TPU v7x, 256 devices: a whole 4x4x8 slice. The times are simulated.
256 devices in a mesh: dp: 8 (over y, core), head: 2 (over z_lo), kv: 16 (over z_hi, x).
Axes of the slice: x: 4, y: 4, z: 8 (z_hi: 4, z_lo: 2; z = z_hi * 2 + z_lo), core: 2. Of those that a mesh axis runs over, the one named last changes fastest.
Arguments:
- teacher_query: bfloat16 [8, 4096, 3584], P('dp', 'kv', 'head'), may hold values from -96 to 96
- teacher_key: bfloat16 [8, 4096, 512], P('dp', 'kv', 'head'), may hold values from -8 to 8
- student_query: bfloat16 [8, 4096, 1792], P('dp', 'kv', 'head'), may hold values from -96 to 96
- student_key: bfloat16 [8, 4096, 256], P('dp', 'kv', 'head'), may hold values from -8 to 8
- pair_table: int32 [14, 2], replicated, may hold values from 0 to 27, as said below
Outputs:
- kl: float32 [8, 14, 4096], P('dp', 'head', 'kv')
- head_loss: float32 [14], P('head')
Inputs may be any that keep to these rules, and one draw needn't show every extreme that they name: `pair_table`: each of the 28 teacher heads appears exactly once in the table.
All inputs are finite; a program needn't handle non-finite values.
Results may differ from a plain program's by a relative error of at most 0.0003.
Values may be sent and summed in bfloat16 or wider, within the bound.
No kernel may reach another device: no remote copies, remote signals or barrier semaphores. Data moves between devices by JAX's collectives and lax.ppermute only.
A program may use at most 64 MiB of HBM per device.

v0:
```python
import math

import jax
import jax.numpy as jnp
from jax import lax
from jax.sharding import Mesh
from jax.sharding import PartitionSpec as P

HT = 28
KVT = 4
DH = 128
HS = 14
KVS = 2
KV = ("kv_0", "kv_1")
DP = ("dp_0", "dp_1")
DP_KV = ("dp_0", "dp_1", "kv_0", "kv_1")


masked_value = -1e30


def from_everyone(shard, axis):
    count = lax.axis_size(axis)
    return lax.all_to_all(
        jnp.broadcast_to(shard[None], (count, *shard.shape)), axis, 0, 0, tiled=True
    )


def joined_along(blocks, dim):
    dims = list(blocks.shape[1:])
    dims[dim] *= blocks.shape[0]
    return jnp.moveaxis(blocks, 0, dim).reshape(dims)


def gathered_copies(shard, axis, dim):
    blocks = from_everyone(shard, axis)
    return joined_along(blocks, dim)


def one_axis_at_a_time(shard, axes):
    for axis in axes:
        shard = lax.psum(shard, axis)
    return shard


def running_softmax(running_max, running_total, logits, causal_mask):
    filled = jnp.where(causal_mask, logits, masked_value)
    new_max = jnp.maximum(running_max, jnp.max(filled, axis=-1))
    rescale = jnp.exp(running_max - new_max)
    weights = jnp.where(causal_mask, jnp.exp(filled - new_max[..., None]), 0.0)
    return (new_max, running_total * rescale + jnp.sum(weights, axis=-1), rescale, weights)


def make_fold(teacher_heads, teacher_select, student_heads, student_select, repeat, query_pos):
    seq_dev, row_count, pair_count, head_dim = teacher_heads.shape
    student_count = student_heads.shape[2]
    scale = 1.0 / math.sqrt(head_dim)
    last_query = query_pos[row_count - 1]

    def fold_step(carry, pieces, start):
        teacher_keys, student_keys = pieces
        key_count = teacher_keys.shape[1]
        block_size = math.gcd(key_count, 512)
        block_total = key_count // block_size
        visible = jnp.clip(last_query // block_size + 1, 0, block_total)

        def one_block(block_index, state):
            t_max, t_total, t_cross, s_max, s_total = state
            offset = block_index * block_size
            t_block = lax.dynamic_slice_in_dim(teacher_keys, offset, block_size, 1).reshape(
                seq_dev, block_size, -1, head_dim
            )
            s_block = lax.dynamic_slice_in_dim(student_keys, offset, block_size, 1).reshape(
                seq_dev, block_size, -1, head_dim
            )
            t_keys = jnp.take(t_block, teacher_select, axis=2)
            s_keys = jnp.take(s_block, student_select, axis=2)
            t_logits = (
                jnp.einsum(
                    "bqpd,bkpd->bpqk", teacher_heads, t_keys, preferred_element_type=jnp.float32
                )
                * scale
            )
            s_logits = (
                jnp.einsum(
                    "bqsd,bksd->bsqk", student_heads, s_keys, preferred_element_type=jnp.float32
                )
                * scale
            )
            key_pos = offset + jnp.arange(block_size, dtype=jnp.int32)
            causal_mask = key_pos[None, :] <= query_pos[:, None]
            t_max, t_total, t_rescale, t_weights = running_softmax(
                t_max, t_total, t_logits, causal_mask
            )
            s_max, s_total, s_rescale, s_weights = running_softmax(
                s_max, s_total, s_logits, causal_mask
            )
            split_logits = t_logits.reshape(seq_dev, student_count, repeat, row_count, block_size)
            gap = (split_logits - s_logits[:, :, None]).reshape(
                seq_dev, pair_count, row_count, block_size
            )
            t_cross = t_cross * t_rescale + jnp.sum(t_weights * gap, axis=-1)
            return (t_max, t_total, t_cross, s_max, s_total)

        return lax.fori_loop(0, visible, one_block, carry)

    pair_shape = (seq_dev, pair_count, row_count)
    student_shape = (seq_dev, student_count, row_count)
    initial = (
        jnp.full(pair_shape, masked_value, jnp.float32),
        jnp.zeros(pair_shape, jnp.float32),
        jnp.zeros(pair_shape, jnp.float32),
        jnp.full(student_shape, masked_value, jnp.float32),
        jnp.zeros(student_shape, jnp.float32),
    )
    return (fold_step, initial)


def finish_pairs(state, repeat):
    t_max, t_total, t_cross, s_max, s_total = state
    seq_dev, pair_count, row_count = t_max.shape
    student_count = s_max.shape[1]
    t_lse = t_max + jnp.log(t_total)
    s_lse = s_max + jnp.log(s_total)
    s_paired = jnp.broadcast_to(
        s_lse[:, :, None], (seq_dev, student_count, repeat, row_count)
    ).reshape(seq_dev, pair_count, row_count)
    return t_cross / t_total - t_lse + s_paired


def per_device(teacher_query, teacher_key, student_query, student_key, pair_table):
    seq_dev, row_count, teacher_width = teacher_query.shape
    n_head = lax.axis_size("head")
    n_kv = lax.axis_size(KV)
    n_data = lax.axis_size(DP)
    head_index = lax.axis_index("head")
    kv_index = lax.axis_index(KV)
    group_teacher = HT // KVT
    group_student = HS // KVS
    local_student = HS // n_head
    local_student_kv = KVS // n_head
    query_pos = kv_index * row_count + jnp.arange(row_count, dtype=jnp.int32)
    all_tq, all_tk = (
        gathered_copies(teacher_query, "head", 2),
        gathered_copies(teacher_key, "head", 2),
    )
    my_pairs = lax.dynamic_slice_in_dim(
        pair_table, head_index * local_student, local_student, 0
    ).reshape(-1)
    teacher_heads = jnp.take(all_tq.reshape(seq_dev, row_count, HT, DH), my_pairs, axis=2)
    teacher_select = my_pairs // group_teacher
    student_heads = student_query.reshape(seq_dev, row_count, local_student, DH)
    student_ids = head_index * local_student + jnp.arange(local_student, dtype=jnp.int32)
    student_select = student_ids // group_student - head_index * local_student_kv
    fold_step, initial = make_fold(
        teacher_heads, teacher_select, student_heads, student_select, 2, query_pos
    )
    state = fold_step(
        initial,
        (
            lax.all_gather(all_tk, KV, axis=1, tiled=True),
            lax.all_gather(student_key, KV, axis=1, tiled=True),
        ),
        jnp.int32(0),
    )
    pair_kl = finish_pairs(state, 2)
    kl_local = jnp.sum(pair_kl.reshape(seq_dev, local_student, 2, row_count), axis=2)
    head_sums = jnp.sum(kl_local, axis=(0, 2))
    total = one_axis_at_a_time(head_sums, DP_KV)
    head_loss = total / (seq_dev * n_data * row_count * n_kv)
    return (kl_local, head_loss)


def solution(mesh):
    split = Mesh(
        mesh.devices.reshape(4, 2, mesh.shape["head"], 4, 4),
        ("dp_0", "dp_1", "head", "kv_0", "kv_1"),
    )
    in_specs = (P(DP, KV, "head"), P(DP, KV, "head"), P(DP, KV, "head"), P(DP, KV, "head"), P())
    out_specs = (P(DP, "head", KV), P("head"))
    return jax.shard_map(
        per_device, mesh=split, in_specs=in_specs, out_specs=out_specs, check_vma=False
    )
```

profile of v0, /device:TPU:1, one launch (start us, length us, event | category | flops | bytes accessed | tf_op | source)
XLA Modules:
  0.0 261.9 jit_solution(12517146968400585087)
XLA Ops:
  7.2 0.7 all-gather.5.cloned.1.call-update
  8.0 1.0 copy.25
  9.0 8.1 %all_to_all.10 = bf16[2,1,256,256]{2,3,1,0:T(8,128)(2,1)} all-to-all(bf16[2,1,256,256]{2,3,1,0:T(8,128)(2,1)S(1)} %broadcast_in_dim.98), channel_id=1, replica_groups=mesh['dp_0'=4,'dp_1'=2,'head'=2,'kv_0'=4,'kv_1'=4] {'head'}, dimensions={0} | all-to-all | bytes 524288 | tf_op jit(solution)/shard_map/all_to_all | solution.py:24
  17.1 1.5 copy.26
  18.6 1.4 broadcast_in_dim.101
  20.0 3.7 %all-to-all-start.1 = ((bf16[2,1,256,1792]{2,3,1,0:T(8,128)(2,1)}), bf16[2,1,256,1792]{2,3,1,0:T(8,128)(2,1)S(1)}, u32[]{:S(2)}, u32[]{:S(2)}) async-start(bf16[2,1,256,1792]{2,3,1,0:T(8,128)(2,1)} %broadcast_in_dim.101), calls=%async_computation.1 | async-start | bytes 3670016 | tf_op jit(solution)/shard_map/all_to_all | solution.py:24
  27.5 1.0 copy.31
  28.5 16.5 %all-to-all-done.1 = bf16[2,1,256,1792]{2,3,1,0:T(8,128)(2,1)S(1)} async-done(((bf16[2,1,256,1792]{2,3,1,0:T(8,128)(2,1)}), bf16[2,1,256,1792]{2,3,1,0:T(8,128)(2,1)S(1)}, u32[]{:S(2)}, u32[]{:S(2)}) %all-to-all-start.1) | async-done | bytes 1835040 | tf_op jit(solution)/shard_map/all_to_all | solution.py:24
  45.0 2.6 copy.29
  47.6 2.2 gather_fusion.1
  50.0 16.4 %all-gather.5.cloned.1.call-done = bf16[1,4096,128]{2,1,0:T(8,128)(2,1)} async-done(((bf16[1,256,128]{2,1,0:T(8,128)(2,1)}), bf16[1,4096,128]{2,1,0:T(8,128)(2,1)}) %all-gather.5.cloned.1.call-update) | async-done | bytes 1048592 | tf_op jit(solution)/shard_map/all_gather | solution.py:162
  66.4 82.6 %all-gather.3.cloned.1.call-done = bf16[1,4096,512]{1,2,0:T(8,128)(2,1)} async-done(((bf16[1,256,512]{1,2,0:T(8,128)(2,1)}), bf16[1,4096,512]{1,2,0:T(8,128)(2,1)}) %all-gather.3.cloned.1.call-update) | async-done | bytes 4194320 | tf_op jit(solution)/shard_map/all_gather | solution.py:161
  149.0 9.1 %while.19 = (s32[]{:T(128)}, f32[1,14,256]{2,1,0:T(8,128)S(1)}, f32[1,14,256]{2,1,0:T(8,128)S(1)}, f32[1,14,256]{2,1,0:T(8,128)S(1)}, f32[1,7,256]{2,1,0:T(8,128...) while((s32[]{:T(128)}, f32[1,14,256]{2,1,0:T(8,128)S(1)}, ...), condition=%wide.region_6.7_spmd.clone, body=%wide.region_0.6_spmd.clone.sunk | while | flops 732774400 | bytes 37899856 | solution.py:105
  149.0 1.1 constant_dynamic-slice_fusion.3
  150.4 0.9 gather_fusion
  151.5 1.4 fusion.28
  152.9 0.9 dynamic-slice_bitcast_fusion.2
  153.9 0.8 select_reduce_fusion.4
  154.7 2.6 fusion.29
  157.3 0.8 select_reduce_fusion.5
  158.5 6.0 %psum.28 = f32[7]{0:T(128)S(1)} all-reduce(f32[7]{0:T(128)S(1)} %reduce_sum.64), channel_id=1, replica_groups=mesh['dp_0'=4,'dp_1'=2,'head'=2,'kv_0'=4,'kv_1'=4] {'dp_0'}, use_global_device_ids=true, to_apply=%region_10.11 | all-reduce | flops 7 | bytes 56 | tf_op jit(solution)/shard_map/psum | solution.py:42
  164.5 7.7 %psum.29 = f32[7]{0:T(128)S(1)} all-reduce(f32[7]{0:T(128)S(1)} %psum.28), channel_id=1, replica_groups=mesh['dp_0'=4,'dp_1'=2,'head'=2,'kv_0'=4,'kv_1'=4] {'dp_1'}, use_global_device_ids=true, to_apply=%region_11.12 | all-reduce | flops 7 | bytes 56 | tf_op jit(solution)/shard_map/psum | solution.py:42
  172.2 63.0 %psum.30 = f32[7]{0:T(128)S(1)} all-reduce(f32[7]{0:T(128)S(1)} %psum.29), channel_id=1, replica_groups=mesh['dp_0'=4,'dp_1'=2,'head'=2,'kv_0'=4,'kv_1'=4] {'kv_0'}, use_global_device_ids=true, to_apply=%region_12.13 | all-reduce | flops 7 | bytes 56 | tf_op jit(solution)/shard_map/psum | solution.py:42
  235.8 18.8 %psum.31 = f32[7]{0:T(128)S(1)} all-reduce(f32[7]{0:T(128)S(1)} %psum.30), channel_id=1, replica_groups=mesh['dp_0'=4,'dp_1'=2,'head'=2,'kv_0'=4,'kv_1'=4] {'kv_1'}, use_global_device_ids=true, to_apply=%region_13.14 | all-reduce | flops 7 | bytes 56 | tf_op jit(solution)/shard_map/psum | solution.py:42
  (51 shorter events, 3.5 us)
Async XLA Ops:
  7.2 19.1 %copy-start = (s32[14,2]{0,1:T(2,128)S(1)}, s32[14,2]{0,1:T(2,128)}, u32[]{:S(2)}) copy-start(s32[14,2]{0,1:T(2,128)} %param.11) | copy-start | bytes 340
  7.2 59.2 %all-gather.5.cloned.1.call-start = ((), (), s32[]{:S(2)}) async-start(), calls=%async_computation.3 | async-start | bytes 1114112 | tf_op jit(solution)/shard_map/all_gather | solution.py:162
  7.9 141.1 %all-gather.3.cloned.1.call-start = ((), (), s32[]{:S(2)}) async-start(), calls=%async_computation.2 | async-start | bytes 4456448 | tf_op jit(solution)/shard_map/all_gather | solution.py:161
  18.6 8.7 %copy-start.1 = (bf16[1,256,896]{2,1,0:T(8,128)(2,1)S(1)}, bf16[1,256,896]{2,1,0:T(8,128)(2,1)}, u32[]{:S(2)}) copy-start(bf16[1,256,896]{2,1,0:T(8,128)(2,1)} %param.9) | copy-start | bytes 1376260
  20.0 25.0 %all-to-all-start.1 = ((bf16[2,1,256,1792]{2,3,1,0:T(8,128)(2,1)}), bf16[2,1,256,1792]{2,3,1,0:T(8,128)(2,1)S(1)}, u32[]{:S(2)}, u32[]{:S(2)}) async-start(bf16[2,1,256,1792]{2,3,1,0:T(8,128)(2,1)} %broadcast_in_dim.101), calls=%async_computation.1 | async-start | bytes 3670016 | tf_op jit(solution)/shard_map/all_to_all | solution.py:24
  151.5 2.4 copy-start.2
Sparse Core Ops, SparseCore 0:
  10.4 55.9 all-gather.4
  68.8 80.1 all-gather.2
where the time goes:
time: 264 us; the launch traced here: 262 us
  waiting for transfers between devices  116 us (44%)
  blocking collectives  104 us (39%)
  between operations  16.8 us (6%)
  local copies, waits for them, and re-layouts  14.7 us (6%)
  other arithmetic  4.56 us (2%)
  starting transfers between devices  3.79 us (1%)
    psum x4, blocking collectives, one_axis_at_a_time(): shard = lax.psum(shard, axis)  95.4 us
    all_gather x1, waiting for transfers between devices, per_device(): lax.all_gather(all_tk, KV, axis=1, tiled=True)  82.6 us
    all_to_all x1, waiting for transfers between devices, from_everyone(): lax.all_to_all(jnp.broadcast_to(shard[None], (count, *shard.shape)), axis...  16.5 us
    all_gather x1, waiting for transfers between devices, per_device(): lax.all_gather(student_key, KV, axis=1, tiled=True)  16.4 us
    all_to_all x1, blocking collectives, from_everyone(): lax.all_to_all(jnp.broadcast_to(shard[None], (count, *shard.shape)), axis...  8.11 us
  transfers between devices with their start and end apart: 3, of which 3 were waited for; matrix products, arithmetic and copies ran while one was open for 4% of the time, Pallas kernels for 0%

commit v1 on v0

v1 whole, which is shorter than its diff:
```python
import functools
import math

import jax
import jax.numpy as jnp
from jax import lax
from jax.experimental import pallas as pl
from jax.experimental.pallas import tpu as pltpu
from jax.sharding import Mesh
from jax.sharding import PartitionSpec as P

HT = 28
KVT = 4
DH = 128
HS = 14
KVS = 2
ROWS = 256
PAIRS = 14
STUDENTS = 7
HEADS = PAIRS + STUDENTS
KV = ("kv_0", "kv_1")
DP = ("dp_0", "dp_1")
LANE = 128
SUB = 8
MASKED = -1e30
LN2 = math.log(2.0)
KAPPA = 1.0 / (LN2 * math.sqrt(DH))


def prepare_kernel(sel, own, other, student, out):
    def put(slot, q):
        q = q.astype(jnp.float32) * KAPPA
        high = q.astype(jnp.bfloat16)
        low = (q - high.astype(jnp.float32)).astype(jnp.bfloat16)
        out[slot, :DH, :] = jnp.transpose(high.astype(jnp.float32)).astype(jnp.bfloat16)
        out[slot, DH:, :] = jnp.transpose(low.astype(jnp.float32)).astype(jnp.bfloat16)

    for s in range(STUDENTS):
        put(PAIRS + s, student[:, s * DH : (s + 1) * DH])
    for p in range(PAIRS):
        lanes = pl.ds(pl.multiple_of(sel[1, p] * DH, DH), DH)

        @pl.when(sel[0, p] == 0)
        def _():
            put(p, own[:, lanes])

        @pl.when(sel[0, p] != 0)
        def _():
            put(p, other[:, lanes])


def prepare(sel, own, other, student):
    vmem = pl.BlockSpec(memory_space=pltpu.VMEM)
    return pl.pallas_call(
        prepare_kernel,
        out_shape=jax.ShapeDtypeStruct((HEADS, 2 * DH, ROWS), jnp.bfloat16),
        in_specs=[pl.BlockSpec(memory_space=pltpu.SMEM), vmem, vmem, vmem],
        out_specs=vmem,
        name="prepare",
    )(sel, own, other, student)


def attend_kernel(n_groups, sizes, info, qt, *refs):
    groups = refs[:n_groups]
    out = refs[n_groups]
    keys, tm, tl, tc, sm, sl, sems = refs[n_groups + 1 :]
    copies = []
    at = 0
    for g in range(n_groups):
        copies.append(
            pltpu.make_async_copy(groups[g], keys.at[pl.ds(at, sizes[g])], sems.at[g])
        )
        at += sizes[g]
    for c in copies:
        c.start()
    for ref in (tm, sm):
        ref[...] = jnp.full_like(ref, MASKED)
    for ref in (tl, tc, sl):
        ref[...] = jnp.zeros_like(ref)
    for c in copies:
        c.wait()
    row_block = info[0, 0]

    def update(logits, mask, m_ref, l_ref, index):
        if mask is not None:
            logits = jnp.where(mask, logits, MASKED)
        folded = logits.reshape(ROWS // SUB, SUB, ROWS)
        old = m_ref[index]
        new = jnp.maximum(old, jnp.max(folded, axis=0))
        weights = jnp.exp2(folded - new[None])
        rescale = jnp.exp2(old - new)
        m_ref[index] = new
        l_ref[index] = l_ref[index] * rescale + jnp.sum(weights, axis=0)
        return weights, rescale

    def block(own_slot, other_slot, masked):
        mask = None
        if masked:
            key_pos = lax.broadcasted_iota(jnp.int32, (ROWS, ROWS), 0)
            row_pos = lax.broadcasted_iota(jnp.int32, (ROWS, ROWS), 1)
            mask = key_pos <= row_pos
        student_keys = keys[own_slot, :, 2 * DH :]
        student_keys = jnp.concatenate([student_keys, student_keys], axis=1)
        for s in range(STUDENTS):
            zs = jnp.dot(student_keys, qt[PAIRS + s], preferred_element_type=jnp.float32)
            update(zs, mask, sm, sl, s)
            for c in range(2):
                p = 2 * s + c
                slot = jnp.where(info[1, p] == 0, own_slot, other_slot)
                lanes = pl.ds(pl.multiple_of(info[2, p] * DH, DH), DH)
                teacher_keys = keys[slot, :, lanes]
                teacher_keys = jnp.concatenate([teacher_keys, teacher_keys], axis=1)
                zt = jnp.dot(teacher_keys, qt[p], preferred_element_type=jnp.float32)
                weights, rescale = update(zt, mask, tm, tl, p)
                gap = (zt - zs).reshape(ROWS // SUB, SUB, ROWS)
                tc[p] = tc[p] * rescale + jnp.sum(weights * gap, axis=0)

    def step(i, carry):
        position = info[3, i]
        own_slot = info[4, i]
        other_slot = info[5, i]

        @pl.when(position < row_block)
        def _():
            block(own_slot, other_slot, False)

        @pl.when(position == row_block)
        def _():
            block(own_slot, other_slot, True)

        return carry

    lax.fori_loop(0, 16, step, 0)

    def merged(m8, l8):
        top = jnp.max(m8, axis=0, keepdims=True)
        factor = jnp.exp2(m8 - top)
        total = jnp.sum(l8 * factor, axis=0, keepdims=True)
        return factor, total, LN2 * top + jnp.log(total)

    for s in range(STUDENTS):
        _, _, s_lse = merged(sm[s], sl[s])
        value = 2.0 * s_lse
        for c in range(2):
            p = 2 * s + c
            factor, total, t_lse = merged(tm[p], tl[p])
            cross = jnp.sum(tc[p] * factor, axis=0, keepdims=True)
            value = value + (LN2 * cross / total - t_lse)
        out[s : s + 1, :] = value


def attend(info, qt, groups):
    sizes = tuple(g.shape[0] for g in groups)
    state = lambda n: pltpu.VMEM((n, SUB, ROWS), jnp.float32)
    return pl.pallas_call(
        functools.partial(attend_kernel, len(groups), sizes),
        out_shape=jax.ShapeDtypeStruct((STUDENTS, ROWS), jnp.float32),
        in_specs=[pl.BlockSpec(memory_space=pltpu.SMEM), pl.BlockSpec(memory_space=pltpu.VMEM)]
        + [pl.BlockSpec(memory_space=pl.ANY)] * len(groups),
        out_specs=pl.BlockSpec(memory_space=pltpu.VMEM),
        scratch_shapes=[
            pltpu.VMEM((sum(sizes), ROWS, 3 * DH), jnp.bfloat16),
            state(PAIRS),
            state(PAIRS),
            state(PAIRS),
            state(STUDENTS),
            state(STUDENTS),
            pltpu.SemaphoreType.DMA((len(groups),)),
        ],
        compiler_params=pltpu.CompilerParams(vmem_limit_bytes=40 * 1024 * 1024),
        name="attend",
    )(info, qt, *groups)


def shift(n, by):
    return [(i, (i + by) % n) for i in range(n)]


def z_place(ring):
    ring %= 8
    return (ring % 2) * 4 + ring // 2


def z_shift(by):
    return [(z_place(i), z_place(i + by)) for i in range(8)]


def per_device(teacher_query, teacher_key, student_query, student_key, pair_table):
    head = lax.axis_index("head")
    z_hi = lax.axis_index("kv_0")
    x = lax.axis_index("kv_1")
    other_query = lax.ppermute(teacher_query, "head", [(0, 1), (1, 0)])
    own_keys = jnp.concatenate([teacher_key, student_key], axis=2)

    ring = {0: own_keys}
    up = down = own_keys
    for step in range(1, 5):
        up = lax.ppermute(up, ("head", "kv_0"), z_shift(1))
        ring[step] = up
        if step < 4:
            down = lax.ppermute(down, ("head", "kv_0"), z_shift(-1))
            ring[8 - step] = down
    column = jnp.concatenate([ring[o] for o in range(8)], axis=0)
    left = lax.ppermute(column, "kv_1", shift(4, 1))
    right = lax.ppermute(column, "kv_1", shift(4, -1))
    far_a = lax.ppermute(left[:4], "kv_1", shift(4, 1))
    far_b = lax.ppermute(right[4:], "kv_1", shift(4, -1))
    groups = [column, left, right, far_a, far_b]

    my_pairs = lax.dynamic_slice_in_dim(pair_table, head * STUDENTS, STUDENTS, 0).reshape(-1)
    sel = jnp.stack([(my_pairs // PAIRS != head).astype(jnp.int32), my_pairs % PAIRS])
    kv_head = my_pairs // (HT // KVT)
    pad = jnp.zeros((2,), jnp.int32)
    xs = jnp.repeat(jnp.arange(4, dtype=jnp.int32), 4)
    m = jnp.tile(jnp.arange(4, dtype=jnp.int32), 4)
    x_of = jnp.mod(x + jnp.array([0, -1, 1, 2], jnp.int32)[xs], 4)
    position = jnp.mod(z_hi - m, 4) * 4 + x_of
    own_slot = xs * 8 + 2 * m
    other_slot = xs * 8 + jnp.mod(2 * m - 1 + 2 * head, 8)
    info = jnp.stack(
        [
            jnp.full((16,), z_hi * 4 + x, jnp.int32),
            jnp.concatenate([(kv_head // 2 != head).astype(jnp.int32), pad]),
            jnp.concatenate([kv_head % 2, pad]),
            position,
            own_slot,
            other_slot,
        ]
    )
    qt = prepare(sel, teacher_query[0], other_query[0], student_query[0])
    kl = attend(info, qt, groups)

    sums = jnp.pad(jnp.sum(kl, axis=1), (0, LANE - STUDENTS))
    everyone = ("dp_0", "dp_1", "kv_0", "kv_1")
    count = lax.axis_size(everyone)
    terms = lax.all_to_all(
        jnp.broadcast_to(sums, (count, LANE)), everyone, 0, 0, tiled=True
    )
    head_loss = jnp.sum(terms, axis=0)[:STUDENTS] / (count * ROWS)
    return (kl[None], head_loss)


def solution(mesh):
    split = Mesh(
        mesh.devices.reshape(4, 2, mesh.shape["head"], 4, 4),
        ("dp_0", "dp_1", "head", "kv_0", "kv_1"),
    )
    in_specs = (P(DP, KV, "head"), P(DP, KV, "head"), P(DP, KV, "head"), P(DP, KV, "head"), P())
    out_specs = (P(DP, "head", KV), P("head"))
    return jax.shard_map(
        per_device, mesh=split, in_specs=in_specs, out_specs=out_specs, check_vma=False
    )
```

time: 264 us -> 165 us (0.62)
  blocking collectives: 104 us -> 0 us
  starting transfers between devices: 3.79 us -> 59.1 us
  waiting for transfers between devices: 116 us -> 78.3 us
  between operations: 16.8 us -> 0.76 us
  Pallas kernels: 0 us -> 9.95 us
  other arithmetic: 4.56 us -> 1.51 us
    all_gather x2 -> x0, waiting for transfers between devices: 99 us -> none  [the longest x1 82.6 us: per_device(): lax.all_gather(all_tk, KV, axis=1, tiled=True)]
    psum x4 -> x0, blocking collectives: 95.4 us -> none  [one_axis_at_a_time(): shard = lax.psum(shard, axis)]
    ppermute x0 -> x12, waiting for transfers between devices: none -> 67.1 us  [the longest x1 30.5 us: per_device(): left = lax.ppermute(column, 'kv_1', shift(4, 1))]
    all_to_all x1, starting transfers between devices: 3.72 us -> 42 us  [per_device(): lax.all_to_all(jnp.broadcast_to(sums, (count, LANE)), everyone, 0, 0, til...]
    ppermute x0 -> x12, starting transfers between devices: none -> 17.1 us  [the longest x3 9.29 us: per_device(): down = lax.ppermute(down, ('head', 'kv_0'), z_shift(-1))]
    pallas_call x0 -> x2, Pallas kernels: none -> 9.95 us  [the longest x1 5.29 us: prepare(): pl.pallas_call(prepare_kernel, out_shape=jax.ShapeDtypeStruct((HEADS, 2 *...]
    all_to_all x1 -> x0, blocking collectives: 8.11 us -> none  [from_everyone(): lax.all_to_all(jnp.broadcast_to(shard[None], (count, *shard.shape)), axis...]
    unnamed x6 -> x14, local copies, waits for them, and re-layouts: 1.21 us -> 8.13 us
  transfers between devices with their start and end apart: 3 -> 13, of which waited for: 3 -> 7; matrix products, arithmetic and copies ran while one was open for 4% -> 6% of each run, Pallas kernels for 0% -> 3%
where the time goes in v1:
time: 165 us
  waiting for transfers between devices  78.3 us (47%)
  starting transfers between devices  59.1 us (36%)
  local copies, waits for them, and re-layouts  15 us (9%)
  Pallas kernels  9.95 us (6%)
    all_to_all x1, starting transfers between devices, per_device(): lax.all_to_all(jnp.broadcast_to(sums, (count, LANE)), everyone, 0, 0, til...  42 us
    ppermute x1, waiting for transfers between devices, per_device(): left = lax.ppermute(column, 'kv_1', shift(4, 1))  30.5 us
    ppermute x4, waiting for transfers between devices, per_device(): up = lax.ppermute(up, ('head', 'kv_0'), z_shift(1))  29.9 us
    all_to_all x1, waiting for transfers between devices, per_device(): lax.all_to_all(jnp.broadcast_to(sums, (count, LANE)), everyone, 0, 0, til...  11.2 us
    ppermute x3, starting transfers between devices, per_device(): down = lax.ppermute(down, ('head', 'kv_0'), z_shift(-1))  9.29 us
    unnamed x14, local copies, waits for them, and re-layouts  8.13 us
    ppermute x1, waiting for transfers between devices, per_device(): far_a = lax.ppermute(left[:4], 'kv_1', shift(4, 1))  6.71 us
    pallas_call x1, Pallas kernels, prepare(): pl.pallas_call(prepare_kernel, out_shape=jax.ShapeDtypeStruct((HEADS, 2 *...  5.29 us
  transfers between devices with their start and end apart: 13, of which 7 were waited for; matrix products, arithmetic and copies ran while one was open for 6% of the time, Pallas kernels for 3%

profile of v1, /device:TPU:1, one launch (start us, length us, event | category | flops | bytes accessed | tf_op | source)
XLA Modules:
  0.0 164.6 jit_solution(10041220760040965172)
XLA Ops:
  0.6 1.6 constant_dynamic-update-slice_fusion.1
  2.2 1.5 constant_dynamic-update-slice_fusion
  3.8 2.5 %collective-permute-start.1 = (bf16[1,256,384]{2,1,0:T(8,128)(2,1)S(1)}, bf16[1,256,384]{2,1,0:T(8,128)(2,1)S(1)}, u32[]{:S(2)}, u32[]{:S(2)}) collective-permute-start(bf16[1,256,384]{2,1,0:T(8,128)(2,1)S(1)} %get-tuple-element.14), channel_id=1, source_target_pairs={{0,16},{16,4},{4,20},{20,8},{8,24},{24,12},{12,28},{28,0},{1,17},{... | collective-permute-start | bytes 589832 | tf_op jit(solution)/shard_map/ppermute | solution.py:198
  6.2 3.9 %collective-permute-start.5 = (bf16[1,256,384]{2,1,0:T(8,128)(2,1)S(1)}, bf16[1,256,384]{2,1,0:T(8,128)(2,1)S(1)}, u32[]{:S(2)}, u32[]{:S(2)}) collective-permute-start(bf16[1,256,384]{2,1,0:T(8,128)(2,1)S(1)} %get-tuple-element.14), channel_id=1, source_target_pairs={{0,28},{16,0},{4,16},{20,4},{8,20},{24,8},{12,24},{28,12},{1,29},{... | collective-permute-start | bytes 589832 | tf_op jit(solution)/shard_map/ppermute | solution.py:201
  10.2 4.6 %collective-permute-done.1 = bf16[1,256,384]{2,1,0:T(8,128)(2,1)S(1)} collective-permute-done((bf16[1,256,384]{2,1,0:T(8,128)(2,1)S(1)}, bf16[1,256,384]{2,1,0:T(8,128)(2,1)S(1)}, u32[]{:S(2)}, u32[]{:S(2)}) %collective-permute-start.1) | collective-permute-done | bytes 196640 | tf_op jit(solution)/shard_map/ppermute | solution.py:198
  14.8 2.7 %collective-permute-start.6 = (bf16[1,256,384]{2,1,0:T(8,128)(2,1)S(1)}, bf16[1,256,384]{2,1,0:T(8,128)(2,1)S(1)}, u32[]{:S(2)}, u32[]{:S(2)}) collective-permute-start(bf16[1,256,384]{2,1,0:T(8,128)(2,1)S(1)} %collective-permute-done.5), channel_id=1, source_target_pairs={{0,28},{16,0},{4,16},{20,4},{8,20},{24,8},{12,24},{28,12},{1,29},{... | collective-permute-start | bytes 589832 | tf_op jit(solution)/shard_map/ppermute | solution.py:201
  17.5 3.7 %collective-permute-done.2 = bf16[1,256,384]{2,1,0:T(8,128)(2,1)S(1)} collective-permute-done((bf16[1,256,384]{2,1,0:T(8,128)(2,1)S(1)}, bf16[1,256,384]{2,1,0:T(8,128)(2,1)S(1)}, u32[]{:S(2)}, u32[]{:S(2)}) %collective-permute-start.2) | collective-permute-done | bytes 196640 | tf_op jit(solution)/shard_map/ppermute | solution.py:198
  21.9 2.7 %collective-permute-start.7 = (bf16[1,256,384]{2,1,0:T(8,128)(2,1)S(1)}, bf16[1,256,384]{2,1,0:T(8,128)(2,1)S(1)}, u32[]{:S(2)}, u32[]{:S(2)}) collective-permute-start(bf16[1,256,384]{2,1,0:T(8,128)(2,1)S(1)} %collective-permute-done.6), channel_id=1, source_target_pairs={{0,28},{16,0},{4,16},{20,4},{8,20},{24,8},{12,24},{28,12},{1,29},{... | collective-permute-start | bytes 589832 | tf_op jit(solution)/shard_map/ppermute | solution.py:201
  24.6 2.4 %collective-permute-done.3 = bf16[1,256,384]{2,1,0:T(8,128)(2,1)S(1)} collective-permute-done((bf16[1,256,384]{2,1,0:T(8,128)(2,1)S(1)}, bf16[1,256,384]{2,1,0:T(8,128)(2,1)S(1)}, u32[]{:S(2)}, u32[]{:S(2)}) %collective-permute-start.3) | collective-permute-done | bytes 196640 | tf_op jit(solution)/shard_map/ppermute | solution.py:198
  26.9 0.7 constant_dynamic-update-slice_fusion.7
  28.3 19.2 %collective-permute-done.4 = bf16[1,256,384]{2,1,0:T(8,128)(2,1)S(1)} collective-permute-done((bf16[1,256,384]{2,1,0:T(8,128)(2,1)S(1)}, bf16[1,256,384]{2,1,0:T(8,128)(2,1)S(1)}, u32[]{:S(2)}, u32[]{:S(2)}) %collective-permute-start.4) | collective-permute-done | bytes 196640 | tf_op jit(solution)/shard_map/ppermute | solution.py:198
  48.2 0.7 constant_dynamic-update-slice_fusion.4
  50.3 1.2 collective-permute-start.8
  51.5 1.5 collective-permute-start.9
  54.5 30.5 %collective-permute-done.8.refs_1_ = bf16[8,256,384]{2,1,0:T(8,128)(2,1)S(1)} collective-permute-done((bf16[8,256,384]{2,1,0:T(8,128)(2,1)}, bf16[8,256,384]{2,1,0:T(8,128)(2,1)S(1)}, u32[]{:S(2)}, u32[]{:S(2)}) %collective-permute-start.8) | collective-permute-done | bytes 1572896 | tf_op jit(solution)/shard_map/ppermute | solution.py:204
  85.0 1.0 slice.14
  85.9 1.0 slice.15
  87.0 2.7 %collective-permute-start.11 = (bf16[4,256,384]{2,1,0:T(8,128)(2,1)}, bf16[4,256,384]{2,1,0:T(8,128)(2,1)}, u32[]{:S(2)}, u32[]{:S(2)}) collective-permute-start(bf16[4,256,384]{2,1,0:T(8,128)(2,1)} %slice.15), channel_id=1, source_target_pairs={{0,3},{1,0},{2,1},{3,2},{4,7},{5,4},{6,5},{7,6},{8,11},{9,8},{10,9... | collective-permute-start | bytes 2359304 | tf_op jit(solution)/shard_map/ppermute | solution.py:207
  91.0 5.3 %prepare.1.qt = bf16[21,256,256]{2,1,0:T(8,128)(2,1)} custom-call(s32[2,14]{1,0:T(2,128)} %pad_add_fusion.sel, bf16[256,1792]{1,0:T(8,128)(2,1)} %bitcast.14, bf16[256,1792]{1,0:T(8,128)(2,1)} %bitcast.5.other, bf16[256,896]{1,0:T(8,128)(2,1)} %bitcast.15), custom_call_target="tpu_custom_call" | custom-call | tf_op jit(solution)/shard_map/prepare/pallas_call | solution.py:54
  96.3 6.7 %collective-permute-done.10.refs_3_ = bf16[4,256,384]{2,1,0:T(8,128)(2,1)} collective-permute-done((bf16[4,256,384]{2,1,0:T(8,128)(2,1)}, bf16[4,256,384]{2,1,0:T(8,128)(2,1)}, u32[]{:S(2)}, u32[]{:S(2)}) %collective-permute-start.10) | collective-permute-done | bytes 786464 | tf_op jit(solution)/shard_map/ppermute | solution.py:206
  103.0 1.8 %copy-done = bf16[21,256,256]{2,1,0:T(8,128)(2,1)S(1)} copy-done((bf16[21,256,256]{2,1,0:T(8,128)(2,1)S(1)}, bf16[21,256,256]{2,1,0:T(8,128)(2,1)}, u32[]{:S(2)}) %copy-start) | copy-done | bytes 2752536
  104.8 4.7 %attend.1 = f32[7,256]{1,0:T(8,128)S(1)} custom-call(s32[6,16]{1,0:T(8,128)S(1)} %stack.23.info, bf16[21,256,256]{2,1,0:T(8,128)(2,1)S(1)} %copy-done, bf16[8,256,384]{2,1,0:T(8,128)(2,1)} %constant_dynamic-update-slice_fusion.2.refs_0_, bf16[8,256,384]{2,1,0:T(8,128)(2,1)S(1)} %collective-permute-done.8.refs_1_, ...), custom_call_target="tpu_custom_call" | custom-call | tf_op jit(solution)/shard_map/attend/pallas_call | solution.py:155
  110.3 42.0 %all-to-all-start = ((f32[128,1,128]{2,1,0:T(1,128)}), f32[128,1,128]{2,1,0:T(1,128)S(1)}, u32[]{:S(2)}, u32[]{:S(2)}) async-start(f32[128,1,128]{2,1,0:T(1,128)} %broadcast_in_dim.17), calls=%async_computation | async-start | bytes 131072 | tf_op jit(solution)/shard_map/all_to_all | solution.py:236
  152.8 11.2 %all-to-all-done = f32[128,1,128]{2,1,0:T(1,128)S(1)} async-done(((f32[128,1,128]{2,1,0:T(1,128)}), f32[128,1,128]{2,1,0:T(1,128)S(1)}, u32[]{:S(2)}, u32[]{:S(2)}) %all-to-all-start) | async-done | bytes 65568 | tf_op jit(solution)/shard_map/all_to_all | solution.py:236
  (61 shorter events, 8.2 us)
Async XLA Ops:
  2.2 50.7 %copy-start.2 = (s32[14,2]{0,1:T(2,128)S(1)}, s32[14,2]{0,1:T(2,128)}, u32[]{:S(2)}) copy-start(s32[14,2]{0,1:T(2,128)} %param.10) | copy-start | bytes 340
  2.2 51.5 %copy-start.1 = (s32[4]{0:T(128)S(1)}, s32[4]{0:T(128)}, u32[]{:S(2)}) copy-start(s32[4]{0:T(128)} %constant.104.clone) | copy-start | bytes 52
  3.8 11.0 %collective-permute-start.1 = (bf16[1,256,384]{2,1,0:T(8,128)(2,1)S(1)}, bf16[1,256,384]{2,1,0:T(8,128)(2,1)S(1)}, u32[]{:S(2)}, u32[]{:S(2)}) collective-permute-start(bf16[1,256,384]{2,1,0:T(8,128)(2,1)S(1)} %get-tuple-element.14), channel_id=1, source_target_pairs={{0,16},{16,4},{4,20},{20,8},{8,24},{24,12},{12,28},{28,0},{1,17},{... | collective-permute-start | bytes 589832 | tf_op jit(solution)/shard_map/ppermute | solution.py:198
  6.2 8.5 %collective-permute-start.5 = (bf16[1,256,384]{2,1,0:T(8,128)(2,1)S(1)}, bf16[1,256,384]{2,1,0:T(8,128)(2,1)S(1)}, u32[]{:S(2)}, u32[]{:S(2)}) collective-permute-start(bf16[1,256,384]{2,1,0:T(8,128)(2,1)S(1)} %get-tuple-element.14), channel_id=1, source_target_pairs={{0,28},{16,0},{4,16},{20,4},{8,20},{24,8},{12,24},{28,12},{1,29},{... | collective-permute-start | bytes 589832 | tf_op jit(solution)/shard_map/ppermute | solution.py:201
  14.8 6.4 %collective-permute-start.2 = (bf16[1,256,384]{2,1,0:T(8,128)(2,1)S(1)}, bf16[1,256,384]{2,1,0:T(8,128)(2,1)S(1)}, u32[]{:S(2)}, u32[]{:S(2)}) collective-permute-start(bf16[1,256,384]{2,1,0:T(8,128)(2,1)S(1)} %collective-permute-done.1), channel_id=1, source_target_pairs={{0,16},{16,4},{4,20},{20,8},{8,24},{24,12},{12,28},{28,0},{1,17},{... | collective-permute-start | bytes 589832 | tf_op jit(solution)/shard_map/ppermute | solution.py:198
  14.8 7.1 %collective-permute-start.6 = (bf16[1,256,384]{2,1,0:T(8,128)(2,1)S(1)}, bf16[1,256,384]{2,1,0:T(8,128)(2,1)S(1)}, u32[]{:S(2)}, u32[]{:S(2)}) collective-permute-start(bf16[1,256,384]{2,1,0:T(8,128)(2,1)S(1)} %collective-permute-done.5), channel_id=1, source_target_pairs={{0,28},{16,0},{4,16},{20,4},{8,20},{24,8},{12,24},{28,12},{1,29},{... | collective-permute-start | bytes 589832 | tf_op jit(solution)/shard_map/ppermute | solution.py:201
  21.2 5.7 %collective-permute-start.3 = (bf16[1,256,384]{2,1,0:T(8,128)(2,1)S(1)}, bf16[1,256,384]{2,1,0:T(8,128)(2,1)S(1)}, u32[]{:S(2)}, u32[]{:S(2)}) collective-permute-start(bf16[1,256,384]{2,1,0:T(8,128)(2,1)S(1)} %collective-permute-done.2), channel_id=1, source_target_pairs={{0,16},{16,4},{4,20},{20,8},{8,24},{24,12},{12,28},{28,0},{1,17},{... | collective-permute-start | bytes 589832 | tf_op jit(solution)/shard_map/ppermute | solution.py:198
  21.2 69.8 %collective-permute-start = (bf16[1,256,1792]{2,1,0:T(8,128)(2,1)}, bf16[1,256,1792]{2,1,0:T(8,128)(2,1)}, u32[]{:S(2)}, u32[]{:S(2)}) collective-permute-start(bf16[1,256,1792]{2,1,0:T(8,128)(2,1)} %param.6), channel_id=1, source_target_pairs={{0,16},{16,0},{1,17},{17,1},{2,18},{18,2},{3,19},{19,3},{4,20},{20... | collective-permute-start | bytes 2752520 | tf_op jit(solution)/shard_map/ppermute | solution.py:192
  21.9 26.3 %collective-permute-start.7 = (bf16[1,256,384]{2,1,0:T(8,128)(2,1)S(1)}, bf16[1,256,384]{2,1,0:T(8,128)(2,1)S(1)}, u32[]{:S(2)}, u32[]{:S(2)}) collective-permute-start(bf16[1,256,384]{2,1,0:T(8,128)(2,1)S(1)} %collective-permute-done.6), channel_id=1, source_target_pairs={{0,28},{16,0},{4,16},{20,4},{8,20},{24,8},{12,24},{28,12},{1,29},{... | collective-permute-start | bytes 589832 | tf_op jit(solution)/shard_map/ppermute | solution.py:201
  26.9 20.6 %collective-permute-start.4 = (bf16[1,256,384]{2,1,0:T(8,128)(2,1)S(1)}, bf16[1,256,384]{2,1,0:T(8,128)(2,1)S(1)}, u32[]{:S(2)}, u32[]{:S(2)}) collective-permute-start(bf16[1,256,384]{2,1,0:T(8,128)(2,1)S(1)} %collective-permute-done.3), channel_id=1, source_target_pairs={{0,16},{16,4},{4,20},{20,8},{8,24},{24,12},{12,28},{28,0},{1,17},{... | collective-permute-start | bytes 589832 | tf_op jit(solution)/shard_map/ppermute | solution.py:198
  50.3 34.7 %collective-permute-start.8 = (bf16[8,256,384]{2,1,0:T(8,128)(2,1)}, bf16[8,256,384]{2,1,0:T(8,128)(2,1)S(1)}, u32[]{:S(2)}, u32[]{:S(2)}) collective-permute-start(bf16[8,256,384]{2,1,0:T(8,128)(2,1)} %constant_dynamic-update-slice_fusion.2.refs_0_), channel_id=1, source_target_pairs={{0,1},{1,2},{2,3},{3,0},{4,5},{5,6},{6,7},{7,4},{8,9},{9,10},{10,1... | collective-permute-start | bytes 4718600 | tf_op jit(solution)/shard_map/ppermute | solution.py:204
  51.5 34.4 %collective-permute-start.9 = (bf16[8,256,384]{2,1,0:T(8,128)(2,1)}, bf16[8,256,384]{2,1,0:T(8,128)(2,1)S(1)}, u32[]{:S(2)}, u32[]{:S(2)}) collective-permute-start(bf16[8,256,384]{2,1,0:T(8,128)(2,1)} %constant_dynamic-update-slice_fusion.2.refs_0_), channel_id=1, source_target_pairs={{0,3},{1,0},{2,1},{3,2},{4,7},{5,4},{6,5},{7,6},{8,11},{9,8},{10,9... | collective-permute-start | bytes 4718600 | tf_op jit(solution)/shard_map/ppermute | solution.py:205
  85.9 17.1 %collective-permute-start.10 = (bf16[4,256,384]{2,1,0:T(8,128)(2,1)}, bf16[4,256,384]{2,1,0:T(8,128)(2,1)}, u32[]{:S(2)}, u32[]{:S(2)}) collective-permute-start(bf16[4,256,384]{2,1,0:T(8,128)(2,1)} %slice.14), channel_id=1, source_target_pairs={{0,1},{1,2},{2,3},{3,0},{4,5},{5,6},{6,7},{7,4},{8,9},{9,10},{10,1... | collective-permute-start | bytes 2359304 | tf_op jit(solution)/shard_map/ppermute | solution.py:206
  87.0 16.1 %collective-permute-start.11 = (bf16[4,256,384]{2,1,0:T(8,128)(2,1)}, bf16[4,256,384]{2,1,0:T(8,128)(2,1)}, u32[]{:S(2)}, u32[]{:S(2)}) collective-permute-start(bf16[4,256,384]{2,1,0:T(8,128)(2,1)} %slice.15), channel_id=1, source_target_pairs={{0,3},{1,0},{2,1},{3,2},{4,7},{5,4},{6,5},{7,6},{8,11},{9,8},{10,9... | collective-permute-start | bytes 2359304 | tf_op jit(solution)/shard_map/ppermute | solution.py:207
  103.0 1.8 %copy-start = (bf16[21,256,256]{2,1,0:T(8,128)(2,1)S(1)}, bf16[21,256,256]{2,1,0:T(8,128)(2,1)}, u32[]{:S(2)}) copy-start(bf16[21,256,256]{2,1,0:T(8,128)(2,1)} %prepare.1.qt) | copy-start | bytes 8257540
  110.3 53.8 %all-to-all-start = ((f32[128,1,128]{2,1,0:T(1,128)}), f32[128,1,128]{2,1,0:T(1,128)S(1)}, u32[]{:S(2)}, u32[]{:S(2)}) async-start(f32[128,1,128]{2,1,0:T(1,128)} %broadcast_in_dim.17), calls=%async_computation | async-start | bytes 131072 | tf_op jit(solution)/shard_map/all_to_all | solution.py:236

commit v2 on v1

v2 whole, which is shorter than its diff:
```python
import functools
import math

import jax
import jax.numpy as jnp
from jax import lax
from jax.experimental import pallas as pl
from jax.experimental.pallas import tpu as pltpu
from jax.sharding import Mesh
from jax.sharding import PartitionSpec as P

HT = 28
KVT = 4
DH = 128
HS = 14
KVS = 2
ROWS = 256
PAIRS = 14
STUDENTS = 7
HEADS = PAIRS + STUDENTS
KV = ("kv_0", "kv_1")
DP = ("dp_0", "dp_1")
LANE = 128
SUB = 8
MASKED = -1e30
LN2 = math.log(2.0)
KAPPA = 1.0 / (LN2 * math.sqrt(DH))


def prepare_kernel(sel, own, other, student, out):
    def put(slot, q):
        q = q.astype(jnp.float32) * KAPPA
        high = q.astype(jnp.bfloat16)
        low = (q - high.astype(jnp.float32)).astype(jnp.bfloat16)
        out[slot, :DH, :] = jnp.transpose(high.astype(jnp.float32)).astype(jnp.bfloat16)
        out[slot, DH:, :] = jnp.transpose(low.astype(jnp.float32)).astype(jnp.bfloat16)

    for s in range(STUDENTS):
        put(PAIRS + s, student[:, s * DH : (s + 1) * DH])
    for p in range(PAIRS):
        lanes = pl.ds(pl.multiple_of(sel[1, p] * DH, DH), DH)

        @pl.when(sel[0, p] == 0)
        def _():
            put(p, own[:, lanes])

        @pl.when(sel[0, p] != 0)
        def _():
            put(p, other[:, lanes])


def prepare(sel, own, other, student):
    vmem = pl.BlockSpec(memory_space=pltpu.VMEM)
    return pl.pallas_call(
        prepare_kernel,
        out_shape=jax.ShapeDtypeStruct((HEADS, 2 * DH, ROWS), jnp.bfloat16),
        in_specs=[pl.BlockSpec(memory_space=pltpu.SMEM), vmem, vmem, vmem],
        out_specs=vmem,
        name="prepare",
    )(sel, own, other, student)


STATE = 3 * PAIRS + 2 * STUDENTS
TL, TC, SM, SL = PAIRS, 2 * PAIRS, 3 * PAIRS, 3 * PAIRS + STUDENTS
HALF = ROWS // 2
PIECES = 5


def attend_kernel(first, last, info, qt, *refs):
    parts = refs[: 2 * PIECES]
    refs = refs[2 * PIECES :]
    if not first:
        before, *refs = refs
    out, keys, *refs = refs
    if last:
        state, sems = refs
    else:
        state = out
        (sems,) = refs
    row_block = info[0, 0]
    needed = info[0, 1] != 0

    def copies():
        for side in range(2):
            for n in range(PIECES):
                slot = min(n, 3)
                rows = pl.ds(0, ROWS) if n < 3 else pl.ds((n - 3) * HALF, HALF)
                yield pltpu.make_async_copy(
                    parts[side * PIECES + n], keys.at[side, slot, rows], sems.at[side, n]
                )

    @pl.when(needed)
    def _():
        for c in copies():
            c.start()

    if first:
        for part, value in ((0, MASKED), (TL, 0.0), (TC, 0.0)):
            state[part : part + PAIRS] = jnp.full((PAIRS, SUB, ROWS), value, jnp.float32)
        for part, value in ((SM, MASKED), (SL, 0.0)):
            state[part : part + STUDENTS] = jnp.full((STUDENTS, SUB, ROWS), value, jnp.float32)
    else:
        state[...] = before[...]

    def update(logits, mask, m_index, l_index):
        if mask is not None:
            logits = jnp.where(mask, logits, MASKED)
        folded = logits.reshape(ROWS // SUB, SUB, ROWS)
        old = state[m_index]
        new = jnp.maximum(old, jnp.max(folded, axis=0))
        weights = jnp.exp2(folded - new[None])
        rescale = jnp.exp2(old - new)
        state[m_index] = new
        state[l_index] = state[l_index] * rescale + jnp.sum(weights, axis=0)
        return weights, rescale

    def block(slot, masked):
        mask = None
        if masked:
            key_pos = lax.broadcasted_iota(jnp.int32, (ROWS, ROWS), 0)
            row_pos = lax.broadcasted_iota(jnp.int32, (ROWS, ROWS), 1)
            mask = key_pos <= row_pos
        student_keys = keys[0, slot, :, 2 * DH :]
        student_keys = jnp.concatenate([student_keys, student_keys], axis=1)
        for s in range(STUDENTS):
            zs = jnp.dot(student_keys, qt[PAIRS + s], preferred_element_type=jnp.float32)
            update(zs, mask, SM + s, SL + s)
            for c in range(2):
                p = 2 * s + c
                lanes = pl.ds(pl.multiple_of(info[2, p] * DH, DH), DH)
                teacher_keys = keys[info[1, p], slot, :, lanes]
                teacher_keys = jnp.concatenate([teacher_keys, teacher_keys], axis=1)
                zt = jnp.dot(teacher_keys, qt[p], preferred_element_type=jnp.float32)
                weights, rescale = update(zt, mask, p, TL + p)
                gap = (zt - zs).reshape(ROWS // SUB, SUB, ROWS)
                state[TC + p] = state[TC + p] * rescale + jnp.sum(weights * gap, axis=0)

    def step(slot, carry):
        position = info[3, slot]

        @pl.when(position < row_block)
        def _():
            block(slot, False)

        if first:

            @pl.when(position == row_block)
            def _():
                block(slot, True)

        return carry

    @pl.when(needed)
    def _():
        for c in copies():
            c.wait()
        lax.fori_loop(0, 4, step, 0)

    if not last:
        return

    def merged(m8, l8):
        top = jnp.max(m8, axis=0, keepdims=True)
        factor = jnp.exp2(m8 - top)
        total = jnp.sum(l8 * factor, axis=0, keepdims=True)
        return factor, total, LN2 * top + jnp.log(total)

    for s in range(STUDENTS):
        _, _, s_lse = merged(state[SM + s], state[SL + s])
        value = 2.0 * s_lse
        for c in range(2):
            p = 2 * s + c
            factor, total, t_lse = merged(state[p], state[TL + p])
            cross = jnp.sum(state[TC + p] * factor, axis=0, keepdims=True)
            value = value + (LN2 * cross / total - t_lse)
        out[s : s + 1, :] = value


def attend(info, qt, parts, state, last):
    first = state is None
    vmem = pl.BlockSpec(memory_space=pltpu.VMEM)
    operands = [info, qt, *parts] + ([] if first else [state])
    state_shape = (STATE, SUB, ROWS)
    scratch = [pltpu.VMEM((2, 4, ROWS, 3 * DH), jnp.bfloat16)]
    if last:
        scratch.append(pltpu.VMEM(state_shape, jnp.float32))
    scratch.append(pltpu.SemaphoreType.DMA((2, PIECES)))
    return pl.pallas_call(
        functools.partial(attend_kernel, first, last),
        out_shape=jax.ShapeDtypeStruct((STUDENTS, ROWS) if last else state_shape, jnp.float32),
        in_specs=[pl.BlockSpec(memory_space=pltpu.SMEM), vmem]
        + [pl.BlockSpec(memory_space=pl.ANY)] * len(parts)
        + ([] if first else [vmem]),
        out_specs=vmem,
        scratch_shapes=scratch,
        compiler_params=pltpu.CompilerParams(vmem_limit_bytes=24 * 1024 * 1024),
        cost_estimate=pl.CostEstimate(
            flops=4 * HEADS * 2 * ROWS * ROWS * 2 * DH,
            bytes_accessed=8 * ROWS * 3 * DH * 2,
            transcendentals=4 * HEADS * ROWS * ROWS,
        ),
        name="attend",
    )(*operands)


CORE = "dp_1"


def per_device(teacher_query, teacher_key, student_query, student_key, pair_table):
    core = lax.axis_index(CORE)
    head = lax.axis_index("head")
    z_hi = lax.axis_index("kv_0")
    x = lax.axis_index("kv_1")
    stays = core == head

    def swap(a):
        return lax.ppermute(a, (CORE, "head"), [(1, 2), (2, 1)])

    def swapped(a):
        return jnp.where(stays, a, swap(a))

    def across(a, chunks):
        pairs = [(c * 4 + z, (1 - c) * 4 + z) for c in range(2) for z in chunks]
        return lax.ppermute(a, (CORE, "kv_0"), pairs)

    def along_x(a, by, chunks):
        pairs = [(z * 4 + i, z * 4 + (i + by) % 4) for z in chunks for i in range(4)]
        return lax.ppermute(a, KV, pairs)

    def along_z(a, pairs):
        return lax.ppermute(a, "kv_0", pairs)

    def gathered(a, chunks):
        left = along_x(a, 1, chunks)
        right = along_x(a, -1, chunks)
        far_a = along_x(left[:HALF], 1, chunks)
        far_b = along_x(right[HALF:], -1, chunks)
        mine = [a, left, right, far_a, far_b]
        return mine + [across(m, chunks) for m in mine]

    keys = swapped(jnp.concatenate([teacher_key[0], student_key[0]], axis=1))
    student = swapped(student_query[0])
    own = swapped(teacher_query[0])
    other = across(own, range(4))

    one_back = along_z(keys, [(0, 1), (1, 2), (2, 3)])
    wrapped = along_z(keys, [(0, 3)])
    two_back = along_z(one_back, [(1, 2), (2, 3)])

    side = core
    my_pairs = lax.dynamic_slice_in_dim(pair_table, side * STUDENTS, STUDENTS, 0).reshape(-1)
    sel = jnp.stack([(my_pairs // PAIRS != side).astype(jnp.int32), my_pairs % PAIRS])
    kv_head = my_pairs // (HT // KVT)
    pad = jnp.zeros((2,), jnp.int32)
    x_of = jnp.mod(x + jnp.array([0, -1, 1, 2], jnp.int32), 4)

    def info(chunk, needed):
        return jnp.stack(
            [
                jnp.pad(jnp.stack([z_hi * 4 + x, needed.astype(jnp.int32)]), (0, 14)),
                jnp.concatenate([(kv_head // 2 != side).astype(jnp.int32), pad]),
                jnp.concatenate([kv_head % 2, pad]),
                jnp.pad(chunk * 4 + x_of, (0, 12)),
            ]
        )

    qt = prepare(sel, own, other, student)
    state = attend(info(z_hi, z_hi >= 0), qt, gathered(keys, range(4)), None, False)
    state = attend(info(z_hi - 1, z_hi >= 1), qt, gathered(one_back, (1, 2, 3)), state, False)
    state = attend(info(z_hi - 3, z_hi == 3), qt, gathered(wrapped, (3,)), state, False)
    kl = attend(info(z_hi - 2, z_hi >= 2), qt, gathered(two_back, (2, 3)), state, True)
    kl = swapped(kl)

    sums = jnp.pad(jnp.sum(kl, axis=1), (0, LANE - STUDENTS))
    everyone = ("dp_0", "dp_1", "kv_0", "kv_1")
    count = lax.axis_size(everyone)
    terms = lax.all_to_all(
        jnp.broadcast_to(sums, (count, LANE)), everyone, 0, 0, tiled=True
    )
    head_loss = jnp.sum(terms, axis=0)[:STUDENTS] / (count * ROWS)
    return (kl[None], head_loss)


def solution(mesh):
    split = Mesh(
        mesh.devices.reshape(4, 2, mesh.shape["head"], 4, 4),
        ("dp_0", "dp_1", "head", "kv_0", "kv_1"),
    )
    in_specs = (P(DP, KV, "head"), P(DP, KV, "head"), P(DP, KV, "head"), P(DP, KV, "head"), P())
    out_specs = (P(DP, "head", KV), P("head"))
    return jax.shard_map(
        per_device, mesh=split, in_specs=in_specs, out_specs=out_specs, check_vma=False
    )
```

time: 165 us -> 216 us (1.31)
  starting transfers between devices: 59.1 us -> 151 us
  waiting for transfers between devices: 78.3 us -> 29.6 us
  other arithmetic: 1.51 us -> 8.78 us
  local copies, waits for them, and re-layouts: 15 us -> 12.4 us
    all_to_all x1, starting transfers between devices: 42 us -> 101 us  [per_device(): lax.all_to_all(jnp.broadcast_to(sums, (count, LANE)), everyone, 0, 0, til...]
    ppermute x12 -> x44, waiting for transfers between devices: 67.1 us -> 18.3 us  [the longest x4 10.6 us: swap(): return lax.ppermute(a, (CORE, 'head'), [(1, 2), (2, 1)])]
    ppermute x12 -> x44, starting transfers between devices: 17.1 us -> 49.7 us  [the longest x16 15.9 us: along_x(): return lax.ppermute(a, KV, pairs)]
    select_n x2 -> x4, other arithmetic: 0.02 us -> 4.17 us  [the longest x3 4.17 us: swapped(): return jnp.where(stays, a, swap(a))]
    concatenate x2 -> x0, local copies, waits for them, and re-layouts: 2.23 us -> none  [the longest x1 1.54 us: per_device(): own_keys = jnp.concatenate([teacher_key, student_key], axis=2)]
    pallas_call x1 -> x4, Pallas kernels: 4.66 us -> 6.88 us  [attend(): pl.pallas_call(functools.partial(attend_kernel, first, last), out_shape=j...]
    unnamed x14 -> x25, local copies, waits for them, and re-layouts: 8.13 us -> 6.39 us
  transfers between devices with their start and end apart: 13 -> 45, of which waited for: 7 -> 7; matrix products, arithmetic and copies ran while one was open for 6% -> 7% of each run, Pallas kernels for 3% -> 5%
where the time goes in v2:
time: 216 us; the launch traced here: 215 us
  starting transfers between devices  151 us (70%)
  waiting for transfers between devices  29.6 us (14%)
  local copies, waits for them, and re-layouts  12.4 us (6%)
  Pallas kernels  11.9 us (6%)
  other arithmetic  8.78 us (4%)
    all_to_all x1, starting transfers between devices, per_device(): lax.all_to_all(jnp.broadcast_to(sums, (count, LANE)), everyone, 0, 0, til...  101 us
    ppermute x16, starting transfers between devices, along_x(): return lax.ppermute(a, KV, pairs)  15.9 us
    ppermute x4, starting transfers between devices, swap(): return lax.ppermute(a, (CORE, 'head'), [(1, 2), (2, 1)])  12.7 us
    ppermute x21, starting transfers between devices, across(): return lax.ppermute(a, (CORE, 'kv_0'), pairs)  11.7 us
    all_to_all x1, waiting for transfers between devices, per_device(): lax.all_to_all(jnp.broadcast_to(sums, (count, LANE)), everyone, 0, 0, til...  11.3 us
    ppermute x4, waiting for transfers between devices, swap(): return lax.ppermute(a, (CORE, 'head'), [(1, 2), (2, 1)])  10.6 us
    ppermute x3, starting transfers between devices, along_z(): return lax.ppermute(a, 'kv_0', pairs)  9.43 us
    pallas_call x4, Pallas kernels, attend(): pl.pallas_call(functools.partial(attend_kernel, first, last), out_shape=j...  6.88 us
  transfers between devices with their start and end apart: 45, of which 7 were waited for; matrix products, arithmetic and copies ran while one was open for 7% of the time, Pallas kernels for 5%

profile of v2, /device:TPU:1, one launch (start us, length us, event | category | flops | bytes accessed | tf_op | source)
XLA Modules:
  0.0 215.0 jit_solution(911605137373509388)
XLA Ops:
  0.6 4.9 %collective-permute-start = (bf16[256,1792]{1,0:T(8,128)(2,1)}, bf16[256,1792]{1,0:T(8,128)(2,1)S(1)}, u32[]{:S(2)}, u32[]{:S(2)}) collective-permute-start(bf16[256,1792]{1,0:T(8,128)(2,1)} %bitcast.34), channel_id=1, source_target_pairs={{16,32},{32,16},{17,33},{33,17},{18,34},{34,18},{19,35},{35,19},{2... | collective-permute-start | bytes 2752520 | tf_op jit(solution)/shard_map/ppermute | solution.py:217
  5.6 1.9 collective-permute-start.2
  8.5 3.6 %collective-permute-start.3 = (bf16[256,384]{1,0:T(8,128)(2,1)S(1)}, bf16[256,384]{1,0:T(8,128)(2,1)S(1)}, u32[]{:S(2)}, u32[]{:S(2)}) collective-permute-start(bf16[256,384]{1,0:T(8,128)(2,1)S(1)} %pad_maximum_fusion), channel_id=1, source_target_pairs={{16,32},{32,16},{17,33},{33,17},{18,34},{34,18},{19,35},{35,19},{2... | collective-permute-start | bytes 589832 | tf_op jit(solution)/shard_map/ppermute | solution.py:217
  16.0 7.9 %collective-permute-done.3 = bf16[256,384]{1,0:T(8,128)(2,1)S(1)} collective-permute-done((bf16[256,384]{1,0:T(8,128)(2,1)S(1)}, bf16[256,384]{1,0:T(8,128)(2,1)S(1)}, u32[]{:S(2)}, u32[]{:S(2)}) %collective-permute-start.3) | collective-permute-done | bytes 196640 | tf_op jit(solution)/shard_map/ppermute | solution.py:217
  24.9 1.3 collective-permute-start.34
  26.1 1.5 collective-permute-start.35
  27.6 1.3 broadcast_select_fusion.own
  29.5 1.2 collective-permute-done.34.refs_1_
  30.7 4.9 %collective-permute-start.4 = (bf16[256,384]{1,0:T(8,128)(2,1)S(1)}, bf16[256,384]{1,0:T(8,128)(2,1)S(1)}, u32[]{:S(2)}, u32[]{:S(2)}) collective-permute-start(bf16[256,384]{1,0:T(8,128)(2,1)S(1)} %broadcast_select_fusion.2.refs_0_), channel_id=1, source_target_pairs={{0,4},{4,8},{8,12},{1,5},{5,9},{9,13},{2,6},{6,10},{10,14},{3,7},{... | collective-permute-start | bytes 589832 | tf_op jit(solution)/shard_map/ppermute | solution.py:231
  35.6 3.9 %collective-permute-start.15 = (bf16[256,384]{1,0:T(8,128)(2,1)S(1)}, bf16[256,384]{1,0:T(8,128)(2,1)S(1)}, u32[]{:S(2)}, u32[]{:S(2)}) collective-permute-start(bf16[256,384]{1,0:T(8,128)(2,1)S(1)} %broadcast_select_fusion.2.refs_0_), channel_id=1, source_target_pairs={{0,12},{1,13},{2,14},{3,15},{16,28},{17,29},{18,30},{19,31},{32,44... | collective-permute-start | bytes 589832 | tf_op jit(solution)/shard_map/ppermute | solution.py:231
  39.7 2.5 %collective-permute-start.37 = (bf16[128,384]{1,0:T(8,128)(2,1)S(1)}, bf16[128,384]{1,0:T(8,128)(2,1)S(1)}, u32[]{:S(2)}, u32[]{:S(2)}) collective-permute-start(bf16[128,384]{1,0:T(8,128)(2,1)S(1)} %slice.43), channel_id=1, source_target_pairs={{0,3},{1,0},{2,1},{3,2},{4,7},{5,4},{6,5},{7,6},{8,11},{9,8},{10,9... | collective-permute-start | bytes 294920 | tf_op jit(solution)/shard_map/ppermute | solution.py:228
  42.3 5.5 %collective-permute-done.15.refs_0_ = bf16[256,384]{1,0:T(8,128)(2,1)S(1)} collective-permute-done((bf16[256,384]{1,0:T(8,128)(2,1)S(1)}, bf16[256,384]{1,0:T(8,128)(2,1)S(1)}, u32[]{:S(2)}, u32[]{:S(2)}) %collective-permute-start.15) | collective-permute-done | bytes 196640 | tf_op jit(solution)/shard_map/ppermute | solution.py:231
  60.3 1.3 collective-permute-start.27
  61.6 1.3 collective-permute-start.28
  62.9 1.3 collective-permute-start.18
  65.2 1.3 collective-permute-start.19
  66.5 1.9 broadcast_select_fusion.1.student
  69.6 5.1 %prepare.1.qt = bf16[21,256,256]{2,1,0:T(8,128)(2,1)} custom-call(s32[2,14]{1,0:T(2,128)} %pad_add_fusion.8.sel, bf16[256,1792]{1,0:T(8,128)(2,1)} %copy-done.5, bf16[256,1792]{1,0:T(8,128)(2,1)} %copy-done.6, bf16[256,896]{1,0:T(8,128)(2,1)} %broadcast_select_fusion.1.student), custom_call_target="tpu_custom_call" | custom-call | tf_op jit(solution)/shard_map/prepare/pallas_call | solution.py:54
  78.1 1.8 copy-done
  81.7 4.6 %attend.4.refs_10_ = f32[56,8,256]{2,1,0:T(8,128)S(1)} custom-call(s32[4,16]{1,0:T(4,128)S(1)} %get-tuple-element.16.info, bf16[21,256,256]{2,1,0:T(8,128)(2,1)S(1)} %copy-done, bf16[256,384]{1,0:T(8,128)(2,1)S(1)} %broadcast_select_fusion.2.refs_0_, bf16[256,384]{1,0:T(8,128)(2,1)S(1)} %collective-permute-done.34.refs_1_, ...), custom_call_target="tpu_custom_call" | custom-call | flops 2818572288 | bytes 1572864 | tf_op jit(solution)/shard_map/attend/pallas_call | solution.py:188
  95.5 2.2 %collective-permute-start.43 = (f32[7,256]{1,0:T(8,128)S(1)}, f32[7,256]{1,0:T(8,128)S(1)}, u32[]{:S(2)}, u32[]{:S(2)}) collective-permute-start(f32[7,256]{1,0:T(8,128)S(1)} %attend.7), channel_id=1, source_target_pairs={{16,32},{32,16},{17,33},{33,17},{18,34},{34,18},{19,35},{35,19},{2... | collective-permute-start | bytes 21512 | tf_op jit(solution)/shard_map/ppermute | solution.py:217
  97.7 2.8 %collective-permute-done.43 = f32[7,256]{1,0:T(8,128)S(1)} collective-permute-done((f32[7,256]{1,0:T(8,128)S(1)}, f32[7,256]{1,0:T(8,128)S(1)}, u32[]{:S(2)}, u32[]{:S(2)}) %collective-permute-start.43) | collective-permute-done | bytes 7200 | tf_op jit(solution)/shard_map/ppermute | solution.py:217
  101.3 101.2 %all-to-all-start = ((f32[128,1,128]{2,1,0:T(1,128)}), f32[128,1,128]{2,1,0:T(1,128)S(1)}, u32[]{:S(2)}, u32[]{:S(2)}) async-start(f32[128,1,128]{2,1,0:T(1,128)} %broadcast_in_dim.7), calls=%async_computation | async-start | bytes 131072 | tf_op jit(solution)/shard_map/all_to_all | solution.py:277
  203.1 11.3 %all-to-all-done = f32[128,1,128]{2,1,0:T(1,128)S(1)} async-done(((f32[128,1,128]{2,1,0:T(1,128)}), f32[128,1,128]{2,1,0:T(1,128)S(1)}, u32[]{:S(2)}, u32[]{:S(2)}) %all-to-all-start) | async-done | bytes 65568 | tf_op jit(solution)/shard_map/all_to_all | solution.py:277
  (143 shorter events, 37.3 us)
Async XLA Ops:
  0.6 27.0 %collective-permute-start = (bf16[256,1792]{1,0:T(8,128)(2,1)}, bf16[256,1792]{1,0:T(8,128)(2,1)S(1)}, u32[]{:S(2)}, u32[]{:S(2)}) collective-permute-start(bf16[256,1792]{1,0:T(8,128)(2,1)} %bitcast.34), channel_id=1, source_target_pairs={{16,32},{32,16},{17,33},{33,17},{18,34},{34,18},{19,35},{35,19},{2... | collective-permute-start | bytes 2752520 | tf_op jit(solution)/shard_map/ppermute | solution.py:217
  5.6 42.2 %collective-permute-start.2 = (bf16[256,896]{1,0:T(8,128)(2,1)}, bf16[256,896]{1,0:T(8,128)(2,1)S(1)}, u32[]{:S(2)}, u32[]{:S(2)}) collective-permute-start(bf16[256,896]{1,0:T(8,128)(2,1)} %bitcast.37), channel_id=1, source_target_pairs={{16,32},{32,16},{17,33},{33,17},{18,34},{34,18},{19,35},{35,19},{2... | collective-permute-start | bytes 1376264 | tf_op jit(solution)/shard_map/ppermute | solution.py:217
  8.5 15.4 %collective-permute-start.3 = (bf16[256,384]{1,0:T(8,128)(2,1)S(1)}, bf16[256,384]{1,0:T(8,128)(2,1)S(1)}, u32[]{:S(2)}, u32[]{:S(2)}) collective-permute-start(bf16[256,384]{1,0:T(8,128)(2,1)S(1)} %pad_maximum_fusion), channel_id=1, source_target_pairs={{16,32},{32,16},{17,33},{33,17},{18,34},{34,18},{19,35},{35,19},{2... | collective-permute-start | bytes 589832 | tf_op jit(solution)/shard_map/ppermute | solution.py:217
  24.9 5.8 %collective-permute-start.34 = (bf16[256,384]{1,0:T(8,128)(2,1)S(1)}, bf16[256,384]{1,0:T(8,128)(2,1)S(1)}, u32[]{:S(2)}, u32[]{:S(2)}) collective-permute-start(bf16[256,384]{1,0:T(8,128)(2,1)S(1)} %broadcast_select_fusion.2.refs_0_), channel_id=1, source_target_pairs={{0,1},{1,2},{2,3},{3,0},{4,5},{5,6},{6,7},{7,4},{8,9},{9,10},{10,1... | collective-permute-start | bytes 589832 | tf_op jit(solution)/shard_map/ppermute | solution.py:228
  26.1 9.4 %collective-permute-start.35 = (bf16[256,384]{1,0:T(8,128)(2,1)S(1)}, bf16[256,384]{1,0:T(8,128)(2,1)S(1)}, u32[]{:S(2)}, u32[]{:S(2)}) collective-permute-start(bf16[256,384]{1,0:T(8,128)(2,1)S(1)} %broadcast_select_fusion.2.refs_0_), channel_id=1, source_target_pairs={{0,3},{1,0},{2,1},{3,2},{4,7},{5,4},{6,5},{7,6},{8,11},{9,8},{10,9... | collective-permute-start | bytes 589832 | tf_op jit(solution)/shard_map/ppermute | solution.py:228
  28.9 35.3 %collective-permute-start.1 = (bf16[256,1792]{1,0:T(8,128)(2,1)S(1)}, bf16[256,1792]{1,0:T(8,128)(2,1)S(1)}, u32[]{:S(2)}, u32[]{:S(2)}) collective-permute-start(bf16[256,1792]{1,0:T(8,128)(2,1)S(1)} %broadcast_select_fusion.own), channel_id=1, source_target_pairs={{0,32},{4,36},{8,40},{12,44},{32,0},{36,4},{40,8},{44,12},{1,33},{... | collective-permute-start | bytes 2752520 | tf_op jit(solution)/shard_map/ppermute | solution.py:224
  29.0 10.5 %collective-permute-start.38 = (bf16[256,384]{1,0:T(8,128)(2,1)S(1)}, bf16[256,384]{1,0:T(8,128)(2,1)S(1)}, u32[]{:S(2)}, u32[]{:S(2)}) collective-permute-start(bf16[256,384]{1,0:T(8,128)(2,1)S(1)} %broadcast_select_fusion.2.refs_0_), channel_id=1, source_target_pairs={{0,32},{4,36},{8,40},{12,44},{32,0},{36,4},{40,8},{44,12},{1,33},{... | collective-permute-start | bytes 589832 | tf_op jit(solution)/shard_map/ppermute | solution.py:224
  30.7 9.1 %collective-permute-start.4 = (bf16[256,384]{1,0:T(8,128)(2,1)S(1)}, bf16[256,384]{1,0:T(8,128)(2,1)S(1)}, u32[]{:S(2)}, u32[]{:S(2)}) collective-permute-start(bf16[256,384]{1,0:T(8,128)(2,1)S(1)} %broadcast_select_fusion.2.refs_0_), channel_id=1, source_target_pairs={{0,4},{4,8},{8,12},{1,5},{5,9},{9,13},{2,6},{6,10},{10,14},{3,7},{... | collective-permute-start | bytes 589832 | tf_op jit(solution)/shard_map/ppermute | solution.py:231
  35.6 12.2 %collective-permute-start.15 = (bf16[256,384]{1,0:T(8,128)(2,1)S(1)}, bf16[256,384]{1,0:T(8,128)(2,1)S(1)}, u32[]{:S(2)}, u32[]{:S(2)}) collective-permute-start(bf16[256,384]{1,0:T(8,128)(2,1)S(1)} %broadcast_select_fusion.2.refs_0_), channel_id=1, source_target_pairs={{0,12},{1,13},{2,14},{3,15},{16,28},{17,29},{18,30},{19,31},{32,44... | collective-permute-start | bytes 589832 | tf_op jit(solution)/shard_map/ppermute | solution.py:231
  39.5 9.0 %collective-permute-start.36 = (bf16[128,384]{1,0:T(8,128)(2,1)S(1)}, bf16[128,384]{1,0:T(8,128)(2,1)S(1)}, u32[]{:S(2)}, u32[]{:S(2)}) collective-permute-start(bf16[128,384]{1,0:T(8,128)(2,1)S(1)} %slice.42), channel_id=1, source_target_pairs={{0,1},{1,2},{2,3},{3,0},{4,5},{5,6},{6,7},{7,4},{8,9},{9,10},{10,1... | collective-permute-start | bytes 294920 | tf_op jit(solution)/shard_map/ppermute | solution.py:228
  39.7 9.3 %collective-permute-start.37 = (bf16[128,384]{1,0:T(8,128)(2,1)S(1)}, bf16[128,384]{1,0:T(8,128)(2,1)S(1)}, u32[]{:S(2)}, u32[]{:S(2)}) collective-permute-start(bf16[128,384]{1,0:T(8,128)(2,1)S(1)} %slice.43), channel_id=1, source_target_pairs={{0,3},{1,0},{2,1},{3,2},{4,7},{5,4},{6,5},{7,6},{8,11},{9,8},{10,9... | collective-permute-start | bytes 294920 | tf_op jit(solution)/shard_map/ppermute | solution.py:228
  55.6 6.0 %collective-permute-start.6 = (bf16[256,384]{1,0:T(8,128)(2,1)S(1)}, bf16[256,384]{1,0:T(8,128)(2,1)S(1)}, u32[]{:S(2)}, u32[]{:S(2)}) collective-permute-start(bf16[256,384]{1,0:T(8,128)(2,1)S(1)} %collective-permute-done.5.refs_0_), channel_id=1, source_target_pairs={{8,9},{9,10},{10,11},{11,8},{12,13},{13,14},{14,15},{15,12},{24,25... | collective-permute-start | bytes 589832 | tf_op jit(solution)/shard_map/ppermute | solution.py:228
  56.3 6.6 %collective-permute-start.7 = (bf16[256,384]{1,0:T(8,128)(2,1)S(1)}, bf16[256,384]{1,0:T(8,128)(2,1)S(1)}, u32[]{:S(2)}, u32[]{:S(2)}) collective-permute-start(bf16[256,384]{1,0:T(8,128)(2,1)S(1)} %collective-permute-done.5.refs_0_), channel_id=1, source_target_pairs={{8,11},{9,8},{10,9},{11,10},{12,15},{13,12},{14,13},{15,14},{24,27... | collective-permute-start | bytes 589832 | tf_op jit(solution)/shard_map/ppermute | solution.py:228
  59.6 15.1 %collective-permute-start.20 = (bf16[256,384]{1,0:T(8,128)(2,1)S(1)}, bf16[256,384]{1,0:T(8,128)(2,1)S(1)}, u32[]{:S(2)}, u32[]{:S(2)}) collective-permute-start(bf16[256,384]{1,0:T(8,128)(2,1)S(1)} %collective-permute-done.15.refs_0_), channel_id=1, source_target_pairs={{12,44},{44,12},{13,45},{45,13},{14,46},{46,14},{15,47},{47,15},{2... | collective-permute-start | bytes 589832 | tf_op jit(solution)/shard_map/ppermute | solution.py:224
  60.3 15.0 %collective-permute-start.27 = (bf16[128,384]{1,0:T(8,128)(2,1)}, bf16[128,384]{1,0:T(8,128)(2,1)}, u32[]{:S(2)}, u32[]{:S(2)}) collective-permute-start(bf16[128,384]{1,0:T(8,128)(2,1)} %slice.40), channel_id=1, source_target_pairs={{4,5},{5,6},{6,7},{7,4},{8,9},{9,10},{10,11},{11,8},{12,13},{13,14... | collective-permute-start | bytes 294920 | tf_op jit(solution)/shard_map/ppermute | solution.py:228
  61.6 14.4 %collective-permute-start.28 = (bf16[128,384]{1,0:T(8,128)(2,1)}, bf16[128,384]{1,0:T(8,128)(2,1)}, u32[]{:S(2)}, u32[]{:S(2)}) collective-permute-start(bf16[128,384]{1,0:T(8,128)(2,1)} %slice.41), channel_id=1, source_target_pairs={{4,7},{5,4},{6,5},{7,6},{8,11},{9,8},{10,9},{11,10},{12,15},{13,12... | collective-permute-start | bytes 294920 | tf_op jit(solution)/shard_map/ppermute | solution.py:228
  62.9 13.8 %collective-permute-start.18 = (bf16[128,384]{1,0:T(8,128)(2,1)}, bf16[128,384]{1,0:T(8,128)(2,1)}, u32[]{:S(2)}, u32[]{:S(2)}) collective-permute-start(bf16[128,384]{1,0:T(8,128)(2,1)} %slice.38), channel_id=1, source_target_pairs={{12,13},{13,14},{14,15},{15,12},{28,29},{29,30},{30,31},{31,28},{4... | collective-permute-start | bytes 294920 | tf_op jit(solution)/shard_map/ppermute | solution.py:228
  65.2 12.3 %collective-permute-start.19 = (bf16[128,384]{1,0:T(8,128)(2,1)}, bf16[128,384]{1,0:T(8,128)(2,1)}, u32[]{:S(2)}, u32[]{:S(2)}) collective-permute-start(bf16[128,384]{1,0:T(8,128)(2,1)} %slice.39), channel_id=1, source_target_pairs={{12,15},{13,12},{14,13},{15,14},{28,31},{29,28},{30,29},{31,30},{4... | collective-permute-start | bytes 294920 | tf_op jit(solution)/shard_map/ppermute | solution.py:228
  74.7 13.0 %collective-permute-start.30 = (bf16[256,384]{1,0:T(8,128)(2,1)S(1)}, bf16[256,384]{1,0:T(8,128)(2,1)S(1)}, u32[]{:S(2)}, u32[]{:S(2)}) collective-permute-start(bf16[256,384]{1,0:T(8,128)(2,1)S(1)} %collective-permute-done.25.refs_1_), channel_id=1, source_target_pairs={{4,36},{8,40},{12,44},{36,4},{40,8},{44,12},{5,37},{9,41},{13,45},... | collective-permute-start | bytes 589832 | tf_op jit(solution)/shard_map/ppermute | solution.py:224
  75.4 13.0 %collective-permute-start.31 = (bf16[256,384]{1,0:T(8,128)(2,1)S(1)}, bf16[256,384]{1,0:T(8,128)(2,1)S(1)}, u32[]{:S(2)}, u32[]{:S(2)}) collective-permute-start(bf16[256,384]{1,0:T(8,128)(2,1)S(1)} %collective-permute-done.26.refs_2_), channel_id=1, source_target_pairs={{4,36},{8,40},{12,44},{36,4},{40,8},{44,12},{5,37},{9,41},{13,45},... | collective-permute-start | bytes 589832 | tf_op jit(solution)/shard_map/ppermute | solution.py:224
  76.1 10.2 %collective-permute-start.32 = (bf16[128,384]{1,0:T(8,128)(2,1)}, bf16[128,384]{1,0:T(8,128)(2,1)S(1)}, u32[]{:S(2)}, u32[]{:S(2)}) collective-permute-start(bf16[128,384]{1,0:T(8,128)(2,1)} %collective-permute-done.27.refs_3_), channel_id=1, source_target_pairs={{4,36},{8,40},{12,44},{36,4},{40,8},{44,12},{5,37},{9,41},{13,45},... | collective-permute-start | bytes 294920 | tf_op jit(solution)/shard_map/ppermute | solution.py:224
  76.8 10.2 %collective-permute-start.33 = (bf16[128,384]{1,0:T(8,128)(2,1)}, bf16[128,384]{1,0:T(8,128)(2,1)S(1)}, u32[]{:S(2)}, u32[]{:S(2)}) collective-permute-start(bf16[128,384]{1,0:T(8,128)(2,1)} %collective-permute-done.28.refs_4_), channel_id=1, source_target_pairs={{4,36},{8,40},{12,44},{36,4},{40,8},{44,12},{5,37},{9,41},{13,45},... | collective-permute-start | bytes 294920 | tf_op jit(solution)/shard_map/ppermute | solution.py:224
  77.4 11.6 %collective-permute-start.23 = (bf16[128,384]{1,0:T(8,128)(2,1)}, bf16[128,384]{1,0:T(8,128)(2,1)S(1)}, u32[]{:S(2)}, u32[]{:S(2)}) collective-permute-start(bf16[128,384]{1,0:T(8,128)(2,1)} %collective-permute-done.18.refs_3_), channel_id=1, source_target_pairs={{12,44},{44,12},{13,45},{45,13},{14,46},{46,14},{15,47},{47,15},{2... | collective-permute-start | bytes 294920 | tf_op jit(solution)/shard_map/ppermute | solution.py:224
  101.3 113.1 %all-to-all-start = ((f32[128,1,128]{2,1,0:T(1,128)}), f32[128,1,128]{2,1,0:T(1,128)S(1)}, u32[]{:S(2)}, u32[]{:S(2)}) async-start(f32[128,1,128]{2,1,0:T(1,128)} %broadcast_in_dim.7), calls=%async_computation | async-start | bytes 131072 | tf_op jit(solution)/shard_map/all_to_all | solution.py:277
  (33 other events, 229.8 us)

commit v3 on v2

v3 whole, which is shorter than its diff:
```python
import functools
import math

import jax
import jax.numpy as jnp
from jax import lax
from jax.experimental import pallas as pl
from jax.experimental.pallas import tpu as pltpu
from jax.sharding import Mesh
from jax.sharding import PartitionSpec as P

HT = 28
KVT = 4
DH = 128
HS = 14
KVS = 2
ROWS = 256
PAIRS = 14
STUDENTS = 7
HEADS = PAIRS + STUDENTS
KV = ("kv_0", "kv_1")
DP = ("dp_0", "dp_1")
LANE = 128
SUB = 8
MASKED = -1e30
LN2 = math.log(2.0)
KAPPA = 1.0 / (LN2 * math.sqrt(DH))


def prepare_kernel(sel, own, other, student, out):
    def put(slot, q):
        q = q.astype(jnp.float32) * KAPPA
        high = q.astype(jnp.bfloat16)
        low = (q - high.astype(jnp.float32)).astype(jnp.bfloat16)
        out[slot, :DH, :] = jnp.transpose(high.astype(jnp.float32)).astype(jnp.bfloat16)
        out[slot, DH:, :] = jnp.transpose(low.astype(jnp.float32)).astype(jnp.bfloat16)

    for s in range(STUDENTS):
        put(PAIRS + s, student[:, s * DH : (s + 1) * DH])
    for p in range(PAIRS):
        lanes = pl.ds(pl.multiple_of(sel[1, p] * DH, DH), DH)

        @pl.when(sel[0, p] == 0)
        def _():
            put(p, own[:, lanes])

        @pl.when(sel[0, p] != 0)
        def _():
            put(p, other[:, lanes])


def prepare(sel, own, other, student):
    vmem = pl.BlockSpec(memory_space=pltpu.VMEM)
    return pl.pallas_call(
        prepare_kernel,
        out_shape=jax.ShapeDtypeStruct((HEADS, 2 * DH, ROWS), jnp.bfloat16),
        in_specs=[pl.BlockSpec(memory_space=pltpu.SMEM), vmem, vmem, vmem],
        out_specs=vmem,
        name="prepare",
    )(sel, own, other, student)


STATE = 3 * PAIRS + 2 * STUDENTS
TL, TC, SM, SL = PAIRS, 2 * PAIRS, 3 * PAIRS, 3 * PAIRS + STUDENTS
OWN = 3
COLUMN = 4 * OWN + 4 * 2


def split_kernel(teacher, student, out):
    out[0] = teacher[:, :DH]
    out[1] = teacher[:, DH:]
    out[2] = student[...]


def split_heads(teacher, student):
    return pl.pallas_call(
        split_kernel,
        out_shape=jax.ShapeDtypeStruct((OWN, ROWS, DH), jnp.bfloat16),
        in_specs=[pl.BlockSpec(memory_space=pltpu.VMEM)] * 2,
        out_specs=pl.BlockSpec(memory_space=pltpu.VMEM),
        name="split_heads",
    )(teacher, student)


def column_kernel(side, *refs):
    ring, out, sems = refs[:8], refs[8], refs[9]

    def move(head):
        copies = []
        for m in range(4):
            own = ring[2 * m]
            other = ring[(2 * m - 1 + 2 * head) % 8]
            copies.append(
                pltpu.make_async_copy(own, out.at[pl.ds(OWN * m, OWN)], sems.at[m])
            )
            copies.append(
                pltpu.make_async_copy(
                    other.at[pl.ds(0, 2)], out.at[pl.ds(4 * OWN + 2 * m, 2)], sems.at[4 + m]
                )
            )
        for c in copies:
            c.start()
        for c in copies:
            c.wait()

    for head in range(2):

        @pl.when(side[0, 0] == head)
        def _():
            move(head)


def column_of(side, ring):
    return pl.pallas_call(
        column_kernel,
        out_shape=jax.ShapeDtypeStruct((COLUMN, ROWS, DH), jnp.bfloat16),
        in_specs=[pl.BlockSpec(memory_space=pltpu.SMEM)]
        + [pl.BlockSpec(memory_space=pl.ANY)] * 8,
        out_specs=pl.BlockSpec(memory_space=pltpu.VMEM),
        scratch_shapes=[pltpu.SemaphoreType.DMA((8,))],
        name="column",
    )(side, *ring)


def attend_kernel(first, last, counts, info, qt, *refs):
    groups = refs[: len(counts)]
    refs = refs[len(counts) :]
    if not first:
        before, *refs = refs
    out, keys, *refs = refs
    if last:
        state, sems = refs
    else:
        state = out
        (sems,) = refs
    row_block = info[0, 0]
    copies = []
    at = 0
    for g, n in enumerate(counts):
        copies.append(pltpu.make_async_copy(groups[g], keys.at[pl.ds(at, n)], sems.at[g]))
        at += n
    columns = at // COLUMN
    for c in copies:
        c.start()

    if first:
        for part, value in ((0, MASKED), (TL, 0.0), (TC, 0.0)):
            state[part : part + PAIRS] = jnp.full((PAIRS, SUB, ROWS), value, jnp.float32)
        for part, value in ((SM, MASKED), (SL, 0.0)):
            state[part : part + STUDENTS] = jnp.full((STUDENTS, SUB, ROWS), value, jnp.float32)
    else:
        state[...] = before[...]
    for c in copies:
        c.wait()

    def update(logits, mask, m_index, l_index):
        if mask is not None:
            logits = jnp.where(mask, logits, MASKED)
        folded = logits.reshape(ROWS // SUB, SUB, ROWS)
        old = state[m_index]
        new = jnp.maximum(old, jnp.max(folded, axis=0))
        weights = jnp.exp2(folded - new[None])
        rescale = jnp.exp2(old - new)
        state[m_index] = new
        state[l_index] = state[l_index] * rescale + jnp.sum(weights, axis=0)
        return weights, rescale

    def block(base, m, masked):
        mask = None
        if masked:
            key_pos = lax.broadcasted_iota(jnp.int32, (ROWS, ROWS), 0)
            row_pos = lax.broadcasted_iota(jnp.int32, (ROWS, ROWS), 1)
            mask = key_pos <= row_pos
        student_keys = keys[base + OWN * m + 2]
        student_keys = jnp.concatenate([student_keys, student_keys], axis=1)
        for s in range(STUDENTS):
            zs = jnp.dot(student_keys, qt[PAIRS + s], preferred_element_type=jnp.float32)
            update(zs, mask, SM + s, SL + s)
            for c in range(2):
                p = 2 * s + c
                teacher_keys = keys[base + info[1, p] + info[2, p] * m]
                teacher_keys = jnp.concatenate([teacher_keys, teacher_keys], axis=1)
                zt = jnp.dot(teacher_keys, qt[p], preferred_element_type=jnp.float32)
                weights, rescale = update(zt, mask, p, TL + p)
                gap = (zt - zs).reshape(ROWS // SUB, SUB, ROWS)
                state[TC + p] = state[TC + p] * rescale + jnp.sum(weights * gap, axis=0)

    def step(i, carry):
        position = info[3, i]
        base = (i // 4) * COLUMN
        m = lax.rem(i, 4)

        @pl.when(position < row_block)
        def _():
            block(base, m, False)

        if first:

            @pl.when(position == row_block)
            def _():
                block(base, m, True)

        return carry

    lax.fori_loop(0, 4 * columns, step, 0)

    if not last:
        return

    def merged(m8, l8):
        top = jnp.max(m8, axis=0, keepdims=True)
        factor = jnp.exp2(m8 - top)
        total = jnp.sum(l8 * factor, axis=0, keepdims=True)
        return factor, total, LN2 * top + jnp.log(total)

    for s in range(STUDENTS):
        _, _, s_lse = merged(state[SM + s], state[SL + s])
        value = 2.0 * s_lse
        for c in range(2):
            p = 2 * s + c
            factor, total, t_lse = merged(state[p], state[TL + p])
            cross = jnp.sum(state[TC + p] * factor, axis=0, keepdims=True)
            value = value + (LN2 * cross / total - t_lse)
        out[s : s + 1, :] = value


def attend(info, qt, groups, state, last):
    first = state is None
    vmem = pl.BlockSpec(memory_space=pltpu.VMEM)
    operands = [info, qt, *groups] + ([] if first else [state])
    state_shape = (STATE, SUB, ROWS)
    counts = tuple(g.shape[0] for g in groups)
    blocks = 4 * sum(counts) // COLUMN
    scratch = [pltpu.VMEM((sum(counts), ROWS, DH), jnp.bfloat16)]
    if last:
        scratch.append(pltpu.VMEM(state_shape, jnp.float32))
    scratch.append(pltpu.SemaphoreType.DMA((len(groups),)))
    return pl.pallas_call(
        functools.partial(attend_kernel, first, last, counts),
        out_shape=jax.ShapeDtypeStruct((STUDENTS, ROWS) if last else state_shape, jnp.float32),
        in_specs=[pl.BlockSpec(memory_space=pltpu.SMEM), vmem]
        + [pl.BlockSpec(memory_space=pl.ANY)] * len(groups)
        + ([] if first else [vmem]),
        out_specs=vmem,
        scratch_shapes=scratch,
        compiler_params=pltpu.CompilerParams(vmem_limit_bytes=24 * 1024 * 1024),
        cost_estimate=pl.CostEstimate(
            flops=blocks * HEADS * 2 * ROWS * ROWS * 2 * DH,
            bytes_accessed=blocks * ROWS * 5 * DH * 2,
            transcendentals=blocks * HEADS * ROWS * ROWS,
        ),
        name="attend",
    )(*operands)


def shift(n, by):
    return [(i, (i + by) % n) for i in range(n)]


def z_place(ring):
    ring %= 8
    return (ring % 2) * 4 + ring // 2


def z_shift(by):
    return [(z_place(i), z_place(i + by)) for i in range(8)]


def per_device(teacher_query, teacher_key, student_query, student_key, pair_table):
    head = lax.axis_index("head")
    z_hi = lax.axis_index("kv_0")
    x = lax.axis_index("kv_1")

    own_keys = split_heads(teacher_key[0], student_key[0])
    ring = {0: own_keys}
    up = down = own_keys
    for step in range(1, 5):
        up = lax.ppermute(up, ("head", "kv_0"), z_shift(1))
        ring[step] = up
        if step < 4:
            down = lax.ppermute(down, ("head", "kv_0"), z_shift(-1))
            ring[8 - step] = down
    column = column_of(head[None, None], [ring[o] for o in range(8)])
    left = lax.ppermute(column, "kv_1", shift(4, 1))
    right = lax.ppermute(column, "kv_1", shift(4, -1))
    late_query, _ = lax.optimization_barrier((teacher_query[0], ring[4]))
    other_query = lax.ppermute(late_query, "head", [(0, 1), (1, 0)])

    my_pairs = lax.dynamic_slice_in_dim(pair_table, head * STUDENTS, STUDENTS, 0).reshape(-1)
    sel = jnp.stack([(my_pairs // PAIRS != head).astype(jnp.int32), my_pairs % PAIRS])
    kv_head = my_pairs // (HT // KVT)
    pad = jnp.zeros((2,), jnp.int32)
    elsewhere = kv_head // 2 != head
    slot = jnp.where(elsewhere, 4 * OWN, 0) + kv_head % 2
    stride = jnp.where(elsewhere, 2, OWN)
    m = jnp.arange(4, dtype=jnp.int32)

    def info(*offsets):
        position = [jnp.mod(z_hi - m, 4) * 4 + jnp.mod(x + o, 4) for o in offsets]
        position = jnp.concatenate(position)
        return jnp.stack(
            [
                jnp.full((16,), z_hi * 4 + x, jnp.int32),
                jnp.concatenate([slot, pad]),
                jnp.concatenate([stride, pad]),
                jnp.pad(position, (0, 16 - position.shape[0])),
            ]
        )

    qt = prepare(sel, teacher_query[0], other_query, student_query[0])
    state = attend(info(0), qt, [column], None, False)
    left, right, state = lax.optimization_barrier((left, right, state))
    half = COLUMN // 2
    far_a = lax.ppermute(left[:half], "kv_1", shift(4, 1))
    far_b = lax.ppermute(right[half:], "kv_1", shift(4, -1))
    state = attend(info(-1, 1), qt, [left, right], state, False)
    kl = attend(info(2), qt, [far_a, far_b], state, True)

    sums = jnp.pad(jnp.sum(kl, axis=1), (0, LANE - STUDENTS))
    everyone = ("dp_0", "dp_1", "kv_0", "kv_1")
    count = lax.axis_size(everyone)
    terms = lax.all_to_all(
        jnp.broadcast_to(sums, (count, LANE)), everyone, 0, 0, tiled=True
    )
    head_loss = jnp.sum(terms, axis=0)[:STUDENTS] / (count * ROWS)
    return (kl[None], head_loss)


def solution(mesh):
    split = Mesh(
        mesh.devices.reshape(4, 2, mesh.shape["head"], 4, 4),
        ("dp_0", "dp_1", "head", "kv_0", "kv_1"),
    )
    in_specs = (P(DP, KV, "head"), P(DP, KV, "head"), P(DP, KV, "head"), P(DP, KV, "head"), P())
    out_specs = (P(DP, "head", KV), P("head"))
    return jax.shard_map(
        per_device, mesh=split, in_specs=in_specs, out_specs=out_specs, check_vma=False
    )
```

time: 216 us -> 122 us (0.56)
  starting transfers between devices: 151 us -> 47.4 us
  waiting for transfers between devices: 29.6 us -> 44.9 us
  other arithmetic: 8.78 us -> 4.79 us
  local copies, waits for them, and re-layouts: 12.4 us -> 8.66 us
  Pallas kernels: 11.9 us -> 15.2 us
    all_to_all x1, starting transfers between devices: 101 us -> 30.2 us  [per_device(): lax.all_to_all(jnp.broadcast_to(sums, (count, LANE)), everyone, 0, 0, til...]
    ppermute x44 -> x12, starting transfers between devices: 49.7 us -> 17.3 us  [the longest x3 9.22 us: per_device(): down = lax.ppermute(down, ('head', 'kv_0'), z_shift(-1))]
    ppermute x44 -> x12, waiting for transfers between devices: 18.3 us -> 33.5 us  [the longest x1 13.9 us: per_device(): other_query = lax.ppermute(late_query, 'head', [(0, 1), (1, 0)])]
    select_n x4 -> x1, other arithmetic: 4.17 us -> 0.63 us  [per_device(): stride = jnp.where(elsewhere, 2, OWN)]
    pallas_call x4 -> x5, Pallas kernels: 6.88 us -> 9.85 us  [the longest x3 5.65 us: attend(): pl.pallas_call(functools.partial(attend_kernel, first, last, counts), out...]
    slice x8 -> x2, local copies, waits for them, and re-layouts: 3.88 us -> 1.18 us  [the longest x1 1.13 us: per_device(): far_b = lax.ppermute(right[half:], 'kv_1', shift(4, -1))]
    unnamed x25 -> x23, local copies, waits for them, and re-layouts: 6.39 us -> 3.98 us
  transfers between devices with their start and end apart: 45 -> 13, of which waited for: 7 -> 8; matrix products, arithmetic and copies ran while one was open for 7% -> 7% of each run, Pallas kernels for 5% -> 8%
where the time goes in v3:
time: 122 us
  starting transfers between devices  47.4 us (39%)
  waiting for transfers between devices  44.9 us (37%)
  Pallas kernels  15.2 us (12%)
  local copies, waits for them, and re-layouts  8.66 us (7%)
  other arithmetic  4.79 us (4%)
    all_to_all x1, starting transfers between devices, per_device(): lax.all_to_all(jnp.broadcast_to(sums, (count, LANE)), everyone, 0, 0, til...  30.2 us
    ppermute x1, waiting for transfers between devices, per_device(): other_query = lax.ppermute(late_query, 'head', [(0, 1), (1, 0)])  13.9 us
    ppermute x4, waiting for transfers between devices, per_device(): up = lax.ppermute(up, ('head', 'kv_0'), z_shift(1))  13.6 us
    all_to_all x1, waiting for transfers between devices, per_device(): lax.all_to_all(jnp.broadcast_to(sums, (count, LANE)), everyone, 0, 0, til...  11.4 us
    ppermute x3, starting transfers between devices, per_device(): down = lax.ppermute(down, ('head', 'kv_0'), z_shift(-1))  9.22 us
    ppermute x1, waiting for transfers between devices, per_device(): far_a = lax.ppermute(left[:half], 'kv_1', shift(4, 1))  5.9 us
    pallas_call x3, Pallas kernels, attend(): pl.pallas_call(functools.partial(attend_kernel, first, last, counts), out...  5.65 us
    pallas_call x1, Pallas kernels, prepare(): pl.pallas_call(prepare_kernel, out_shape=jax.ShapeDtypeStruct((HEADS, 2 *...  5.38 us
  transfers between devices with their start and end apart: 13, of which 8 were waited for; matrix products, arithmetic and copies ran while one was open for 7% of the time, Pallas kernels for 8%

profile of v3, /device:TPU:1, one launch (start us, length us, event | category | flops | bytes accessed | tf_op | source)
XLA Modules:
  0.0 121.8 jit_solution(14418072126466362685)
XLA Ops:
  0.6 1.6 %split_heads.1.refs_0_ = bf16[3,256,128]{2,1,0:T(8,128)(2,1)} custom-call(bf16[256,256]{1,0:T(8,128)(2,1)} %bitcast.23, bf16[256,128]{1,0:T(8,128)(2,1)} %bitcast.24), custom_call_target="tpu_custom_call" | custom-call | tf_op jit(solution)/shard_map/split_heads/pallas_call | solution.py:76
  2.2 2.5 %collective-permute-start = (bf16[3,256,128]{2,1,0:T(8,128)(2,1)}, bf16[3,256,128]{2,1,0:T(8,128)(2,1)S(1)}, u32[]{:S(2)}, u32[]{:S(2)}) collective-permute-start(bf16[3,256,128]{2,1,0:T(8,128)(2,1)} %split_heads.1.refs_0_), channel_id=1, source_target_pairs={{0,16},{16,4},{4,20},{20,8},{8,24},{24,12},{12,28},{28,0},{1,17},{... | collective-permute-start | bytes 589832 | tf_op jit(solution)/shard_map/ppermute | solution.py:278
  4.7 3.9 %collective-permute-start.5 = (bf16[3,256,128]{2,1,0:T(8,128)(2,1)}, bf16[3,256,128]{2,1,0:T(8,128)(2,1)S(1)}, u32[]{:S(2)}, u32[]{:S(2)}) collective-permute-start(bf16[3,256,128]{2,1,0:T(8,128)(2,1)} %split_heads.1.refs_0_), channel_id=1, source_target_pairs={{0,28},{16,0},{4,16},{20,4},{8,20},{24,8},{12,24},{28,12},{1,29},{... | collective-permute-start | bytes 589832 | tf_op jit(solution)/shard_map/ppermute | solution.py:281
  10.6 2.9 %collective-permute-done.refs_1_ = bf16[3,256,128]{2,1,0:T(8,128)(2,1)S(1)} collective-permute-done((bf16[3,256,128]{2,1,0:T(8,128)(2,1)}, bf16[3,256,128]{2,1,0:T(8,128)(2,1)S(1)}, u32[]{:S(2)}, u32[]{:S(2)}) %collective-permute-start) | collective-permute-done | bytes 196640 | tf_op jit(solution)/shard_map/ppermute | solution.py:278
  14.1 2.7 %collective-permute-start.6 = (bf16[3,256,128]{2,1,0:T(8,128)(2,1)S(1)}, bf16[3,256,128]{2,1,0:T(8,128)(2,1)S(1)}, u32[]{:S(2)}, u32[]{:S(2)}) collective-permute-start(bf16[3,256,128]{2,1,0:T(8,128)(2,1)S(1)} %collective-permute-done.5.refs_7_), channel_id=1, source_target_pairs={{0,28},{16,0},{4,16},{20,4},{8,20},{24,8},{12,24},{28,12},{1,29},{... | collective-permute-start | bytes 589832 | tf_op jit(solution)/shard_map/ppermute | solution.py:281
  16.8 3.1 %collective-permute-done.1.refs_2_ = bf16[3,256,128]{2,1,0:T(8,128)(2,1)S(1)} collective-permute-done((bf16[3,256,128]{2,1,0:T(8,128)(2,1)S(1)}, bf16[3,256,128]{2,1,0:T(8,128)(2,1)S(1)}, u32[]{:S(2)}, u32[]{:S(2)}) %collective-permute-start.1) | collective-permute-done | bytes 196640 | tf_op jit(solution)/shard_map/ppermute | solution.py:278
  20.5 2.6 %collective-permute-start.7 = (bf16[3,256,128]{2,1,0:T(8,128)(2,1)S(1)}, bf16[3,256,128]{2,1,0:T(8,128)(2,1)S(1)}, u32[]{:S(2)}, u32[]{:S(2)}) collective-permute-start(bf16[3,256,128]{2,1,0:T(8,128)(2,1)S(1)} %collective-permute-done.6.refs_6_), channel_id=1, source_target_pairs={{0,28},{16,0},{4,16},{20,4},{8,20},{24,8},{12,24},{28,12},{1,29},{... | collective-permute-start | bytes 589832 | tf_op jit(solution)/shard_map/ppermute | solution.py:281
  23.1 2.5 %collective-permute-done.2.refs_3_ = bf16[3,256,128]{2,1,0:T(8,128)(2,1)S(1)} collective-permute-done((bf16[3,256,128]{2,1,0:T(8,128)(2,1)S(1)}, bf16[3,256,128]{2,1,0:T(8,128)(2,1)S(1)}, u32[]{:S(2)}, u32[]{:S(2)}) %collective-permute-start.2) | collective-permute-done | bytes 196640 | tf_op jit(solution)/shard_map/ppermute | solution.py:278
  26.2 5.1 %collective-permute-done.3.refs_4_ = bf16[3,256,128]{2,1,0:T(8,128)(2,1)S(1)} collective-permute-done((bf16[3,256,128]{2,1,0:T(8,128)(2,1)S(1)}, bf16[3,256,128]{2,1,0:T(8,128)(2,1)S(1)}, u32[]{:S(2)}, u32[]{:S(2)}) %collective-permute-start.3) | collective-permute-done | bytes 196640 | tf_op jit(solution)/shard_map/ppermute | solution.py:278
  32.0 2.6 %column.1.refs_0_ = bf16[20,256,128]{2,1,0:T(8,128)(2,1)} custom-call(s32[1,1]{1,0:T(1,128)} %bitcast.7.side, bf16[3,256,128]{2,1,0:T(8,128)(2,1)} %split_heads.1.refs_0_, bf16[3,256,128]{2,1,0:T(8,128)(2,1)} %copy-done.4, bf16[3,256,128]{2,1,0:T(8,128)(2,1)} %copy-done.6, bf16[3,256,128]{2,1,0:T(8,128)(2,1)} %copy-done.8, bf16[3,256,128]{2,1,0:T(8,128)(2,1)} %copy-done.10, ...), custom_call_target="tpu_custom_call" | custom-call | tf_op jit(solution)/shard_map/column/pallas_call | solution.py:114
  34.6 1.3 %collective-permute-start.8 = (bf16[20,256,128]{2,1,0:T(8,128)(2,1)}, bf16[20,256,128]{2,1,0:T(8,128)(2,1)S(1)}, u32[]{:S(2)}, u32[]{:S(2)}) collective-permute-start(bf16[20,256,128]{2,1,0:T(8,128)(2,1)} %column.1.refs_0_), channel_id=1, source_target_pairs={{0,1},{1,2},{2,3},{3,0},{4,5},{5,6},{6,7},{7,4},{8,9},{9,10},{10,1... | collective-permute-start | bytes 3932168 | tf_op jit(solution)/shard_map/ppermute | solution.py:284
  35.9 1.5 %collective-permute-start.9 = (bf16[20,256,128]{2,1,0:T(8,128)(2,1)}, bf16[20,256,128]{2,1,0:T(8,128)(2,1)}, u32[]{:S(2)}, u32[]{:S(2)}) collective-permute-start(bf16[20,256,128]{2,1,0:T(8,128)(2,1)} %column.1.refs_0_), channel_id=1, source_target_pairs={{0,3},{1,0},{2,1},{3,2},{4,7},{5,4},{6,5},{7,6},{8,11},{9,8},{10,9... | collective-permute-start | bytes 3932168 | tf_op jit(solution)/shard_map/ppermute | solution.py:285
  40.6 13.9 %collective-permute-done.4.other = bf16[256,1792]{1,0:T(8,128)(2,1)S(1)} collective-permute-done((bf16[256,1792]{1,0:T(8,128)(2,1)S(1)}, bf16[256,1792]{1,0:T(8,128)(2,1)S(1)}, u32[]{:S(2)}, u32[]{:S(2)}) %collective-permute-start.4) | collective-permute-done | bytes 917536 | tf_op jit(solution)/shard_map/ppermute | solution.py:287
  54.4 0.9 copy-done.3
  55.4 5.4 %prepare.1.qt = bf16[21,256,256]{2,1,0:T(8,128)(2,1)} custom-call(s32[2,14]{1,0:T(2,128)} %pad_add_fusion.4.sel, bf16[256,1792]{1,0:T(8,128)(2,1)} %bitcast.19, bf16[256,1792]{1,0:T(8,128)(2,1)} %copy-done.3, bf16[256,896]{1,0:T(8,128)(2,1)} %bitcast.21), custom_call_target="tpu_custom_call" | custom-call | tf_op jit(solution)/shard_map/prepare/pallas_call | solution.py:54
  60.8 1.8 %copy-done = bf16[21,256,256]{2,1,0:T(8,128)(2,1)S(1)} copy-done((bf16[21,256,256]{2,1,0:T(8,128)(2,1)S(1)}, bf16[21,256,256]{2,1,0:T(8,128)(2,1)}, u32[]{:S(2)}) %copy-start) | copy-done | bytes 2752536
  62.5 2.4 %attend.3.refs_2_ = f32[56,8,256]{2,1,0:T(8,128)S(1)} custom-call(s32[4,16]{1,0:T(4,128)S(1)} %get-tuple-element.21.info, bf16[21,256,256]{2,1,0:T(8,128)(2,1)S(1)} %copy-done, bf16[20,256,128]{2,1,0:T(8,128)(2,1)S(1)} %copy-done.1), custom_call_target="tpu_custom_call" | custom-call | flops 2818572288 | bytes 1310720 | tf_op jit(solution)/shard_map/attend/pallas_call | solution.py:238
  65.1 1.1 slice.10
  66.3 2.7 %collective-permute-start.11 = (bf16[10,256,128]{2,1,0:T(8,128)(2,1)S(1)}, bf16[10,256,128]{2,1,0:T(8,128)(2,1)S(1)}, u32[]{:S(2)}, u32[]{:S(2)}) collective-permute-start(bf16[10,256,128]{2,1,0:T(8,128)(2,1)S(1)} %slice.10), channel_id=1, source_target_pairs={{0,3},{1,0},{2,1},{3,2},{4,7},{5,4},{6,5},{7,6},{8,11},{9,8},{10,9... | collective-permute-start | bytes 1966088 | tf_op jit(solution)/shard_map/ppermute | solution.py:315
  69.0 2.0 %attend.4.refs_2_ = f32[56,8,256]{2,1,0:T(8,128)S(1)} custom-call(s32[4,16]{1,0:T(4,128)S(1)} %get-tuple-element.20.info, bf16[21,256,256]{2,1,0:T(8,128)(2,1)S(1)} %copy-done, bf16[20,256,128]{2,1,0:T(8,128)(2,1)S(1)} %collective-permute-done.8.refs_0_, bf16[20,256,128]{2,1,0:T(8,128)(2,1)} %collective-permute-done.9.refs_1_, f32[56,8,256]{2,1,0:T(8,128)S(1)} %attend.3.refs_2_), custom_call_target="tpu_custom_call" | custom-call | flops 5637144576 | bytes 2621440 | tf_op jit(solution)/shard_map/attend/pallas_call | solution.py:238
  71.0 5.9 %collective-permute-done.10.refs_0_ = bf16[10,256,128]{2,1,0:T(8,128)(2,1)S(1)} collective-permute-done((bf16[10,256,128]{2,1,0:T(8,128)(2,1)S(1)}, bf16[10,256,128]{2,1,0:T(8,128)(2,1)S(1)}, u32[]{:S(2)}, u32[]{:S(2)}) %collective-permute-start.10) | collective-permute-done | bytes 655392 | tf_op jit(solution)/shard_map/ppermute | solution.py:314
  77.1 1.2 %attend.5 = f32[7,256]{1,0:T(8,128)S(1)} custom-call(s32[4,16]{1,0:T(4,128)S(1)} %get-tuple-element.22.info, bf16[21,256,256]{2,1,0:T(8,128)(2,1)S(1)} %copy-done, bf16[10,256,128]{2,1,0:T(8,128)(2,1)S(1)} %collective-permute-done.10.refs_0_, bf16[10,256,128]{2,1,0:T(8,128)(2,1)S(1)} %collective-permute-done.11.refs_1_, f32[56,8,256]{2,1,0:T(8,128)S(1)} %attend.4.refs_2_), custom_call_target="tpu_custom_call" | custom-call | flops 2818572288 | bytes 1310720 | tf_op jit(solution)/shard_map/attend/pallas_call | solution.py:238
  79.1 30.2 %all-to-all-start = ((f32[128,1,128]{2,1,0:T(1,128)}), f32[128,1,128]{2,1,0:T(1,128)S(1)}, u32[]{:S(2)}, u32[]{:S(2)}) async-start(f32[128,1,128]{2,1,0:T(1,128)} %broadcast_in_dim.23), calls=%async_computation | async-start | bytes 131072 | tf_op jit(solution)/shard_map/all_to_all | solution.py:322
  109.9 11.4 %all-to-all-done = f32[128,1,128]{2,1,0:T(1,128)S(1)} async-done(((f32[128,1,128]{2,1,0:T(1,128)}), f32[128,1,128]{2,1,0:T(1,128)S(1)}, u32[]{:S(2)}, u32[]{:S(2)}) %all-to-all-start) | async-done | bytes 65568 | tf_op jit(solution)/shard_map/all_to_all | solution.py:322
  (65 shorter events, 9.9 us)
Async XLA Ops:
  2.2 11.2 %collective-permute-start = (bf16[3,256,128]{2,1,0:T(8,128)(2,1)}, bf16[3,256,128]{2,1,0:T(8,128)(2,1)S(1)}, u32[]{:S(2)}, u32[]{:S(2)}) collective-permute-start(bf16[3,256,128]{2,1,0:T(8,128)(2,1)} %split_heads.1.refs_0_), channel_id=1, source_target_pairs={{0,16},{16,4},{4,20},{20,8},{8,24},{24,12},{12,28},{28,0},{1,17},{... | collective-permute-start | bytes 589832 | tf_op jit(solution)/shard_map/ppermute | solution.py:278
  4.7 9.4 %collective-permute-start.5 = (bf16[3,256,128]{2,1,0:T(8,128)(2,1)}, bf16[3,256,128]{2,1,0:T(8,128)(2,1)S(1)}, u32[]{:S(2)}, u32[]{:S(2)}) collective-permute-start(bf16[3,256,128]{2,1,0:T(8,128)(2,1)} %split_heads.1.refs_0_), channel_id=1, source_target_pairs={{0,28},{16,0},{4,16},{20,4},{8,20},{24,8},{12,24},{28,12},{1,29},{... | collective-permute-start | bytes 589832 | tf_op jit(solution)/shard_map/ppermute | solution.py:281
  13.4 17.9 %copy-start.4 = (bf16[3,256,128]{2,1,0:T(8,128)(2,1)}, bf16[3,256,128]{2,1,0:T(8,128)(2,1)S(1)}, u32[]{:S(2)}) copy-start(bf16[3,256,128]{2,1,0:T(8,128)(2,1)S(1)} %collective-permute-done.refs_1_) | copy-start | bytes 589828
  13.5 6.4 %collective-permute-start.1 = (bf16[3,256,128]{2,1,0:T(8,128)(2,1)S(1)}, bf16[3,256,128]{2,1,0:T(8,128)(2,1)S(1)}, u32[]{:S(2)}, u32[]{:S(2)}) collective-permute-start(bf16[3,256,128]{2,1,0:T(8,128)(2,1)S(1)} %collective-permute-done.refs_1_), channel_id=1, source_target_pairs={{0,16},{16,4},{4,20},{20,8},{8,24},{24,12},{12,28},{28,0},{1,17},{... | collective-permute-start | bytes 589832 | tf_op jit(solution)/shard_map/ppermute | solution.py:278
  14.1 17.2 %copy-start.5 = (bf16[3,256,128]{2,1,0:T(8,128)(2,1)}, bf16[3,256,128]{2,1,0:T(8,128)(2,1)S(1)}, u32[]{:S(2)}) copy-start(bf16[3,256,128]{2,1,0:T(8,128)(2,1)S(1)} %collective-permute-done.5.refs_7_) | copy-start | bytes 589828
  14.1 6.3 %collective-permute-start.6 = (bf16[3,256,128]{2,1,0:T(8,128)(2,1)S(1)}, bf16[3,256,128]{2,1,0:T(8,128)(2,1)S(1)}, u32[]{:S(2)}, u32[]{:S(2)}) collective-permute-start(bf16[3,256,128]{2,1,0:T(8,128)(2,1)S(1)} %collective-permute-done.5.refs_7_), channel_id=1, source_target_pairs={{0,28},{16,0},{4,16},{20,4},{8,20},{24,8},{12,24},{28,12},{1,29},{... | collective-permute-start | bytes 589832 | tf_op jit(solution)/shard_map/ppermute | solution.py:281
  19.9 11.5 %copy-start.6 = (bf16[3,256,128]{2,1,0:T(8,128)(2,1)}, bf16[3,256,128]{2,1,0:T(8,128)(2,1)S(1)}, u32[]{:S(2)}) copy-start(bf16[3,256,128]{2,1,0:T(8,128)(2,1)S(1)} %collective-permute-done.1.refs_2_) | copy-start | bytes 589828
  19.9 5.7 %collective-permute-start.2 = (bf16[3,256,128]{2,1,0:T(8,128)(2,1)S(1)}, bf16[3,256,128]{2,1,0:T(8,128)(2,1)S(1)}, u32[]{:S(2)}, u32[]{:S(2)}) collective-permute-start(bf16[3,256,128]{2,1,0:T(8,128)(2,1)S(1)} %collective-permute-done.1.refs_2_), channel_id=1, source_target_pairs={{0,16},{16,4},{4,20},{20,8},{8,24},{24,12},{12,28},{28,0},{1,17},{... | collective-permute-start | bytes 589832 | tf_op jit(solution)/shard_map/ppermute | solution.py:278
  20.5 10.9 %copy-start.7 = (bf16[3,256,128]{2,1,0:T(8,128)(2,1)}, bf16[3,256,128]{2,1,0:T(8,128)(2,1)S(1)}, u32[]{:S(2)}) copy-start(bf16[3,256,128]{2,1,0:T(8,128)(2,1)S(1)} %collective-permute-done.6.refs_6_) | copy-start | bytes 589828
  20.5 5.8 %collective-permute-start.7 = (bf16[3,256,128]{2,1,0:T(8,128)(2,1)S(1)}, bf16[3,256,128]{2,1,0:T(8,128)(2,1)S(1)}, u32[]{:S(2)}, u32[]{:S(2)}) collective-permute-start(bf16[3,256,128]{2,1,0:T(8,128)(2,1)S(1)} %collective-permute-done.6.refs_6_), channel_id=1, source_target_pairs={{0,28},{16,0},{4,16},{20,4},{8,20},{24,8},{12,24},{28,12},{1,29},{... | collective-permute-start | bytes 589832 | tf_op jit(solution)/shard_map/ppermute | solution.py:281
  25.6 5.8 %copy-start.8 = (bf16[3,256,128]{2,1,0:T(8,128)(2,1)}, bf16[3,256,128]{2,1,0:T(8,128)(2,1)S(1)}, u32[]{:S(2)}) copy-start(bf16[3,256,128]{2,1,0:T(8,128)(2,1)S(1)} %collective-permute-done.2.refs_3_) | copy-start | bytes 589828
  25.6 5.7 %collective-permute-start.3 = (bf16[3,256,128]{2,1,0:T(8,128)(2,1)S(1)}, bf16[3,256,128]{2,1,0:T(8,128)(2,1)S(1)}, u32[]{:S(2)}, u32[]{:S(2)}) collective-permute-start(bf16[3,256,128]{2,1,0:T(8,128)(2,1)S(1)} %collective-permute-done.2.refs_3_), channel_id=1, source_target_pairs={{0,16},{16,4},{4,20},{20,8},{8,24},{24,12},{12,28},{28,0},{1,17},{... | collective-permute-start | bytes 589832 | tf_op jit(solution)/shard_map/ppermute | solution.py:278
  26.2 5.1 %copy-start.9 = (bf16[3,256,128]{2,1,0:T(8,128)(2,1)}, bf16[3,256,128]{2,1,0:T(8,128)(2,1)S(1)}, u32[]{:S(2)}) copy-start(bf16[3,256,128]{2,1,0:T(8,128)(2,1)S(1)} %collective-permute-done.7.refs_5_) | copy-start | bytes 589828
  31.3 0.7 copy-start.10
  32.0 5.4 %copy-start.2 = (bf16[1,256,1792]{2,1,0:T(8,128)(2,1)S(1)}, bf16[1,256,1792]{2,1,0:T(8,128)(2,1)}, u32[]{:S(2)}) copy-start(bf16[1,256,1792]{2,1,0:T(8,128)(2,1)} %param.5) | copy-start | bytes 2752516
  34.6 30.3 %collective-permute-start.8 = (bf16[20,256,128]{2,1,0:T(8,128)(2,1)}, bf16[20,256,128]{2,1,0:T(8,128)(2,1)S(1)}, u32[]{:S(2)}, u32[]{:S(2)}) collective-permute-start(bf16[20,256,128]{2,1,0:T(8,128)(2,1)} %column.1.refs_0_), channel_id=1, source_target_pairs={{0,1},{1,2},{2,3},{3,0},{4,5},{5,6},{6,7},{7,4},{8,9},{9,10},{10,1... | collective-permute-start | bytes 3932168 | tf_op jit(solution)/shard_map/ppermute | solution.py:284
  35.9 29.1 %collective-permute-start.9 = (bf16[20,256,128]{2,1,0:T(8,128)(2,1)}, bf16[20,256,128]{2,1,0:T(8,128)(2,1)}, u32[]{:S(2)}, u32[]{:S(2)}) collective-permute-start(bf16[20,256,128]{2,1,0:T(8,128)(2,1)} %column.1.refs_0_), channel_id=1, source_target_pairs={{0,3},{1,0},{2,1},{3,2},{4,7},{5,4},{6,5},{7,6},{8,11},{9,8},{10,9... | collective-permute-start | bytes 3932168 | tf_op jit(solution)/shard_map/ppermute | solution.py:285
  37.4 17.1 %collective-permute-start.4 = (bf16[256,1792]{1,0:T(8,128)(2,1)S(1)}, bf16[256,1792]{1,0:T(8,128)(2,1)S(1)}, u32[]{:S(2)}, u32[]{:S(2)}) collective-permute-start(bf16[256,1792]{1,0:T(8,128)(2,1)S(1)} %bitcast.20), channel_id=1, source_target_pairs={{0,16},{16,0},{1,17},{17,1},{2,18},{18,2},{3,19},{19,3},{4,20},{20... | collective-permute-start | bytes 2752520 | tf_op jit(solution)/shard_map/ppermute | solution.py:287
  54.4 0.9 copy-start.3
  55.4 5.4 %copy-start.1 = (bf16[20,256,128]{2,1,0:T(8,128)(2,1)S(1)}, bf16[20,256,128]{2,1,0:T(8,128)(2,1)}, u32[]{:S(2)}) copy-start(bf16[20,256,128]{2,1,0:T(8,128)(2,1)} %column.1.refs_0_) | copy-start | bytes 3932164
  60.8 1.8 %copy-start = (bf16[21,256,256]{2,1,0:T(8,128)(2,1)S(1)}, bf16[21,256,256]{2,1,0:T(8,128)(2,1)}, u32[]{:S(2)}) copy-start(bf16[21,256,256]{2,1,0:T(8,128)(2,1)} %prepare.1.qt) | copy-start | bytes 8257540
  65.0 11.9 %collective-permute-start.10 = (bf16[10,256,128]{2,1,0:T(8,128)(2,1)S(1)}, bf16[10,256,128]{2,1,0:T(8,128)(2,1)S(1)}, u32[]{:S(2)}, u32[]{:S(2)}) collective-permute-start(bf16[10,256,128]{2,1,0:T(8,128)(2,1)S(1)} %slice.9), channel_id=1, source_target_pairs={{0,1},{1,2},{2,3},{3,0},{4,5},{5,6},{6,7},{7,4},{8,9},{9,10},{10,1... | collective-permute-start | bytes 1966088 | tf_op jit(solution)/shard_map/ppermute | solution.py:314
  66.3 10.8 %collective-permute-start.11 = (bf16[10,256,128]{2,1,0:T(8,128)(2,1)S(1)}, bf16[10,256,128]{2,1,0:T(8,128)(2,1)S(1)}, u32[]{:S(2)}, u32[]{:S(2)}) collective-permute-start(bf16[10,256,128]{2,1,0:T(8,128)(2,1)S(1)} %slice.10), channel_id=1, source_target_pairs={{0,3},{1,0},{2,1},{3,2},{4,7},{5,4},{6,5},{7,6},{8,11},{9,8},{10,9... | collective-permute-start | bytes 1966088 | tf_op jit(solution)/shard_map/ppermute | solution.py:315
  79.1 42.1 %all-to-all-start = ((f32[128,1,128]{2,1,0:T(1,128)}), f32[128,1,128]{2,1,0:T(1,128)S(1)}, u32[]{:S(2)}, u32[]{:S(2)}) async-start(f32[128,1,128]{2,1,0:T(1,128)} %broadcast_in_dim.23), calls=%async_computation | async-start | bytes 131072 | tf_op jit(solution)/shard_map/all_to_all | solution.py:322

commit v4 on v3

v4 whole, which is shorter than its diff:
```python
import functools
import math

import jax
import jax.numpy as jnp
from jax import lax
from jax.experimental import pallas as pl
from jax.experimental.pallas import tpu as pltpu
from jax.sharding import Mesh
from jax.sharding import PartitionSpec as P


HT = 28
KVT = 4
DH = 128
ROWS = 256
PAIRS = 14
STUDENTS = 7
HEADS = PAIRS + STUDENTS
GROUP = HT // KVT
KV = ("kv_0", "kv_1")
DP = ("dp_0", "dp_1")
LANE = 128
SUB = 8
MASKED = -1e30
LN2 = math.log(2.0)
KAPPA = 1.0 / (LN2 * math.sqrt(DH))
STATE = 3 * PAIRS + 2 * STUDENTS
TL, TC, SM, SL = PAIRS, 2 * PAIRS, 3 * PAIRS, 3 * PAIRS + STUDENTS
OWN = 3
OTHER = 2
CHUNK = OWN + OTHER
REST = 3 * CHUNK
SENT = 9
MIB = 1024 * 1024
SMEM = pl.BlockSpec(memory_space=pltpu.SMEM)
VMEM = pl.BlockSpec(memory_space=pltpu.VMEM)
ANY = pl.BlockSpec(memory_space=pl.ANY)


def heads_of(n):
    return jax.ShapeDtypeStruct((n, ROWS, DH), jnp.bfloat16)


def small(limit):
    return pltpu.CompilerParams(vmem_limit_bytes=limit * MIB)


def run_all(copies):
    for c in copies:
        c.start()
    for c in copies:
        c.wait()


def split_kernel(teacher, student, out):
    out[0] = teacher[:, :DH]
    out[1] = teacher[:, DH:]
    out[2] = student[...]


def split_heads(teacher, student):
    return pl.pallas_call(
        split_kernel,
        out_shape=heads_of(OWN),
        in_specs=[VMEM, VMEM],
        out_specs=VMEM,
        compiler_params=small(2),
        name="split_heads",
    )(teacher, student)


def queries_kernel(place, table, query, sent, more, sems):
    head = place[0, 0]
    theirs = (1 - head) * STUDENTS

    def each(act):
        rank = jnp.int32(0)
        for p in range(PAIRS):
            teacher = table[theirs + p // 2, p % 2]
            mine = lax.div(teacher, PAIRS) == head
            lanes = pl.ds(pl.multiple_of(lax.rem(teacher, PAIRS) * DH, DH), DH)

            @pl.when(jnp.logical_and(mine, rank < SENT))
            def _():
                act(pltpu.make_async_copy(query.at[:, lanes], sent.at[rank], sems.at[p]))

            @pl.when(jnp.logical_and(mine, rank >= SENT))
            def _():
                act(pltpu.make_async_copy(query.at[:, lanes], more.at[rank - SENT], sems.at[p]))

            rank = rank + mine.astype(jnp.int32)

    each(lambda c: c.start())
    each(lambda c: c.wait())


def queries_for_other(place, table, query):
    return pl.pallas_call(
        queries_kernel,
        out_shape=(heads_of(SENT), heads_of(PAIRS - SENT)),
        in_specs=[SMEM, SMEM, ANY],
        out_specs=(VMEM, VMEM),
        scratch_shapes=[pltpu.SemaphoreType.DMA((PAIRS,))],
        compiler_params=small(4),
        name="queries_for_other",
    )(place, table, query)


def own_chunk_kernel(place, own, ring_1, ring_7, out, sems):
    for head, pair in enumerate((ring_7, ring_1)):

        @pl.when(place[0, 0] == head)
        def _():
            run_all(
                [
                    pltpu.make_async_copy(own, out.at[pl.ds(0, OWN)], sems.at[0]),
                    pltpu.make_async_copy(
                        pair.at[pl.ds(0, OTHER)], out.at[pl.ds(OWN, OTHER)], sems.at[1]
                    ),
                ]
            )


def own_chunk(place, own, ring_1, ring_7):
    return pl.pallas_call(
        own_chunk_kernel,
        out_shape=heads_of(CHUNK),
        in_specs=[SMEM, ANY, ANY, ANY],
        out_specs=VMEM,
        scratch_shapes=[pltpu.SemaphoreType.DMA((2,))],
        compiler_params=small(2),
        name="own_chunk",
    )(place, own, ring_1, ring_7)


def rest_kernel(place, *refs):
    ring, out, sems = refs[:7], refs[7], refs[8]
    for head in range(2):

        @pl.when(place[0, 0] == head)
        def _():
            copies = []
            for m in range(1, 4):
                own = ring[2 * m - 1]
                other = ring[(2 * m - 1 + 2 * head) - 1]
                copies.append(
                    pltpu.make_async_copy(
                        own, out.at[pl.ds(OWN * (m - 1), OWN)], sems.at[m - 1]
                    )
                )
                copies.append(
                    pltpu.make_async_copy(
                        other.at[pl.ds(0, OTHER)],
                        out.at[pl.ds(3 * OWN + OTHER * (m - 1), OTHER)],
                        sems.at[m + 2],
                    )
                )
            run_all(copies)


def rest_of(place, ring):
    return pl.pallas_call(
        rest_kernel,
        out_shape=heads_of(REST),
        in_specs=[SMEM] + [ANY] * 7,
        out_specs=VMEM,
        scratch_shapes=[pltpu.SemaphoreType.DMA((6,))],
        compiler_params=small(4),
        name="rest_of",
    )(place, *ring)


def scaled(q):
    q = q.astype(jnp.float32) * KAPPA
    high = q.astype(jnp.bfloat16)
    low = (q - high.astype(jnp.float32)).astype(jnp.bfloat16)
    return jnp.concatenate([high, low], axis=1)


def fill_queries(place, table, own, sent, more, student, rows):
    head = place[0, 0]
    for s in range(STUDENTS):
        rows[PAIRS + s] = scaled(student[:, s * DH : (s + 1) * DH])
    rank = jnp.int32(0)
    for p in range(PAIRS):
        teacher = table[head * STUDENTS + p // 2, p % 2]
        mine = lax.div(teacher, PAIRS) == head
        lanes = pl.ds(pl.multiple_of(lax.rem(teacher, PAIRS) * DH, DH), DH)

        @pl.when(mine)
        def _():
            rows[p] = scaled(own[:, lanes])

        @pl.when(jnp.logical_and(jnp.logical_not(mine), rank < SENT))
        def _():
            rows[p] = scaled(sent[rank])

        @pl.when(jnp.logical_and(jnp.logical_not(mine), rank >= SENT))
        def _():
            rows[p] = scaled(more[rank - SENT])

        rank = rank + 1 - mine.astype(jnp.int32)


def attend_kernel(first, last, counts, blocks, place, table, plan, *refs):
    refs = list(refs)
    take = lambda n: [refs.pop(0) for _ in range(n)]
    groups = take(len(counts))
    if first:
        own, sent, more, student = take(4)
        state, rows = take(2)
    else:
        rows, before = take(2)
        if last:
            out, sums = take(2)
        else:
            (state,) = take(1)
    (keys,) = take(1)
    if last:
        (state,) = take(1)
    (sems,) = refs
    head, z_hi, x = place[0, 0], place[0, 1], place[0, 2]
    row_block = z_hi * 4 + x

    copies = []
    at = 0
    for g, n in enumerate(counts):
        copies.append(pltpu.make_async_copy(groups[g], keys.at[pl.ds(at, n)], sems.at[g]))
        at += n
    for c in copies:
        c.start()
    if first:
        for part, value in ((0, MASKED), (TL, 0.0), (TC, 0.0)):
            state[part : part + PAIRS] = jnp.full((PAIRS, SUB, ROWS), value, jnp.float32)
        for part, value in ((SM, MASKED), (SL, 0.0)):
            state[part : part + STUDENTS] = jnp.full((STUDENTS, SUB, ROWS), value, jnp.float32)
        fill_queries(place, table, own, sent, more, student, rows)
    else:
        state[...] = before[...]
    for c in copies:
        c.wait()

    def product(k, p):
        return lax.dot_general(
            jnp.concatenate([k, k], axis=1),
            rows[p],
            (((1,), (1,)), ((), ())),
            preferred_element_type=jnp.float32,
        )

    def update(logits, mask, m_index, l_index):
        if mask is not None:
            logits = jnp.where(mask, logits, MASKED)
        folded = logits.reshape(ROWS // SUB, SUB, ROWS)
        old = state[m_index]
        new = jnp.maximum(old, jnp.max(folded, axis=0))
        weights = jnp.exp2(folded - new[None])
        rescale = jnp.exp2(old - new)
        state[m_index] = new
        state[l_index] = state[l_index] * rescale + jnp.sum(weights, axis=0)
        return weights, rescale

    def block(own_at, other_at, masked):
        mask = None
        if masked:
            key_pos = lax.broadcasted_iota(jnp.int32, (ROWS, ROWS), 0)
            row_pos = lax.broadcasted_iota(jnp.int32, (ROWS, ROWS), 1)
            mask = key_pos <= row_pos
        student_keys = keys[own_at + 2]
        for s in range(STUDENTS):
            zs = product(student_keys, PAIRS + s)
            update(zs, mask, SM + s, SL + s)
            for c in range(2):
                p = 2 * s + c
                kv_head = lax.div(table[head * STUDENTS + s, c], GROUP)
                base = jnp.where(lax.div(kv_head, 2) == head, own_at, other_at)
                zt = product(keys[base + lax.rem(kv_head, 2)], p)
                weights, rescale = update(zt, mask, p, TL + p)
                gap = (zt - zs).reshape(ROWS // SUB, SUB, ROWS)
                state[TC + p] = state[TC + p] * rescale + jnp.sum(weights * gap, axis=0)

    def step(i, carry):
        chunk = lax.bitwise_and(z_hi - plan[0, i], 3)
        position = chunk * 4 + lax.bitwise_and(x + plan[1, i], 3)

        @pl.when(position < row_block)
        def _():
            block(plan[2, i], plan[3, i], False)

        if first:

            @pl.when(position == row_block)
            def _():
                block(plan[2, i], plan[3, i], True)

        return carry

    lax.fori_loop(0, blocks, step, 0)

    if not last:
        return

    def merged(m8, l8):
        top = jnp.max(m8, axis=0, keepdims=True)
        factor = jnp.exp2(m8 - top)
        total = jnp.sum(l8 * factor, axis=0, keepdims=True)
        return factor, total, LN2 * top + jnp.log(total)

    lane = lax.broadcasted_iota(jnp.int32, (1, LANE), 1)
    line = jnp.zeros((1, LANE), jnp.float32)
    for s in range(STUDENTS):
        _, _, s_lse = merged(state[SM + s], state[SL + s])
        value = 2.0 * s_lse
        for c in range(2):
            p = 2 * s + c
            factor, total, t_lse = merged(state[p], state[TL + p])
            cross = jnp.sum(state[TC + p] * factor, axis=0, keepdims=True)
            value = value + (LN2 * cross / total - t_lse)
        out[s : s + 1, :] = value
        line = jnp.where(lane == s, jnp.sum(value, axis=1, keepdims=True), line)
    sums[...] = jnp.broadcast_to(line, sums.shape)


def attend(place, table, plan, groups, queries=None, rows=None, state=None, copies_out=0):
    first = queries is not None
    last = copies_out > 0
    counts = tuple(g.shape[0] for g in groups)
    blocks = plan.shape[1]
    state_shape = jax.ShapeDtypeStruct((STATE, SUB, ROWS), jnp.float32)
    rows_shape = jax.ShapeDtypeStruct((HEADS, ROWS, 2 * DH), jnp.bfloat16)
    if first:
        extra, out_shape = list(queries), (state_shape, rows_shape)
    elif last:
        extra = [rows, state]
        out_shape = (
            jax.ShapeDtypeStruct((STUDENTS, ROWS), jnp.float32),
            jax.ShapeDtypeStruct((copies_out, LANE), jnp.float32),
        )
    else:
        extra, out_shape = [rows, state], state_shape
    scratch = [pltpu.VMEM((sum(counts), ROWS, DH), jnp.bfloat16)]
    if last:
        scratch.append(pltpu.VMEM(state_shape.shape, jnp.float32))
    scratch.append(pltpu.SemaphoreType.DMA((len(groups),)))
    return pl.pallas_call(
        functools.partial(attend_kernel, first, last, counts, blocks),
        out_shape=out_shape,
        in_specs=[SMEM] * 3 + [ANY] * len(groups) + [VMEM] * len(extra),
        out_specs=jax.tree.map(lambda _: VMEM, out_shape),
        scratch_shapes=scratch,
        compiler_params=small(24),
        cost_estimate=pl.CostEstimate(
            flops=blocks * HEADS * 2 * ROWS * ROWS * 2 * DH,
            bytes_accessed=blocks * ROWS * CHUNK * DH * 2,
            transcendentals=blocks * HEADS * ROWS * ROWS,
        ),
        name="attend",
    )(place, table, plan, *groups, *extra)


def shift(n, by):
    return [(i, (i + by) % n) for i in range(n)]


def z_place(ring):
    ring %= 8
    return (ring % 2) * 4 + ring // 2


def z_shift(by):
    return [(z_place(i), z_place(i + by)) for i in range(8)]


def plan_of(blocks):
    return jnp.array([list(row) for row in zip(*blocks)], jnp.int32)


def rest_blocks(by, base):
    return [
        (m, by, base + OWN * (m - 1), base + 3 * OWN + OTHER * (m - 1)) for m in range(1, 4)
    ]


def program(teacher_query, teacher_key, student_query, student_key, pair_table):
    head = lax.axis_index("head")
    place = jnp.stack([head, lax.axis_index("kv_0"), lax.axis_index("kv_1")])[None]

    along_x = lambda a, by: lax.ppermute(a, "kv_1", shift(4, by))
    along_z = lambda a, by: lax.ppermute(a, ("head", "kv_0"), z_shift(by))
    other_side = [(0, 1), (1, 0)]

    ring = {0: split_heads(teacher_key[0], student_key[0])}
    ring[1] = along_z(ring[0], 1)
    ring[7] = along_z(ring[0], -1)
    sent, more = queries_for_other(place, pair_table, teacher_query[0])
    sent, ring[1], ring[7] = lax.optimization_barrier((sent, ring[1], ring[7]))
    sent = lax.ppermute(sent, "head", other_side)
    mine = own_chunk(place, ring[0], ring[1], ring[7])
    near = [mine, along_x(mine, 1), along_x(mine, -1), along_x(mine, 2)]
    for step in range(2, 5):
        ring[step] = along_z(ring[step - 1], 1)
        if step < 4:
            ring[8 - step] = along_z(ring[9 - step], -1)
    my_pairs = lax.dynamic_slice_in_dim(pair_table, head * STUDENTS, STUDENTS, 0)
    count = jnp.sum((my_pairs // PAIRS != head).astype(jnp.int32))
    more = lax.cond(
        count > SENT, lambda q: lax.ppermute(q, "head", other_side), lambda q: q, more
    )

    rest = rest_of(place, [ring[o] for o in range(1, 8)])
    left, right = along_x(rest, 1), along_x(rest, -1)
    near_plan = [(0, by, CHUNK * n, CHUNK * n + OWN) for n, by in enumerate((0, -1, 1, 2))]
    state, rows = attend(
        place,
        pair_table,
        plan_of(near_plan + rest_blocks(0, 4 * CHUNK)),
        near + [rest],
        queries=(teacher_query[0], sent, more, student_query[0]),
    )
    left, right, state = lax.optimization_barrier((left, right, state))
    cut = (REST + 1) // 2
    far = [along_x(left[:cut], 1), along_x(right[cut:], -1)]
    state = attend(
        place,
        pair_table,
        plan_of(rest_blocks(-1, 0) + rest_blocks(1, REST)),
        [left, right],
        rows=rows,
        state=state,
    )
    everyone = ("dp_0", "dp_1", "kv_0", "kv_1")
    devices = lax.axis_size(everyone)
    kl, sums = attend(
        place,
        pair_table,
        plan_of(rest_blocks(2, 0)),
        far,
        rows=rows,
        state=state,
        copies_out=devices,
    )
    terms = lax.all_to_all(sums, everyone, 0, 0, tiled=True)
    head_loss = jnp.sum(terms, axis=0)[:STUDENTS] / (devices * ROWS)
    return (kl[None], head_loss)


def solution(mesh):
    split = Mesh(
        mesh.devices.reshape(4, 2, mesh.shape["head"], 4, 4),
        ("dp_0", "dp_1", "head", "kv_0", "kv_1"),
    )
    in_specs = (P(DP, KV, "head"), P(DP, KV, "head"), P(DP, KV, "head"), P(DP, KV, "head"), P())
    out_specs = (P(DP, "head", KV), P("head"))
    return jax.shard_map(
        program, mesh=split, in_specs=in_specs, out_specs=out_specs, check_vma=False
    )
```

time: 122 us -> 132 us (1.082)
  starting transfers between devices: 47.4 us -> 55.4 us
  waiting for transfers between devices: 44.9 us -> 50.7 us
  other arithmetic: 4.79 us -> 2.14 us
    ppermute x12 -> x15, starting transfers between devices: 17.3 us -> 28.2 us  [the longest x7 16.4 us: program(): along_x = lambda a, by: lax.ppermute(a, 'kv_1', shift(4, by))]
    ppermute x12 -> x15, waiting for transfers between devices: 33.5 us -> 39.4 us  [the longest x7 28.8 us: program(): along_x = lambda a, by: lax.ppermute(a, 'kv_1', shift(4, by))]
    all_to_all x1, starting transfers between devices: 30.2 us -> 27.2 us  [program(): terms = lax.all_to_all(sums, everyone, 0, 0, tiled=True)]
    another operation x6 -> x0, local copies, waits for them, and re-layouts: 1.93 us -> none  [info(): jnp.stack([jnp.full((16,), z_hi * 4 + x, jnp.int32), jnp.concatenate([slo...]
    reduce_sum x2, other arithmetic: 0.15 us -> 1.55 us  [the longest x1 1.4 us: program(): count = jnp.sum((my_pairs // PAIRS != head).astype(jnp.int32))]
    unnamed x23 -> x18, local copies, waits for them, and re-layouts: 3.98 us -> 5.32 us
    pallas_call x6 -> x7, Pallas kernels: 15.2 us -> 14 us  [the longest x3 9.04 us: attend(): pl.pallas_call(functools.partial(attend_kernel, first, last, counts, bloc...]
  transfers between devices with their start and end apart: 13 -> 16, of which waited for: 8 -> 8; matrix products, arithmetic and copies ran while one was open for 7% -> 3% of each run, Pallas kernels for 8% -> 9%
where the time goes in v4:
time: 132 us; the launch traced here: 131 us
  starting transfers between devices  55.4 us (42%)
  waiting for transfers between devices  50.7 us (38%)
  Pallas kernels  14 us (11%)
  local copies, waits for them, and re-layouts  7.45 us (6%)
  other arithmetic  2.14 us (2%)
  between operations  1.44 us (1%)
    ppermute x7, waiting for transfers between devices, program(): along_x = lambda a, by: lax.ppermute(a, 'kv_1', shift(4, by))  28.8 us
    all_to_all x1, starting transfers between devices, program(): terms = lax.all_to_all(sums, everyone, 0, 0, tiled=True)  27.2 us
    ppermute x7, starting transfers between devices, program(): along_x = lambda a, by: lax.ppermute(a, 'kv_1', shift(4, by))  16.4 us
    ppermute x7, starting transfers between devices, program(): along_z = lambda a, by: lax.ppermute(a, ('head', 'kv_0'), z_shift(by))  11.8 us
    all_to_all x1, waiting for transfers between devices, program(): terms = lax.all_to_all(sums, everyone, 0, 0, tiled=True)  11.2 us
    ppermute x7, waiting for transfers between devices, program(): along_z = lambda a, by: lax.ppermute(a, ('head', 'kv_0'), z_shift(by))  10.6 us
    pallas_call x3, Pallas kernels, attend(): pl.pallas_call(functools.partial(attend_kernel, first, last, counts, bloc...  9.04 us
    unnamed x18, local copies, waits for them, and re-layouts  5.32 us
  transfers between devices with their start and end apart: 16, of which 8 were waited for; matrix products, arithmetic and copies ran while one was open for 3% of the time, Pallas kernels for 9%

profile of v4, /device:TPU:1, one launch (start us, length us, event | category | flops | bytes accessed | tf_op | source)
XLA Modules:
  0.0 131.1 jit_solution(3042195954892301034)
XLA Ops:
  2.4 6.5 %collective-permute-start.2 = (bf16[3,256,128]{2,1,0:T(8,128)(2,1)S(1)}, bf16[3,256,128]{2,1,0:T(8,128)(2,1)S(1)}, u32[]{:S(2)}, u32[]{:S(2)}) collective-permute-start(bf16[3,256,128]{2,1,0:T(8,128)(2,1)S(1)} %split_heads.1.own), channel_id=1, source_target_pairs={{0,28},{16,0},{4,16},{20,4},{8,20},{24,8},{12,24},{28,12},{1,29},{... | collective-permute-start | bytes 589832 | tf_op jit(solution)/shard_map/ppermute | solution.py:390
  9.7 1.2 copy-done
  10.9 2.1 %queries_for_other.1 = (bf16[9,256,128]{2,1,0:T(8,128)(2,1)S(1)}, bf16[5,256,128]{2,1,0:T(8,128)(2,1)}) custom-call(s32[1,3]{1,0:T(1,128)S(1)} %add_bitcast_fusion.place, s32[14,2]{1,0:T(8,128)S(1)} %copy.18.table, bf16[256,1792]{1,0:T(8,128)(2,1)S(1)} %bitcast.13), custom_call_target="tpu_custom_call" | custom-call | tf_op jit(solution)/shard_map/queries_for_other/pallas_call | solution.py:99
  13.0 2.6 %collective-permute-done.1.refs_0_.ring_1 = bf16[3,256,128]{2,1,0:T(8,128)(2,1)S(1)} collective-permute-done((bf16[3,256,128]{2,1,0:T(8,128)(2,1)S(1)}, bf16[3,256,128]{2,1,0:T(8,128)(2,1)S(1)}, u32[]{:S(2)}, u32[]{:S(2)}) %collective-permute-start.1) | collective-permute-done | bytes 196640 | tf_op jit(solution)/shard_map/ppermute | solution.py:390
  15.6 2.7 %collective-permute-start.6 = (bf16[3,256,128]{2,1,0:T(8,128)(2,1)S(1)}, bf16[3,256,128]{2,1,0:T(8,128)(2,1)S(1)}, u32[]{:S(2)}, u32[]{:S(2)}) collective-permute-start(bf16[3,256,128]{2,1,0:T(8,128)(2,1)S(1)} %collective-permute-done.2.refs_6_.ring_7), channel_id=1, source_target_pairs={{0,28},{16,0},{4,16},{20,4},{8,20},{24,8},{12,24},{28,12},{1,29},{... | collective-permute-start | bytes 589832 | tf_op jit(solution)/shard_map/ppermute | solution.py:390
  18.3 3.1 %collective-permute-done.3.refs_1_ = bf16[3,256,128]{2,1,0:T(8,128)(2,1)S(1)} collective-permute-done((bf16[3,256,128]{2,1,0:T(8,128)(2,1)S(1)}, bf16[3,256,128]{2,1,0:T(8,128)(2,1)S(1)}, u32[]{:S(2)}, u32[]{:S(2)}) %collective-permute-start.3) | collective-permute-done | bytes 196640 | tf_op jit(solution)/shard_map/ppermute | solution.py:390
  21.4 2.7 %collective-permute-start.7 = (bf16[3,256,128]{2,1,0:T(8,128)(2,1)S(1)}, bf16[3,256,128]{2,1,0:T(8,128)(2,1)S(1)}, u32[]{:S(2)}, u32[]{:S(2)}) collective-permute-start(bf16[3,256,128]{2,1,0:T(8,128)(2,1)S(1)} %collective-permute-done.6.refs_5_), channel_id=1, source_target_pairs={{0,28},{16,0},{4,16},{20,4},{8,20},{24,8},{12,24},{28,12},{1,29},{... | collective-permute-start | bytes 589832 | tf_op jit(solution)/shard_map/ppermute | solution.py:390
  24.0 3.0 %collective-permute-done.4.refs_2_ = bf16[3,256,128]{2,1,0:T(8,128)(2,1)S(1)} collective-permute-done((bf16[3,256,128]{2,1,0:T(8,128)(2,1)S(1)}, bf16[3,256,128]{2,1,0:T(8,128)(2,1)S(1)}, u32[]{:S(2)}, u32[]{:S(2)}) %collective-permute-start.4) | collective-permute-done | bytes 196640 | tf_op jit(solution)/shard_map/ppermute | solution.py:390
  28.1 2.8 %collective-permute-start.12 = (bf16[5,256,128]{2,1,0:T(8,128)(2,1)S(1)}, bf16[5,256,128]{2,1,0:T(8,128)(2,1)S(1)}, u32[]{:S(2)}, u32[]{:S(2)}) collective-permute-start(bf16[5,256,128]{2,1,0:T(8,128)(2,1)S(1)} %own_chunk.1.refs_0_), channel_id=1, source_target_pairs={{0,2},{1,3},{2,0},{3,1},{4,6},{5,7},{6,4},{7,5},{8,10},{9,11},{10,... | collective-permute-start | bytes 983048 | tf_op jit(solution)/shard_map/ppermute | solution.py:389
  30.9 1.9 %collective-permute-done.5.refs_3_ = bf16[3,256,128]{2,1,0:T(8,128)(2,1)S(1)} collective-permute-done((bf16[3,256,128]{2,1,0:T(8,128)(2,1)S(1)}, bf16[3,256,128]{2,1,0:T(8,128)(2,1)S(1)}, u32[]{:S(2)}, u32[]{:S(2)}) %collective-permute-start.5) | collective-permute-done | bytes 196640 | tf_op jit(solution)/shard_map/ppermute | solution.py:390
  32.8 1.9 %rest_of.1.refs_4_ = bf16[15,256,128]{2,1,0:T(8,128)(2,1)S(1)} custom-call(s32[1,3]{1,0:T(1,128)S(1)} %add_bitcast_fusion.place, bf16[3,256,128]{2,1,0:T(8,128)(2,1)S(1)} %collective-permute-done.1.refs_0_.ring_1, bf16[3,256,128]{2,1,0:T(8,128)(2,1)S(1)} %collective-permute-done.3.refs_1_, bf16[3,256,128]{2,1,0:T(8,128)(2,1)S(1)} %collective-permute-done.4.refs_2_, ...), custom_call_target="tpu_custom_call" | custom-call | tf_op jit(solution)/shard_map/rest_of/pallas_call | solution.py:163
  34.7 2.6 %collective-permute-start.9 = (bf16[15,256,128]{2,1,0:T(8,128)(2,1)S(1)}, bf16[15,256,128]{2,1,0:T(8,128)(2,1)}, u32[]{:S(2)}, u32[]{:S(2)}) collective-permute-start(bf16[15,256,128]{2,1,0:T(8,128)(2,1)S(1)} %rest_of.1.refs_4_), channel_id=1, source_target_pairs={{0,3},{1,0},{2,1},{3,2},{4,7},{5,4},{6,5},{7,6},{8,11},{9,8},{10,9... | collective-permute-start | bytes 2949128 | tf_op jit(solution)/shard_map/ppermute | solution.py:389
  37.3 1.4 %fusion = s32[]{:T(128)} fusion(s32[14,2]{0,1:T(2,128)} %param.14, s32[]{:T(128)S(6)} %select_n.8, s32[]{:T(128)} %axis_index.33), kind=kLoop, calls=%fused_computation.2 | loop fusion | flops 153 | bytes 68 | tf_op jit(solution)/shard_map/reduce_sum | solution.py:406
  39.3 2.8 %collective-permute-start.11 = (bf16[5,256,128]{2,1,0:T(8,128)(2,1)S(1)}, bf16[5,256,128]{2,1,0:T(8,128)(2,1)S(1)}, u32[]{:S(2)}, u32[]{:S(2)}) collective-permute-start(bf16[5,256,128]{2,1,0:T(8,128)(2,1)S(1)} %own_chunk.1.refs_0_), channel_id=1, source_target_pairs={{0,3},{1,0},{2,1},{3,2},{4,7},{5,4},{6,5},{7,6},{8,11},{9,8},{10,9... | collective-permute-start | bytes 983048 | tf_op jit(solution)/shard_map/ppermute | solution.py:389
  42.1 23.6 %collective-permute-done.11.refs_2_ = bf16[5,256,128]{2,1,0:T(8,128)(2,1)S(1)} collective-permute-done((bf16[5,256,128]{2,1,0:T(8,128)(2,1)S(1)}, bf16[5,256,128]{2,1,0:T(8,128)(2,1)S(1)}, u32[]{:S(2)}, u32[]{:S(2)}) %collective-permute-start.11) | collective-permute-done | bytes 327712 | tf_op jit(solution)/shard_map/ppermute | solution.py:389
  66.7 4.8 %attend.3 = (f32[56,8,256]{2,1,0:T(8,128)S(1)}, bf16[21,256,256]{2,1,0:T(8,128)(2,1)S(1)}) custom-call(s32[1,3]{1,0:T(1,128)S(1)} %add_bitcast_fusion.place, s32[14,2]{1,0:T(8,128)S(1)} %copy.18.table, s32[4,7]{1,0:T(4,128)S(1)} %copy-done.7, bf16[5,256,128]{2,1,0:T(8,128)(2,1)S(1)} %own_chunk.1.refs_0_, ...), custom_call_target="tpu_custom_call" | custom-call | flops 4932501504 | bytes 2293760 | tf_op jit(solution)/shard_map/attend/pallas_call | solution.py:346
  72.7 3.2 %collective-permute-start.14 = (bf16[8,256,128]{2,1,0:T(8,128)(2,1)S(1)}, bf16[8,256,128]{2,1,0:T(8,128)(2,1)S(1)}, u32[]{:S(2)}, u32[]{:S(2)}) collective-permute-start(bf16[8,256,128]{2,1,0:T(8,128)(2,1)S(1)} %slice.9), channel_id=1, source_target_pairs={{0,1},{1,2},{2,3},{3,0},{4,5},{5,6},{6,7},{7,4},{8,9},{9,10},{10,1... | collective-permute-start | bytes 1572872 | tf_op jit(solution)/shard_map/ppermute | solution.py:389
  77.0 5.0 %collective-permute-start.15 = (bf16[7,256,128]{2,1,0:T(8,128)(2,1)S(1)}, bf16[7,256,128]{2,1,0:T(8,128)(2,1)S(1)}, u32[]{:S(2)}, u32[]{:S(2)}) collective-permute-start(bf16[7,256,128]{2,1,0:T(8,128)(2,1)S(1)} %slice.10), channel_id=1, source_target_pairs={{0,3},{1,0},{2,1},{3,2},{4,7},{5,4},{6,5},{7,6},{8,11},{9,8},{10,9... | collective-permute-start | bytes 1376264 | tf_op jit(solution)/shard_map/ppermute | solution.py:389
  82.0 2.2 %attend.4.refs_3_ = f32[56,8,256]{2,1,0:T(8,128)S(1)} custom-call(s32[1,3]{1,0:T(1,128)S(1)} %add_bitcast_fusion.place, s32[14,2]{1,0:T(8,128)S(1)} %copy.18.table, s32[4,6]{1,0:T(4,128)S(1)} %copy-done.6, bf16[15,256,128]{2,1,0:T(8,128)(2,1)} %collective-permute-done.8.refs_0_, bf16[15,256,128]{2,1,0:T(8,128)(2,1)} %collective-permute-done.9.refs_1_, ...), custom_call_target="tpu_custom_call" | custom-call | flops 4227858432 | bytes 1966080 | tf_op jit(solution)/shard_map/attend/pallas_call | solution.py:346
  84.2 3.9 %collective-permute-done.15.refs_1_ = bf16[7,256,128]{2,1,0:T(8,128)(2,1)S(1)} collective-permute-done((bf16[7,256,128]{2,1,0:T(8,128)(2,1)S(1)}, bf16[7,256,128]{2,1,0:T(8,128)(2,1)S(1)}, u32[]{:S(2)}, u32[]{:S(2)}) %collective-permute-start.15) | collective-permute-done | bytes 458784 | tf_op jit(solution)/shard_map/ppermute | solution.py:389
  88.1 1.3 collective-permute-done.14.refs_0_
  89.4 2.0 %attend.5 = (f32[7,256]{1,0:T(8,128)S(1)}, f32[128,128]{1,0:T(8,128)}) custom-call(s32[1,3]{1,0:T(1,128)S(1)} %add_bitcast_fusion.place, s32[14,2]{1,0:T(8,128)S(1)} %copy.18.table, s32[4,3]{1,0:T(4,128)S(1)} %copy-done.5, bf16[8,256,128]{2,1,0:T(8,128)(2,1)S(1)} %collective-permute-done.14.refs_0_, ...), custom_call_target="tpu_custom_call" | custom-call | flops 2113929216 | bytes 983040 | tf_op jit(solution)/shard_map/attend/pallas_call | solution.py:346
  91.4 27.2 %all-to-all-start = ((f32[128,1,128]{2,1,0:T(1,128)}), f32[128,1,128]{2,1,0:T(1,128)S(1)}, u32[]{:S(2)}, u32[]{:S(2)}) async-start(f32[128,1,128]{2,1,0:T(1,128)} %bitcast.10), calls=%async_computation | async-start | bytes 131072 | tf_op jit(solution)/shard_map/all_to_all | solution.py:443
  119.2 11.2 %all-to-all-done = f32[128,1,128]{2,1,0:T(1,128)S(1)} async-done(((f32[128,1,128]{2,1,0:T(1,128)}), f32[128,1,128]{2,1,0:T(1,128)S(1)}, u32[]{:S(2)}, u32[]{:S(2)}) %all-to-all-start) | async-done | bytes 65568 | tf_op jit(solution)/shard_map/all_to_all | solution.py:443
  (40 shorter events, 8.1 us)
Async XLA Ops:
  0.6 65.0 %copy-start.7 = (s32[4,7]{1,0:T(4,128)S(1)}, s32[4,7]{1,0:T(4,128)}, u32[]{:S(2)}) copy-start(s32[4,7]{1,0:T(4,128)} %constant.40.clone.plan) | copy-start | bytes 340
  0.6 0.9 copy-start.2
  1.6 0.8 copy-start.3
  2.4 10.6 %collective-permute-start.2 = (bf16[3,256,128]{2,1,0:T(8,128)(2,1)S(1)}, bf16[3,256,128]{2,1,0:T(8,128)(2,1)S(1)}, u32[]{:S(2)}, u32[]{:S(2)}) collective-permute-start(bf16[3,256,128]{2,1,0:T(8,128)(2,1)S(1)} %split_heads.1.own), channel_id=1, source_target_pairs={{0,28},{16,0},{4,16},{20,4},{8,20},{24,8},{12,24},{28,12},{1,29},{... | collective-permute-start | bytes 589832 | tf_op jit(solution)/shard_map/ppermute | solution.py:390
  8.9 6.7 %collective-permute-start.1 = (bf16[3,256,128]{2,1,0:T(8,128)(2,1)S(1)}, bf16[3,256,128]{2,1,0:T(8,128)(2,1)S(1)}, u32[]{:S(2)}, u32[]{:S(2)}) collective-permute-start(bf16[3,256,128]{2,1,0:T(8,128)(2,1)S(1)} %split_heads.1.own), channel_id=1, source_target_pairs={{0,16},{16,4},{4,20},{20,8},{8,24},{24,12},{12,28},{28,0},{1,17},{... | collective-permute-start | bytes 589832 | tf_op jit(solution)/shard_map/ppermute | solution.py:390
  9.7 1.2 copy-start
  10.9 54.8 %copy-start.1 = (bf16[1,256,1792]{2,1,0:T(8,128)(2,1)S(1)}, bf16[1,256,1792]{2,1,0:T(8,128)(2,1)}, u32[]{:S(2)}) copy-start(bf16[1,256,1792]{2,1,0:T(8,128)(2,1)} %param.10) | copy-start | bytes 2752516
  15.6 5.7 %collective-permute-start.3 = (bf16[3,256,128]{2,1,0:T(8,128)(2,1)S(1)}, bf16[3,256,128]{2,1,0:T(8,128)(2,1)S(1)}, u32[]{:S(2)}, u32[]{:S(2)}) collective-permute-start(bf16[3,256,128]{2,1,0:T(8,128)(2,1)S(1)} %collective-permute-done.1.refs_0_.ring_1), channel_id=1, source_target_pairs={{0,16},{16,4},{4,20},{20,8},{8,24},{24,12},{12,28},{28,0},{1,17},{... | collective-permute-start | bytes 589832 | tf_op jit(solution)/shard_map/ppermute | solution.py:390
  15.6 5.7 %collective-permute-start.6 = (bf16[3,256,128]{2,1,0:T(8,128)(2,1)S(1)}, bf16[3,256,128]{2,1,0:T(8,128)(2,1)S(1)}, u32[]{:S(2)}, u32[]{:S(2)}) collective-permute-start(bf16[3,256,128]{2,1,0:T(8,128)(2,1)S(1)} %collective-permute-done.2.refs_6_.ring_7), channel_id=1, source_target_pairs={{0,28},{16,0},{4,16},{20,4},{8,20},{24,8},{12,24},{28,12},{1,29},{... | collective-permute-start | bytes 589832 | tf_op jit(solution)/shard_map/ppermute | solution.py:390
  21.3 5.7 %collective-permute-start.4 = (bf16[3,256,128]{2,1,0:T(8,128)(2,1)S(1)}, bf16[3,256,128]{2,1,0:T(8,128)(2,1)S(1)}, u32[]{:S(2)}, u32[]{:S(2)}) collective-permute-start(bf16[3,256,128]{2,1,0:T(8,128)(2,1)S(1)} %collective-permute-done.3.refs_1_), channel_id=1, source_target_pairs={{0,16},{16,4},{4,20},{20,8},{8,24},{24,12},{12,28},{28,0},{1,17},{... | collective-permute-start | bytes 589832 | tf_op jit(solution)/shard_map/ppermute | solution.py:390
  21.4 9.6 %collective-permute-start.7 = (bf16[3,256,128]{2,1,0:T(8,128)(2,1)S(1)}, bf16[3,256,128]{2,1,0:T(8,128)(2,1)S(1)}, u32[]{:S(2)}, u32[]{:S(2)}) collective-permute-start(bf16[3,256,128]{2,1,0:T(8,128)(2,1)S(1)} %collective-permute-done.6.refs_5_), channel_id=1, source_target_pairs={{0,28},{16,0},{4,16},{20,4},{8,20},{24,8},{12,24},{28,12},{1,29},{... | collective-permute-start | bytes 589832 | tf_op jit(solution)/shard_map/ppermute | solution.py:390
  27.1 5.7 %collective-permute-start.5 = (bf16[3,256,128]{2,1,0:T(8,128)(2,1)S(1)}, bf16[3,256,128]{2,1,0:T(8,128)(2,1)S(1)}, u32[]{:S(2)}, u32[]{:S(2)}) collective-permute-start(bf16[3,256,128]{2,1,0:T(8,128)(2,1)S(1)} %collective-permute-done.4.refs_2_), channel_id=1, source_target_pairs={{0,16},{16,4},{4,20},{20,8},{8,24},{24,12},{12,28},{28,0},{1,17},{... | collective-permute-start | bytes 589832 | tf_op jit(solution)/shard_map/ppermute | solution.py:390
  28.1 14.0 %collective-permute-start.12 = (bf16[5,256,128]{2,1,0:T(8,128)(2,1)S(1)}, bf16[5,256,128]{2,1,0:T(8,128)(2,1)S(1)}, u32[]{:S(2)}, u32[]{:S(2)}) collective-permute-start(bf16[5,256,128]{2,1,0:T(8,128)(2,1)S(1)} %own_chunk.1.refs_0_), channel_id=1, source_target_pairs={{0,2},{1,3},{2,0},{3,1},{4,6},{5,7},{6,4},{7,5},{8,10},{9,11},{10,... | collective-permute-start | bytes 983048 | tf_op jit(solution)/shard_map/ppermute | solution.py:389
  30.9 34.8 %collective-permute-start.13 = (bf16[9,256,128]{2,1,0:T(8,128)(2,1)S(1)}, bf16[9,256,128]{2,1,0:T(8,128)(2,1)}, u32[]{:S(2)}, u32[]{:S(2)}) collective-permute-start(bf16[9,256,128]{2,1,0:T(8,128)(2,1)S(1)} %get-tuple-element.22), channel_id=1, source_target_pairs={{0,16},{16,0},{1,17},{17,1},{2,18},{18,2},{3,19},{19,3},{4,20},{20... | collective-permute-start | bytes 1769480 | tf_op jit(solution)/shard_map/ppermute | solution.py:398
  34.7 36.9 %collective-permute-start.9 = (bf16[15,256,128]{2,1,0:T(8,128)(2,1)S(1)}, bf16[15,256,128]{2,1,0:T(8,128)(2,1)}, u32[]{:S(2)}, u32[]{:S(2)}) collective-permute-start(bf16[15,256,128]{2,1,0:T(8,128)(2,1)S(1)} %rest_of.1.refs_4_), channel_id=1, source_target_pairs={{0,3},{1,0},{2,1},{3,2},{4,7},{5,4},{6,5},{7,6},{8,11},{9,8},{10,9... | collective-permute-start | bytes 2949128 | tf_op jit(solution)/shard_map/ppermute | solution.py:389
  37.3 34.3 %collective-permute-start.8 = (bf16[15,256,128]{2,1,0:T(8,128)(2,1)S(1)}, bf16[15,256,128]{2,1,0:T(8,128)(2,1)}, u32[]{:S(2)}, u32[]{:S(2)}) collective-permute-start(bf16[15,256,128]{2,1,0:T(8,128)(2,1)S(1)} %rest_of.1.refs_4_), channel_id=1, source_target_pairs={{0,1},{1,2},{2,3},{3,0},{4,5},{5,6},{6,7},{7,4},{8,9},{9,10},{10,1... | collective-permute-start | bytes 2949128 | tf_op jit(solution)/shard_map/ppermute | solution.py:389
  39.3 26.4 %collective-permute-start.11 = (bf16[5,256,128]{2,1,0:T(8,128)(2,1)S(1)}, bf16[5,256,128]{2,1,0:T(8,128)(2,1)S(1)}, u32[]{:S(2)}, u32[]{:S(2)}) collective-permute-start(bf16[5,256,128]{2,1,0:T(8,128)(2,1)S(1)} %own_chunk.1.refs_0_), channel_id=1, source_target_pairs={{0,3},{1,0},{2,1},{3,2},{4,7},{5,4},{6,5},{7,6},{8,11},{9,8},{10,9... | collective-permute-start | bytes 983048 | tf_op jit(solution)/shard_map/ppermute | solution.py:389
  42.1 23.6 %collective-permute-start.10 = (bf16[5,256,128]{2,1,0:T(8,128)(2,1)S(1)}, bf16[5,256,128]{2,1,0:T(8,128)(2,1)S(1)}, u32[]{:S(2)}, u32[]{:S(2)}) collective-permute-start(bf16[5,256,128]{2,1,0:T(8,128)(2,1)S(1)} %own_chunk.1.refs_0_), channel_id=1, source_target_pairs={{0,1},{1,2},{2,3},{3,0},{4,5},{5,6},{6,7},{7,4},{8,9},{9,10},{10,1... | collective-permute-start | bytes 983048 | tf_op jit(solution)/shard_map/ppermute | solution.py:389
  65.7 1.0 copy-start.4
  66.7 15.3 %copy-start.6 = (s32[4,6]{1,0:T(4,128)S(1)}, s32[4,6]{1,0:T(4,128)}, u32[]{:S(2)}) copy-start(s32[4,6]{1,0:T(4,128)} %constant.41.clone.plan) | copy-start | bytes 292
  72.7 16.7 %collective-permute-start.14 = (bf16[8,256,128]{2,1,0:T(8,128)(2,1)S(1)}, bf16[8,256,128]{2,1,0:T(8,128)(2,1)S(1)}, u32[]{:S(2)}, u32[]{:S(2)}) collective-permute-start(bf16[8,256,128]{2,1,0:T(8,128)(2,1)S(1)} %slice.9), channel_id=1, source_target_pairs={{0,1},{1,2},{2,3},{3,0},{4,5},{5,6},{6,7},{7,4},{8,9},{9,10},{10,1... | collective-permute-start | bytes 1572872 | tf_op jit(solution)/shard_map/ppermute | solution.py:389
  77.0 11.2 %collective-permute-start.15 = (bf16[7,256,128]{2,1,0:T(8,128)(2,1)S(1)}, bf16[7,256,128]{2,1,0:T(8,128)(2,1)S(1)}, u32[]{:S(2)}, u32[]{:S(2)}) collective-permute-start(bf16[7,256,128]{2,1,0:T(8,128)(2,1)S(1)} %slice.10), channel_id=1, source_target_pairs={{0,3},{1,0},{2,1},{3,2},{4,7},{5,4},{6,5},{7,6},{8,11},{9,8},{10,9... | collective-permute-start | bytes 1376264 | tf_op jit(solution)/shard_map/ppermute | solution.py:389
  82.0 7.4 %copy-start.5 = (s32[4,3]{1,0:T(4,128)S(1)}, s32[4,3]{1,0:T(4,128)}, u32[]{:S(2)}) copy-start(s32[4,3]{1,0:T(4,128)} %constant.42.clone.plan) | copy-start | bytes 148
  91.4 39.1 %all-to-all-start = ((f32[128,1,128]{2,1,0:T(1,128)}), f32[128,1,128]{2,1,0:T(1,128)S(1)}, u32[]{:S(2)}, u32[]{:S(2)}) async-start(f32[128,1,128]{2,1,0:T(1,128)} %bitcast.10), calls=%async_computation | async-start | bytes 131072 | tf_op jit(solution)/shard_map/all_to_all | solution.py:443

commit v5 on v4

--- a/solution.py
+++ b/solution.py
@@ -30,12 +30,12 @@
 OWN = 3
 OTHER = 2
 CHUNK = OWN + OTHER
-REST = 3 * CHUNK
 SENT = 9
 MIB = 1024 * 1024
 SMEM = pl.BlockSpec(memory_space=pltpu.SMEM)
 VMEM = pl.BlockSpec(memory_space=pltpu.VMEM)
 ANY = pl.BlockSpec(memory_space=pl.ANY)
+HBM = pl.BlockSpec(memory_space=pltpu.HBM)
 
 
 def heads_of(n):
@@ -53,24 +53,29 @@
         c.wait()
 
 
-def split_kernel(teacher, student, out):
-    out[0] = teacher[:, :DH]
-    out[1] = teacher[:, DH:]
-    out[2] = student[...]
+def split_kernel(teacher, student, out, sems):
+    run_all(
+        [
+            pltpu.make_async_copy(teacher.at[:, pl.ds(0, DH)], out.at[0], sems.at[0]),
+            pltpu.make_async_copy(teacher.at[:, pl.ds(DH, DH)], out.at[1], sems.at[1]),
+            pltpu.make_async_copy(student, out.at[2], sems.at[2]),
+        ]
+    )
 
 
 def split_heads(teacher, student):
     return pl.pallas_call(
         split_kernel,
         out_shape=heads_of(OWN),
-        in_specs=[VMEM, VMEM],
+        in_specs=[HBM, HBM],
         out_specs=VMEM,
+        scratch_shapes=[pltpu.SemaphoreType.DMA((3,))],
         compiler_params=small(2),
         name="split_heads",
     )(teacher, student)
 
 
-def queries_kernel(place, table, query, sent, more, sems):
+def queries_kernel(place, table, query, sent, more, count, sems):
     head = place[0, 0]
     theirs = (1 - head) * STUDENTS
 
@@ -90,17 +95,22 @@
                 act(pltpu.make_async_copy(query.at[:, lanes], more.at[rank - SENT], sems.at[p]))
 
             rank = rank + mine.astype(jnp.int32)
-
-    each(lambda c: c.start())
+        return rank
+
+    count[0, 0] = each(lambda c: c.start())
     each(lambda c: c.wait())
 
 
 def queries_for_other(place, table, query):
     return pl.pallas_call(
         queries_kernel,
-        out_shape=(heads_of(SENT), heads_of(PAIRS - SENT)),
-        in_specs=[SMEM, SMEM, ANY],
-        out_specs=(VMEM, VMEM),
+        out_shape=(
+            heads_of(SENT),
+            heads_of(PAIRS - SENT),
+            jax.ShapeDtypeStruct((1, 1), jnp.int32),
+        ),
+        in_specs=[SMEM, SMEM, HBM],
+        out_specs=(VMEM, VMEM, SMEM),
         scratch_shapes=[pltpu.SemaphoreType.DMA((PAIRS,))],
         compiler_params=small(4),
         name="queries_for_other",
@@ -134,41 +144,39 @@
     )(place, own, ring_1, ring_7)
 
 
-def rest_kernel(place, *refs):
-    ring, out, sems = refs[:7], refs[7], refs[8]
+def rest_kernel(chunks, place, *refs):
+    ring, out, sems = refs[:-2], refs[-2], refs[-1]
     for head in range(2):
 
         @pl.when(place[0, 0] == head)
         def _():
             copies = []
-            for m in range(1, 4):
-                own = ring[2 * m - 1]
-                other = ring[(2 * m - 1 + 2 * head) - 1]
+            for n in range(chunks):
+                own, other = ring[3 * n], ring[3 * n + 1 + head]
                 copies.append(
-                    pltpu.make_async_copy(
-                        own, out.at[pl.ds(OWN * (m - 1), OWN)], sems.at[m - 1]
-                    )
+                    pltpu.make_async_copy(own, out.at[pl.ds(CHUNK * n, OWN)], sems.at[n, 0])
                 )
                 copies.append(
                     pltpu.make_async_copy(
                         other.at[pl.ds(0, OTHER)],
-                        out.at[pl.ds(3 * OWN + OTHER * (m - 1), OTHER)],
-                        sems.at[m + 2],
+                        out.at[pl.ds(CHUNK * n + OWN, OTHER)],
+                        sems.at[n, 1],
                     )
                 )
             run_all(copies)
 
 
-def rest_of(place, ring):
+def rest_of(place, ring, chunks):
+    parts = [ring[o] for m in chunks for o in (2 * m, 2 * m - 1, (2 * m + 1) % 8)]
     return pl.pallas_call(
-        rest_kernel,
-        out_shape=heads_of(REST),
-        in_specs=[SMEM] + [ANY] * 7,
+        functools.partial(rest_kernel, len(chunks)),
+        out_shape=heads_of(CHUNK * len(chunks)),
+        in_specs=[SMEM] + [ANY] * len(parts),
         out_specs=VMEM,
-        scratch_shapes=[pltpu.SemaphoreType.DMA((6,))],
+        scratch_shapes=[pltpu.SemaphoreType.DMA((len(chunks), 2))],
         compiler_params=small(4),
         name="rest_of",
-    )(place, *ring)
+    )(place, *parts)
 
 
 def scaled(q):
@@ -217,17 +225,27 @@
         else:
             (state,) = take(1)
     (keys,) = take(1)
+    if first:
+        own_vmem, student_vmem = take(2)
     if last:
         (state,) = take(1)
     (sems,) = refs
     head, z_hi, x = place[0, 0], place[0, 1], place[0, 2]
     row_block = z_hi * 4 + x
 
-    copies = []
+    copies, arrivals = [], []
     at = 0
     for g, n in enumerate(counts):
         copies.append(pltpu.make_async_copy(groups[g], keys.at[pl.ds(at, n)], sems.at[g]))
+        arrivals.append((at // CHUNK, copies[-1]))
         at += n
+    if first:
+        inputs = [
+            pltpu.make_async_copy(own, own_vmem, sems.at[len(counts)]),
+            pltpu.make_async_copy(student, student_vmem, sems.at[len(counts) + 1]),
+        ]
+        for c in inputs:
+            c.start()
     for c in copies:
         c.start()
     if first:
@@ -235,11 +253,11 @@
             state[part : part + PAIRS] = jnp.full((PAIRS, SUB, ROWS), value, jnp.float32)
         for part, value in ((SM, MASKED), (SL, 0.0)):
             state[part : part + STUDENTS] = jnp.full((STUDENTS, SUB, ROWS), value, jnp.float32)
-        fill_queries(place, table, own, sent, more, student, rows)
+        for c in inputs:
+            c.wait()
+        fill_queries(place, table, own_vmem, sent, more, student_vmem, rows)
     else:
         state[...] = before[...]
-    for c in copies:
-        c.wait()
 
     def product(k, p):
         return lax.dot_general(
@@ -281,18 +299,24 @@
                 state[TC + p] = state[TC + p] * rescale + jnp.sum(weights * gap, axis=0)
 
     def step(i, carry):
+        for at_block, c in arrivals:
+
+            @pl.when(i == at_block)
+            def _():
+                c.wait()
+
         chunk = lax.bitwise_and(z_hi - plan[0, i], 3)
         position = chunk * 4 + lax.bitwise_and(x + plan[1, i], 3)
 
         @pl.when(position < row_block)
         def _():
-            block(plan[2, i], plan[3, i], False)
+            block(CHUNK * i, CHUNK * i + OWN, False)
 
         if first:
 
             @pl.when(position == row_block)
             def _():
-                block(plan[2, i], plan[3, i], True)
+                block(CHUNK * i, CHUNK * i + OWN, True)
 
         return carry
 
@@ -339,14 +363,18 @@
         )
     else:
         extra, out_shape = [rows, state], state_shape
+    extra_specs = [HBM, VMEM, VMEM, HBM] if first else [VMEM, VMEM]
     scratch = [pltpu.VMEM((sum(counts), ROWS, DH), jnp.bfloat16)]
+    if first:
+        scratch.append(pltpu.VMEM((ROWS, PAIRS * DH), jnp.bfloat16))
+        scratch.append(pltpu.VMEM((ROWS, STUDENTS * DH), jnp.bfloat16))
     if last:
         scratch.append(pltpu.VMEM(state_shape.shape, jnp.float32))
-    scratch.append(pltpu.SemaphoreType.DMA((len(groups),)))
+    scratch.append(pltpu.SemaphoreType.DMA((len(groups) + 2,)))
     return pl.pallas_call(
         functools.partial(attend_kernel, first, last, counts, blocks),
         out_shape=out_shape,
-        in_specs=[SMEM] * 3 + [ANY] * len(groups) + [VMEM] * len(extra),
+        in_specs=[SMEM] * 3 + [ANY] * len(groups) + extra_specs,
         out_specs=jax.tree.map(lambda _: VMEM, out_shape),
         scratch_shapes=scratch,
         compiler_params=small(24),
@@ -376,12 +404,6 @@
     return jnp.array([list(row) for row in zip(*blocks)], jnp.int32)
 
 
-def rest_blocks(by, base):
-    return [
-        (m, by, base + OWN * (m - 1), base + 3 * OWN + OTHER * (m - 1)) for m in range(1, 4)
-    ]
-
-
 def program(teacher_query, teacher_key, student_query, student_key, pair_table):
     head = lax.axis_index("head")
     place = jnp.stack([head, lax.axis_index("kv_0"), lax.axis_index("kv_1")])[None]
@@ -391,41 +413,47 @@
     other_side = [(0, 1), (1, 0)]
 
     ring = {0: split_heads(teacher_key[0], student_key[0])}
+    sent, more, count = queries_for_other(place, pair_table, teacher_query[0])
     ring[1] = along_z(ring[0], 1)
     ring[7] = along_z(ring[0], -1)
-    sent, more = queries_for_other(place, pair_table, teacher_query[0])
-    sent, ring[1], ring[7] = lax.optimization_barrier((sent, ring[1], ring[7]))
     sent = lax.ppermute(sent, "head", other_side)
     mine = own_chunk(place, ring[0], ring[1], ring[7])
-    near = [mine, along_x(mine, 1), along_x(mine, -1), along_x(mine, 2)]
+    near_a = along_x(mine, 1)
+    near_b = along_x(mine, -1)
+    near_c = along_x(near_a[:OTHER], 1)
+    near_d = along_x(near_b[OTHER:], -1)
     for step in range(2, 5):
         ring[step] = along_z(ring[step - 1], 1)
         if step < 4:
             ring[8 - step] = along_z(ring[9 - step], -1)
-    my_pairs = lax.dynamic_slice_in_dim(pair_table, head * STUDENTS, STUDENTS, 0)
-    count = jnp.sum((my_pairs // PAIRS != head).astype(jnp.int32))
     more = lax.cond(
-        count > SENT, lambda q: lax.ppermute(q, "head", other_side), lambda q: q, more
-    )
-
-    rest = rest_of(place, [ring[o] for o in range(1, 8)])
-    left, right = along_x(rest, 1), along_x(rest, -1)
-    near_plan = [(0, by, CHUNK * n, CHUNK * n + OWN) for n, by in enumerate((0, -1, 1, 2))]
+        count[0, 0] > SENT, lambda q: lax.ppermute(q, "head", other_side), lambda q: q, more
+    )
+
+    rest_13 = rest_of(place, ring, (1, 3))
+    left_13 = along_x(rest_13, 1)
+    right_13 = along_x(rest_13, -1)
+    rest_2 = rest_of(place, ring, (2,))
+    left_2 = along_x(rest_2, 1)
+    right_2 = along_x(rest_2, -1)
     state, rows = attend(
         place,
         pair_table,
-        plan_of(near_plan + rest_blocks(0, 4 * CHUNK)),
-        near + [rest],
+        plan_of([(0, 0), (0, -1), (0, 1), (0, 2), (1, 0), (3, 0), (2, 0)]),
+        [mine, near_a, near_b, near_c, near_d, rest_13, rest_2],
         queries=(teacher_query[0], sent, more, student_query[0]),
     )
-    left, right, state = lax.optimization_barrier((left, right, state))
-    cut = (REST + 1) // 2
-    far = [along_x(left[:cut], 1), along_x(right[cut:], -1)]
+    left_13, right_13, left_2, right_2, state = lax.optimization_barrier(
+        (left_13, right_13, left_2, right_2, state)
+    )
+    far_1 = along_x(left_13[:CHUNK], 1)
+    far_3 = along_x(right_13[CHUNK:], -1)
+    far_2 = along_x(left_2, 1)
     state = attend(
         place,
         pair_table,
-        plan_of(rest_blocks(-1, 0) + rest_blocks(1, REST)),
-        [left, right],
+        plan_of([(1, -1), (3, -1), (1, 1), (3, 1), (2, -1), (2, 1)]),
+        [left_13, right_13, left_2, right_2],
         rows=rows,
         state=state,
     )
@@ -434,8 +462,8 @@
     kl, sums = attend(
         place,
         pair_table,
-        plan_of(rest_blocks(2, 0)),
-        far,
+        plan_of([(1, 2), (3, 2), (2, 2)]),
+        [far_1, far_3, far_2],
         rows=rows,
         state=state,
         copies_out=devices,

time: 132 us -> 129 us (0.977)
  starting transfers between devices: 55.4 us -> 62 us
  waiting for transfers between devices: 50.7 us -> 45.8 us
  local copies, waits for them, and re-layouts: 7.45 us -> 4.38 us
  other arithmetic: 2.14 us -> 0.74 us
    ppermute x7 -> x11, waiting for transfers between devices: 28.8 us -> 18.6 us  [program(): along_x = lambda a, by: lax.ppermute(a, 'kv_1', shift(4, by))]
    all_to_all x1, starting transfers between devices: 27.2 us -> 34.5 us  [program(): terms = lax.all_to_all(sums, everyone, 0, 0, tiled=True)]
    ppermute x7, waiting for transfers between devices: 10.6 us -> 15.9 us  [program(): along_z = lambda a, by: lax.ppermute(a, ('head', 'kv_0'), z_shift(by))]
    slice x2 -> x4, local copies, waits for them, and re-layouts: 2.13 us -> 0.07 us  [the longest x1 0.02 us: program(): far_1 = along_x(left_13[:CHUNK], 1)]
    reduce_sum x1 -> x0, other arithmetic: 1.4 us -> none  [program(): count = jnp.sum((my_pairs // PAIRS != head).astype(jnp.int32))]
    ppermute x7 -> x11, starting transfers between devices: 16.4 us -> 16.6 us  [program(): along_x = lambda a, by: lax.ppermute(a, 'kv_1', shift(4, by))]
  transfers between devices with their start and end apart: 16 -> 20, of which waited for: 8 -> 9; matrix products, arithmetic and copies ran while one was open for 3% -> 1% of each run, Pallas kernels for 9% -> 10%
where the time goes in v5:
time: 129 us
  starting transfers between devices  62 us (48%)
  waiting for transfers between devices  45.8 us (36%)
  Pallas kernels  14.4 us (11%)
  local copies, waits for them, and re-layouts  4.38 us (3%)
  between operations  1.49 us (1%)
    all_to_all x1, starting transfers between devices, program(): terms = lax.all_to_all(sums, everyone, 0, 0, tiled=True)  34.5 us
    ppermute x11, waiting for transfers between devices, program(): along_x = lambda a, by: lax.ppermute(a, 'kv_1', shift(4, by))  18.6 us
    ppermute x11, starting transfers between devices, program(): along_x = lambda a, by: lax.ppermute(a, 'kv_1', shift(4, by))  16.6 us
    ppermute x7, waiting for transfers between devices, program(): along_z = lambda a, by: lax.ppermute(a, ('head', 'kv_0'), z_shift(by))  15.9 us
    all_to_all x1, waiting for transfers between devices, program(): terms = lax.all_to_all(sums, everyone, 0, 0, tiled=True)  11.2 us
    ppermute x7, starting transfers between devices, program(): along_z = lambda a, by: lax.ppermute(a, ('head', 'kv_0'), z_shift(by))  10.8 us
    pallas_call x3, Pallas kernels, attend(): pl.pallas_call(functools.partial(attend_kernel, first, last, counts, bloc...  8.71 us
    unnamed x18, local copies, waits for them, and re-layouts  4.31 us
  transfers between devices with their start and end apart: 20, of which 9 were waited for; matrix products, arithmetic and copies ran while one was open for 1% of the time, Pallas kernels for 10%

profile of v5, /device:TPU:1, one launch (start us, length us, event | category | flops | bytes accessed | tf_op | source)
XLA Modules:
  0.0 128.8 jit_solution(1613847356673719307)
XLA Ops:
  2.5 2.5 %collective-permute-start.1 = (bf16[3,256,128]{2,1,0:T(8,128)(2,1)S(1)}, bf16[3,256,128]{2,1,0:T(8,128)(2,1)S(1)}, u32[]{:S(2)}, u32[]{:S(2)}) collective-permute-start(bf16[3,256,128]{2,1,0:T(8,128)(2,1)S(1)} %split_heads.1.own), channel_id=1, source_target_pairs={{0,16},{16,4},{4,20},{20,8},{8,24},{24,12},{12,28},{28,0},{1,17},{... | collective-permute-start | bytes 589832 | tf_op jit(solution)/shard_map/ppermute | solution.py:412
  5.1 4.0 %collective-permute-start.4 = (bf16[3,256,128]{2,1,0:T(8,128)(2,1)S(1)}, bf16[3,256,128]{2,1,0:T(8,128)(2,1)S(1)}, u32[]{:S(2)}, u32[]{:S(2)}) collective-permute-start(bf16[3,256,128]{2,1,0:T(8,128)(2,1)S(1)} %split_heads.1.own), channel_id=1, source_target_pairs={{0,28},{16,0},{4,16},{20,4},{8,20},{24,8},{12,24},{28,12},{1,29},{... | collective-permute-start | bytes 589832 | tf_op jit(solution)/shard_map/ppermute | solution.py:412
  9.1 4.5 %collective-permute-done.1.refs_1_.ring_1 = bf16[3,256,128]{2,1,0:T(8,128)(2,1)S(1)} collective-permute-done((bf16[3,256,128]{2,1,0:T(8,128)(2,1)S(1)}, bf16[3,256,128]{2,1,0:T(8,128)(2,1)S(1)}, u32[]{:S(2)}, u32[]{:S(2)}) %collective-permute-start.1) | collective-permute-done | bytes 196640 | tf_op jit(solution)/shard_map/ppermute | solution.py:412
  15.6 2.1 %queries_for_other.1 = (bf16[9,256,128]{2,1,0:T(8,128)(2,1)}, bf16[5,256,128]{2,1,0:T(8,128)(2,1)S(1)}, s32[1,1]{1,0:T(1,128)}) custom-call(s32[1,3]{1,0:T(1,128)S(1)} %add_bitcast_fusion.place, s32[14,2]{1,0:T(8,128)S(1)} %copy.18.table, bf16[256,1792]{1,0:T(8,128)(2,1)S(1)} %bitcast.14), custom_call_target="tpu_custom_call" | custom-call | tf_op jit(solution)/shard_map/queries_for_other/pallas_call | solution.py:105
  17.9 2.7 %collective-permute-start.5 = (bf16[3,256,128]{2,1,0:T(8,128)(2,1)S(1)}, bf16[3,256,128]{2,1,0:T(8,128)(2,1)S(1)}, u32[]{:S(2)}, u32[]{:S(2)}) collective-permute-start(bf16[3,256,128]{2,1,0:T(8,128)(2,1)S(1)} %collective-permute-done.4.refs_5_.ring_7), channel_id=1, source_target_pairs={{0,28},{16,0},{4,16},{20,4},{8,20},{24,8},{12,24},{28,12},{1,29},{... | collective-permute-start | bytes 589832 | tf_op jit(solution)/shard_map/ppermute | solution.py:412
  21.6 2.6 %collective-permute-start.13 = (bf16[5,256,128]{2,1,0:T(8,128)(2,1)S(1)}, bf16[5,256,128]{2,1,0:T(8,128)(2,1)S(1)}, u32[]{:S(2)}, u32[]{:S(2)}) collective-permute-start(bf16[5,256,128]{2,1,0:T(8,128)(2,1)S(1)} %own_chunk.1.refs_0_), channel_id=1, source_target_pairs={{0,3},{1,0},{2,1},{3,2},{4,7},{5,4},{6,5},{7,6},{8,11},{9,8},{10,9... | collective-permute-start | bytes 983048 | tf_op jit(solution)/shard_map/ppermute | solution.py:411
  25.0 11.0 %collective-permute-done.5.refs_3_ = bf16[3,256,128]{2,1,0:T(8,128)(2,1)S(1)} collective-permute-done((bf16[3,256,128]{2,1,0:T(8,128)(2,1)S(1)}, bf16[3,256,128]{2,1,0:T(8,128)(2,1)S(1)}, u32[]{:S(2)}, u32[]{:S(2)}) %collective-permute-start.5) | collective-permute-done | bytes 196640 | tf_op jit(solution)/shard_map/ppermute | solution.py:412
  35.9 1.5 %collective-permute-start.9 = (bf16[3,256,128]{2,1,0:T(8,128)(2,1)S(1)}, bf16[3,256,128]{2,1,0:T(8,128)(2,1)S(1)}, u32[]{:S(2)}, u32[]{:S(2)}) collective-permute-start(bf16[3,256,128]{2,1,0:T(8,128)(2,1)S(1)} %collective-permute-done.3.refs_2_.refs_1_), channel_id=1, source_target_pairs={{0,16},{16,4},{4,20},{20,8},{8,24},{24,12},{12,28},{28,0},{1,17},{... | collective-permute-start | bytes 589832 | tf_op jit(solution)/shard_map/ppermute | solution.py:412
  37.4 2.6 %collective-permute-start.15 = (bf16[3,256,128]{2,1,0:T(8,128)(2,1)S(1)}, bf16[3,256,128]{2,1,0:T(8,128)(2,1)S(1)}, u32[]{:S(2)}, u32[]{:S(2)}) collective-permute-start(bf16[3,256,128]{2,1,0:T(8,128)(2,1)S(1)} %slice.21), channel_id=1, source_target_pairs={{0,3},{1,0},{2,1},{3,2},{4,7},{5,4},{6,5},{7,6},{8,11},{9,8},{10,9... | collective-permute-start | bytes 589832 | tf_op jit(solution)/shard_map/ppermute | solution.py:411
  40.4 1.4 %rest_of.2.refs_5_ = bf16[10,256,128]{2,1,0:T(8,128)(2,1)S(1)} custom-call(s32[1,3]{1,0:T(1,128)S(1)} %add_bitcast_fusion.place, bf16[3,256,128]{2,1,0:T(8,128)(2,1)S(1)} %collective-permute-done.2.refs_0_, bf16[3,256,128]{2,1,0:T(8,128)(2,1)S(1)} %collective-permute-done.1.refs_1_.ring_1, bf16[3,256,128]{2,1,0:T(8,128)(2,1)S(1)} %collective-permute-done.3.refs_2_.refs_1_, ...), custom_call_target="tpu_custom_call" | custom-call | tf_op jit(solution)/shard_map/rest_of/pallas_call | solution.py:171
  41.9 1.3 %collective-permute-start.7 = (bf16[10,256,128]{2,1,0:T(8,128)(2,1)S(1)}, bf16[10,256,128]{2,1,0:T(8,128)(2,1)S(1)}, u32[]{:S(2)}, u32[]{:S(2)}) collective-permute-start(bf16[10,256,128]{2,1,0:T(8,128)(2,1)S(1)} %rest_of.2.refs_5_), channel_id=1, source_target_pairs={{0,1},{1,2},{2,3},{3,0},{4,5},{5,6},{6,7},{7,4},{8,9},{9,10},{10,1... | collective-permute-start | bytes 1966088 | tf_op jit(solution)/shard_map/ppermute | solution.py:411
  43.2 1.5 %collective-permute-start.8 = (bf16[10,256,128]{2,1,0:T(8,128)(2,1)S(1)}, bf16[10,256,128]{2,1,0:T(8,128)(2,1)S(1)}, u32[]{:S(2)}, u32[]{:S(2)}) collective-permute-start(bf16[10,256,128]{2,1,0:T(8,128)(2,1)S(1)} %rest_of.2.refs_5_), channel_id=1, source_target_pairs={{0,3},{1,0},{2,1},{3,2},{4,7},{5,4},{6,5},{7,6},{8,11},{9,8},{10,9... | collective-permute-start | bytes 1966088 | tf_op jit(solution)/shard_map/ppermute | solution.py:411
  45.8 1.5 %collective-permute-start.10 = (bf16[5,256,128]{2,1,0:T(8,128)(2,1)S(1)}, bf16[5,256,128]{2,1,0:T(8,128)(2,1)S(1)}, u32[]{:S(2)}, u32[]{:S(2)}) collective-permute-start(bf16[5,256,128]{2,1,0:T(8,128)(2,1)S(1)} %rest_of.3.refs_6_), channel_id=1, source_target_pairs={{0,1},{1,2},{2,3},{3,0},{4,5},{5,6},{6,7},{7,4},{8,9},{9,10},{10,1... | collective-permute-start | bytes 983048 | tf_op jit(solution)/shard_map/ppermute | solution.py:411
  47.2 11.8 %collective-permute-done.14.refs_3_ = bf16[2,256,128]{2,1,0:T(8,128)(2,1)S(1)} collective-permute-done((bf16[2,256,128]{2,1,0:T(8,128)(2,1)S(1)}, bf16[2,256,128]{2,1,0:T(8,128)(2,1)S(1)}, u32[]{:S(2)}, u32[]{:S(2)}) %collective-permute-start.14) | collective-permute-done | bytes 131104 | tf_op jit(solution)/shard_map/ppermute | solution.py:411
  59.0 1.3 collective-permute-start.11
  60.3 5.2 %attend.3 = (f32[56,8,256]{2,1,0:T(8,128)S(1)}, bf16[21,256,256]{2,1,0:T(8,128)(2,1)S(1)}) custom-call(s32[1,3]{1,0:T(1,128)S(1)} %add_bitcast_fusion.place, s32[14,2]{1,0:T(8,128)S(1)} %copy.18.table, s32[2,7]{1,0:T(2,128)S(1)} %copy-done.7, bf16[5,256,128]{2,1,0:T(8,128)(2,1)S(1)} %own_chunk.1.refs_0_, ...), custom_call_target="tpu_custom_call" | custom-call | flops 4932501504 | bytes 2293760 | tf_op jit(solution)/shard_map/attend/pallas_call | solution.py:374
  66.1 1.7 %collective-permute-start.17 = (bf16[5,256,128]{2,1,0:T(8,128)(2,1)S(1)}, bf16[5,256,128]{2,1,0:T(8,128)(2,1)S(1)}, u32[]{:S(2)}, u32[]{:S(2)}) collective-permute-start(bf16[5,256,128]{2,1,0:T(8,128)(2,1)S(1)} %slice.17), channel_id=1, source_target_pairs={{0,1},{1,2},{2,3},{3,0},{4,5},{5,6},{6,7},{7,4},{8,9},{9,10},{10,1... | collective-permute-start | bytes 983048 | tf_op jit(solution)/shard_map/ppermute | solution.py:411
  67.8 4.2 %collective-permute-start.18 = (bf16[5,256,128]{2,1,0:T(8,128)(2,1)S(1)}, bf16[5,256,128]{2,1,0:T(8,128)(2,1)S(1)}, u32[]{:S(2)}, u32[]{:S(2)}) collective-permute-start(bf16[5,256,128]{2,1,0:T(8,128)(2,1)S(1)} %slice.18), channel_id=1, source_target_pairs={{0,3},{1,0},{2,1},{3,2},{4,7},{5,4},{6,5},{7,6},{8,11},{9,8},{10,9... | collective-permute-start | bytes 983048 | tf_op jit(solution)/shard_map/ppermute | solution.py:411
  72.0 1.5 %attend.4.refs_4_ = f32[56,8,256]{2,1,0:T(8,128)S(1)} custom-call(s32[1,3]{1,0:T(1,128)S(1)} %add_bitcast_fusion.place, s32[14,2]{1,0:T(8,128)S(1)} %copy.18.table, s32[2,6]{1,0:T(2,128)S(1)} %copy-done.6, bf16[10,256,128]{2,1,0:T(8,128)(2,1)S(1)} %collective-permute-done.7.refs_0_, bf16[10,256,128]{2,1,0:T(8,128)(2,1)S(1)} %collective-permute-done.8.refs_1_, ...), custom_call_target="tpu_custom_call" | custom-call | flops 4227858432 | bytes 1966080 | tf_op jit(solution)/shard_map/attend/pallas_call | solution.py:374
  73.5 2.8 %collective-permute-done.17.refs_0_ = bf16[5,256,128]{2,1,0:T(8,128)(2,1)S(1)} collective-permute-done((bf16[5,256,128]{2,1,0:T(8,128)(2,1)S(1)}, bf16[5,256,128]{2,1,0:T(8,128)(2,1)S(1)}, u32[]{:S(2)}, u32[]{:S(2)}) %collective-permute-start.17) | collective-permute-done | bytes 327712 | tf_op jit(solution)/shard_map/ppermute | solution.py:411
  76.5 3.3 %collective-permute-done.19.refs_2_ = bf16[5,256,128]{2,1,0:T(8,128)(2,1)S(1)} collective-permute-done((bf16[5,256,128]{2,1,0:T(8,128)(2,1)S(1)}, bf16[5,256,128]{2,1,0:T(8,128)(2,1)S(1)}, u32[]{:S(2)}, u32[]{:S(2)}) %collective-permute-start.19) | collective-permute-done | bytes 327712 | tf_op jit(solution)/shard_map/ppermute | solution.py:411
  79.8 2.0 %attend.5 = (f32[7,256]{1,0:T(8,128)S(1)}, f32[128,128]{1,0:T(8,128)}) custom-call(s32[1,3]{1,0:T(1,128)S(1)} %add_bitcast_fusion.place, s32[14,2]{1,0:T(8,128)S(1)} %copy.18.table, s32[2,3]{1,0:T(2,128)S(1)} %copy-done.5, bf16[5,256,128]{2,1,0:T(8,128)(2,1)S(1)} %collective-permute-done.17.refs_0_, ...), custom_call_target="tpu_custom_call" | custom-call | flops 2113929216 | bytes 983040 | tf_op jit(solution)/shard_map/attend/pallas_call | solution.py:374
  81.8 34.5 %all-to-all-start = ((f32[128,1,128]{2,1,0:T(1,128)}), f32[128,1,128]{2,1,0:T(1,128)S(1)}, u32[]{:S(2)}, u32[]{:S(2)}) async-start(f32[128,1,128]{2,1,0:T(1,128)} %bitcast.11), calls=%async_computation | async-start | bytes 131072 | tf_op jit(solution)/shard_map/all_to_all | solution.py:471
  116.9 11.2 %all-to-all-done = f32[128,1,128]{2,1,0:T(1,128)S(1)} async-done(((f32[128,1,128]{2,1,0:T(1,128)}), f32[128,1,128]{2,1,0:T(1,128)S(1)}, u32[]{:S(2)}, u32[]{:S(2)}) %all-to-all-start) | async-done | bytes 65568 | tf_op jit(solution)/shard_map/all_to_all | solution.py:471
  (50 shorter events, 8.7 us)
Async XLA Ops:
  2.5 11.1 %collective-permute-start.1 = (bf16[3,256,128]{2,1,0:T(8,128)(2,1)S(1)}, bf16[3,256,128]{2,1,0:T(8,128)(2,1)S(1)}, u32[]{:S(2)}, u32[]{:S(2)}) collective-permute-start(bf16[3,256,128]{2,1,0:T(8,128)(2,1)S(1)} %split_heads.1.own), channel_id=1, source_target_pairs={{0,16},{16,4},{4,20},{20,8},{8,24},{24,12},{12,28},{28,0},{1,17},{... | collective-permute-start | bytes 589832 | tf_op jit(solution)/shard_map/ppermute | solution.py:412
  5.1 12.8 %collective-permute-start.4 = (bf16[3,256,128]{2,1,0:T(8,128)(2,1)S(1)}, bf16[3,256,128]{2,1,0:T(8,128)(2,1)S(1)}, u32[]{:S(2)}, u32[]{:S(2)}) collective-permute-start(bf16[3,256,128]{2,1,0:T(8,128)(2,1)S(1)} %split_heads.1.own), channel_id=1, source_target_pairs={{0,28},{16,0},{4,16},{20,4},{8,20},{24,8},{12,24},{28,12},{1,29},{... | collective-permute-start | bytes 589832 | tf_op jit(solution)/shard_map/ppermute | solution.py:412
  13.6 7.0 %collective-permute-start.2 = (bf16[3,256,128]{2,1,0:T(8,128)(2,1)S(1)}, bf16[3,256,128]{2,1,0:T(8,128)(2,1)S(1)}, u32[]{:S(2)}, u32[]{:S(2)}) collective-permute-start(bf16[3,256,128]{2,1,0:T(8,128)(2,1)S(1)} %collective-permute-done.1.refs_1_.ring_1), channel_id=1, source_target_pairs={{0,16},{16,4},{4,20},{20,8},{8,24},{24,12},{12,28},{28,0},{1,17},{... | collective-permute-start | bytes 589832 | tf_op jit(solution)/shard_map/ppermute | solution.py:412
  15.6 44.7 %copy-start.1 = (bf16[1,256,1792]{2,1,0:T(8,128)(2,1)S(1)}, bf16[1,256,1792]{2,1,0:T(8,128)(2,1)}, u32[]{:S(2)}) copy-start(bf16[1,256,1792]{2,1,0:T(8,128)(2,1)} %param.10) | copy-start | bytes 2752516
  15.6 44.7 %copy-start.7 = (s32[2,7]{1,0:T(2,128)S(1)}, s32[2,7]{1,0:T(2,128)}, u32[]{:S(2)}) copy-start(s32[2,7]{1,0:T(2,128)} %constant.27.clone.plan) | copy-start | bytes 172
  17.8 28.0 %collective-permute-start.16 = (bf16[9,256,128]{2,1,0:T(8,128)(2,1)}, bf16[9,256,128]{2,1,0:T(8,128)(2,1)S(1)}, u32[]{:S(2)}, u32[]{:S(2)}) collective-permute-start(bf16[9,256,128]{2,1,0:T(8,128)(2,1)} %get-tuple-element.19), channel_id=1, source_target_pairs={{0,16},{16,0},{1,17},{17,1},{2,18},{18,2},{3,19},{19,3},{4,20},{20... | collective-permute-start | bytes 1769480 | tf_op jit(solution)/shard_map/ppermute | solution.py:419
  17.9 18.0 %collective-permute-start.5 = (bf16[3,256,128]{2,1,0:T(8,128)(2,1)S(1)}, bf16[3,256,128]{2,1,0:T(8,128)(2,1)S(1)}, u32[]{:S(2)}, u32[]{:S(2)}) collective-permute-start(bf16[3,256,128]{2,1,0:T(8,128)(2,1)S(1)} %collective-permute-done.4.refs_5_.ring_7), channel_id=1, source_target_pairs={{0,28},{16,0},{4,16},{20,4},{8,20},{24,8},{12,24},{28,12},{1,29},{... | collective-permute-start | bytes 589832 | tf_op jit(solution)/shard_map/ppermute | solution.py:412
  20.6 15.3 %collective-permute-start.3 = (bf16[3,256,128]{2,1,0:T(8,128)(2,1)S(1)}, bf16[3,256,128]{2,1,0:T(8,128)(2,1)S(1)}, u32[]{:S(2)}, u32[]{:S(2)}) collective-permute-start(bf16[3,256,128]{2,1,0:T(8,128)(2,1)S(1)} %collective-permute-done.2.refs_0_), channel_id=1, source_target_pairs={{0,16},{16,4},{4,20},{20,8},{8,24},{24,12},{12,28},{28,0},{1,17},{... | collective-permute-start | bytes 589832 | tf_op jit(solution)/shard_map/ppermute | solution.py:412
  21.6 15.8 %collective-permute-start.13 = (bf16[5,256,128]{2,1,0:T(8,128)(2,1)S(1)}, bf16[5,256,128]{2,1,0:T(8,128)(2,1)S(1)}, u32[]{:S(2)}, u32[]{:S(2)}) collective-permute-start(bf16[5,256,128]{2,1,0:T(8,128)(2,1)S(1)} %own_chunk.1.refs_0_), channel_id=1, source_target_pairs={{0,3},{1,0},{2,1},{3,2},{4,7},{5,4},{6,5},{7,6},{8,11},{9,8},{10,9... | collective-permute-start | bytes 983048 | tf_op jit(solution)/shard_map/ppermute | solution.py:411
  24.9 35.4 %copy-start.4 = (bf16[1,256,896]{2,1,0:T(8,128)(2,1)S(1)}, bf16[1,256,896]{2,1,0:T(8,128)(2,1)}, u32[]{:S(2)}) copy-start(bf16[1,256,896]{2,1,0:T(8,128)(2,1)} %param.12) | copy-start | bytes 1376260
  24.9 18.3 %collective-permute-start.12 = (bf16[5,256,128]{2,1,0:T(8,128)(2,1)S(1)}, bf16[5,256,128]{2,1,0:T(8,128)(2,1)S(1)}, u32[]{:S(2)}, u32[]{:S(2)}) collective-permute-start(bf16[5,256,128]{2,1,0:T(8,128)(2,1)S(1)} %own_chunk.1.refs_0_), channel_id=1, source_target_pairs={{0,1},{1,2},{2,3},{3,0},{4,5},{5,6},{6,7},{7,4},{8,9},{9,10},{10,1... | collective-permute-start | bytes 983048 | tf_op jit(solution)/shard_map/ppermute | solution.py:411
  35.9 4.5 %collective-permute-start.6 = (bf16[3,256,128]{2,1,0:T(8,128)(2,1)S(1)}, bf16[3,256,128]{2,1,0:T(8,128)(2,1)S(1)}, u32[]{:S(2)}, u32[]{:S(2)}) collective-permute-start(bf16[3,256,128]{2,1,0:T(8,128)(2,1)S(1)} %collective-permute-done.5.refs_3_), channel_id=1, source_target_pairs={{0,28},{16,0},{4,16},{20,4},{8,20},{24,8},{12,24},{28,12},{1,29},{... | collective-permute-start | bytes 589832 | tf_op jit(solution)/shard_map/ppermute | solution.py:412
  35.9 8.7 %collective-permute-start.9 = (bf16[3,256,128]{2,1,0:T(8,128)(2,1)S(1)}, bf16[3,256,128]{2,1,0:T(8,128)(2,1)S(1)}, u32[]{:S(2)}, u32[]{:S(2)}) collective-permute-start(bf16[3,256,128]{2,1,0:T(8,128)(2,1)S(1)} %collective-permute-done.3.refs_2_.refs_1_), channel_id=1, source_target_pairs={{0,16},{16,4},{4,20},{20,8},{8,24},{24,12},{12,28},{28,0},{1,17},{... | collective-permute-start | bytes 589832 | tf_op jit(solution)/shard_map/ppermute | solution.py:412
  37.4 22.9 %collective-permute-start.15 = (bf16[3,256,128]{2,1,0:T(8,128)(2,1)S(1)}, bf16[3,256,128]{2,1,0:T(8,128)(2,1)S(1)}, u32[]{:S(2)}, u32[]{:S(2)}) collective-permute-start(bf16[3,256,128]{2,1,0:T(8,128)(2,1)S(1)} %slice.21), channel_id=1, source_target_pairs={{0,3},{1,0},{2,1},{3,2},{4,7},{5,4},{6,5},{7,6},{8,11},{9,8},{10,9... | collective-permute-start | bytes 589832 | tf_op jit(solution)/shard_map/ppermute | solution.py:411
  41.9 24.2 %collective-permute-start.7 = (bf16[10,256,128]{2,1,0:T(8,128)(2,1)S(1)}, bf16[10,256,128]{2,1,0:T(8,128)(2,1)S(1)}, u32[]{:S(2)}, u32[]{:S(2)}) collective-permute-start(bf16[10,256,128]{2,1,0:T(8,128)(2,1)S(1)} %rest_of.2.refs_5_), channel_id=1, source_target_pairs={{0,1},{1,2},{2,3},{3,0},{4,5},{5,6},{6,7},{7,4},{8,9},{9,10},{10,1... | collective-permute-start | bytes 1966088 | tf_op jit(solution)/shard_map/ppermute | solution.py:411
  43.2 22.9 %collective-permute-start.8 = (bf16[10,256,128]{2,1,0:T(8,128)(2,1)S(1)}, bf16[10,256,128]{2,1,0:T(8,128)(2,1)S(1)}, u32[]{:S(2)}, u32[]{:S(2)}) collective-permute-start(bf16[10,256,128]{2,1,0:T(8,128)(2,1)S(1)} %rest_of.2.refs_5_), channel_id=1, source_target_pairs={{0,3},{1,0},{2,1},{3,2},{4,7},{5,4},{6,5},{7,6},{8,11},{9,8},{10,9... | collective-permute-start | bytes 1966088 | tf_op jit(solution)/shard_map/ppermute | solution.py:411
  44.7 14.3 %collective-permute-start.14 = (bf16[2,256,128]{2,1,0:T(8,128)(2,1)S(1)}, bf16[2,256,128]{2,1,0:T(8,128)(2,1)S(1)}, u32[]{:S(2)}, u32[]{:S(2)}) collective-permute-start(bf16[2,256,128]{2,1,0:T(8,128)(2,1)S(1)} %slice.20), channel_id=1, source_target_pairs={{0,1},{1,2},{2,3},{3,0},{4,5},{5,6},{6,7},{7,4},{8,9},{9,10},{10,1... | collective-permute-start | bytes 393224 | tf_op jit(solution)/shard_map/ppermute | solution.py:411
  45.8 20.3 %collective-permute-start.10 = (bf16[5,256,128]{2,1,0:T(8,128)(2,1)S(1)}, bf16[5,256,128]{2,1,0:T(8,128)(2,1)S(1)}, u32[]{:S(2)}, u32[]{:S(2)}) collective-permute-start(bf16[5,256,128]{2,1,0:T(8,128)(2,1)S(1)} %rest_of.3.refs_6_), channel_id=1, source_target_pairs={{0,1},{1,2},{2,3},{3,0},{4,5},{5,6},{6,7},{7,4},{8,9},{9,10},{10,1... | collective-permute-start | bytes 983048 | tf_op jit(solution)/shard_map/ppermute | solution.py:411
  59.0 7.0 %collective-permute-start.11 = (bf16[5,256,128]{2,1,0:T(8,128)(2,1)S(1)}, bf16[5,256,128]{2,1,0:T(8,128)(2,1)S(1)}, u32[]{:S(2)}, u32[]{:S(2)}) collective-permute-start(bf16[5,256,128]{2,1,0:T(8,128)(2,1)S(1)} %rest_of.3.refs_6_), channel_id=1, source_target_pairs={{0,3},{1,0},{2,1},{3,2},{4,7},{5,4},{6,5},{7,6},{8,11},{9,8},{10,9... | collective-permute-start | bytes 983048 | tf_op jit(solution)/shard_map/ppermute | solution.py:411
  60.3 11.7 %copy-start.6 = (s32[2,6]{1,0:T(2,128)S(1)}, s32[2,6]{1,0:T(2,128)}, u32[]{:S(2)}) copy-start(s32[2,6]{1,0:T(2,128)} %constant.28.clone.plan) | copy-start | bytes 148
  66.1 10.2 %collective-permute-start.17 = (bf16[5,256,128]{2,1,0:T(8,128)(2,1)S(1)}, bf16[5,256,128]{2,1,0:T(8,128)(2,1)S(1)}, u32[]{:S(2)}, u32[]{:S(2)}) collective-permute-start(bf16[5,256,128]{2,1,0:T(8,128)(2,1)S(1)} %slice.17), channel_id=1, source_target_pairs={{0,1},{1,2},{2,3},{3,0},{4,5},{5,6},{6,7},{7,4},{8,9},{9,10},{10,1... | collective-permute-start | bytes 983048 | tf_op jit(solution)/shard_map/ppermute | solution.py:411
  67.8 8.8 %collective-permute-start.18 = (bf16[5,256,128]{2,1,0:T(8,128)(2,1)S(1)}, bf16[5,256,128]{2,1,0:T(8,128)(2,1)S(1)}, u32[]{:S(2)}, u32[]{:S(2)}) collective-permute-start(bf16[5,256,128]{2,1,0:T(8,128)(2,1)S(1)} %slice.18), channel_id=1, source_target_pairs={{0,3},{1,0},{2,1},{3,2},{4,7},{5,4},{6,5},{7,6},{8,11},{9,8},{10,9... | collective-permute-start | bytes 983048 | tf_op jit(solution)/shard_map/ppermute | solution.py:411
  72.0 7.9 %collective-permute-start.19 = (bf16[5,256,128]{2,1,0:T(8,128)(2,1)S(1)}, bf16[5,256,128]{2,1,0:T(8,128)(2,1)S(1)}, u32[]{:S(2)}, u32[]{:S(2)}) collective-permute-start(bf16[5,256,128]{2,1,0:T(8,128)(2,1)S(1)} %collective-permute-done.10.refs_2_), channel_id=1, source_target_pairs={{0,1},{1,2},{2,3},{3,0},{4,5},{5,6},{6,7},{7,4},{8,9},{9,10},{10,1... | collective-permute-start | bytes 983048 | tf_op jit(solution)/shard_map/ppermute | solution.py:411
  81.8 46.3 %all-to-all-start = ((f32[128,1,128]{2,1,0:T(1,128)}), f32[128,1,128]{2,1,0:T(1,128)S(1)}, u32[]{:S(2)}, u32[]{:S(2)}) async-start(f32[128,1,128]{2,1,0:T(1,128)} %bitcast.11), calls=%async_computation | async-start | bytes 131072 | tf_op jit(solution)/shard_map/all_to_all | solution.py:471
  (4 other events, 10.8 us)

commit v6 on v5

--- a/solution.py
+++ b/solution.py
@@ -30,7 +30,8 @@
 OWN = 3
 OTHER = 2
 CHUNK = OWN + OTHER
-SENT = 9
+PIECES = (2, 2, 2, 3)
+SENT = sum(PIECES)
 MIB = 1024 * 1024
 SMEM = pl.BlockSpec(memory_space=pltpu.SMEM)
 VMEM = pl.BlockSpec(memory_space=pltpu.VMEM)
@@ -75,7 +76,7 @@
     )(teacher, student)
 
 
-def queries_kernel(place, table, query, sent, more, count, sems):
+def queries_kernel(place, table, query, sent, count, sems):
     head = place[0, 0]
     theirs = (1 - head) * STUDENTS
 
@@ -86,13 +87,9 @@
             mine = lax.div(teacher, PAIRS) == head
             lanes = pl.ds(pl.multiple_of(lax.rem(teacher, PAIRS) * DH, DH), DH)
 
-            @pl.when(jnp.logical_and(mine, rank < SENT))
+            @pl.when(mine)
             def _():
                 act(pltpu.make_async_copy(query.at[:, lanes], sent.at[rank], sems.at[p]))
-
-            @pl.when(jnp.logical_and(mine, rank >= SENT))
-            def _():
-                act(pltpu.make_async_copy(query.at[:, lanes], more.at[rank - SENT], sems.at[p]))
 
             rank = rank + mine.astype(jnp.int32)
         return rank
@@ -104,13 +101,9 @@
 def queries_for_other(place, table, query):
     return pl.pallas_call(
         queries_kernel,
-        out_shape=(
-            heads_of(SENT),
-            heads_of(PAIRS - SENT),
-            jax.ShapeDtypeStruct((1, 1), jnp.int32),
-        ),
-        in_specs=[SMEM, SMEM, HBM],
-        out_specs=(VMEM, VMEM, SMEM),
+        out_shape=(heads_of(PAIRS), jax.ShapeDtypeStruct((1, 1), jnp.int32)),
+        in_specs=[SMEM, SMEM, ANY],
+        out_specs=(VMEM, SMEM),
         scratch_shapes=[pltpu.SemaphoreType.DMA((PAIRS,))],
         compiler_params=small(4),
         name="queries_for_other",
@@ -186,27 +179,42 @@
     return jnp.concatenate([high, low], axis=1)
 
 
-def fill_queries(place, table, own, sent, more, student, rows):
+def prepare_kernel(place, table, own, student, rows):
     head = place[0, 0]
     for s in range(STUDENTS):
         rows[PAIRS + s] = scaled(student[:, s * DH : (s + 1) * DH])
+    for p in range(PAIRS):
+        teacher = table[head * STUDENTS + p // 2, p % 2]
+        lanes = pl.ds(pl.multiple_of(lax.rem(teacher, PAIRS) * DH, DH), DH)
+
+        @pl.when(lax.div(teacher, PAIRS) == head)
+        def _():
+            rows[p] = scaled(own[:, lanes])
+
+
+def prepare(place, table, own, student):
+    return pl.pallas_call(
+        prepare_kernel,
+        out_shape=jax.ShapeDtypeStruct((HEADS, ROWS, 2 * DH), jnp.bfloat16),
+        in_specs=[SMEM, SMEM, VMEM, VMEM],
+        out_specs=VMEM,
+        compiler_params=small(8),
+        cost_estimate=pl.CostEstimate(
+            flops=HEADS * ROWS * DH * 64, bytes_accessed=HEADS * ROWS * DH * 6, transcendentals=0
+        ),
+        name="prepare",
+    )(place, table, own, student)
+
+
+def fill_received(place, table, received, rows):
+    head = place[0, 0]
     rank = jnp.int32(0)
     for p in range(PAIRS):
-        teacher = table[head * STUDENTS + p // 2, p % 2]
-        mine = lax.div(teacher, PAIRS) == head
-        lanes = pl.ds(pl.multiple_of(lax.rem(teacher, PAIRS) * DH, DH), DH)
-
-        @pl.when(mine)
+        mine = lax.div(table[head * STUDENTS + p // 2, p % 2], PAIRS) == head
+
+        @pl.when(jnp.logical_not(mine))
         def _():
-            rows[p] = scaled(own[:, lanes])
-
-        @pl.when(jnp.logical_and(jnp.logical_not(mine), rank < SENT))
-        def _():
-            rows[p] = scaled(sent[rank])
-
-        @pl.when(jnp.logical_and(jnp.logical_not(mine), rank >= SENT))
-        def _():
-            rows[p] = scaled(more[rank - SENT])
+            rows[p] = scaled(received[rank])
 
         rank = rank + 1 - mine.astype(jnp.int32)
 
@@ -216,7 +224,8 @@
     take = lambda n: [refs.pop(0) for _ in range(n)]
     groups = take(len(counts))
     if first:
-        own, sent, more, student = take(4)
+        pieces = take(len(PIECES) + 1)
+        take(1)
         state, rows = take(2)
     else:
         rows, before = take(2)
@@ -226,7 +235,7 @@
             (state,) = take(1)
     (keys,) = take(1)
     if first:
-        own_vmem, student_vmem = take(2)
+        (received,) = take(1)
     if last:
         (state,) = take(1)
     (sems,) = refs
@@ -240,10 +249,16 @@
         arrivals.append((at // CHUNK, copies[-1]))
         at += n
     if first:
-        inputs = [
-            pltpu.make_async_copy(own, own_vmem, sems.at[len(counts)]),
-            pltpu.make_async_copy(student, student_vmem, sems.at[len(counts) + 1]),
-        ]
+        inputs = []
+        rank = 0
+        for n, piece in enumerate(pieces):
+            length = piece.shape[0]
+            inputs.append(
+                pltpu.make_async_copy(
+                    piece, received.at[pl.ds(rank, length)], sems.at[len(counts) + n]
+                )
+            )
+            rank += length
         for c in inputs:
             c.start()
     for c in copies:
@@ -255,7 +270,7 @@
             state[part : part + STUDENTS] = jnp.full((STUDENTS, SUB, ROWS), value, jnp.float32)
         for c in inputs:
             c.wait()
-        fill_queries(place, table, own_vmem, sent, more, student_vmem, rows)
+        fill_received(place, table, received, rows)
     else:
         state[...] = before[...]
 
@@ -346,7 +361,7 @@
     sums[...] = jnp.broadcast_to(line, sums.shape)
 
 
-def attend(place, table, plan, groups, queries=None, rows=None, state=None, copies_out=0):
+def attend(place, table, plan, groups, rows, queries=None, state=None, copies_out=0):
     first = queries is not None
     last = copies_out > 0
     counts = tuple(g.shape[0] for g in groups)
@@ -354,7 +369,7 @@
     state_shape = jax.ShapeDtypeStruct((STATE, SUB, ROWS), jnp.float32)
     rows_shape = jax.ShapeDtypeStruct((HEADS, ROWS, 2 * DH), jnp.bfloat16)
     if first:
-        extra, out_shape = list(queries), (state_shape, rows_shape)
+        extra, out_shape = [*queries, rows], (state_shape, rows_shape)
     elif last:
         extra = [rows, state]
         out_shape = (
@@ -363,20 +378,20 @@
         )
     else:
         extra, out_shape = [rows, state], state_shape
-    extra_specs = [HBM, VMEM, VMEM, HBM] if first else [VMEM, VMEM]
+    extra_specs = [ANY] * (len(PIECES) + 1) + [VMEM] if first else [VMEM, VMEM]
     scratch = [pltpu.VMEM((sum(counts), ROWS, DH), jnp.bfloat16)]
     if first:
-        scratch.append(pltpu.VMEM((ROWS, PAIRS * DH), jnp.bfloat16))
-        scratch.append(pltpu.VMEM((ROWS, STUDENTS * DH), jnp.bfloat16))
+        scratch.append(pltpu.VMEM((PAIRS, ROWS, DH), jnp.bfloat16))
     if last:
         scratch.append(pltpu.VMEM(state_shape.shape, jnp.float32))
-    scratch.append(pltpu.SemaphoreType.DMA((len(groups) + 2,)))
+    scratch.append(pltpu.SemaphoreType.DMA((len(groups) + len(PIECES) + 1,)))
     return pl.pallas_call(
         functools.partial(attend_kernel, first, last, counts, blocks),
         out_shape=out_shape,
         in_specs=[SMEM] * 3 + [ANY] * len(groups) + extra_specs,
         out_specs=jax.tree.map(lambda _: VMEM, out_shape),
         scratch_shapes=scratch,
+        input_output_aliases={3 + len(groups) + len(extra) - 1: 1} if first else {},
         compiler_params=small(24),
         cost_estimate=pl.CostEstimate(
             flops=blocks * HEADS * 2 * ROWS * ROWS * 2 * DH,
@@ -413,10 +428,22 @@
     other_side = [(0, 1), (1, 0)]
 
     ring = {0: split_heads(teacher_key[0], student_key[0])}
-    sent, more, count = queries_for_other(place, pair_table, teacher_query[0])
+    chosen, count = queries_for_other(place, pair_table, teacher_query[0])
     ring[1] = along_z(ring[0], 1)
     ring[7] = along_z(ring[0], -1)
-    sent = lax.ppermute(sent, "head", other_side)
+    pieces, rank = [], 0
+    for length in PIECES:
+        piece = chosen[rank : rank + length]
+        pieces.append(lax.ppermute(piece, "head", other_side))
+        rank += length
+    more = lax.cond(
+        count[0, 0] > SENT,
+        lambda q: lax.ppermute(q, "head", other_side),
+        lambda q: q,
+        chosen[SENT:],
+    )
+    more, ring[1], ring[7] = lax.optimization_barrier((more, ring[1], ring[7]))
+    rows = prepare(place, pair_table, teacher_query[0], student_query[0])
     mine = own_chunk(place, ring[0], ring[1], ring[7])
     near_a = along_x(mine, 1)
     near_b = along_x(mine, -1)
@@ -426,9 +453,6 @@
         ring[step] = along_z(ring[step - 1], 1)
         if step < 4:
             ring[8 - step] = along_z(ring[9 - step], -1)
-    more = lax.cond(
-        count[0, 0] > SENT, lambda q: lax.ppermute(q, "head", other_side), lambda q: q, more
-    )
 
     rest_13 = rest_of(place, ring, (1, 3))
     left_13 = along_x(rest_13, 1)
@@ -441,7 +465,8 @@
         pair_table,
         plan_of([(0, 0), (0, -1), (0, 1), (0, 2), (1, 0), (3, 0), (2, 0)]),
         [mine, near_a, near_b, near_c, near_d, rest_13, rest_2],
-        queries=(teacher_query[0], sent, more, student_query[0]),
+        rows,
+        queries=(*pieces, more),
     )
     left_13, right_13, left_2, right_2, state = lax.optimization_barrier(
         (left_13, right_13, left_2, right_2, state)
@@ -454,7 +479,7 @@
         pair_table,
         plan_of([(1, -1), (3, -1), (1, 1), (3, 1), (2, -1), (2, 1)]),
         [left_13, right_13, left_2, right_2],
-        rows=rows,
+        rows,
         state=state,
     )
     everyone = ("dp_0", "dp_1", "kv_0", "kv_1")
@@ -464,7 +489,7 @@
         pair_table,
         plan_of([(1, 2), (3, 2), (2, 2)]),
         [far_1, far_3, far_2],
-        rows=rows,
+        rows,
         state=state,
         copies_out=devices,
     )

time: 129 us -> 120 us (0.930)
  waiting for transfers between devices: 45.8 us -> 29.5 us
  starting transfers between devices: 62 us -> 67.9 us
    ppermute x7, waiting for transfers between devices: 15.9 us -> 1.47 us  [program(): along_z = lambda a, by: lax.ppermute(a, ('head', 'kv_0'), z_shift(by))]
    ppermute x1 -> x4, starting transfers between devices: 0.09 us -> 3.3 us  [program(): pieces.append(lax.ppermute(piece, 'head', other_side))]
    ppermute x11, waiting for transfers between devices: 18.6 us -> 15.9 us  [program(): along_x = lambda a, by: lax.ppermute(a, 'kv_1', shift(4, by))]
    ppermute x7, starting transfers between devices: 10.8 us -> 12.7 us  [program(): along_z = lambda a, by: lax.ppermute(a, ('head', 'kv_0'), z_shift(by))]
    all_to_all x1, starting transfers between devices: 34.5 us -> 36.1 us  [program(): terms = lax.all_to_all(sums, everyone, 0, 0, tiled=True)]
    pallas_call x1 -> x2, Pallas kernels: 2.14 us -> 3 us  [the longest x1 1.79 us: queries_for_other(): pl.pallas_call(queries_kernel, out_shape=(heads_of(PAIRS), jax.ShapeDtype...]
  transfers between devices with their start and end apart: 20 -> 23, of which waited for: 9 -> 11; matrix products, arithmetic and copies ran while one was open for 1% -> 1% of each run, Pallas kernels for 10% -> 11%
where the time goes in v6:
time: 120 us; the launch traced here: 119 us
  starting transfers between devices  67.9 us (57%)
  waiting for transfers between devices  29.5 us (25%)
  Pallas kernels  15.2 us (13%)
  local copies, waits for them, and re-layouts  4.45 us (4%)
  between operations  1.68 us (1%)
    all_to_all x1, starting transfers between devices, program(): terms = lax.all_to_all(sums, everyone, 0, 0, tiled=True)  36.1 us
    ppermute x11, waiting for transfers between devices, program(): along_x = lambda a, by: lax.ppermute(a, 'kv_1', shift(4, by))  15.9 us
    ppermute x11, starting transfers between devices, program(): along_x = lambda a, by: lax.ppermute(a, 'kv_1', shift(4, by))  15.7 us
    ppermute x7, starting transfers between devices, program(): along_z = lambda a, by: lax.ppermute(a, ('head', 'kv_0'), z_shift(by))  12.7 us
    all_to_all x1, waiting for transfers between devices, program(): terms = lax.all_to_all(sums, everyone, 0, 0, tiled=True)  11.2 us
    pallas_call x3, Pallas kernels, attend(): pl.pallas_call(functools.partial(attend_kernel, first, last, counts, bloc...  8.65 us
    unnamed x18, local copies, waits for them, and re-layouts  4.31 us
    ppermute x4, starting transfers between devices, program(): pieces.append(lax.ppermute(piece, 'head', other_side))  3.3 us
  transfers between devices with their start and end apart: 23, of which 11 were waited for; matrix products, arithmetic and copies ran while one was open for 1% of the time, Pallas kernels for 11%

profile of v6, /device:TPU:1, one launch (start us, length us, event | category | flops | bytes accessed | tf_op | source)
XLA Modules:
  0.0 119.4 jit_solution(5578177920892503315)
XLA Ops:
  2.5 2.5 %collective-permute-start.1 = (bf16[3,256,128]{2,1,0:T(8,128)(2,1)S(1)}, bf16[3,256,128]{2,1,0:T(8,128)(2,1)S(1)}, u32[]{:S(2)}, u32[]{:S(2)}) collective-permute-start(bf16[3,256,128]{2,1,0:T(8,128)(2,1)S(1)} %split_heads.1.own), channel_id=1, source_target_pairs={{0,16},{16,4},{4,20},{20,8},{8,24},{24,12},{12,28},{28,0},{1,17},{... | collective-permute-start | bytes 589832 | tf_op jit(solution)/shard_map/ppermute | solution.py:427
  5.1 4.0 %collective-permute-start.2 = (bf16[3,256,128]{2,1,0:T(8,128)(2,1)S(1)}, bf16[3,256,128]{2,1,0:T(8,128)(2,1)S(1)}, u32[]{:S(2)}, u32[]{:S(2)}) collective-permute-start(bf16[3,256,128]{2,1,0:T(8,128)(2,1)S(1)} %split_heads.1.own), channel_id=1, source_target_pairs={{0,28},{16,0},{4,16},{20,4},{8,20},{24,8},{12,24},{28,12},{1,29},{... | collective-permute-start | bytes 589832 | tf_op jit(solution)/shard_map/ppermute | solution.py:427
  11.1 1.8 %queries_for_other.1 = (bf16[14,256,128]{2,1,0:T(8,128)(2,1)S(1)}, s32[1,1]{1,0:T(1,128)}) custom-call(s32[1,3]{1,0:T(1,128)S(1)} %add_bitcast_fusion.place, s32[14,2]{1,0:T(8,128)S(1)} %copy.21.table, bf16[256,1792]{1,0:T(8,128)(2,1)S(1)} %bitcast.14), custom_call_target="tpu_custom_call" | custom-call | tf_op jit(solution)/shard_map/queries_for_other/pallas_call | solution.py:102
  13.8 2.7 %collective-permute-start.5 = (bf16[3,256,128]{2,1,0:T(8,128)(2,1)S(1)}, bf16[3,256,128]{2,1,0:T(8,128)(2,1)S(1)}, u32[]{:S(2)}, u32[]{:S(2)}) collective-permute-start(bf16[3,256,128]{2,1,0:T(8,128)(2,1)S(1)} %collective-permute-done.2.refs_5_.ring_7), channel_id=1, source_target_pairs={{0,28},{16,0},{4,16},{20,4},{8,20},{24,8},{12,24},{28,12},{1,29},{... | collective-permute-start | bytes 589832 | tf_op jit(solution)/shard_map/ppermute | solution.py:427
  17.6 2.6 %collective-permute-start.13 = (bf16[5,256,128]{2,1,0:T(8,128)(2,1)S(1)}, bf16[5,256,128]{2,1,0:T(8,128)(2,1)S(1)}, u32[]{:S(2)}, u32[]{:S(2)}) collective-permute-start(bf16[5,256,128]{2,1,0:T(8,128)(2,1)S(1)} %own_chunk.1.refs_0_), channel_id=1, source_target_pairs={{0,3},{1,0},{2,1},{3,2},{4,7},{5,4},{6,5},{7,6},{8,11},{9,8},{10,9... | collective-permute-start | bytes 983048 | tf_op jit(solution)/shard_map/ppermute | solution.py:426
  23.1 2.0 %collective-permute-start.6 = (bf16[3,256,128]{2,1,0:T(8,128)(2,1)S(1)}, bf16[3,256,128]{2,1,0:T(8,128)(2,1)S(1)}, u32[]{:S(2)}, u32[]{:S(2)}) collective-permute-start(bf16[3,256,128]{2,1,0:T(8,128)(2,1)S(1)} %collective-permute-done.5.refs_3_), channel_id=1, source_target_pairs={{0,28},{16,0},{4,16},{20,4},{8,20},{24,8},{12,24},{28,12},{1,29},{... | collective-permute-start | bytes 589832 | tf_op jit(solution)/shard_map/ppermute | solution.py:427
  26.6 2.2 %collective-permute-start.18 = (bf16[2,256,128]{2,1,0:T(8,128)(2,1)S(1)}, bf16[2,256,128]{2,1,0:T(8,128)(2,1)S(1)}, u32[]{:S(2)}, u32[]{:S(2)}) collective-permute-start(bf16[2,256,128]{2,1,0:T(8,128)(2,1)S(1)} %get-tuple-element.39), channel_id=1, source_target_pairs={{0,16},{16,0},{1,17},{17,1},{2,18},{18,2},{3,19},{19,3},{4,20},{20... | collective-permute-start | bytes 393224 | tf_op jit(solution)/shard_map/ppermute | solution.py:437
  28.9 2.5 %collective-permute-start.15 = (bf16[3,256,128]{2,1,0:T(8,128)(2,1)S(1)}, bf16[3,256,128]{2,1,0:T(8,128)(2,1)S(1)}, u32[]{:S(2)}, u32[]{:S(2)}) collective-permute-start(bf16[3,256,128]{2,1,0:T(8,128)(2,1)S(1)} %slice.47), channel_id=1, source_target_pairs={{0,3},{1,0},{2,1},{3,2},{4,7},{5,4},{6,5},{7,6},{8,11},{9,8},{10,9... | collective-permute-start | bytes 589832 | tf_op jit(solution)/shard_map/ppermute | solution.py:426
  31.5 1.4 %rest_of.2.refs_5_ = bf16[10,256,128]{2,1,0:T(8,128)(2,1)S(1)} custom-call(s32[1,3]{1,0:T(1,128)S(1)} %add_bitcast_fusion.place, bf16[3,256,128]{2,1,0:T(8,128)(2,1)S(1)} %collective-permute-done.3.refs_0_, bf16[3,256,128]{2,1,0:T(8,128)(2,1)S(1)} %collective-permute-done.1.refs_1_.ring_1, bf16[3,256,128]{2,1,0:T(8,128)(2,1)S(1)} %collective-permute-done.4.refs_2_.refs_1_, ...), custom_call_target="tpu_custom_call" | custom-call | tf_op jit(solution)/shard_map/rest_of/pallas_call | solution.py:164
  34.2 1.7 %collective-permute-start.8 = (bf16[10,256,128]{2,1,0:T(8,128)(2,1)S(1)}, bf16[10,256,128]{2,1,0:T(8,128)(2,1)S(1)}, u32[]{:S(2)}, u32[]{:S(2)}) collective-permute-start(bf16[10,256,128]{2,1,0:T(8,128)(2,1)S(1)} %rest_of.2.refs_5_), channel_id=1, source_target_pairs={{0,3},{1,0},{2,1},{3,2},{4,7},{5,4},{6,5},{7,6},{8,11},{9,8},{10,9... | collective-permute-start | bytes 1966088 | tf_op jit(solution)/shard_map/ppermute | solution.py:426
  36.1 1.2 %prepare.1.refs_12_ = bf16[21,256,256]{2,1,0:T(8,128)(2,1)S(1)} custom-call(s32[1,3]{1,0:T(1,128)S(1)} %add_bitcast_fusion.place, s32[14,2]{1,0:T(8,128)S(1)} %copy.21.table, bf16[256,1792]{1,0:T(8,128)(2,1)S(1)} %bitcast.15, bf16[256,896]{1,0:T(8,128)(2,1)S(1)} %bitcast.16), custom_call_target="tpu_custom_call" | custom-call | flops 44040192 | bytes 4128768 | tf_op jit(solution)/shard_map/prepare/pallas_call | solution.py:196
  39.3 8.4 %collective-permute-done.14.refs_3_ = bf16[2,256,128]{2,1,0:T(8,128)(2,1)S(1)} collective-permute-done((bf16[2,256,128]{2,1,0:T(8,128)(2,1)S(1)}, bf16[2,256,128]{2,1,0:T(8,128)(2,1)S(1)}, u32[]{:S(2)}, u32[]{:S(2)}) %collective-permute-start.14) | collective-permute-done | bytes 131104 | tf_op jit(solution)/shard_map/ppermute | solution.py:426
  47.7 2.5 %collective-permute-start.11 = (bf16[5,256,128]{2,1,0:T(8,128)(2,1)S(1)}, bf16[5,256,128]{2,1,0:T(8,128)(2,1)S(1)}, u32[]{:S(2)}, u32[]{:S(2)}) collective-permute-start(bf16[5,256,128]{2,1,0:T(8,128)(2,1)S(1)} %rest_of.3.refs_6_), channel_id=1, source_target_pairs={{0,3},{1,0},{2,1},{3,2},{4,7},{5,4},{6,5},{7,6},{8,11},{9,8},{10,9... | collective-permute-start | bytes 983048 | tf_op jit(solution)/shard_map/ppermute | solution.py:426
  50.2 5.1 %attend.3 = (f32[56,8,256]{2,1,0:T(8,128)S(1)}, bf16[21,256,256]{2,1,0:T(8,128)(2,1)S(1)}) custom-call(s32[1,3]{1,0:T(1,128)S(1)} %add_bitcast_fusion.place, s32[14,2]{1,0:T(8,128)S(1)} %copy.21.table, s32[2,7]{1,0:T(2,128)S(1)} %copy-done.7, bf16[5,256,128]{2,1,0:T(8,128)(2,1)S(1)} %own_chunk.1.refs_0_, ...), custom_call_target="tpu_custom_call", output_to_operand_aliasing={{1}: (15, {})} | custom-call | flops 4932501504 | bytes 2293760 | tf_op jit(solution)/shard_map/attend/pallas_call | solution.py:388
  55.3 1.2 %collective-permute-done.11.refs_3_ = bf16[5,256,128]{2,1,0:T(8,128)(2,1)S(1)} collective-permute-done((bf16[5,256,128]{2,1,0:T(8,128)(2,1)S(1)}, bf16[5,256,128]{2,1,0:T(8,128)(2,1)S(1)}, u32[]{:S(2)}, u32[]{:S(2)}) %collective-permute-start.11) | collective-permute-done | bytes 327712 | tf_op jit(solution)/shard_map/ppermute | solution.py:426
  56.6 1.3 %collective-permute-start.20 = (bf16[5,256,128]{2,1,0:T(8,128)(2,1)S(1)}, bf16[5,256,128]{2,1,0:T(8,128)(2,1)S(1)}, u32[]{:S(2)}, u32[]{:S(2)}) collective-permute-start(bf16[5,256,128]{2,1,0:T(8,128)(2,1)S(1)} %slice.43), channel_id=1, source_target_pairs={{0,1},{1,2},{2,3},{3,0},{4,5},{5,6},{6,7},{7,4},{8,9},{9,10},{10,1... | collective-permute-start | bytes 983048 | tf_op jit(solution)/shard_map/ppermute | solution.py:426
  57.9 3.0 %collective-permute-start.21 = (bf16[5,256,128]{2,1,0:T(8,128)(2,1)S(1)}, bf16[5,256,128]{2,1,0:T(8,128)(2,1)S(1)}, u32[]{:S(2)}, u32[]{:S(2)}) collective-permute-start(bf16[5,256,128]{2,1,0:T(8,128)(2,1)S(1)} %slice.44), channel_id=1, source_target_pairs={{0,3},{1,0},{2,1},{3,2},{4,7},{5,4},{6,5},{7,6},{8,11},{9,8},{10,9... | collective-permute-start | bytes 983048 | tf_op jit(solution)/shard_map/ppermute | solution.py:426
  61.0 1.5 %attend.4.refs_4_ = f32[56,8,256]{2,1,0:T(8,128)S(1)} custom-call(s32[1,3]{1,0:T(1,128)S(1)} %add_bitcast_fusion.place, s32[14,2]{1,0:T(8,128)S(1)} %copy.21.table, s32[2,6]{1,0:T(2,128)S(1)} %copy-done.6, bf16[10,256,128]{2,1,0:T(8,128)(2,1)S(1)} %collective-permute-done.7.refs_0_, bf16[10,256,128]{2,1,0:T(8,128)(2,1)S(1)} %collective-permute-done.8.refs_1_, ...), custom_call_target="tpu_custom_call" | custom-call | flops 4227858432 | bytes 1966080 | tf_op jit(solution)/shard_map/attend/pallas_call | solution.py:388
  62.5 2.8 %collective-permute-done.20.refs_0_ = bf16[5,256,128]{2,1,0:T(8,128)(2,1)S(1)} collective-permute-done((bf16[5,256,128]{2,1,0:T(8,128)(2,1)S(1)}, bf16[5,256,128]{2,1,0:T(8,128)(2,1)S(1)}, u32[]{:S(2)}, u32[]{:S(2)}) %collective-permute-start.20) | collective-permute-done | bytes 327712 | tf_op jit(solution)/shard_map/ppermute | solution.py:426
  65.3 2.0 %collective-permute-done.21.refs_1_ = bf16[5,256,128]{2,1,0:T(8,128)(2,1)S(1)} collective-permute-done((bf16[5,256,128]{2,1,0:T(8,128)(2,1)S(1)}, bf16[5,256,128]{2,1,0:T(8,128)(2,1)S(1)}, u32[]{:S(2)}, u32[]{:S(2)}) %collective-permute-start.21) | collective-permute-done | bytes 327712 | tf_op jit(solution)/shard_map/ppermute | solution.py:426
  67.3 1.5 %collective-permute-done.22.refs_2_ = bf16[5,256,128]{2,1,0:T(8,128)(2,1)S(1)} collective-permute-done((bf16[5,256,128]{2,1,0:T(8,128)(2,1)S(1)}, bf16[5,256,128]{2,1,0:T(8,128)(2,1)S(1)}, u32[]{:S(2)}, u32[]{:S(2)}) %collective-permute-start.22) | collective-permute-done | bytes 327712 | tf_op jit(solution)/shard_map/ppermute | solution.py:426
  68.8 2.0 %attend.5 = (f32[7,256]{1,0:T(8,128)S(1)}, f32[128,128]{1,0:T(8,128)}) custom-call(s32[1,3]{1,0:T(1,128)S(1)} %add_bitcast_fusion.place, s32[14,2]{1,0:T(8,128)S(1)} %copy.21.table, s32[2,3]{1,0:T(2,128)S(1)} %copy-done.5, bf16[5,256,128]{2,1,0:T(8,128)(2,1)S(1)} %collective-permute-done.20.refs_0_, ...), custom_call_target="tpu_custom_call" | custom-call | flops 2113929216 | bytes 983040 | tf_op jit(solution)/shard_map/attend/pallas_call | solution.py:388
  70.8 36.1 %all-to-all-start = ((f32[128,1,128]{2,1,0:T(1,128)}), f32[128,1,128]{2,1,0:T(1,128)S(1)}, u32[]{:S(2)}, u32[]{:S(2)}) async-start(f32[128,1,128]{2,1,0:T(1,128)} %bitcast.11), calls=%async_computation | async-start | bytes 131072 | tf_op jit(solution)/shard_map/all_to_all | solution.py:496
  107.6 11.2 %all-to-all-done = f32[128,1,128]{2,1,0:T(1,128)S(1)} async-done(((f32[128,1,128]{2,1,0:T(1,128)}), f32[128,1,128]{2,1,0:T(1,128)S(1)}, u32[]{:S(2)}, u32[]{:S(2)}) %all-to-all-start) | async-done | bytes 65568 | tf_op jit(solution)/shard_map/all_to_all | solution.py:496
  (60 shorter events, 14.4 us)
Async XLA Ops:
  2.5 11.2 %collective-permute-start.1 = (bf16[3,256,128]{2,1,0:T(8,128)(2,1)S(1)}, bf16[3,256,128]{2,1,0:T(8,128)(2,1)S(1)}, u32[]{:S(2)}, u32[]{:S(2)}) collective-permute-start(bf16[3,256,128]{2,1,0:T(8,128)(2,1)S(1)} %split_heads.1.own), channel_id=1, source_target_pairs={{0,16},{16,4},{4,20},{20,8},{8,24},{24,12},{12,28},{28,0},{1,17},{... | collective-permute-start | bytes 589832 | tf_op jit(solution)/shard_map/ppermute | solution.py:427
  5.1 8.7 %collective-permute-start.2 = (bf16[3,256,128]{2,1,0:T(8,128)(2,1)S(1)}, bf16[3,256,128]{2,1,0:T(8,128)(2,1)S(1)}, u32[]{:S(2)}, u32[]{:S(2)}) collective-permute-start(bf16[3,256,128]{2,1,0:T(8,128)(2,1)S(1)} %split_heads.1.own), channel_id=1, source_target_pairs={{0,28},{16,0},{4,16},{20,4},{8,20},{24,8},{12,24},{28,12},{1,29},{... | collective-permute-start | bytes 589832 | tf_op jit(solution)/shard_map/ppermute | solution.py:427
  12.9 23.1 %copy-start.1 = (bf16[1,256,1792]{2,1,0:T(8,128)(2,1)S(1)}, bf16[1,256,1792]{2,1,0:T(8,128)(2,1)}, u32[]{:S(2)}) copy-start(bf16[1,256,1792]{2,1,0:T(8,128)(2,1)} %param.10) | copy-start | bytes 2752516
  13.7 6.7 %collective-permute-start.3 = (bf16[3,256,128]{2,1,0:T(8,128)(2,1)S(1)}, bf16[3,256,128]{2,1,0:T(8,128)(2,1)S(1)}, u32[]{:S(2)}, u32[]{:S(2)}) collective-permute-start(bf16[3,256,128]{2,1,0:T(8,128)(2,1)S(1)} %collective-permute-done.1.refs_1_.ring_1), channel_id=1, source_target_pairs={{0,16},{16,4},{4,20},{20,8},{8,24},{24,12},{12,28},{28,0},{1,17},{... | collective-permute-start | bytes 589832 | tf_op jit(solution)/shard_map/ppermute | solution.py:427
  13.8 9.2 %collective-permute-start.5 = (bf16[3,256,128]{2,1,0:T(8,128)(2,1)S(1)}, bf16[3,256,128]{2,1,0:T(8,128)(2,1)S(1)}, u32[]{:S(2)}, u32[]{:S(2)}) collective-permute-start(bf16[3,256,128]{2,1,0:T(8,128)(2,1)S(1)} %collective-permute-done.2.refs_5_.ring_7), channel_id=1, source_target_pairs={{0,28},{16,0},{4,16},{20,4},{8,20},{24,8},{12,24},{28,12},{1,29},{... | collective-permute-start | bytes 589832 | tf_op jit(solution)/shard_map/ppermute | solution.py:427
  16.5 5.6 %collective-permute-start.16 = (bf16[2,256,128]{2,1,0:T(8,128)(2,1)S(1)}, bf16[2,256,128]{2,1,0:T(8,128)(2,1)S(1)}, u32[]{:S(2)}, u32[]{:S(2)}) collective-permute-start(bf16[2,256,128]{2,1,0:T(8,128)(2,1)S(1)} %get-tuple-element.41), channel_id=1, source_target_pairs={{0,16},{16,0},{1,17},{17,1},{2,18},{18,2},{3,19},{19,3},{4,20},{20... | collective-permute-start | bytes 393224 | tf_op jit(solution)/shard_map/ppermute | solution.py:437
  17.6 11.2 %collective-permute-start.13 = (bf16[5,256,128]{2,1,0:T(8,128)(2,1)S(1)}, bf16[5,256,128]{2,1,0:T(8,128)(2,1)S(1)}, u32[]{:S(2)}, u32[]{:S(2)}) collective-permute-start(bf16[5,256,128]{2,1,0:T(8,128)(2,1)S(1)} %own_chunk.1.refs_0_), channel_id=1, source_target_pairs={{0,3},{1,0},{2,1},{3,2},{4,7},{5,4},{6,5},{7,6},{8,11},{9,8},{10,9... | collective-permute-start | bytes 983048 | tf_op jit(solution)/shard_map/ppermute | solution.py:426
  20.5 5.7 %collective-permute-start.4 = (bf16[3,256,128]{2,1,0:T(8,128)(2,1)S(1)}, bf16[3,256,128]{2,1,0:T(8,128)(2,1)S(1)}, u32[]{:S(2)}, u32[]{:S(2)}) collective-permute-start(bf16[3,256,128]{2,1,0:T(8,128)(2,1)S(1)} %collective-permute-done.3.refs_0_), channel_id=1, source_target_pairs={{0,16},{16,4},{4,20},{20,8},{8,24},{24,12},{12,28},{28,0},{1,17},{... | collective-permute-start | bytes 589832 | tf_op jit(solution)/shard_map/ppermute | solution.py:427
  21.6 12.5 %collective-permute-start.12 = (bf16[5,256,128]{2,1,0:T(8,128)(2,1)S(1)}, bf16[5,256,128]{2,1,0:T(8,128)(2,1)S(1)}, u32[]{:S(2)}, u32[]{:S(2)}) collective-permute-start(bf16[5,256,128]{2,1,0:T(8,128)(2,1)S(1)} %own_chunk.1.refs_0_), channel_id=1, source_target_pairs={{0,1},{1,2},{2,3},{3,0},{4,5},{5,6},{6,7},{7,4},{8,9},{9,10},{10,1... | collective-permute-start | bytes 983048 | tf_op jit(solution)/shard_map/ppermute | solution.py:426
  22.1 4.4 %collective-permute-start.17 = (bf16[2,256,128]{2,1,0:T(8,128)(2,1)S(1)}, bf16[2,256,128]{2,1,0:T(8,128)(2,1)S(1)}, u32[]{:S(2)}, u32[]{:S(2)}) collective-permute-start(bf16[2,256,128]{2,1,0:T(8,128)(2,1)S(1)} %get-tuple-element.40), channel_id=1, source_target_pairs={{0,16},{16,0},{1,17},{17,1},{2,18},{18,2},{3,19},{19,3},{4,20},{20... | collective-permute-start | bytes 393224 | tf_op jit(solution)/shard_map/ppermute | solution.py:437
  23.1 5.9 %collective-permute-start.6 = (bf16[3,256,128]{2,1,0:T(8,128)(2,1)S(1)}, bf16[3,256,128]{2,1,0:T(8,128)(2,1)S(1)}, u32[]{:S(2)}, u32[]{:S(2)}) collective-permute-start(bf16[3,256,128]{2,1,0:T(8,128)(2,1)S(1)} %collective-permute-done.5.refs_3_), channel_id=1, source_target_pairs={{0,28},{16,0},{4,16},{20,4},{8,20},{24,8},{12,24},{28,12},{1,29},{... | collective-permute-start | bytes 589832 | tf_op jit(solution)/shard_map/ppermute | solution.py:427
  26.2 9.7 %collective-permute-start.9 = (bf16[3,256,128]{2,1,0:T(8,128)(2,1)S(1)}, bf16[3,256,128]{2,1,0:T(8,128)(2,1)S(1)}, u32[]{:S(2)}, u32[]{:S(2)}) collective-permute-start(bf16[3,256,128]{2,1,0:T(8,128)(2,1)S(1)} %collective-permute-done.4.refs_2_.refs_1_), channel_id=1, source_target_pairs={{0,16},{16,4},{4,20},{20,8},{8,24},{24,12},{12,28},{28,0},{1,17},{... | collective-permute-start | bytes 589832 | tf_op jit(solution)/shard_map/ppermute | solution.py:427
  26.6 6.7 %collective-permute-start.18 = (bf16[2,256,128]{2,1,0:T(8,128)(2,1)S(1)}, bf16[2,256,128]{2,1,0:T(8,128)(2,1)S(1)}, u32[]{:S(2)}, u32[]{:S(2)}) collective-permute-start(bf16[2,256,128]{2,1,0:T(8,128)(2,1)S(1)} %get-tuple-element.39), channel_id=1, source_target_pairs={{0,16},{16,0},{1,17},{17,1},{2,18},{18,2},{3,19},{19,3},{4,20},{20... | collective-permute-start | bytes 393224 | tf_op jit(solution)/shard_map/ppermute | solution.py:437
  28.8 9.5 %collective-permute-start.19 = (bf16[3,256,128]{2,1,0:T(8,128)(2,1)S(1)}, bf16[3,256,128]{2,1,0:T(8,128)(2,1)S(1)}, u32[]{:S(2)}, u32[]{:S(2)}) collective-permute-start(bf16[3,256,128]{2,1,0:T(8,128)(2,1)S(1)} %slice.42), channel_id=1, source_target_pairs={{0,16},{16,0},{1,17},{17,1},{2,18},{18,2},{3,19},{19,3},{4,20},{20... | collective-permute-start | bytes 589832 | tf_op jit(solution)/shard_map/ppermute | solution.py:437
  28.9 21.3 %collective-permute-start.15 = (bf16[3,256,128]{2,1,0:T(8,128)(2,1)S(1)}, bf16[3,256,128]{2,1,0:T(8,128)(2,1)S(1)}, u32[]{:S(2)}, u32[]{:S(2)}) collective-permute-start(bf16[3,256,128]{2,1,0:T(8,128)(2,1)S(1)} %slice.47), channel_id=1, source_target_pairs={{0,3},{1,0},{2,1},{3,2},{4,7},{5,4},{6,5},{7,6},{8,11},{9,8},{10,9... | collective-permute-start | bytes 589832 | tf_op jit(solution)/shard_map/ppermute | solution.py:426
  33.2 23.3 %collective-permute-start.7 = (bf16[10,256,128]{2,1,0:T(8,128)(2,1)S(1)}, bf16[10,256,128]{2,1,0:T(8,128)(2,1)S(1)}, u32[]{:S(2)}, u32[]{:S(2)}) collective-permute-start(bf16[10,256,128]{2,1,0:T(8,128)(2,1)S(1)} %rest_of.2.refs_5_), channel_id=1, source_target_pairs={{0,1},{1,2},{2,3},{3,0},{4,5},{5,6},{6,7},{7,4},{8,9},{9,10},{10,1... | collective-permute-start | bytes 1966088 | tf_op jit(solution)/shard_map/ppermute | solution.py:426
  34.2 22.4 %collective-permute-start.8 = (bf16[10,256,128]{2,1,0:T(8,128)(2,1)S(1)}, bf16[10,256,128]{2,1,0:T(8,128)(2,1)S(1)}, u32[]{:S(2)}, u32[]{:S(2)}) collective-permute-start(bf16[10,256,128]{2,1,0:T(8,128)(2,1)S(1)} %rest_of.2.refs_5_), channel_id=1, source_target_pairs={{0,3},{1,0},{2,1},{3,2},{4,7},{5,4},{6,5},{7,6},{8,11},{9,8},{10,9... | collective-permute-start | bytes 1966088 | tf_op jit(solution)/shard_map/ppermute | solution.py:426
  35.9 11.7 %collective-permute-start.14 = (bf16[2,256,128]{2,1,0:T(8,128)(2,1)S(1)}, bf16[2,256,128]{2,1,0:T(8,128)(2,1)S(1)}, u32[]{:S(2)}, u32[]{:S(2)}) collective-permute-start(bf16[2,256,128]{2,1,0:T(8,128)(2,1)S(1)} %slice.46), channel_id=1, source_target_pairs={{0,1},{1,2},{2,3},{3,0},{4,5},{5,6},{6,7},{7,4},{8,9},{9,10},{10,1... | collective-permute-start | bytes 393224 | tf_op jit(solution)/shard_map/ppermute | solution.py:426
  38.3 17.0 %collective-permute-start.10 = (bf16[5,256,128]{2,1,0:T(8,128)(2,1)S(1)}, bf16[5,256,128]{2,1,0:T(8,128)(2,1)S(1)}, u32[]{:S(2)}, u32[]{:S(2)}) collective-permute-start(bf16[5,256,128]{2,1,0:T(8,128)(2,1)S(1)} %rest_of.3.refs_6_), channel_id=1, source_target_pairs={{0,1},{1,2},{2,3},{3,0},{4,5},{5,6},{6,7},{7,4},{8,9},{9,10},{10,1... | collective-permute-start | bytes 983048 | tf_op jit(solution)/shard_map/ppermute | solution.py:426
  47.7 8.9 %collective-permute-start.11 = (bf16[5,256,128]{2,1,0:T(8,128)(2,1)S(1)}, bf16[5,256,128]{2,1,0:T(8,128)(2,1)S(1)}, u32[]{:S(2)}, u32[]{:S(2)}) collective-permute-start(bf16[5,256,128]{2,1,0:T(8,128)(2,1)S(1)} %rest_of.3.refs_6_), channel_id=1, source_target_pairs={{0,3},{1,0},{2,1},{3,2},{4,7},{5,4},{6,5},{7,6},{8,11},{9,8},{10,9... | collective-permute-start | bytes 983048 | tf_op jit(solution)/shard_map/ppermute | solution.py:426
  56.6 8.7 %collective-permute-start.20 = (bf16[5,256,128]{2,1,0:T(8,128)(2,1)S(1)}, bf16[5,256,128]{2,1,0:T(8,128)(2,1)S(1)}, u32[]{:S(2)}, u32[]{:S(2)}) collective-permute-start(bf16[5,256,128]{2,1,0:T(8,128)(2,1)S(1)} %slice.43), channel_id=1, source_target_pairs={{0,1},{1,2},{2,3},{3,0},{4,5},{5,6},{6,7},{7,4},{8,9},{9,10},{10,1... | collective-permute-start | bytes 983048 | tf_op jit(solution)/shard_map/ppermute | solution.py:426
  57.9 9.4 %collective-permute-start.21 = (bf16[5,256,128]{2,1,0:T(8,128)(2,1)S(1)}, bf16[5,256,128]{2,1,0:T(8,128)(2,1)S(1)}, u32[]{:S(2)}, u32[]{:S(2)}) collective-permute-start(bf16[5,256,128]{2,1,0:T(8,128)(2,1)S(1)} %slice.44), channel_id=1, source_target_pairs={{0,3},{1,0},{2,1},{3,2},{4,7},{5,4},{6,5},{7,6},{8,11},{9,8},{10,9... | collective-permute-start | bytes 983048 | tf_op jit(solution)/shard_map/ppermute | solution.py:426
  60.9 7.9 %collective-permute-start.22 = (bf16[5,256,128]{2,1,0:T(8,128)(2,1)S(1)}, bf16[5,256,128]{2,1,0:T(8,128)(2,1)S(1)}, u32[]{:S(2)}, u32[]{:S(2)}) collective-permute-start(bf16[5,256,128]{2,1,0:T(8,128)(2,1)S(1)} %collective-permute-done.10.refs_2_), channel_id=1, source_target_pairs={{0,1},{1,2},{2,3},{3,0},{4,5},{5,6},{6,7},{7,4},{8,9},{9,10},{10,1... | collective-permute-start | bytes 983048 | tf_op jit(solution)/shard_map/ppermute | solution.py:426
  70.8 47.9 %all-to-all-start = ((f32[128,1,128]{2,1,0:T(1,128)}), f32[128,1,128]{2,1,0:T(1,128)S(1)}, u32[]{:S(2)}, u32[]{:S(2)}) async-start(f32[128,1,128]{2,1,0:T(1,128)} %bitcast.11), calls=%async_computation | async-start | bytes 131072 | tf_op jit(solution)/shard_map/all_to_all | solution.py:496
  (7 other events, 73.8 us)

commit v7 on v6

--- a/solution.py
+++ b/solution.py
@@ -23,6 +23,7 @@
 LANE = 128
 SUB = 8
 MASKED = -1e30
+LARGE = 2.0**100
 LN2 = math.log(2.0)
 KAPPA = 1.0 / (LN2 * math.sqrt(DH))
 STATE = 3 * PAIRS + 2 * STUDENTS
@@ -235,10 +236,10 @@
             (state,) = take(1)
     (keys,) = take(1)
     if first:
-        (received,) = take(1)
+        received, entry = take(2)
     if last:
         (state,) = take(1)
-    (sems,) = refs
+    offsets, sems = refs
     head, z_hi, x = place[0, 0], place[0, 1], place[0, 2]
     row_block = z_hi * 4 + x
 
@@ -264,15 +265,17 @@
     for c in copies:
         c.start()
     if first:
-        for part, value in ((0, MASKED), (TL, 0.0), (TC, 0.0)):
-            state[part : part + PAIRS] = jnp.full((PAIRS, SUB, ROWS), value, jnp.float32)
-        for part, value in ((SM, MASKED), (SL, 0.0)):
-            state[part : part + STUDENTS] = jnp.full((STUDENTS, SUB, ROWS), value, jnp.float32)
         for c in inputs:
             c.wait()
         fill_received(place, table, received, rows)
     else:
+        entry = before
         state[...] = before[...]
+
+    for p in range(PAIRS):
+        kv_head = lax.div(table[head * STUDENTS + p // 2, p % 2], GROUP)
+        side = jnp.where(lax.div(kv_head, 2) == head, 0, OWN)
+        offsets[p] = side + lax.rem(kv_head, 2)
 
     def product(k, p):
         return lax.dot_general(
@@ -282,36 +285,74 @@
             preferred_element_type=jnp.float32,
         )
 
-    def update(logits, mask, m_index, l_index):
-        if mask is not None:
+    def folded(a):
+        return a.reshape(ROWS // SUB, SUB, ROWS)
+
+    def own_block():
+        key_pos = lax.broadcasted_iota(jnp.int32, (ROWS, ROWS), 0)
+        row_pos = lax.broadcasted_iota(jnp.int32, (ROWS, ROWS), 1)
+        mask = key_pos <= row_pos
+
+        def begin(logits, m_index, l_index):
             logits = jnp.where(mask, logits, MASKED)
-        folded = logits.reshape(ROWS // SUB, SUB, ROWS)
-        old = state[m_index]
-        new = jnp.maximum(old, jnp.max(folded, axis=0))
-        weights = jnp.exp2(folded - new[None])
-        rescale = jnp.exp2(old - new)
-        state[m_index] = new
-        state[l_index] = state[l_index] * rescale + jnp.sum(weights, axis=0)
-        return weights, rescale
-
-    def block(own_at, other_at, masked):
-        mask = None
-        if masked:
-            key_pos = lax.broadcasted_iota(jnp.int32, (ROWS, ROWS), 0)
-            row_pos = lax.broadcasted_iota(jnp.int32, (ROWS, ROWS), 1)
-            mask = key_pos <= row_pos
-        student_keys = keys[own_at + 2]
+            top = jnp.max(logits, axis=0, keepdims=True)
+            weights = folded(jnp.exp2(logits - top))
+            state[m_index] = jnp.broadcast_to(top, (SUB, ROWS))
+            state[l_index] = jnp.sum(weights, axis=0)
+            return weights
+
+        for s in range(STUDENTS):
+            zs = product(keys[2], PAIRS + s)
+            begin(zs, SM + s, SL + s)
+            for c in range(2):
+                p = 2 * s + c
+                zt = product(keys[offsets[p]], p)
+                weights = begin(zt, p, TL + p)
+                state[TC + p] = jnp.sum(weights * folded(zt - zs), axis=0)
+
+    def block(base):
+        def add(logits, m_index, l_index):
+            weights = jnp.exp2(folded(logits) - state[m_index][None])
+            state[l_index] = state[l_index] + jnp.sum(weights, axis=0)
+            return weights
+
+        student_keys = keys[base + 2]
         for s in range(STUDENTS):
             zs = product(student_keys, PAIRS + s)
-            update(zs, mask, SM + s, SL + s)
+            add(zs, SM + s, SL + s)
             for c in range(2):
                 p = 2 * s + c
-                kv_head = lax.div(table[head * STUDENTS + s, c], GROUP)
-                base = jnp.where(lax.div(kv_head, 2) == head, own_at, other_at)
-                zt = product(keys[base + lax.rem(kv_head, 2)], p)
-                weights, rescale = update(zt, mask, p, TL + p)
-                gap = (zt - zs).reshape(ROWS // SUB, SUB, ROWS)
-                state[TC + p] = state[TC + p] * rescale + jnp.sum(weights * gap, axis=0)
+                zt = product(keys[base + offsets[p]], p)
+                weights = add(zt, p, TL + p)
+                state[TC + p] = state[TC + p] + jnp.sum(weights * folded(zt - zs), axis=0)
+
+    def exact_block(base):
+        def add(logits, m_index, l_index):
+            logits = folded(logits)
+            old = state[m_index]
+            new = jnp.maximum(old, jnp.max(logits, axis=0))
+            weights = jnp.exp2(logits - new[None])
+            rescale = jnp.exp2(old - new)
+            state[m_index] = new
+            state[l_index] = state[l_index] * rescale + jnp.sum(weights, axis=0)
+            return weights, rescale
+
+        def student(s, carry):
+            zs = product(keys[base + 2], PAIRS + s)
+            add(zs, SM + s, SL + s)
+            for c in range(2):
+                p = 2 * s + c
+                zt = product(keys[base + offsets[p]], p)
+                weights, rescale = add(zt, p, TL + p)
+                cross = jnp.sum(weights * folded(zt - zs), axis=0)
+                state[TC + p] = state[TC + p] * rescale + cross
+            return carry
+
+        lax.fori_loop(0, STUDENTS, student, 0)
+
+    def visible(i):
+        chunk = lax.bitwise_and(z_hi - plan[0, i], 3)
+        return chunk * 4 + lax.bitwise_and(x + plan[1, i], 3) < row_block
 
     def step(i, carry):
         for at_block, c in arrivals:
@@ -320,22 +361,34 @@
             def _():
                 c.wait()
 
-        chunk = lax.bitwise_and(z_hi - plan[0, i], 3)
-        position = chunk * 4 + lax.bitwise_and(x + plan[1, i], 3)
-
-        @pl.when(position < row_block)
+        @pl.when(visible(i))
         def _():
-            block(CHUNK * i, CHUNK * i + OWN, False)
-
-        if first:
-
-            @pl.when(position == row_block)
-            def _():
-                block(CHUNK * i, CHUNK * i + OWN, True)
+            block(CHUNK * i)
 
         return carry
 
-    lax.fori_loop(0, blocks, step, 0)
+    def exact_step(i, carry):
+        @pl.when(visible(i))
+        def _():
+            exact_block(CHUNK * i)
+
+        return carry
+
+    if first:
+        arrivals[0][1].wait()
+        arrivals = arrivals[1:]
+        own_block()
+        entry[...] = state[...]
+    lax.fori_loop(int(first), blocks, step, 0)
+
+    largest = jnp.maximum(
+        jnp.max(state[TL : TL + PAIRS]), jnp.max(state[SL : SL + STUDENTS])
+    )
+
+    @pl.when(largest > LARGE)
+    def _():
+        state[...] = entry[...]
+        lax.fori_loop(int(first), blocks, exact_step, 0)
 
     if not last:
         return
@@ -382,8 +435,10 @@
     scratch = [pltpu.VMEM((sum(counts), ROWS, DH), jnp.bfloat16)]
     if first:
         scratch.append(pltpu.VMEM((PAIRS, ROWS, DH), jnp.bfloat16))
+        scratch.append(pltpu.VMEM(state_shape.shape, jnp.float32))
     if last:
         scratch.append(pltpu.VMEM(state_shape.shape, jnp.float32))
+    scratch.append(pltpu.SMEM((PAIRS,), jnp.int32))
     scratch.append(pltpu.SemaphoreType.DMA((len(groups) + len(PIECES) + 1,)))
     return pl.pallas_call(
         functools.partial(attend_kernel, first, last, counts, blocks),

time: 120 us -> 147 us (1.23)
  starting transfers between devices: 67.9 us -> 95.2 us
    all_to_all x1, starting transfers between devices: 36.1 us -> 55.5 us  [program(): terms = lax.all_to_all(sums, everyone, 0, 0, tiled=True)]
    ppermute x11, starting transfers between devices: 15.7 us -> 23.7 us  [program(): along_x = lambda a, by: lax.ppermute(a, 'kv_1', shift(4, by))]
  transfers between devices with their start and end apart: 23 -> 23, of which waited for: 11 -> 10; matrix products, arithmetic and copies ran while one was open for 1% -> 1% of each run, Pallas kernels for 11% -> 9%
where the time goes in v7:
time: 147 us
  starting transfers between devices  95.2 us (65%)
  waiting for transfers between devices  29 us (20%)
  Pallas kernels  15.9 us (11%)
  local copies, waits for them, and re-layouts  4.45 us (3%)
  between operations  1.67 us (1%)
    all_to_all x1, starting transfers between devices, program(): terms = lax.all_to_all(sums, everyone, 0, 0, tiled=True)  55.5 us
    ppermute x11, starting transfers between devices, program(): along_x = lambda a, by: lax.ppermute(a, 'kv_1', shift(4, by))  23.7 us
    ppermute x11, waiting for transfers between devices, program(): along_x = lambda a, by: lax.ppermute(a, 'kv_1', shift(4, by))  15.5 us
    ppermute x7, starting transfers between devices, program(): along_z = lambda a, by: lax.ppermute(a, ('head', 'kv_0'), z_shift(by))  12.7 us
    all_to_all x1, waiting for transfers between devices, program(): terms = lax.all_to_all(sums, everyone, 0, 0, tiled=True)  11.2 us
    pallas_call x3, Pallas kernels, attend(): pl.pallas_call(functools.partial(attend_kernel, first, last, counts, bloc...  9.31 us
    unnamed x18, local copies, waits for them, and re-layouts  4.31 us
    ppermute x4, starting transfers between devices, program(): pieces.append(lax.ppermute(piece, 'head', other_side))  3.3 us
  transfers between devices with their start and end apart: 23, of which 10 were waited for; matrix products, arithmetic and copies ran while one was open for 1% of the time, Pallas kernels for 9%

profile of v7, /device:TPU:1, one launch (start us, length us, event | category | flops | bytes accessed | tf_op | source)
XLA Modules:
  0.0 146.9 jit_solution(2946533093295433974)
XLA Ops:
  2.5 2.5 %collective-permute-start.1 = (bf16[3,256,128]{2,1,0:T(8,128)(2,1)S(1)}, bf16[3,256,128]{2,1,0:T(8,128)(2,1)S(1)}, u32[]{:S(2)}, u32[]{:S(2)}) collective-permute-start(bf16[3,256,128]{2,1,0:T(8,128)(2,1)S(1)} %split_heads.1.own), channel_id=1, source_target_pairs={{0,16},{16,4},{4,20},{20,8},{8,24},{24,12},{12,28},{28,0},{1,17},{... | collective-permute-start | bytes 589832 | tf_op jit(solution)/shard_map/ppermute | solution.py:482
  5.1 4.0 %collective-permute-start.2 = (bf16[3,256,128]{2,1,0:T(8,128)(2,1)S(1)}, bf16[3,256,128]{2,1,0:T(8,128)(2,1)S(1)}, u32[]{:S(2)}, u32[]{:S(2)}) collective-permute-start(bf16[3,256,128]{2,1,0:T(8,128)(2,1)S(1)} %split_heads.1.own), channel_id=1, source_target_pairs={{0,28},{16,0},{4,16},{20,4},{8,20},{24,8},{12,24},{28,12},{1,29},{... | collective-permute-start | bytes 589832 | tf_op jit(solution)/shard_map/ppermute | solution.py:482
  11.1 1.8 %queries_for_other.1 = (bf16[14,256,128]{2,1,0:T(8,128)(2,1)S(1)}, s32[1,1]{1,0:T(1,128)}) custom-call(s32[1,3]{1,0:T(1,128)S(1)} %add_bitcast_fusion.place, s32[14,2]{1,0:T(8,128)S(1)} %copy.21.table, bf16[256,1792]{1,0:T(8,128)(2,1)S(1)} %bitcast.14), custom_call_target="tpu_custom_call" | custom-call | tf_op jit(solution)/shard_map/queries_for_other/pallas_call | solution.py:103
  13.8 2.7 %collective-permute-start.5 = (bf16[3,256,128]{2,1,0:T(8,128)(2,1)S(1)}, bf16[3,256,128]{2,1,0:T(8,128)(2,1)S(1)}, u32[]{:S(2)}, u32[]{:S(2)}) collective-permute-start(bf16[3,256,128]{2,1,0:T(8,128)(2,1)S(1)} %collective-permute-done.2.refs_5_.ring_7), channel_id=1, source_target_pairs={{0,28},{16,0},{4,16},{20,4},{8,20},{24,8},{12,24},{28,12},{1,29},{... | collective-permute-start | bytes 589832 | tf_op jit(solution)/shard_map/ppermute | solution.py:482
  17.6 2.6 %collective-permute-start.13 = (bf16[5,256,128]{2,1,0:T(8,128)(2,1)S(1)}, bf16[5,256,128]{2,1,0:T(8,128)(2,1)S(1)}, u32[]{:S(2)}, u32[]{:S(2)}) collective-permute-start(bf16[5,256,128]{2,1,0:T(8,128)(2,1)S(1)} %own_chunk.1.refs_0_), channel_id=1, source_target_pairs={{0,3},{1,0},{2,1},{3,2},{4,7},{5,4},{6,5},{7,6},{8,11},{9,8},{10,9... | collective-permute-start | bytes 983048 | tf_op jit(solution)/shard_map/ppermute | solution.py:481
  20.5 1.2 collective-permute-start.4
  23.1 2.0 %collective-permute-start.6 = (bf16[3,256,128]{2,1,0:T(8,128)(2,1)S(1)}, bf16[3,256,128]{2,1,0:T(8,128)(2,1)S(1)}, u32[]{:S(2)}, u32[]{:S(2)}) collective-permute-start(bf16[3,256,128]{2,1,0:T(8,128)(2,1)S(1)} %collective-permute-done.5.refs_3_), channel_id=1, source_target_pairs={{0,28},{16,0},{4,16},{20,4},{8,20},{24,8},{12,24},{28,12},{1,29},{... | collective-permute-start | bytes 589832 | tf_op jit(solution)/shard_map/ppermute | solution.py:482
  25.0 1.2 collective-permute-done.4.refs_2_.refs_1_
  26.6 2.2 %collective-permute-start.18 = (bf16[2,256,128]{2,1,0:T(8,128)(2,1)S(1)}, bf16[2,256,128]{2,1,0:T(8,128)(2,1)S(1)}, u32[]{:S(2)}, u32[]{:S(2)}) collective-permute-start(bf16[2,256,128]{2,1,0:T(8,128)(2,1)S(1)} %get-tuple-element.39), channel_id=1, source_target_pairs={{0,16},{16,0},{1,17},{17,1},{2,18},{18,2},{3,19},{19,3},{4,20},{20... | collective-permute-start | bytes 393224 | tf_op jit(solution)/shard_map/ppermute | solution.py:492
  28.9 2.5 %collective-permute-start.15 = (bf16[3,256,128]{2,1,0:T(8,128)(2,1)S(1)}, bf16[3,256,128]{2,1,0:T(8,128)(2,1)S(1)}, u32[]{:S(2)}, u32[]{:S(2)}) collective-permute-start(bf16[3,256,128]{2,1,0:T(8,128)(2,1)S(1)} %slice.47), channel_id=1, source_target_pairs={{0,3},{1,0},{2,1},{3,2},{4,7},{5,4},{6,5},{7,6},{8,11},{9,8},{10,9... | collective-permute-start | bytes 589832 | tf_op jit(solution)/shard_map/ppermute | solution.py:481
  31.5 1.4 rest_of.2.refs_5_
  34.2 1.7 %collective-permute-start.8 = (bf16[10,256,128]{2,1,0:T(8,128)(2,1)S(1)}, bf16[10,256,128]{2,1,0:T(8,128)(2,1)S(1)}, u32[]{:S(2)}, u32[]{:S(2)}) collective-permute-start(bf16[10,256,128]{2,1,0:T(8,128)(2,1)S(1)} %rest_of.2.refs_5_), channel_id=1, source_target_pairs={{0,3},{1,0},{2,1},{3,2},{4,7},{5,4},{6,5},{7,6},{8,11},{9,8},{10,9... | collective-permute-start | bytes 1966088 | tf_op jit(solution)/shard_map/ppermute | solution.py:481
  36.1 1.2 prepare.1.refs_12_
  39.3 8.4 %collective-permute-done.14.refs_3_ = bf16[2,256,128]{2,1,0:T(8,128)(2,1)S(1)} collective-permute-done((bf16[2,256,128]{2,1,0:T(8,128)(2,1)S(1)}, bf16[2,256,128]{2,1,0:T(8,128)(2,1)S(1)}, u32[]{:S(2)}, u32[]{:S(2)}) %collective-permute-start.14) | collective-permute-done | bytes 131104 | tf_op jit(solution)/shard_map/ppermute | solution.py:481
  47.7 2.5 %collective-permute-start.11 = (bf16[5,256,128]{2,1,0:T(8,128)(2,1)S(1)}, bf16[5,256,128]{2,1,0:T(8,128)(2,1)S(1)}, u32[]{:S(2)}, u32[]{:S(2)}) collective-permute-start(bf16[5,256,128]{2,1,0:T(8,128)(2,1)S(1)} %rest_of.3.refs_6_), channel_id=1, source_target_pairs={{0,3},{1,0},{2,1},{3,2},{4,7},{5,4},{6,5},{7,6},{8,11},{9,8},{10,9... | collective-permute-start | bytes 983048 | tf_op jit(solution)/shard_map/ppermute | solution.py:481
  50.2 5.2 %attend.3 = (f32[56,8,256]{2,1,0:T(8,128)S(1)}, bf16[21,256,256]{2,1,0:T(8,128)(2,1)S(1)}) custom-call(s32[1,3]{1,0:T(1,128)S(1)} %add_bitcast_fusion.place, s32[14,2]{1,0:T(8,128)S(1)} %copy.21.table, s32[2,7]{1,0:T(2,128)S(1)} %copy-done.7, bf16[5,256,128]{2,1,0:T(8,128)(2,1)S(1)} %own_chunk.1.refs_0_, ...), custom_call_target="tpu_custom_call", output_to_operand_aliasing={{1}: (15, {})} | custom-call | flops 4932501504 | bytes 2293760 | tf_op jit(solution)/shard_map/attend/pallas_call | solution.py:443
  56.6 2.4 %collective-permute-start.20 = (bf16[5,256,128]{2,1,0:T(8,128)(2,1)S(1)}, bf16[5,256,128]{2,1,0:T(8,128)(2,1)S(1)}, u32[]{:S(2)}, u32[]{:S(2)}) collective-permute-start(bf16[5,256,128]{2,1,0:T(8,128)(2,1)S(1)} %slice.43), channel_id=1, source_target_pairs={{0,1},{1,2},{2,3},{3,0},{4,5},{5,6},{6,7},{7,4},{8,9},{9,10},{10,1... | collective-permute-start | bytes 983048 | tf_op jit(solution)/shard_map/ppermute | solution.py:481
  59.0 9.9 %collective-permute-start.21 = (bf16[5,256,128]{2,1,0:T(8,128)(2,1)S(1)}, bf16[5,256,128]{2,1,0:T(8,128)(2,1)S(1)}, u32[]{:S(2)}, u32[]{:S(2)}) collective-permute-start(bf16[5,256,128]{2,1,0:T(8,128)(2,1)S(1)} %slice.44), channel_id=1, source_target_pairs={{0,3},{1,0},{2,1},{3,2},{4,7},{5,4},{6,5},{7,6},{8,11},{9,8},{10,9... | collective-permute-start | bytes 983048 | tf_op jit(solution)/shard_map/ppermute | solution.py:481
  68.9 1.9 %attend.4.refs_4_ = f32[56,8,256]{2,1,0:T(8,128)S(1)} custom-call(s32[1,3]{1,0:T(1,128)S(1)} %add_bitcast_fusion.place, s32[14,2]{1,0:T(8,128)S(1)} %copy.21.table, s32[2,6]{1,0:T(2,128)S(1)} %copy-done.6, bf16[10,256,128]{2,1,0:T(8,128)(2,1)S(1)} %collective-permute-done.7.refs_0_, bf16[10,256,128]{2,1,0:T(8,128)(2,1)S(1)} %collective-permute-done.8.refs_1_, ...), custom_call_target="tpu_custom_call" | custom-call | flops 4227858432 | bytes 1966080 | tf_op jit(solution)/shard_map/attend/pallas_call | solution.py:443
  70.9 2.4 %collective-permute-done.20.refs_0_ = bf16[5,256,128]{2,1,0:T(8,128)(2,1)S(1)} collective-permute-done((bf16[5,256,128]{2,1,0:T(8,128)(2,1)S(1)}, bf16[5,256,128]{2,1,0:T(8,128)(2,1)S(1)}, u32[]{:S(2)}, u32[]{:S(2)}) %collective-permute-start.20) | collective-permute-done | bytes 327712 | tf_op jit(solution)/shard_map/ppermute | solution.py:481
  73.3 3.5 %collective-permute-done.22.refs_2_ = bf16[5,256,128]{2,1,0:T(8,128)(2,1)S(1)} collective-permute-done((bf16[5,256,128]{2,1,0:T(8,128)(2,1)S(1)}, bf16[5,256,128]{2,1,0:T(8,128)(2,1)S(1)}, u32[]{:S(2)}, u32[]{:S(2)}) %collective-permute-start.22) | collective-permute-done | bytes 327712 | tf_op jit(solution)/shard_map/ppermute | solution.py:481
  76.8 2.2 %attend.5 = (f32[7,256]{1,0:T(8,128)S(1)}, f32[128,128]{1,0:T(8,128)}) custom-call(s32[1,3]{1,0:T(1,128)S(1)} %add_bitcast_fusion.place, s32[14,2]{1,0:T(8,128)S(1)} %copy.21.table, s32[2,3]{1,0:T(2,128)S(1)} %copy-done.5, bf16[5,256,128]{2,1,0:T(8,128)(2,1)S(1)} %collective-permute-done.20.refs_0_, ...), custom_call_target="tpu_custom_call" | custom-call | flops 2113929216 | bytes 983040 | tf_op jit(solution)/shard_map/attend/pallas_call | solution.py:443
  79.0 55.5 %all-to-all-start = ((f32[128,1,128]{2,1,0:T(1,128)}), f32[128,1,128]{2,1,0:T(1,128)S(1)}, u32[]{:S(2)}, u32[]{:S(2)}) async-start(f32[128,1,128]{2,1,0:T(1,128)} %bitcast.11), calls=%async_computation | async-start | bytes 131072 | tf_op jit(solution)/shard_map/all_to_all | solution.py:551
  135.0 11.2 %all-to-all-done = f32[128,1,128]{2,1,0:T(1,128)S(1)} async-done(((f32[128,1,128]{2,1,0:T(1,128)}), f32[128,1,128]{2,1,0:T(1,128)S(1)}, u32[]{:S(2)}, u32[]{:S(2)}) %all-to-all-start) | async-done | bytes 65568 | tf_op jit(solution)/shard_map/all_to_all | solution.py:551
  (60 shorter events, 13.1 us)
Async XLA Ops:
  2.5 11.2 %collective-permute-start.1 = (bf16[3,256,128]{2,1,0:T(8,128)(2,1)S(1)}, bf16[3,256,128]{2,1,0:T(8,128)(2,1)S(1)}, u32[]{:S(2)}, u32[]{:S(2)}) collective-permute-start(bf16[3,256,128]{2,1,0:T(8,128)(2,1)S(1)} %split_heads.1.own), channel_id=1, source_target_pairs={{0,16},{16,4},{4,20},{20,8},{8,24},{24,12},{12,28},{28,0},{1,17},{... | collective-permute-start | bytes 589832 | tf_op jit(solution)/shard_map/ppermute | solution.py:482
  5.1 8.7 %collective-permute-start.2 = (bf16[3,256,128]{2,1,0:T(8,128)(2,1)S(1)}, bf16[3,256,128]{2,1,0:T(8,128)(2,1)S(1)}, u32[]{:S(2)}, u32[]{:S(2)}) collective-permute-start(bf16[3,256,128]{2,1,0:T(8,128)(2,1)S(1)} %split_heads.1.own), channel_id=1, source_target_pairs={{0,28},{16,0},{4,16},{20,4},{8,20},{24,8},{12,24},{28,12},{1,29},{... | collective-permute-start | bytes 589832 | tf_op jit(solution)/shard_map/ppermute | solution.py:482
  13.7 6.7 %collective-permute-start.3 = (bf16[3,256,128]{2,1,0:T(8,128)(2,1)S(1)}, bf16[3,256,128]{2,1,0:T(8,128)(2,1)S(1)}, u32[]{:S(2)}, u32[]{:S(2)}) collective-permute-start(bf16[3,256,128]{2,1,0:T(8,128)(2,1)S(1)} %collective-permute-done.1.refs_1_.ring_1), channel_id=1, source_target_pairs={{0,16},{16,4},{4,20},{20,8},{8,24},{24,12},{12,28},{28,0},{1,17},{... | collective-permute-start | bytes 589832 | tf_op jit(solution)/shard_map/ppermute | solution.py:482
  13.8 9.2 %collective-permute-start.5 = (bf16[3,256,128]{2,1,0:T(8,128)(2,1)S(1)}, bf16[3,256,128]{2,1,0:T(8,128)(2,1)S(1)}, u32[]{:S(2)}, u32[]{:S(2)}) collective-permute-start(bf16[3,256,128]{2,1,0:T(8,128)(2,1)S(1)} %collective-permute-done.2.refs_5_.ring_7), channel_id=1, source_target_pairs={{0,28},{16,0},{4,16},{20,4},{8,20},{24,8},{12,24},{28,12},{1,29},{... | collective-permute-start | bytes 589832 | tf_op jit(solution)/shard_map/ppermute | solution.py:482
  16.5 5.6 %collective-permute-start.16 = (bf16[2,256,128]{2,1,0:T(8,128)(2,1)S(1)}, bf16[2,256,128]{2,1,0:T(8,128)(2,1)S(1)}, u32[]{:S(2)}, u32[]{:S(2)}) collective-permute-start(bf16[2,256,128]{2,1,0:T(8,128)(2,1)S(1)} %get-tuple-element.41), channel_id=1, source_target_pairs={{0,16},{16,0},{1,17},{17,1},{2,18},{18,2},{3,19},{19,3},{4,20},{20... | collective-permute-start | bytes 393224 | tf_op jit(solution)/shard_map/ppermute | solution.py:492
  17.6 11.2 %collective-permute-start.13 = (bf16[5,256,128]{2,1,0:T(8,128)(2,1)S(1)}, bf16[5,256,128]{2,1,0:T(8,128)(2,1)S(1)}, u32[]{:S(2)}, u32[]{:S(2)}) collective-permute-start(bf16[5,256,128]{2,1,0:T(8,128)(2,1)S(1)} %own_chunk.1.refs_0_), channel_id=1, source_target_pairs={{0,3},{1,0},{2,1},{3,2},{4,7},{5,4},{6,5},{7,6},{8,11},{9,8},{10,9... | collective-permute-start | bytes 983048 | tf_op jit(solution)/shard_map/ppermute | solution.py:481
  20.5 5.7 %collective-permute-start.4 = (bf16[3,256,128]{2,1,0:T(8,128)(2,1)S(1)}, bf16[3,256,128]{2,1,0:T(8,128)(2,1)S(1)}, u32[]{:S(2)}, u32[]{:S(2)}) collective-permute-start(bf16[3,256,128]{2,1,0:T(8,128)(2,1)S(1)} %collective-permute-done.3.refs_0_), channel_id=1, source_target_pairs={{0,16},{16,4},{4,20},{20,8},{8,24},{24,12},{12,28},{28,0},{1,17},{... | collective-permute-start | bytes 589832 | tf_op jit(solution)/shard_map/ppermute | solution.py:482
  21.6 12.5 %collective-permute-start.12 = (bf16[5,256,128]{2,1,0:T(8,128)(2,1)S(1)}, bf16[5,256,128]{2,1,0:T(8,128)(2,1)S(1)}, u32[]{:S(2)}, u32[]{:S(2)}) collective-permute-start(bf16[5,256,128]{2,1,0:T(8,128)(2,1)S(1)} %own_chunk.1.refs_0_), channel_id=1, source_target_pairs={{0,1},{1,2},{2,3},{3,0},{4,5},{5,6},{6,7},{7,4},{8,9},{9,10},{10,1... | collective-permute-start | bytes 983048 | tf_op jit(solution)/shard_map/ppermute | solution.py:481
  22.1 4.4 %collective-permute-start.17 = (bf16[2,256,128]{2,1,0:T(8,128)(2,1)S(1)}, bf16[2,256,128]{2,1,0:T(8,128)(2,1)S(1)}, u32[]{:S(2)}, u32[]{:S(2)}) collective-permute-start(bf16[2,256,128]{2,1,0:T(8,128)(2,1)S(1)} %get-tuple-element.40), channel_id=1, source_target_pairs={{0,16},{16,0},{1,17},{17,1},{2,18},{18,2},{3,19},{19,3},{4,20},{20... | collective-permute-start | bytes 393224 | tf_op jit(solution)/shard_map/ppermute | solution.py:492
  23.1 5.9 %collective-permute-start.6 = (bf16[3,256,128]{2,1,0:T(8,128)(2,1)S(1)}, bf16[3,256,128]{2,1,0:T(8,128)(2,1)S(1)}, u32[]{:S(2)}, u32[]{:S(2)}) collective-permute-start(bf16[3,256,128]{2,1,0:T(8,128)(2,1)S(1)} %collective-permute-done.5.refs_3_), channel_id=1, source_target_pairs={{0,28},{16,0},{4,16},{20,4},{8,20},{24,8},{12,24},{28,12},{1,29},{... | collective-permute-start | bytes 589832 | tf_op jit(solution)/shard_map/ppermute | solution.py:482
  26.2 9.7 %collective-permute-start.9 = (bf16[3,256,128]{2,1,0:T(8,128)(2,1)S(1)}, bf16[3,256,128]{2,1,0:T(8,128)(2,1)S(1)}, u32[]{:S(2)}, u32[]{:S(2)}) collective-permute-start(bf16[3,256,128]{2,1,0:T(8,128)(2,1)S(1)} %collective-permute-done.4.refs_2_.refs_1_), channel_id=1, source_target_pairs={{0,16},{16,4},{4,20},{20,8},{8,24},{24,12},{12,28},{28,0},{1,17},{... | collective-permute-start | bytes 589832 | tf_op jit(solution)/shard_map/ppermute | solution.py:482
  26.6 6.7 %collective-permute-start.18 = (bf16[2,256,128]{2,1,0:T(8,128)(2,1)S(1)}, bf16[2,256,128]{2,1,0:T(8,128)(2,1)S(1)}, u32[]{:S(2)}, u32[]{:S(2)}) collective-permute-start(bf16[2,256,128]{2,1,0:T(8,128)(2,1)S(1)} %get-tuple-element.39), channel_id=1, source_target_pairs={{0,16},{16,0},{1,17},{17,1},{2,18},{18,2},{3,19},{19,3},{4,20},{20... | collective-permute-start | bytes 393224 | tf_op jit(solution)/shard_map/ppermute | solution.py:492
  28.8 9.5 %collective-permute-start.19 = (bf16[3,256,128]{2,1,0:T(8,128)(2,1)S(1)}, bf16[3,256,128]{2,1,0:T(8,128)(2,1)S(1)}, u32[]{:S(2)}, u32[]{:S(2)}) collective-permute-start(bf16[3,256,128]{2,1,0:T(8,128)(2,1)S(1)} %slice.42), channel_id=1, source_target_pairs={{0,16},{16,0},{1,17},{17,1},{2,18},{18,2},{3,19},{19,3},{4,20},{20... | collective-permute-start | bytes 589832 | tf_op jit(solution)/shard_map/ppermute | solution.py:492
  28.9 21.3 %collective-permute-start.15 = (bf16[3,256,128]{2,1,0:T(8,128)(2,1)S(1)}, bf16[3,256,128]{2,1,0:T(8,128)(2,1)S(1)}, u32[]{:S(2)}, u32[]{:S(2)}) collective-permute-start(bf16[3,256,128]{2,1,0:T(8,128)(2,1)S(1)} %slice.47), channel_id=1, source_target_pairs={{0,3},{1,0},{2,1},{3,2},{4,7},{5,4},{6,5},{7,6},{8,11},{9,8},{10,9... | collective-permute-start | bytes 589832 | tf_op jit(solution)/shard_map/ppermute | solution.py:481
  33.2 23.3 %collective-permute-start.7 = (bf16[10,256,128]{2,1,0:T(8,128)(2,1)S(1)}, bf16[10,256,128]{2,1,0:T(8,128)(2,1)S(1)}, u32[]{:S(2)}, u32[]{:S(2)}) collective-permute-start(bf16[10,256,128]{2,1,0:T(8,128)(2,1)S(1)} %rest_of.2.refs_5_), channel_id=1, source_target_pairs={{0,1},{1,2},{2,3},{3,0},{4,5},{5,6},{6,7},{7,4},{8,9},{9,10},{10,1... | collective-permute-start | bytes 1966088 | tf_op jit(solution)/shard_map/ppermute | solution.py:481
  34.2 22.4 %collective-permute-start.8 = (bf16[10,256,128]{2,1,0:T(8,128)(2,1)S(1)}, bf16[10,256,128]{2,1,0:T(8,128)(2,1)S(1)}, u32[]{:S(2)}, u32[]{:S(2)}) collective-permute-start(bf16[10,256,128]{2,1,0:T(8,128)(2,1)S(1)} %rest_of.2.refs_5_), channel_id=1, source_target_pairs={{0,3},{1,0},{2,1},{3,2},{4,7},{5,4},{6,5},{7,6},{8,11},{9,8},{10,9... | collective-permute-start | bytes 1966088 | tf_op jit(solution)/shard_map/ppermute | solution.py:481
  35.9 11.7 %collective-permute-start.14 = (bf16[2,256,128]{2,1,0:T(8,128)(2,1)S(1)}, bf16[2,256,128]{2,1,0:T(8,128)(2,1)S(1)}, u32[]{:S(2)}, u32[]{:S(2)}) collective-permute-start(bf16[2,256,128]{2,1,0:T(8,128)(2,1)S(1)} %slice.46), channel_id=1, source_target_pairs={{0,1},{1,2},{2,3},{3,0},{4,5},{5,6},{6,7},{7,4},{8,9},{9,10},{10,1... | collective-permute-start | bytes 393224 | tf_op jit(solution)/shard_map/ppermute | solution.py:481
  38.3 30.6 %copy-start.6 = (s32[2,6]{1,0:T(2,128)S(1)}, s32[2,6]{1,0:T(2,128)}, u32[]{:S(2)}) copy-start(s32[2,6]{1,0:T(2,128)} %constant.28.clone.plan) | copy-start | bytes 148
  38.3 17.1 %collective-permute-start.10 = (bf16[5,256,128]{2,1,0:T(8,128)(2,1)S(1)}, bf16[5,256,128]{2,1,0:T(8,128)(2,1)S(1)}, u32[]{:S(2)}, u32[]{:S(2)}) collective-permute-start(bf16[5,256,128]{2,1,0:T(8,128)(2,1)S(1)} %rest_of.3.refs_6_), channel_id=1, source_target_pairs={{0,1},{1,2},{2,3},{3,0},{4,5},{5,6},{6,7},{7,4},{8,9},{9,10},{10,1... | collective-permute-start | bytes 983048 | tf_op jit(solution)/shard_map/ppermute | solution.py:481
  47.7 8.9 %collective-permute-start.11 = (bf16[5,256,128]{2,1,0:T(8,128)(2,1)S(1)}, bf16[5,256,128]{2,1,0:T(8,128)(2,1)S(1)}, u32[]{:S(2)}, u32[]{:S(2)}) collective-permute-start(bf16[5,256,128]{2,1,0:T(8,128)(2,1)S(1)} %rest_of.3.refs_6_), channel_id=1, source_target_pairs={{0,3},{1,0},{2,1},{3,2},{4,7},{5,4},{6,5},{7,6},{8,11},{9,8},{10,9... | collective-permute-start | bytes 983048 | tf_op jit(solution)/shard_map/ppermute | solution.py:481
  56.6 16.7 %collective-permute-start.20 = (bf16[5,256,128]{2,1,0:T(8,128)(2,1)S(1)}, bf16[5,256,128]{2,1,0:T(8,128)(2,1)S(1)}, u32[]{:S(2)}, u32[]{:S(2)}) collective-permute-start(bf16[5,256,128]{2,1,0:T(8,128)(2,1)S(1)} %slice.43), channel_id=1, source_target_pairs={{0,1},{1,2},{2,3},{3,0},{4,5},{5,6},{6,7},{7,4},{8,9},{9,10},{10,1... | collective-permute-start | bytes 983048 | tf_op jit(solution)/shard_map/ppermute | solution.py:481
  59.0 14.3 %collective-permute-start.21 = (bf16[5,256,128]{2,1,0:T(8,128)(2,1)S(1)}, bf16[5,256,128]{2,1,0:T(8,128)(2,1)S(1)}, u32[]{:S(2)}, u32[]{:S(2)}) collective-permute-start(bf16[5,256,128]{2,1,0:T(8,128)(2,1)S(1)} %slice.44), channel_id=1, source_target_pairs={{0,3},{1,0},{2,1},{3,2},{4,7},{5,4},{6,5},{7,6},{8,11},{9,8},{10,9... | collective-permute-start | bytes 983048 | tf_op jit(solution)/shard_map/ppermute | solution.py:481
  68.9 7.9 %collective-permute-start.22 = (bf16[5,256,128]{2,1,0:T(8,128)(2,1)S(1)}, bf16[5,256,128]{2,1,0:T(8,128)(2,1)S(1)}, u32[]{:S(2)}, u32[]{:S(2)}) collective-permute-start(bf16[5,256,128]{2,1,0:T(8,128)(2,1)S(1)} %collective-permute-done.10.refs_2_), channel_id=1, source_target_pairs={{0,1},{1,2},{2,3},{3,0},{4,5},{5,6},{6,7},{7,4},{8,9},{9,10},{10,1... | collective-permute-start | bytes 983048 | tf_op jit(solution)/shard_map/ppermute | solution.py:481
  79.0 67.3 %all-to-all-start = ((f32[128,1,128]{2,1,0:T(1,128)}), f32[128,1,128]{2,1,0:T(1,128)S(1)}, u32[]{:S(2)}, u32[]{:S(2)}) async-start(f32[128,1,128]{2,1,0:T(1,128)} %bitcast.11), calls=%async_computation | async-start | bytes 131072 | tf_op jit(solution)/shard_map/all_to_all | solution.py:551
  (7 other events, 74.3 us)

commit v8 on v7

--- a/solution.py
+++ b/solution.py
@@ -31,7 +31,7 @@
 OWN = 3
 OTHER = 2
 CHUNK = OWN + OTHER
-PIECES = (2, 2, 2, 3)
+PIECES = (3, 3, 3)
 SENT = sum(PIECES)
 MIB = 1024 * 1024
 SMEM = pl.BlockSpec(memory_space=pltpu.SMEM)
@@ -77,14 +77,15 @@
     )(teacher, student)
 
 
-def queries_kernel(place, table, query, sent, count, sems):
+def queries_kernel(place, table, query, *refs):
+    pieces, (count, sent, sems) = refs[:-3], refs[-3:]
     head = place[0, 0]
     theirs = (1 - head) * STUDENTS
 
     def each(act):
         rank = jnp.int32(0)
         for p in range(PAIRS):
-            teacher = table[theirs + p // 2, p % 2]
+            teacher = table[p % 2, theirs + p // 2]
             mine = lax.div(teacher, PAIRS) == head
             lanes = pl.ds(pl.multiple_of(lax.rem(teacher, PAIRS) * DH, DH), DH)
 
@@ -97,79 +98,51 @@
 
     count[0, 0] = each(lambda c: c.start())
     each(lambda c: c.wait())
+    rank = 0
+    for piece in pieces:
+        piece[...] = sent[rank : rank + piece.shape[0]]
+        rank += piece.shape[0]
 
 
 def queries_for_other(place, table, query):
     return pl.pallas_call(
         queries_kernel,
-        out_shape=(heads_of(PAIRS), jax.ShapeDtypeStruct((1, 1), jnp.int32)),
+        out_shape=(
+            *(heads_of(n) for n in (*PIECES, PAIRS - SENT)),
+            jax.ShapeDtypeStruct((1, 1), jnp.int32),
+        ),
         in_specs=[SMEM, SMEM, ANY],
-        out_specs=(VMEM, SMEM),
-        scratch_shapes=[pltpu.SemaphoreType.DMA((PAIRS,))],
+        out_specs=(*[VMEM] * (len(PIECES) + 1), SMEM),
+        scratch_shapes=[
+            pltpu.VMEM((PAIRS, ROWS, DH), jnp.bfloat16),
+            pltpu.SemaphoreType.DMA((PAIRS,)),
+        ],
         compiler_params=small(4),
         name="queries_for_other",
     )(place, table, query)
 
 
-def own_chunk_kernel(place, own, ring_1, ring_7, out, sems):
-    for head, pair in enumerate((ring_7, ring_1)):
+def chunks_kernel(place, *refs):
+    ring, out = refs[:-1], refs[-1]
+    for head in range(2):
 
         @pl.when(place[0, 0] == head)
         def _():
-            run_all(
-                [
-                    pltpu.make_async_copy(own, out.at[pl.ds(0, OWN)], sems.at[0]),
-                    pltpu.make_async_copy(
-                        pair.at[pl.ds(0, OTHER)], out.at[pl.ds(OWN, OTHER)], sems.at[1]
-                    ),
-                ]
-            )
-
-
-def own_chunk(place, own, ring_1, ring_7):
+            for n in range(len(ring) // 3):
+                own, other = ring[3 * n], ring[3 * n + 1 + head]
+                out[CHUNK * n : CHUNK * n + OWN] = own[...]
+                out[CHUNK * n + OWN : CHUNK * (n + 1)] = other[:OTHER]
+
+
+def chunks_of(place, ring, chunks):
+    parts = [ring[o % 8] for m in chunks for o in (2 * m, 2 * m - 1, 2 * m + 1)]
     return pl.pallas_call(
-        own_chunk_kernel,
-        out_shape=heads_of(CHUNK),
-        in_specs=[SMEM, ANY, ANY, ANY],
+        chunks_kernel,
+        out_shape=heads_of(CHUNK * len(chunks)),
+        in_specs=[SMEM] + [VMEM] * len(parts),
         out_specs=VMEM,
-        scratch_shapes=[pltpu.SemaphoreType.DMA((2,))],
-        compiler_params=small(2),
-        name="own_chunk",
-    )(place, own, ring_1, ring_7)
-
-
-def rest_kernel(chunks, place, *refs):
-    ring, out, sems = refs[:-2], refs[-2], refs[-1]
-    for head in range(2):
-
-        @pl.when(place[0, 0] == head)
-        def _():
-            copies = []
-            for n in range(chunks):
-                own, other = ring[3 * n], ring[3 * n + 1 + head]
-                copies.append(
-                    pltpu.make_async_copy(own, out.at[pl.ds(CHUNK * n, OWN)], sems.at[n, 0])
-                )
-                copies.append(
-                    pltpu.make_async_copy(
-                        other.at[pl.ds(0, OTHER)],
-                        out.at[pl.ds(CHUNK * n + OWN, OTHER)],
-                        sems.at[n, 1],
-                    )
-                )
-            run_all(copies)
-
-
-def rest_of(place, ring, chunks):
-    parts = [ring[o] for m in chunks for o in (2 * m, 2 * m - 1, (2 * m + 1) % 8)]
-    return pl.pallas_call(
-        functools.partial(rest_kernel, len(chunks)),
-        out_shape=heads_of(CHUNK * len(chunks)),
-        in_specs=[SMEM] + [ANY] * len(parts),
-        out_specs=VMEM,
-        scratch_shapes=[pltpu.SemaphoreType.DMA((len(chunks), 2))],
         compiler_params=small(4),
-        name="rest_of",
+        name="chunks_of",
     )(place, *parts)
 
 
@@ -185,7 +158,7 @@
     for s in range(STUDENTS):
         rows[PAIRS + s] = scaled(student[:, s * DH : (s + 1) * DH])
     for p in range(PAIRS):
-        teacher = table[head * STUDENTS + p // 2, p % 2]
+        teacher = table[p % 2, head * STUDENTS + p // 2]
         lanes = pl.ds(pl.multiple_of(lax.rem(teacher, PAIRS) * DH, DH), DH)
 
         @pl.when(lax.div(teacher, PAIRS) == head)
@@ -211,7 +184,7 @@
     head = place[0, 0]
     rank = jnp.int32(0)
     for p in range(PAIRS):
-        mine = lax.div(table[head * STUDENTS + p // 2, p % 2], PAIRS) == head
+        mine = lax.div(table[p % 2, head * STUDENTS + p // 2], PAIRS) == head
 
         @pl.when(jnp.logical_not(mine))
         def _():
@@ -273,7 +246,7 @@
         state[...] = before[...]
 
     for p in range(PAIRS):
-        kv_head = lax.div(table[head * STUDENTS + p // 2, p % 2], GROUP)
+        kv_head = lax.div(table[p % 2, head * STUDENTS + p // 2], GROUP)
         side = jnp.where(lax.div(kv_head, 2) == head, 0, OWN)
         offsets[p] = side + lax.rem(kv_head, 2)
 
@@ -476,6 +449,7 @@
 
 def program(teacher_query, teacher_key, student_query, student_key, pair_table):
     head = lax.axis_index("head")
+    table = pair_table.T
     place = jnp.stack([head, lax.axis_index("kv_0"), lax.axis_index("kv_1")])[None]
 
     along_x = lambda a, by: lax.ppermute(a, "kv_1", shift(4, by))
@@ -483,23 +457,19 @@
     other_side = [(0, 1), (1, 0)]
 
     ring = {0: split_heads(teacher_key[0], student_key[0])}
-    chosen, count = queries_for_other(place, pair_table, teacher_query[0])
+    *chosen, count = queries_for_other(place, table, teacher_query[0])
     ring[1] = along_z(ring[0], 1)
     ring[7] = along_z(ring[0], -1)
-    pieces, rank = [], 0
-    for length in PIECES:
-        piece = chosen[rank : rank + length]
-        pieces.append(lax.ppermute(piece, "head", other_side))
-        rank += length
+    pieces = [lax.ppermute(piece, "head", other_side) for piece in chosen[:-1]]
     more = lax.cond(
         count[0, 0] > SENT,
         lambda q: lax.ppermute(q, "head", other_side),
         lambda q: q,
-        chosen[SENT:],
+        chosen[-1],
     )
     more, ring[1], ring[7] = lax.optimization_barrier((more, ring[1], ring[7]))
-    rows = prepare(place, pair_table, teacher_query[0], student_query[0])
-    mine = own_chunk(place, ring[0], ring[1], ring[7])
+    rows = prepare(place, table, teacher_query[0], student_query[0])
+    mine = chunks_of(place, ring, (0,))
     near_a = along_x(mine, 1)
     near_b = along_x(mine, -1)
     near_c = along_x(near_a[:OTHER], 1)
@@ -509,15 +479,15 @@
         if step < 4:
             ring[8 - step] = along_z(ring[9 - step], -1)
 
-    rest_13 = rest_of(place, ring, (1, 3))
+    rest_13 = chunks_of(place, ring, (1, 3))
     left_13 = along_x(rest_13, 1)
     right_13 = along_x(rest_13, -1)
-    rest_2 = rest_of(place, ring, (2,))
+    rest_2 = chunks_of(place, ring, (2,))
     left_2 = along_x(rest_2, 1)
     right_2 = along_x(rest_2, -1)
     state, rows = attend(
         place,
-        pair_table,
+        table,
         plan_of([(0, 0), (0, -1), (0, 1), (0, 2), (1, 0), (3, 0), (2, 0)]),
         [mine, near_a, near_b, near_c, near_d, rest_13, rest_2],
         rows,
@@ -531,7 +501,7 @@
     far_2 = along_x(left_2, 1)
     state = attend(
         place,
-        pair_table,
+        table,
         plan_of([(1, -1), (3, -1), (1, 1), (3, 1), (2, -1), (2, 1)]),
         [left_13, right_13, left_2, right_2],
         rows,
@@ -541,7 +511,7 @@
     devices = lax.axis_size(everyone)
     kl, sums = attend(
         place,
-        pair_table,
+        table,
         plan_of([(1, 2), (3, 2), (2, 2)]),
         [far_1, far_3, far_2],
         rows,

time: 147 us -> 146 us (level)
  Pallas kernels: 15.9 us -> 13.7 us
  waiting for transfers between devices: 29 us -> 30.5 us
    pallas_call x4, Pallas kernels: 5.22 us -> 3.42 us  [the longest x3 1.74 us: chunks_of(): pl.pallas_call(chunks_kernel, out_shape=heads_of(CHUNK * len(chunks)), in...]
    ppermute x4 -> x3, starting transfers between devices: 3.3 us -> 1.51 us  [program(): pieces = [lax.ppermute(piece, 'head', other_side) for piece in chosen[:-1]]]
    ppermute x7, starting transfers between devices: 12.7 us -> 14.3 us  [program(): along_z = lambda a, by: lax.ppermute(a, ('head', 'kv_0'), z_shift(by))]
    unnamed x18 -> x21, local copies, waits for them, and re-layouts: 4.31 us -> 4.23 us
  transfers between devices with their start and end apart: 23 -> 22, of which waited for: 10 -> 10; matrix products, arithmetic and copies ran while one was open for 1% -> 0% of each run, Pallas kernels for 9% -> 8%
where the time goes in v8:
time: 146 us
  starting transfers between devices  95.4 us (65%)
  waiting for transfers between devices  30.5 us (21%)
  Pallas kernels  13.7 us (9%)
  local copies, waits for them, and re-layouts  4.3 us (3%)
  between operations  1.48 us (1%)
    all_to_all x1, starting transfers between devices, program(): terms = lax.all_to_all(sums, everyone, 0, 0, tiled=True)  56.9 us
    ppermute x11, starting transfers between devices, program(): along_x = lambda a, by: lax.ppermute(a, 'kv_1', shift(4, by))  22.7 us
    ppermute x11, waiting for transfers between devices, program(): along_x = lambda a, by: lax.ppermute(a, 'kv_1', shift(4, by))  15.5 us
    ppermute x7, starting transfers between devices, program(): along_z = lambda a, by: lax.ppermute(a, ('head', 'kv_0'), z_shift(by))  14.3 us
    all_to_all x1, waiting for transfers between devices, program(): terms = lax.all_to_all(sums, everyone, 0, 0, tiled=True)  11.3 us
    pallas_call x3, Pallas kernels, attend(): pl.pallas_call(functools.partial(attend_kernel, first, last, counts, bloc...  9.02 us
    unnamed x21, local copies, waits for them, and re-layouts  4.23 us
  transfers between devices with their start and end apart: 22, of which 10 were waited for; matrix products, arithmetic and copies ran while one was open for 0% of the time, Pallas kernels for 8%

profile of v8, /device:TPU:1, one launch (start us, length us, event | category | flops | bytes accessed | tf_op | source)
XLA Modules:
  0.0 146.1 jit_solution(1965830887762570207)
XLA Ops:
  2.5 2.5 %collective-permute-start.1 = (bf16[3,256,128]{2,1,0:T(8,128)(2,1)S(1)}, bf16[3,256,128]{2,1,0:T(8,128)(2,1)S(1)}, u32[]{:S(2)}, u32[]{:S(2)}) collective-permute-start(bf16[3,256,128]{2,1,0:T(8,128)(2,1)S(1)} %split_heads.1.refs_0_), channel_id=1, source_target_pairs={{0,16},{16,4},{4,20},{20,8},{8,24},{24,12},{12,28},{28,0},{1,17},{... | collective-permute-start | bytes 589832 | tf_op jit(solution)/shard_map/ppermute | solution.py:456
  5.1 4.0 %collective-permute-start.2 = (bf16[3,256,128]{2,1,0:T(8,128)(2,1)S(1)}, bf16[3,256,128]{2,1,0:T(8,128)(2,1)S(1)}, u32[]{:S(2)}, u32[]{:S(2)}) collective-permute-start(bf16[3,256,128]{2,1,0:T(8,128)(2,1)S(1)} %split_heads.1.refs_0_), channel_id=1, source_target_pairs={{0,28},{16,0},{4,16},{20,4},{8,20},{24,8},{12,24},{28,12},{1,29},{... | collective-permute-start | bytes 589832 | tf_op jit(solution)/shard_map/ppermute | solution.py:456
  9.2 1.2 copy-done
  11.0 1.7 %queries_for_other.1 = (bf16[3,256,128]{2,1,0:T(8,128)(2,1)S(1)}, bf16[3,256,128]{2,1,0:T(8,128)(2,1)S(1)}, bf16[3,256,128]{2,1,0:T(8,128)(2,1)S(1)}, bf16[5,256,128]{2,1,0:T(8,128)(2,1)S(1)}, s32[1,1]{1,0:T(1,128)}) custom-call(s32[1,3]{1,0:T(1,128)S(1)} %add_bitcast_fusion.place, s32[2,14]{1,0:T(2,128)S(1)} %bitcast.21, bf16[256,1792]{1,0:T(8,128)(2,1)S(1)} %bitcast.15), custom_call_target="tpu_custom_call" | custom-call | tf_op jit(solution)/shard_map/queries_for_other/pallas_call | solution.py:108
  13.6 2.7 %collective-permute-start.5 = (bf16[3,256,128]{2,1,0:T(8,128)(2,1)S(1)}, bf16[3,256,128]{2,1,0:T(8,128)(2,1)S(1)}, u32[]{:S(2)}, u32[]{:S(2)}) collective-permute-start(bf16[3,256,128]{2,1,0:T(8,128)(2,1)S(1)} %collective-permute-done.2.refs_5_.refs_1_), channel_id=1, source_target_pairs={{0,28},{16,0},{4,16},{20,4},{8,20},{24,8},{12,24},{28,12},{1,29},{... | collective-permute-start | bytes 589832 | tf_op jit(solution)/shard_map/ppermute | solution.py:456
  16.9 2.6 %collective-permute-start.13 = (bf16[5,256,128]{2,1,0:T(8,128)(2,1)S(1)}, bf16[5,256,128]{2,1,0:T(8,128)(2,1)S(1)}, u32[]{:S(2)}, u32[]{:S(2)}) collective-permute-start(bf16[5,256,128]{2,1,0:T(8,128)(2,1)S(1)} %chunks_of.5.refs_0_), channel_id=1, source_target_pairs={{0,3},{1,0},{2,1},{3,2},{4,7},{5,4},{6,5},{7,6},{8,11},{9,8},{10,9... | collective-permute-start | bytes 983048 | tf_op jit(solution)/shard_map/ppermute | solution.py:455
  21.3 2.7 %collective-permute-start.6 = (bf16[3,256,128]{2,1,0:T(8,128)(2,1)S(1)}, bf16[3,256,128]{2,1,0:T(8,128)(2,1)S(1)}, u32[]{:S(2)}, u32[]{:S(2)}) collective-permute-start(bf16[3,256,128]{2,1,0:T(8,128)(2,1)S(1)} %collective-permute-done.5.refs_3_), channel_id=1, source_target_pairs={{0,28},{16,0},{4,16},{20,4},{8,20},{24,8},{12,24},{28,12},{1,29},{... | collective-permute-start | bytes 589832 | tf_op jit(solution)/shard_map/ppermute | solution.py:456
  23.9 1.8 %collective-permute-done.4.refs_2_.refs_1_ = bf16[3,256,128]{2,1,0:T(8,128)(2,1)S(1)} collective-permute-done((bf16[3,256,128]{2,1,0:T(8,128)(2,1)S(1)}, bf16[3,256,128]{2,1,0:T(8,128)(2,1)S(1)}, u32[]{:S(2)}, u32[]{:S(2)}) %collective-permute-start.4) | collective-permute-done | bytes 196640 | tf_op jit(solution)/shard_map/ppermute | solution.py:456
  25.8 1.5 %collective-permute-start.9 = (bf16[3,256,128]{2,1,0:T(8,128)(2,1)S(1)}, bf16[3,256,128]{2,1,0:T(8,128)(2,1)S(1)}, u32[]{:S(2)}, u32[]{:S(2)}) collective-permute-start(bf16[3,256,128]{2,1,0:T(8,128)(2,1)S(1)} %collective-permute-done.4.refs_2_.refs_1_), channel_id=1, source_target_pairs={{0,16},{16,4},{4,20},{20,8},{8,24},{24,12},{12,28},{28,0},{1,17},{... | collective-permute-start | bytes 589832 | tf_op jit(solution)/shard_map/ppermute | solution.py:456
  27.3 1.5 %collective-permute-start.18 = (bf16[3,256,128]{2,1,0:T(8,128)(2,1)S(1)}, bf16[3,256,128]{2,1,0:T(8,128)(2,1)S(1)}, u32[]{:S(2)}, u32[]{:S(2)}) collective-permute-start(bf16[3,256,128]{2,1,0:T(8,128)(2,1)S(1)} %get-tuple-element.30), channel_id=1, source_target_pairs={{0,16},{16,0},{1,17},{17,1},{2,18},{18,2},{3,19},{19,3},{4,20},{20... | collective-permute-start | bytes 589832 | tf_op jit(solution)/shard_map/ppermute | solution.py:463
  28.8 2.6 %collective-permute-start.15 = (bf16[3,256,128]{2,1,0:T(8,128)(2,1)S(1)}, bf16[3,256,128]{2,1,0:T(8,128)(2,1)S(1)}, u32[]{:S(2)}, u32[]{:S(2)}) collective-permute-start(bf16[3,256,128]{2,1,0:T(8,128)(2,1)S(1)} %slice.21), channel_id=1, source_target_pairs={{0,3},{1,0},{2,1},{3,2},{4,7},{5,4},{6,5},{7,6},{8,11},{9,8},{10,9... | collective-permute-start | bytes 589832 | tf_op jit(solution)/shard_map/ppermute | solution.py:455
  32.1 2.7 %collective-permute-start.8 = (bf16[10,256,128]{2,1,0:T(8,128)(2,1)S(1)}, bf16[10,256,128]{2,1,0:T(8,128)(2,1)S(1)}, u32[]{:S(2)}, u32[]{:S(2)}) collective-permute-start(bf16[10,256,128]{2,1,0:T(8,128)(2,1)S(1)} %chunks_of.3.refs_5_), channel_id=1, source_target_pairs={{0,3},{1,0},{2,1},{3,2},{4,7},{5,4},{6,5},{7,6},{8,11},{9,8},{10,9... | collective-permute-start | bytes 1966088 | tf_op jit(solution)/shard_map/ppermute | solution.py:455
  37.7 1.5 %collective-permute-start.10 = (bf16[5,256,128]{2,1,0:T(8,128)(2,1)S(1)}, bf16[5,256,128]{2,1,0:T(8,128)(2,1)S(1)}, u32[]{:S(2)}, u32[]{:S(2)}) collective-permute-start(bf16[5,256,128]{2,1,0:T(8,128)(2,1)S(1)} %chunks_of.4.refs_6_), channel_id=1, source_target_pairs={{0,1},{1,2},{2,3},{3,0},{4,5},{5,6},{6,7},{7,4},{8,9},{9,10},{10,1... | collective-permute-start | bytes 983048 | tf_op jit(solution)/shard_map/ppermute | solution.py:455
  39.2 7.4 %collective-permute-done.14.refs_3_ = bf16[2,256,128]{2,1,0:T(8,128)(2,1)S(1)} collective-permute-done((bf16[2,256,128]{2,1,0:T(8,128)(2,1)S(1)}, bf16[2,256,128]{2,1,0:T(8,128)(2,1)S(1)}, u32[]{:S(2)}, u32[]{:S(2)}) %collective-permute-start.14) | collective-permute-done | bytes 131104 | tf_op jit(solution)/shard_map/ppermute | solution.py:455
  47.8 5.1 %attend.3 = (f32[56,8,256]{2,1,0:T(8,128)S(1)}, bf16[21,256,256]{2,1,0:T(8,128)(2,1)S(1)}) custom-call(s32[1,3]{1,0:T(1,128)S(1)} %add_bitcast_fusion.place, s32[2,14]{1,0:T(2,128)S(1)} %bitcast.23, s32[2,7]{1,0:T(2,128)S(1)} %copy-done.9, bf16[5,256,128]{2,1,0:T(8,128)(2,1)S(1)} %chunks_of.5.refs_0_, ...), custom_call_target="tpu_custom_call", output_to_operand_aliasing={{1}: (14, {})} | custom-call | flops 4932501504 | bytes 2293760 | tf_op jit(solution)/shard_map/attend/pallas_call | solution.py:416
  53.6 1.3 collective-permute-done.11.refs_3_
  55.0 3.0 %collective-permute-start.19 = (bf16[5,256,128]{2,1,0:T(8,128)(2,1)S(1)}, bf16[5,256,128]{2,1,0:T(8,128)(2,1)S(1)}, u32[]{:S(2)}, u32[]{:S(2)}) collective-permute-start(bf16[5,256,128]{2,1,0:T(8,128)(2,1)S(1)} %slice.17), channel_id=1, source_target_pairs={{0,1},{1,2},{2,3},{3,0},{4,5},{5,6},{6,7},{7,4},{8,9},{9,10},{10,1... | collective-permute-start | bytes 983048 | tf_op jit(solution)/shard_map/ppermute | solution.py:455
  58.0 8.7 %collective-permute-start.20 = (bf16[5,256,128]{2,1,0:T(8,128)(2,1)S(1)}, bf16[5,256,128]{2,1,0:T(8,128)(2,1)S(1)}, u32[]{:S(2)}, u32[]{:S(2)}) collective-permute-start(bf16[5,256,128]{2,1,0:T(8,128)(2,1)S(1)} %slice.18), channel_id=1, source_target_pairs={{0,3},{1,0},{2,1},{3,2},{4,7},{5,4},{6,5},{7,6},{8,11},{9,8},{10,9... | collective-permute-start | bytes 983048 | tf_op jit(solution)/shard_map/ppermute | solution.py:455
  66.7 1.8 %attend.4.refs_4_ = f32[56,8,256]{2,1,0:T(8,128)S(1)} custom-call(s32[1,3]{1,0:T(1,128)S(1)} %add_bitcast_fusion.place, s32[2,14]{1,0:T(2,128)S(1)} %bitcast.24, s32[2,6]{1,0:T(2,128)S(1)} %copy-done.8, bf16[10,256,128]{2,1,0:T(8,128)(2,1)S(1)} %collective-permute-done.7.refs_0_, bf16[10,256,128]{2,1,0:T(8,128)(2,1)S(1)} %collective-permute-done.8.refs_1_, ...), custom_call_target="tpu_custom_call" | custom-call | flops 4227858432 | bytes 1966080 | tf_op jit(solution)/shard_map/attend/pallas_call | solution.py:416
  68.5 2.5 %collective-permute-done.19.refs_0_ = bf16[5,256,128]{2,1,0:T(8,128)(2,1)S(1)} collective-permute-done((bf16[5,256,128]{2,1,0:T(8,128)(2,1)S(1)}, bf16[5,256,128]{2,1,0:T(8,128)(2,1)S(1)}, u32[]{:S(2)}, u32[]{:S(2)}) %collective-permute-start.19) | collective-permute-done | bytes 327712 | tf_op jit(solution)/shard_map/ppermute | solution.py:455
  71.0 3.5 %collective-permute-done.21.refs_2_ = bf16[5,256,128]{2,1,0:T(8,128)(2,1)S(1)} collective-permute-done((bf16[5,256,128]{2,1,0:T(8,128)(2,1)S(1)}, bf16[5,256,128]{2,1,0:T(8,128)(2,1)S(1)}, u32[]{:S(2)}, u32[]{:S(2)}) %collective-permute-start.21) | collective-permute-done | bytes 327712 | tf_op jit(solution)/shard_map/ppermute | solution.py:455
  74.5 2.1 %attend.5 = (f32[7,256]{1,0:T(8,128)S(1)}, f32[128,128]{1,0:T(8,128)}) custom-call(s32[1,3]{1,0:T(1,128)S(1)} %add_bitcast_fusion.place, s32[2,14]{1,0:T(2,128)S(1)} %bitcast.25, s32[2,3]{1,0:T(2,128)S(1)} %copy-done.7, bf16[5,256,128]{2,1,0:T(8,128)(2,1)S(1)} %collective-permute-done.19.refs_0_, bf16[5,256,128]{2,1,0:T(8,128)(2,1)S(1)} %collective-permute-done.20.refs_1_, ...), custom_call_target="tpu_custom_call" | custom-call | flops 2113929216 | bytes 983040 | tf_op jit(solution)/shard_map/attend/pallas_call | solution.py:416
  76.6 56.9 %all-to-all-start = ((f32[128,1,128]{2,1,0:T(1,128)}), f32[128,1,128]{2,1,0:T(1,128)S(1)}, u32[]{:S(2)}, u32[]{:S(2)}) async-start(f32[128,1,128]{2,1,0:T(1,128)} %bitcast.12), calls=%async_computation | async-start | bytes 131072 | tf_op jit(solution)/shard_map/all_to_all | solution.py:521
  134.1 11.3 %all-to-all-done = f32[128,1,128]{2,1,0:T(1,128)S(1)} async-done(((f32[128,1,128]{2,1,0:T(1,128)}), f32[128,1,128]{2,1,0:T(1,128)S(1)}, u32[]{:S(2)}, u32[]{:S(2)}) %all-to-all-start) | async-done | bytes 65568 | tf_op jit(solution)/shard_map/all_to_all | solution.py:521
  (58 shorter events, 12.1 us)
Async XLA Ops:
  0.6 34.3 %copy-start.6 = (s32[14,2]{0,1:T(2,128)S(1)}, s32[14,2]{0,1:T(2,128)}, u32[]{:S(2)}) copy-start(s32[14,2]{0,1:T(2,128)} %param.14) | copy-start | bytes 340
  2.5 11.1 %collective-permute-start.1 = (bf16[3,256,128]{2,1,0:T(8,128)(2,1)S(1)}, bf16[3,256,128]{2,1,0:T(8,128)(2,1)S(1)}, u32[]{:S(2)}, u32[]{:S(2)}) collective-permute-start(bf16[3,256,128]{2,1,0:T(8,128)(2,1)S(1)} %split_heads.1.refs_0_), channel_id=1, source_target_pairs={{0,16},{16,4},{4,20},{20,8},{8,24},{24,12},{12,28},{28,0},{1,17},{... | collective-permute-start | bytes 589832 | tf_op jit(solution)/shard_map/ppermute | solution.py:456
  5.1 8.5 %collective-permute-start.2 = (bf16[3,256,128]{2,1,0:T(8,128)(2,1)S(1)}, bf16[3,256,128]{2,1,0:T(8,128)(2,1)S(1)}, u32[]{:S(2)}, u32[]{:S(2)}) collective-permute-start(bf16[3,256,128]{2,1,0:T(8,128)(2,1)S(1)} %split_heads.1.refs_0_), channel_id=1, source_target_pairs={{0,28},{16,0},{4,16},{20,4},{8,20},{24,8},{12,24},{28,12},{1,29},{... | collective-permute-start | bytes 589832 | tf_op jit(solution)/shard_map/ppermute | solution.py:456
  13.6 6.4 %collective-permute-start.3 = (bf16[3,256,128]{2,1,0:T(8,128)(2,1)S(1)}, bf16[3,256,128]{2,1,0:T(8,128)(2,1)S(1)}, u32[]{:S(2)}, u32[]{:S(2)}) collective-permute-start(bf16[3,256,128]{2,1,0:T(8,128)(2,1)S(1)} %collective-permute-done.1.refs_1_.refs_2_), channel_id=1, source_target_pairs={{0,16},{16,4},{4,20},{20,8},{8,24},{24,12},{12,28},{28,0},{1,17},{... | collective-permute-start | bytes 589832 | tf_op jit(solution)/shard_map/ppermute | solution.py:456
  13.6 7.6 %collective-permute-start.5 = (bf16[3,256,128]{2,1,0:T(8,128)(2,1)S(1)}, bf16[3,256,128]{2,1,0:T(8,128)(2,1)S(1)}, u32[]{:S(2)}, u32[]{:S(2)}) collective-permute-start(bf16[3,256,128]{2,1,0:T(8,128)(2,1)S(1)} %collective-permute-done.2.refs_5_.refs_1_), channel_id=1, source_target_pairs={{0,28},{16,0},{4,16},{20,4},{8,20},{24,8},{12,24},{28,12},{1,29},{... | collective-permute-start | bytes 589832 | tf_op jit(solution)/shard_map/ppermute | solution.py:456
  16.3 7.6 %collective-permute-start.16 = (bf16[3,256,128]{2,1,0:T(8,128)(2,1)S(1)}, bf16[3,256,128]{2,1,0:T(8,128)(2,1)S(1)}, u32[]{:S(2)}, u32[]{:S(2)}) collective-permute-start(bf16[3,256,128]{2,1,0:T(8,128)(2,1)S(1)} %get-tuple-element.28), channel_id=1, source_target_pairs={{0,16},{16,0},{1,17},{17,1},{2,18},{18,2},{3,19},{19,3},{4,20},{20... | collective-permute-start | bytes 589832 | tf_op jit(solution)/shard_map/ppermute | solution.py:463
  16.9 10.4 %collective-permute-start.13 = (bf16[5,256,128]{2,1,0:T(8,128)(2,1)S(1)}, bf16[5,256,128]{2,1,0:T(8,128)(2,1)S(1)}, u32[]{:S(2)}, u32[]{:S(2)}) collective-permute-start(bf16[5,256,128]{2,1,0:T(8,128)(2,1)S(1)} %chunks_of.5.refs_0_), channel_id=1, source_target_pairs={{0,3},{1,0},{2,1},{3,2},{4,7},{5,4},{6,5},{7,6},{8,11},{9,8},{10,9... | collective-permute-start | bytes 983048 | tf_op jit(solution)/shard_map/ppermute | solution.py:455
  20.0 5.7 %collective-permute-start.4 = (bf16[3,256,128]{2,1,0:T(8,128)(2,1)S(1)}, bf16[3,256,128]{2,1,0:T(8,128)(2,1)S(1)}, u32[]{:S(2)}, u32[]{:S(2)}) collective-permute-start(bf16[3,256,128]{2,1,0:T(8,128)(2,1)S(1)} %collective-permute-done.3.refs_0_), channel_id=1, source_target_pairs={{0,16},{16,4},{4,20},{20,8},{8,24},{24,12},{12,28},{28,0},{1,17},{... | collective-permute-start | bytes 589832 | tf_op jit(solution)/shard_map/ppermute | solution.py:456
  20.9 11.2 %collective-permute-start.12 = (bf16[5,256,128]{2,1,0:T(8,128)(2,1)S(1)}, bf16[5,256,128]{2,1,0:T(8,128)(2,1)S(1)}, u32[]{:S(2)}, u32[]{:S(2)}) collective-permute-start(bf16[5,256,128]{2,1,0:T(8,128)(2,1)S(1)} %chunks_of.5.refs_0_), channel_id=1, source_target_pairs={{0,1},{1,2},{2,3},{3,0},{4,5},{5,6},{6,7},{7,4},{8,9},{9,10},{10,1... | collective-permute-start | bytes 983048 | tf_op jit(solution)/shard_map/ppermute | solution.py:455
  21.3 7.6 %collective-permute-start.6 = (bf16[3,256,128]{2,1,0:T(8,128)(2,1)S(1)}, bf16[3,256,128]{2,1,0:T(8,128)(2,1)S(1)}, u32[]{:S(2)}, u32[]{:S(2)}) collective-permute-start(bf16[3,256,128]{2,1,0:T(8,128)(2,1)S(1)} %collective-permute-done.5.refs_3_), channel_id=1, source_target_pairs={{0,28},{16,0},{4,16},{20,4},{8,20},{24,8},{12,24},{28,12},{1,29},{... | collective-permute-start | bytes 589832 | tf_op jit(solution)/shard_map/ppermute | solution.py:456
  23.9 8.1 %collective-permute-start.17 = (bf16[3,256,128]{2,1,0:T(8,128)(2,1)S(1)}, bf16[3,256,128]{2,1,0:T(8,128)(2,1)S(1)}, u32[]{:S(2)}, u32[]{:S(2)}) collective-permute-start(bf16[3,256,128]{2,1,0:T(8,128)(2,1)S(1)} %get-tuple-element.29), channel_id=1, source_target_pairs={{0,16},{16,0},{1,17},{17,1},{2,18},{18,2},{3,19},{19,3},{4,20},{20... | collective-permute-start | bytes 589832 | tf_op jit(solution)/shard_map/ppermute | solution.py:463
  25.8 9.0 %collective-permute-start.9 = (bf16[3,256,128]{2,1,0:T(8,128)(2,1)S(1)}, bf16[3,256,128]{2,1,0:T(8,128)(2,1)S(1)}, u32[]{:S(2)}, u32[]{:S(2)}) collective-permute-start(bf16[3,256,128]{2,1,0:T(8,128)(2,1)S(1)} %collective-permute-done.4.refs_2_.refs_1_), channel_id=1, source_target_pairs={{0,16},{16,4},{4,20},{20,8},{8,24},{24,12},{12,28},{28,0},{1,17},{... | collective-permute-start | bytes 589832 | tf_op jit(solution)/shard_map/ppermute | solution.py:456
  27.3 10.4 %collective-permute-start.18 = (bf16[3,256,128]{2,1,0:T(8,128)(2,1)S(1)}, bf16[3,256,128]{2,1,0:T(8,128)(2,1)S(1)}, u32[]{:S(2)}, u32[]{:S(2)}) collective-permute-start(bf16[3,256,128]{2,1,0:T(8,128)(2,1)S(1)} %get-tuple-element.30), channel_id=1, source_target_pairs={{0,16},{16,0},{1,17},{17,1},{2,18},{18,2},{3,19},{19,3},{4,20},{20... | collective-permute-start | bytes 589832 | tf_op jit(solution)/shard_map/ppermute | solution.py:463
  28.8 19.0 %collective-permute-start.15 = (bf16[3,256,128]{2,1,0:T(8,128)(2,1)S(1)}, bf16[3,256,128]{2,1,0:T(8,128)(2,1)S(1)}, u32[]{:S(2)}, u32[]{:S(2)}) collective-permute-start(bf16[3,256,128]{2,1,0:T(8,128)(2,1)S(1)} %slice.21), channel_id=1, source_target_pairs={{0,3},{1,0},{2,1},{3,2},{4,7},{5,4},{6,5},{7,6},{8,11},{9,8},{10,9... | collective-permute-start | bytes 589832 | tf_op jit(solution)/shard_map/ppermute | solution.py:455
  32.0 22.9 %collective-permute-start.7 = (bf16[10,256,128]{2,1,0:T(8,128)(2,1)S(1)}, bf16[10,256,128]{2,1,0:T(8,128)(2,1)S(1)}, u32[]{:S(2)}, u32[]{:S(2)}) collective-permute-start(bf16[10,256,128]{2,1,0:T(8,128)(2,1)S(1)} %chunks_of.3.refs_5_), channel_id=1, source_target_pairs={{0,1},{1,2},{2,3},{3,0},{4,5},{5,6},{6,7},{7,4},{8,9},{9,10},{10,1... | collective-permute-start | bytes 1966088 | tf_op jit(solution)/shard_map/ppermute | solution.py:455
  32.1 22.8 %collective-permute-start.8 = (bf16[10,256,128]{2,1,0:T(8,128)(2,1)S(1)}, bf16[10,256,128]{2,1,0:T(8,128)(2,1)S(1)}, u32[]{:S(2)}, u32[]{:S(2)}) collective-permute-start(bf16[10,256,128]{2,1,0:T(8,128)(2,1)S(1)} %chunks_of.3.refs_5_), channel_id=1, source_target_pairs={{0,3},{1,0},{2,1},{3,2},{4,7},{5,4},{6,5},{7,6},{8,11},{9,8},{10,9... | collective-permute-start | bytes 1966088 | tf_op jit(solution)/shard_map/ppermute | solution.py:455
  34.8 11.8 %collective-permute-start.14 = (bf16[2,256,128]{2,1,0:T(8,128)(2,1)S(1)}, bf16[2,256,128]{2,1,0:T(8,128)(2,1)S(1)}, u32[]{:S(2)}, u32[]{:S(2)}) collective-permute-start(bf16[2,256,128]{2,1,0:T(8,128)(2,1)S(1)} %slice.20), channel_id=1, source_target_pairs={{0,1},{1,2},{2,3},{3,0},{4,5},{5,6},{6,7},{7,4},{8,9},{9,10},{10,1... | collective-permute-start | bytes 393224 | tf_op jit(solution)/shard_map/ppermute | solution.py:455
  36.7 30.0 %copy-start.8 = (s32[2,6]{1,0:T(2,128)S(1)}, s32[2,6]{1,0:T(2,128)}, u32[]{:S(2)}) copy-start(s32[2,6]{1,0:T(2,128)} %constant.28.clone.plan) | copy-start | bytes 148
  37.7 15.9 %collective-permute-start.10 = (bf16[5,256,128]{2,1,0:T(8,128)(2,1)S(1)}, bf16[5,256,128]{2,1,0:T(8,128)(2,1)S(1)}, u32[]{:S(2)}, u32[]{:S(2)}) collective-permute-start(bf16[5,256,128]{2,1,0:T(8,128)(2,1)S(1)} %chunks_of.4.refs_6_), channel_id=1, source_target_pairs={{0,1},{1,2},{2,3},{3,0},{4,5},{5,6},{6,7},{7,4},{8,9},{9,10},{10,1... | collective-permute-start | bytes 983048 | tf_op jit(solution)/shard_map/ppermute | solution.py:455
  46.6 8.3 %collective-permute-start.11 = (bf16[5,256,128]{2,1,0:T(8,128)(2,1)S(1)}, bf16[5,256,128]{2,1,0:T(8,128)(2,1)S(1)}, u32[]{:S(2)}, u32[]{:S(2)}) collective-permute-start(bf16[5,256,128]{2,1,0:T(8,128)(2,1)S(1)} %chunks_of.4.refs_6_), channel_id=1, source_target_pairs={{0,3},{1,0},{2,1},{3,2},{4,7},{5,4},{6,5},{7,6},{8,11},{9,8},{10,9... | collective-permute-start | bytes 983048 | tf_op jit(solution)/shard_map/ppermute | solution.py:455
  55.0 16.0 %collective-permute-start.19 = (bf16[5,256,128]{2,1,0:T(8,128)(2,1)S(1)}, bf16[5,256,128]{2,1,0:T(8,128)(2,1)S(1)}, u32[]{:S(2)}, u32[]{:S(2)}) collective-permute-start(bf16[5,256,128]{2,1,0:T(8,128)(2,1)S(1)} %slice.17), channel_id=1, source_target_pairs={{0,1},{1,2},{2,3},{3,0},{4,5},{5,6},{6,7},{7,4},{8,9},{9,10},{10,1... | collective-permute-start | bytes 983048 | tf_op jit(solution)/shard_map/ppermute | solution.py:455
  58.0 13.0 %collective-permute-start.20 = (bf16[5,256,128]{2,1,0:T(8,128)(2,1)S(1)}, bf16[5,256,128]{2,1,0:T(8,128)(2,1)S(1)}, u32[]{:S(2)}, u32[]{:S(2)}) collective-permute-start(bf16[5,256,128]{2,1,0:T(8,128)(2,1)S(1)} %slice.18), channel_id=1, source_target_pairs={{0,3},{1,0},{2,1},{3,2},{4,7},{5,4},{6,5},{7,6},{8,11},{9,8},{10,9... | collective-permute-start | bytes 983048 | tf_op jit(solution)/shard_map/ppermute | solution.py:455
  66.7 7.9 %collective-permute-start.21 = (bf16[5,256,128]{2,1,0:T(8,128)(2,1)S(1)}, bf16[5,256,128]{2,1,0:T(8,128)(2,1)S(1)}, u32[]{:S(2)}, u32[]{:S(2)}) collective-permute-start(bf16[5,256,128]{2,1,0:T(8,128)(2,1)S(1)} %collective-permute-done.10.refs_2_), channel_id=1, source_target_pairs={{0,1},{1,2},{2,3},{3,0},{4,5},{5,6},{6,7},{7,4},{8,9},{9,10},{10,1... | collective-permute-start | bytes 983048 | tf_op jit(solution)/shard_map/ppermute | solution.py:455
  76.6 68.8 %all-to-all-start = ((f32[128,1,128]{2,1,0:T(1,128)}), f32[128,1,128]{2,1,0:T(1,128)S(1)}, u32[]{:S(2)}, u32[]{:S(2)}) async-start(f32[128,1,128]{2,1,0:T(1,128)} %bitcast.12), calls=%async_computation | async-start | bytes 131072 | tf_op jit(solution)/shard_map/all_to_all | solution.py:521
  (8 other events, 75.2 us)

commit v9 on v8

--- a/solution.py
+++ b/solution.py
@@ -31,7 +31,7 @@
 OWN = 3
 OTHER = 2
 CHUNK = OWN + OTHER
-PIECES = (3, 3, 3)
+PIECES = (2, 2, 5)
 SENT = sum(PIECES)
 MIB = 1024 * 1024
 SMEM = pl.BlockSpec(memory_space=pltpu.SMEM)
@@ -212,16 +212,12 @@
         received, entry = take(2)
     if last:
         (state,) = take(1)
-    offsets, sems = refs
+    offsets = refs[0]
+    if first:
+        sems = refs[1]
     head, z_hi, x = place[0, 0], place[0, 1], place[0, 2]
     row_block = z_hi * 4 + x
 
-    copies, arrivals = [], []
-    at = 0
-    for g, n in enumerate(counts):
-        copies.append(pltpu.make_async_copy(groups[g], keys.at[pl.ds(at, n)], sems.at[g]))
-        arrivals.append((at // CHUNK, copies[-1]))
-        at += n
     if first:
         inputs = []
         rank = 0
@@ -229,15 +225,12 @@
             length = piece.shape[0]
             inputs.append(
                 pltpu.make_async_copy(
-                    piece, received.at[pl.ds(rank, length)], sems.at[len(counts) + n]
+                    piece, received.at[pl.ds(rank, length)], sems.at[n]
                 )
             )
             rank += length
         for c in inputs:
             c.start()
-    for c in copies:
-        c.start()
-    if first:
         for c in inputs:
             c.wait()
         fill_received(place, table, received, rows)
@@ -249,6 +242,25 @@
         kv_head = lax.div(table[p % 2, head * STUDENTS + p // 2], GROUP)
         side = jnp.where(lax.div(kv_head, 2) == head, 0, OWN)
         offsets[p] = side + lax.rem(kv_head, 2)
+
+    def place_keys(i):
+        at = 0
+        for g, n in enumerate(counts):
+            if n % CHUNK == 0:
+                lo = at // CHUNK
+
+                @pl.when(jnp.logical_and(i >= lo, i < lo + n // CHUNK))
+                def _():
+                    keys[...] = groups[g][pl.ds((i - lo) * CHUNK, CHUNK)]
+
+            else:
+                inside = at % CHUNK
+
+                @pl.when(i == at // CHUNK)
+                def _():
+                    keys[inside : inside + n] = groups[g][...]
+
+            at += n
 
     def product(k, p):
         return lax.dot_general(
@@ -283,23 +295,23 @@
                 weights = begin(zt, p, TL + p)
                 state[TC + p] = jnp.sum(weights * folded(zt - zs), axis=0)
 
-    def block(base):
+    def block():
         def add(logits, m_index, l_index):
             weights = jnp.exp2(folded(logits) - state[m_index][None])
             state[l_index] = state[l_index] + jnp.sum(weights, axis=0)
             return weights
 
-        student_keys = keys[base + 2]
+        student_keys = keys[2]
         for s in range(STUDENTS):
             zs = product(student_keys, PAIRS + s)
             add(zs, SM + s, SL + s)
             for c in range(2):
                 p = 2 * s + c
-                zt = product(keys[base + offsets[p]], p)
+                zt = product(keys[offsets[p]], p)
                 weights = add(zt, p, TL + p)
                 state[TC + p] = state[TC + p] + jnp.sum(weights * folded(zt - zs), axis=0)
 
-    def exact_block(base):
+    def exact_block():
         def add(logits, m_index, l_index):
             logits = folded(logits)
             old = state[m_index]
@@ -311,11 +323,11 @@
             return weights, rescale
 
         def student(s, carry):
-            zs = product(keys[base + 2], PAIRS + s)
+            zs = product(keys[2], PAIRS + s)
             add(zs, SM + s, SL + s)
             for c in range(2):
                 p = 2 * s + c
-                zt = product(keys[base + offsets[p]], p)
+                zt = product(keys[offsets[p]], p)
                 weights, rescale = add(zt, p, TL + p)
                 cross = jnp.sum(weights * folded(zt - zs), axis=0)
                 state[TC + p] = state[TC + p] * rescale + cross
@@ -328,28 +340,23 @@
         return chunk * 4 + lax.bitwise_and(x + plan[1, i], 3) < row_block
 
     def step(i, carry):
-        for at_block, c in arrivals:
-
-            @pl.when(i == at_block)
-            def _():
-                c.wait()
-
         @pl.when(visible(i))
         def _():
-            block(CHUNK * i)
+            place_keys(i)
+            block()
 
         return carry
 
     def exact_step(i, carry):
         @pl.when(visible(i))
         def _():
-            exact_block(CHUNK * i)
+            place_keys(i)
+            exact_block()
 
         return carry
 
     if first:
-        arrivals[0][1].wait()
-        arrivals = arrivals[1:]
+        keys[...] = groups[0][...]
         own_block()
         entry[...] = state[...]
     lax.fori_loop(int(first), blocks, step, 0)
@@ -405,18 +412,19 @@
     else:
         extra, out_shape = [rows, state], state_shape
     extra_specs = [ANY] * (len(PIECES) + 1) + [VMEM] if first else [VMEM, VMEM]
-    scratch = [pltpu.VMEM((sum(counts), ROWS, DH), jnp.bfloat16)]
+    scratch = [pltpu.VMEM((CHUNK, ROWS, DH), jnp.bfloat16)]
     if first:
         scratch.append(pltpu.VMEM((PAIRS, ROWS, DH), jnp.bfloat16))
         scratch.append(pltpu.VMEM(state_shape.shape, jnp.float32))
     if last:
         scratch.append(pltpu.VMEM(state_shape.shape, jnp.float32))
     scratch.append(pltpu.SMEM((PAIRS,), jnp.int32))
-    scratch.append(pltpu.SemaphoreType.DMA((len(groups) + len(PIECES) + 1,)))
+    if first:
+        scratch.append(pltpu.SemaphoreType.DMA((len(PIECES) + 1,)))
     return pl.pallas_call(
         functools.partial(attend_kernel, first, last, counts, blocks),
         out_shape=out_shape,
-        in_specs=[SMEM] * 3 + [ANY] * len(groups) + extra_specs,
+        in_specs=[SMEM] * 3 + [VMEM] * len(groups) + extra_specs,
         out_specs=jax.tree.map(lambda _: VMEM, out_shape),
         scratch_shapes=scratch,
         input_output_aliases={3 + len(groups) + len(extra) - 1: 1} if first else {},
@@ -430,17 +438,9 @@
     )(place, table, plan, *groups, *extra)
 
 
-def shift(n, by):
-    return [(i, (i + by) % n) for i in range(n)]
-
-
 def z_place(ring):
     ring %= 8
     return (ring % 2) * 4 + ring // 2
-
-
-def z_shift(by):
-    return [(z_place(i), z_place(i + by)) for i in range(8)]
 
 
 def plan_of(blocks):
@@ -452,14 +452,20 @@
     table = pair_table.T
     place = jnp.stack([head, lax.axis_index("kv_0"), lax.axis_index("kv_1")])[None]
 
-    along_x = lambda a, by: lax.ppermute(a, "kv_1", shift(4, by))
-    along_z = lambda a, by: lax.ppermute(a, ("head", "kv_0"), z_shift(by))
+    def along_x(a, by, chunks, sources=range(4)):
+        pairs = [(c * 4 + i, c * 4 + (i + by) % 4) for c in chunks for i in sources]
+        return lax.ppermute(a, KV, pairs)
+
+    def along_z(a, by, sources):
+        pairs = [(z_place(i), z_place(i + by)) for i in sources]
+        return lax.ppermute(a, ("head", "kv_0"), pairs)
+
     other_side = [(0, 1), (1, 0)]
 
     ring = {0: split_heads(teacher_key[0], student_key[0])}
     *chosen, count = queries_for_other(place, table, teacher_query[0])
-    ring[1] = along_z(ring[0], 1)
-    ring[7] = along_z(ring[0], -1)
+    ring[1] = along_z(ring[0], 1, range(7))
+    ring[7] = along_z(ring[0], -1, (0, 1, 2, 3, 5, 7))
     pieces = [lax.ppermute(piece, "head", other_side) for piece in chosen[:-1]]
     more = lax.cond(
         count[0, 0] > SENT,
@@ -470,21 +476,21 @@
     more, ring[1], ring[7] = lax.optimization_barrier((more, ring[1], ring[7]))
     rows = prepare(place, table, teacher_query[0], student_query[0])
     mine = chunks_of(place, ring, (0,))
-    near_a = along_x(mine, 1)
-    near_b = along_x(mine, -1)
-    near_c = along_x(near_a[:OTHER], 1)
-    near_d = along_x(near_b[OTHER:], -1)
+    near_a = along_x(mine, 1, range(4), (0, 1, 2))
+    near_b = along_x(mine, -1, range(4), (0, 1))
+    near_c = along_x(near_a[:OTHER], 1, range(4), (1, 2))
+    near_d = along_x(near_b[OTHER:], -1, range(4), (3, 0))
     for step in range(2, 5):
-        ring[step] = along_z(ring[step - 1], 1)
+        ring[step] = along_z(ring[step - 1], 1, range(step - 1, 7))
         if step < 4:
-            ring[8 - step] = along_z(ring[9 - step], -1)
+            ring[8 - step] = along_z(ring[9 - step], -1, (7, 0, 1 if step == 2 else 6))
 
     rest_13 = chunks_of(place, ring, (1, 3))
-    left_13 = along_x(rest_13, 1)
-    right_13 = along_x(rest_13, -1)
+    left_13 = along_x(rest_13, 1, (1, 2, 3))
+    right_13 = along_x(rest_13, -1, (1, 2, 3))
     rest_2 = chunks_of(place, ring, (2,))
-    left_2 = along_x(rest_2, 1)
-    right_2 = along_x(rest_2, -1)
+    left_2 = along_x(rest_2, 1, (2, 3))
+    right_2 = along_x(rest_2, -1, (2, 3))
     state, rows = attend(
         place,
         table,
@@ -493,12 +499,13 @@
         rows,
         queries=(*pieces, more),
     )
-    left_13, right_13, left_2, right_2, state = lax.optimization_barrier(
-        (left_13, right_13, left_2, right_2, state)
-    )
-    far_1 = along_x(left_13[:CHUNK], 1)
-    far_3 = along_x(right_13[CHUNK:], -1)
-    far_2 = along_x(left_2, 1)
+    left_13, right_13, state = lax.optimization_barrier((left_13, right_13, state))
+    cut_1 = left_13[:CHUNK]
+    cut_3 = right_13[CHUNK:]
+    far_1 = along_x(cut_1, 1, (1, 2, 3))
+    far_3 = along_x(cut_3, -1, (3,))
+    left_2, right_2, state = lax.optimization_barrier((left_2, right_2, state))
+    far_2 = along_x(left_2, 1, (2, 3))
     state = attend(
         place,
         table,

time: 146 us -> 171 us (1.17)
  starting transfers between devices: 95.4 us -> 135 us
  waiting for transfers between devices: 30.5 us -> 16.6 us
  Pallas kernels: 13.7 us -> 11 us
    all_to_all x1, starting transfers between devices: 56.9 us -> 98.3 us  [program(): terms = lax.all_to_all(sums, everyone, 0, 0, tiled=True)]
    ppermute x18, waiting for transfers between devices: 18.1 us -> 0.76 us  [the longest x7 0.73 us: along_z(): return lax.ppermute(a, ('head', 'kv_0'), pairs)]
    ppermute x3, waiting for transfers between devices: 1.03 us -> 4.47 us  [program(): pieces = [lax.ppermute(piece, 'head', other_side) for piece in chosen[:-1]]]
    pallas_call x3, Pallas kernels: 9.02 us -> 6.34 us  [attend(): pl.pallas_call(functools.partial(attend_kernel, first, last, counts, bloc...]
  transfers between devices with their start and end apart: 22 -> 22, of which waited for: 10 -> 4; matrix products, arithmetic and copies ran while one was open for 0% -> 0% of each run, Pallas kernels for 8% -> 5%
where the time goes in v9:
time: 171 us; the launch traced here: 170 us
  starting transfers between devices  135 us (79%)
  waiting for transfers between devices  16.6 us (10%)
  Pallas kernels  11 us (6%)
  local copies, waits for them, and re-layouts  4.31 us (3%)
  between operations  1.79 us (1%)
    all_to_all x1, starting transfers between devices, program(): terms = lax.all_to_all(sums, everyone, 0, 0, tiled=True)  98.3 us
    ppermute x7, starting transfers between devices, along_z(): return lax.ppermute(a, ('head', 'kv_0'), pairs)  23 us
    ppermute x11, starting transfers between devices, along_x(): return lax.ppermute(a, KV, pairs)  12.5 us
    all_to_all x1, waiting for transfers between devices, program(): terms = lax.all_to_all(sums, everyone, 0, 0, tiled=True)  11.4 us
    pallas_call x3, Pallas kernels, attend(): pl.pallas_call(functools.partial(attend_kernel, first, last, counts, bloc...  6.34 us
    ppermute x3, waiting for transfers between devices, program(): pieces = [lax.ppermute(piece, 'head', other_side) for piece in chosen[:-1]]  4.47 us
    unnamed x21, local copies, waits for them, and re-layouts  4.24 us
  transfers between devices with their start and end apart: 22, of which 4 were waited for; matrix products, arithmetic and copies ran while one was open for 0% of the time, Pallas kernels for 5%

profile of v9, /device:TPU:1, one launch (start us, length us, event | category | flops | bytes accessed | tf_op | source)
XLA Modules:
  0.0 169.9 jit_solution(5682438289408419908)
XLA Ops:
  0.7 0.9 copy-done.3
  1.6 0.8 copy-done.4
  2.5 4.4 %collective-permute-start.1 = (bf16[3,256,128]{2,1,0:T(8,128)(2,1)S(1)}, bf16[3,256,128]{2,1,0:T(8,128)(2,1)S(1)}, u32[]{:S(2)}, u32[]{:S(2)}) collective-permute-start(bf16[3,256,128]{2,1,0:T(8,128)(2,1)S(1)} %split_heads.1.refs_0_), channel_id=1, source_target_pairs={{0,16},{16,4},{4,20},{20,8},{8,24},{24,12},{12,28},{1,17},{17,5},{... | collective-permute-start | bytes 589832 | tf_op jit(solution)/shard_map/ppermute | solution.py:461
  6.9 5.2 %collective-permute-start.2 = (bf16[3,256,128]{2,1,0:T(8,128)(2,1)S(1)}, bf16[3,256,128]{2,1,0:T(8,128)(2,1)S(1)}, u32[]{:S(2)}, u32[]{:S(2)}) collective-permute-start(bf16[3,256,128]{2,1,0:T(8,128)(2,1)S(1)} %split_heads.1.refs_0_), channel_id=1, source_target_pairs={{0,28},{16,0},{4,16},{20,4},{24,8},{28,12},{1,29},{17,1},{5,17},{2... | collective-permute-start | bytes 589832 | tf_op jit(solution)/shard_map/ppermute | solution.py:461
  12.2 1.2 copy-done
  14.1 1.7 queries_for_other.1
  17.7 4.4 %collective-permute-start.10 = (bf16[5,256,128]{2,1,0:T(8,128)(2,1)S(1)}, bf16[5,256,128]{2,1,0:T(8,128)(2,1)S(1)}, u32[]{:S(2)}, u32[]{:S(2)}) collective-permute-start(bf16[5,256,128]{2,1,0:T(8,128)(2,1)S(1)} %chunks_of.4.refs_0_), channel_id=1, source_target_pairs={{0,3},{1,0},{4,7},{5,4},{8,11},{9,8},{12,15},{13,12},{16,19},{17,1... | collective-permute-start | bytes 983048 | tf_op jit(solution)/shard_map/ppermute | solution.py:457
  22.1 5.2 %collective-permute-start.5 = (bf16[3,256,128]{2,1,0:T(8,128)(2,1)S(1)}, bf16[3,256,128]{2,1,0:T(8,128)(2,1)S(1)}, u32[]{:S(2)}, u32[]{:S(2)}) collective-permute-start(bf16[3,256,128]{2,1,0:T(8,128)(2,1)S(1)} %collective-permute-done.2.refs_5_.refs_1_), channel_id=1, source_target_pairs={{28,12},{0,28},{16,0},{29,13},{1,29},{17,1},{30,14},{2,30},{18,2},... | collective-permute-start | bytes 589832 | tf_op jit(solution)/shard_map/ppermute | solution.py:461
  28.0 1.3 collective-permute-start.9
  29.9 6.2 %collective-permute-start.6 = (bf16[3,256,128]{2,1,0:T(8,128)(2,1)S(1)}, bf16[3,256,128]{2,1,0:T(8,128)(2,1)S(1)}, u32[]{:S(2)}, u32[]{:S(2)}) collective-permute-start(bf16[3,256,128]{2,1,0:T(8,128)(2,1)S(1)} %collective-permute-done.5.refs_3_), channel_id=1, source_target_pairs={{28,12},{0,28},{12,24},{29,13},{1,29},{13,25},{30,14},{2,30},{14,2... | collective-permute-start | bytes 589832 | tf_op jit(solution)/shard_map/ppermute | solution.py:461
  36.9 1.5 collective-permute-start.15
  38.7 1.3 collective-permute-start.12
  40.6 4.5 %collective-permute-done.15.refs_8_ = bf16[2,256,128]{2,1,0:T(8,128)(2,1)S(1)} collective-permute-done((bf16[2,256,128]{2,1,0:T(8,128)(2,1)S(1)}, bf16[2,256,128]{2,1,0:T(8,128)(2,1)S(1)}, u32[]{:S(2)}, u32[]{:S(2)}) %collective-permute-start.15) | collective-permute-done | bytes 131104 | tf_op jit(solution)/shard_map/ppermute | solution.py:469
  45.1 0.7 collective-permute-start.7
  45.8 0.7 collective-permute-start.8
  47.2 1.1 prepare.1.refs_11_
  48.9 0.7 collective-permute-start.19
  49.6 0.7 collective-permute-start.20
  50.4 3.5 %attend.3 = (f32[56,8,256]{2,1,0:T(8,128)S(1)}, bf16[21,256,256]{2,1,0:T(8,128)(2,1)S(1)}) custom-call(s32[1,3]{1,0:T(1,128)S(1)} %add_bitcast_fusion.place, s32[2,14]{1,0:T(2,128)S(1)} %bitcast.23, s32[2,7]{1,0:T(2,128)S(1)} %copy-done.9, bf16[5,256,128]{2,1,0:T(8,128)(2,1)S(1)} %chunks_of.4.refs_0_, ...), custom_call_target="tpu_custom_call", output_to_operand_aliasing={{1}: (14, {})} | custom-call | flops 4932501504 | bytes 2293760 | tf_op jit(solution)/shard_map/attend/pallas_call | solution.py:424
  53.9 0.7 collective-permute-start.21
  56.1 1.1 attend.4.refs_4_
  57.2 1.7 %attend.5 = (f32[7,256]{1,0:T(8,128)S(1)}, f32[128,128]{1,0:T(8,128)}) custom-call(s32[1,3]{1,0:T(1,128)S(1)} %add_bitcast_fusion.place, s32[2,14]{1,0:T(2,128)S(1)} %bitcast.25, s32[2,3]{1,0:T(2,128)S(1)} %copy-done.7, bf16[5,256,128]{2,1,0:T(8,128)(2,1)S(1)} %collective-permute-done.17.refs_0_, bf16[5,256,128]{2,1,0:T(8,128)(2,1)S(1)} %collective-permute-done.18.refs_1_, ...), custom_call_target="tpu_custom_call" | custom-call | flops 2113929216 | bytes 983040 | tf_op jit(solution)/shard_map/attend/pallas_call | solution.py:424
  58.9 98.3 %all-to-all-start = ((f32[128,1,128]{2,1,0:T(1,128)}), f32[128,1,128]{2,1,0:T(1,128)S(1)}, u32[]{:S(2)}, u32[]{:S(2)}) async-start(f32[128,1,128]{2,1,0:T(1,128)} %bitcast.12), calls=%async_computation | async-start | bytes 131072 | tf_op jit(solution)/shard_map/all_to_all | solution.py:528
  157.9 11.4 %all-to-all-done = f32[128,1,128]{2,1,0:T(1,128)S(1)} async-done(((f32[128,1,128]{2,1,0:T(1,128)}), f32[128,1,128]{2,1,0:T(1,128)S(1)}, u32[]{:S(2)}, u32[]{:S(2)}) %all-to-all-start) | async-done | bytes 65568 | tf_op jit(solution)/shard_map/all_to_all | solution.py:528
  (58 shorter events, 9.0 us)
Async XLA Ops:
  0.6 46.6 %copy-start.6 = (s32[14,2]{0,1:T(2,128)S(1)}, s32[14,2]{0,1:T(2,128)}, u32[]{:S(2)}) copy-start(s32[14,2]{0,1:T(2,128)} %param.14) | copy-start | bytes 340
  2.5 13.9 %collective-permute-start.1 = (bf16[3,256,128]{2,1,0:T(8,128)(2,1)S(1)}, bf16[3,256,128]{2,1,0:T(8,128)(2,1)S(1)}, u32[]{:S(2)}, u32[]{:S(2)}) collective-permute-start(bf16[3,256,128]{2,1,0:T(8,128)(2,1)S(1)} %split_heads.1.refs_0_), channel_id=1, source_target_pairs={{0,16},{16,4},{4,20},{20,8},{8,24},{24,12},{12,28},{1,17},{17,5},{... | collective-permute-start | bytes 589832 | tf_op jit(solution)/shard_map/ppermute | solution.py:461
  6.9 9.5 %collective-permute-start.2 = (bf16[3,256,128]{2,1,0:T(8,128)(2,1)S(1)}, bf16[3,256,128]{2,1,0:T(8,128)(2,1)S(1)}, u32[]{:S(2)}, u32[]{:S(2)}) collective-permute-start(bf16[3,256,128]{2,1,0:T(8,128)(2,1)S(1)} %split_heads.1.refs_0_), channel_id=1, source_target_pairs={{0,28},{16,0},{4,16},{20,4},{24,8},{28,12},{1,29},{17,1},{5,17},{2... | collective-permute-start | bytes 589832 | tf_op jit(solution)/shard_map/ppermute | solution.py:461
  14.1 33.1 %copy-start.2 = (bf16[1,256,896]{2,1,0:T(8,128)(2,1)S(1)}, bf16[1,256,896]{2,1,0:T(8,128)(2,1)}, u32[]{:S(2)}) copy-start(bf16[1,256,896]{2,1,0:T(8,128)(2,1)} %param.12) | copy-start | bytes 1376260
  16.5 10.8 %collective-permute-start.3 = (bf16[3,256,128]{2,1,0:T(8,128)(2,1)S(1)}, bf16[3,256,128]{2,1,0:T(8,128)(2,1)S(1)}, u32[]{:S(2)}, u32[]{:S(2)}) collective-permute-start(bf16[3,256,128]{2,1,0:T(8,128)(2,1)S(1)} %collective-permute-done.1.refs_1_.refs_2_), channel_id=1, source_target_pairs={{16,4},{4,20},{20,8},{8,24},{24,12},{12,28},{17,5},{5,21},{21,9},{... | collective-permute-start | bytes 589832 | tf_op jit(solution)/shard_map/ppermute | solution.py:461
  17.7 19.2 %collective-permute-start.10 = (bf16[5,256,128]{2,1,0:T(8,128)(2,1)S(1)}, bf16[5,256,128]{2,1,0:T(8,128)(2,1)S(1)}, u32[]{:S(2)}, u32[]{:S(2)}) collective-permute-start(bf16[5,256,128]{2,1,0:T(8,128)(2,1)S(1)} %chunks_of.4.refs_0_), channel_id=1, source_target_pairs={{0,3},{1,0},{4,7},{5,4},{8,11},{9,8},{12,15},{13,12},{16,19},{17,1... | collective-permute-start | bytes 983048 | tf_op jit(solution)/shard_map/ppermute | solution.py:457
  22.1 7.8 %collective-permute-start.5 = (bf16[3,256,128]{2,1,0:T(8,128)(2,1)S(1)}, bf16[3,256,128]{2,1,0:T(8,128)(2,1)S(1)}, u32[]{:S(2)}, u32[]{:S(2)}) collective-permute-start(bf16[3,256,128]{2,1,0:T(8,128)(2,1)S(1)} %collective-permute-done.2.refs_5_.refs_1_), channel_id=1, source_target_pairs={{28,12},{0,28},{16,0},{29,13},{1,29},{17,1},{30,14},{2,30},{18,2},... | collective-permute-start | bytes 589832 | tf_op jit(solution)/shard_map/ppermute | solution.py:461
  27.3 8.9 %collective-permute-start.4 = (bf16[3,256,128]{2,1,0:T(8,128)(2,1)S(1)}, bf16[3,256,128]{2,1,0:T(8,128)(2,1)S(1)}, u32[]{:S(2)}, u32[]{:S(2)}) collective-permute-start(bf16[3,256,128]{2,1,0:T(8,128)(2,1)S(1)} %collective-permute-done.3.refs_0_), channel_id=1, source_target_pairs={{4,20},{20,8},{8,24},{24,12},{12,28},{5,21},{21,9},{9,25},{25,13},... | collective-permute-start | bytes 589832 | tf_op jit(solution)/shard_map/ppermute | solution.py:461
  28.0 17.8 %collective-permute-start.9 = (bf16[5,256,128]{2,1,0:T(8,128)(2,1)S(1)}, bf16[5,256,128]{2,1,0:T(8,128)(2,1)S(1)}, u32[]{:S(2)}, u32[]{:S(2)}) collective-permute-start(bf16[5,256,128]{2,1,0:T(8,128)(2,1)S(1)} %chunks_of.4.refs_0_), channel_id=1, source_target_pairs={{0,1},{1,2},{2,3},{4,5},{5,6},{6,7},{8,9},{9,10},{10,11},{12,13},{... | collective-permute-start | bytes 983048 | tf_op jit(solution)/shard_map/ppermute | solution.py:457
  29.3 6.8 %collective-permute-start.14 = (bf16[2,256,128]{2,1,0:T(8,128)(2,1)S(1)}, bf16[2,256,128]{2,1,0:T(8,128)(2,1)S(1)}, u32[]{:S(2)}, u32[]{:S(2)}) collective-permute-start(bf16[2,256,128]{2,1,0:T(8,128)(2,1)S(1)} %get-tuple-element.29), channel_id=1, source_target_pairs={{0,16},{16,0},{1,17},{17,1},{2,18},{18,2},{3,19},{19,3},{4,20},{20... | collective-permute-start | bytes 393224 | tf_op jit(solution)/shard_map/ppermute | solution.py:469
  29.9 8.8 %collective-permute-start.6 = (bf16[3,256,128]{2,1,0:T(8,128)(2,1)S(1)}, bf16[3,256,128]{2,1,0:T(8,128)(2,1)S(1)}, u32[]{:S(2)}, u32[]{:S(2)}) collective-permute-start(bf16[3,256,128]{2,1,0:T(8,128)(2,1)S(1)} %collective-permute-done.5.refs_3_), channel_id=1, source_target_pairs={{28,12},{0,28},{12,24},{29,13},{1,29},{13,25},{30,14},{2,30},{14,2... | collective-permute-start | bytes 589832 | tf_op jit(solution)/shard_map/ppermute | solution.py:461
  36.1 12.8 %collective-permute-start.16 = (bf16[5,256,128]{2,1,0:T(8,128)(2,1)S(1)}, bf16[5,256,128]{2,1,0:T(8,128)(2,1)S(1)}, u32[]{:S(2)}, u32[]{:S(2)}) collective-permute-start(bf16[5,256,128]{2,1,0:T(8,128)(2,1)S(1)} %get-tuple-element.31), channel_id=1, source_target_pairs={{0,16},{16,0},{1,17},{17,1},{2,18},{18,2},{3,19},{19,3},{4,20},{20... | collective-permute-start | bytes 983048 | tf_op jit(solution)/shard_map/ppermute | solution.py:469
  36.2 10.3 %collective-permute-start.13 = (bf16[3,256,128]{2,1,0:T(8,128)(2,1)S(1)}, bf16[3,256,128]{2,1,0:T(8,128)(2,1)S(1)}, u32[]{:S(2)}, u32[]{:S(2)}) collective-permute-start(bf16[3,256,128]{2,1,0:T(8,128)(2,1)S(1)} %collective-permute-done.4.refs_2_.refs_1_), channel_id=1, source_target_pairs={{20,8},{8,24},{24,12},{12,28},{21,9},{9,25},{25,13},{13,29},{22,10... | collective-permute-start | bytes 589832 | tf_op jit(solution)/shard_map/ppermute | solution.py:461
  36.9 8.1 %collective-permute-start.15 = (bf16[2,256,128]{2,1,0:T(8,128)(2,1)S(1)}, bf16[2,256,128]{2,1,0:T(8,128)(2,1)S(1)}, u32[]{:S(2)}, u32[]{:S(2)}) collective-permute-start(bf16[2,256,128]{2,1,0:T(8,128)(2,1)S(1)} %get-tuple-element.30), channel_id=1, source_target_pairs={{0,16},{16,0},{1,17},{17,1},{2,18},{18,2},{3,19},{19,3},{4,20},{20... | collective-permute-start | bytes 393224 | tf_op jit(solution)/shard_map/ppermute | solution.py:469
  38.7 11.6 %collective-permute-start.12 = (bf16[3,256,128]{2,1,0:T(8,128)(2,1)S(1)}, bf16[3,256,128]{2,1,0:T(8,128)(2,1)S(1)}, u32[]{:S(2)}, u32[]{:S(2)}) collective-permute-start(bf16[3,256,128]{2,1,0:T(8,128)(2,1)S(1)} %slice.21), channel_id=1, source_target_pairs={{3,2},{0,3},{7,6},{4,7},{11,10},{8,11},{15,14},{12,15},{19,18},{16... | collective-permute-start | bytes 589832 | tf_op jit(solution)/shard_map/ppermute | solution.py:457
  45.1 8.8 %collective-permute-start.7 = (bf16[10,256,128]{2,1,0:T(8,128)(2,1)S(1)}, bf16[10,256,128]{2,1,0:T(8,128)(2,1)S(1)}, u32[]{:S(2)}, u32[]{:S(2)}) collective-permute-start(bf16[10,256,128]{2,1,0:T(8,128)(2,1)S(1)} %chunks_of.3.refs_5_), channel_id=1, source_target_pairs={{4,5},{5,6},{6,7},{7,4},{8,9},{9,10},{10,11},{11,8},{12,13},{13,14... | collective-permute-start | bytes 1966088 | tf_op jit(solution)/shard_map/ppermute | solution.py:457
  45.8 8.1 %collective-permute-start.8 = (bf16[10,256,128]{2,1,0:T(8,128)(2,1)S(1)}, bf16[10,256,128]{2,1,0:T(8,128)(2,1)S(1)}, u32[]{:S(2)}, u32[]{:S(2)}) collective-permute-start(bf16[10,256,128]{2,1,0:T(8,128)(2,1)S(1)} %chunks_of.3.refs_5_), channel_id=1, source_target_pairs={{4,7},{5,4},{6,5},{7,6},{8,11},{9,8},{10,9},{11,10},{12,15},{13,12... | collective-permute-start | bytes 1966088 | tf_op jit(solution)/shard_map/ppermute | solution.py:457
  46.5 3.1 %collective-permute-start.11 = (bf16[2,256,128]{2,1,0:T(8,128)(2,1)S(1)}, bf16[2,256,128]{2,1,0:T(8,128)(2,1)S(1)}, u32[]{:S(2)}, u32[]{:S(2)}) collective-permute-start(bf16[2,256,128]{2,1,0:T(8,128)(2,1)S(1)} %slice.20), channel_id=1, source_target_pairs={{1,2},{2,3},{5,6},{6,7},{9,10},{10,11},{13,14},{14,15},{17,18},{18... | collective-permute-start | bytes 393224 | tf_op jit(solution)/shard_map/ppermute | solution.py:457
  48.9 5.0 %collective-permute-start.19 = (bf16[5,256,128]{2,1,0:T(8,128)(2,1)S(1)}, bf16[5,256,128]{2,1,0:T(8,128)(2,1)S(1)}, u32[]{:S(2)}, u32[]{:S(2)}) collective-permute-start(bf16[5,256,128]{2,1,0:T(8,128)(2,1)S(1)} %chunks_of.5.refs_6_), channel_id=1, source_target_pairs={{8,9},{9,10},{10,11},{11,8},{12,13},{13,14},{14,15},{15,12},{24,25... | collective-permute-start | bytes 983048 | tf_op jit(solution)/shard_map/ppermute | solution.py:457
  49.6 4.3 %collective-permute-start.20 = (bf16[5,256,128]{2,1,0:T(8,128)(2,1)S(1)}, bf16[5,256,128]{2,1,0:T(8,128)(2,1)S(1)}, u32[]{:S(2)}, u32[]{:S(2)}) collective-permute-start(bf16[5,256,128]{2,1,0:T(8,128)(2,1)S(1)} %chunks_of.5.refs_6_), channel_id=1, source_target_pairs={{8,11},{9,8},{10,9},{11,10},{12,15},{13,12},{14,13},{15,14},{24,27... | collective-permute-start | bytes 983048 | tf_op jit(solution)/shard_map/ppermute | solution.py:457
  53.9 3.2 %collective-permute-start.21 = (bf16[5,256,128]{2,1,0:T(8,128)(2,1)S(1)}, bf16[5,256,128]{2,1,0:T(8,128)(2,1)S(1)}, u32[]{:S(2)}, u32[]{:S(2)}) collective-permute-start(bf16[5,256,128]{2,1,0:T(8,128)(2,1)S(1)} %collective-permute-done.19.refs_2_), channel_id=1, source_target_pairs={{8,9},{9,10},{10,11},{11,8},{12,13},{13,14},{14,15},{15,12},{24,25... | collective-permute-start | bytes 983048 | tf_op jit(solution)/shard_map/ppermute | solution.py:457
  54.7 2.5 %collective-permute-start.17 = (bf16[5,256,128]{2,1,0:T(8,128)(2,1)S(1)}, bf16[5,256,128]{2,1,0:T(8,128)(2,1)S(1)}, u32[]{:S(2)}, u32[]{:S(2)}) collective-permute-start(bf16[5,256,128]{2,1,0:T(8,128)(2,1)S(1)} %slice.17), channel_id=1, source_target_pairs={{4,5},{5,6},{6,7},{7,4},{8,9},{9,10},{10,11},{11,8},{12,13},{13,14... | collective-permute-start | bytes 983048 | tf_op jit(solution)/shard_map/ppermute | solution.py:457
  55.4 1.8 %collective-permute-start.18 = (bf16[5,256,128]{2,1,0:T(8,128)(2,1)S(1)}, bf16[5,256,128]{2,1,0:T(8,128)(2,1)S(1)}, u32[]{:S(2)}, u32[]{:S(2)}) collective-permute-start(bf16[5,256,128]{2,1,0:T(8,128)(2,1)S(1)} %slice.18), channel_id=1, source_target_pairs={{12,15},{13,12},{14,13},{15,14},{28,31},{29,28},{30,29},{31,30},{4... | collective-permute-start | bytes 983048 | tf_op jit(solution)/shard_map/ppermute | solution.py:457
  58.9 110.3 %all-to-all-start = ((f32[128,1,128]{2,1,0:T(1,128)}), f32[128,1,128]{2,1,0:T(1,128)S(1)}, u32[]{:S(2)}, u32[]{:S(2)}) async-start(f32[128,1,128]{2,1,0:T(1,128)} %bitcast.12), calls=%async_computation | async-start | bytes 131072 | tf_op jit(solution)/shard_map/all_to_all | solution.py:528
  (8 other events, 54.8 us)

commit v10 on v9

--- a/solution.py
+++ b/solution.py
@@ -31,7 +31,7 @@
 OWN = 3
 OTHER = 2
 CHUNK = OWN + OTHER
-PIECES = (2, 2, 5)
+PIECES = (4, 5)
 SENT = sum(PIECES)
 MIB = 1024 * 1024
 SMEM = pl.BlockSpec(memory_space=pltpu.SMEM)
@@ -438,9 +438,17 @@
     )(place, table, plan, *groups, *extra)
 
 
+def shift(n, by):
+    return [(i, (i + by) % n) for i in range(n)]
+
+
 def z_place(ring):
     ring %= 8
     return (ring % 2) * 4 + ring // 2
+
+
+def z_shift(by):
+    return [(z_place(i), z_place(i + by)) for i in range(8)]
 
 
 def plan_of(blocks):
@@ -452,20 +460,14 @@
     table = pair_table.T
     place = jnp.stack([head, lax.axis_index("kv_0"), lax.axis_index("kv_1")])[None]
 
-    def along_x(a, by, chunks, sources=range(4)):
-        pairs = [(c * 4 + i, c * 4 + (i + by) % 4) for c in chunks for i in sources]
-        return lax.ppermute(a, KV, pairs)
-
-    def along_z(a, by, sources):
-        pairs = [(z_place(i), z_place(i + by)) for i in sources]
-        return lax.ppermute(a, ("head", "kv_0"), pairs)
-
+    along_x = lambda a, by: lax.ppermute(a, "kv_1", shift(4, by))
+    along_z = lambda a, by: lax.ppermute(a, ("head", "kv_0"), z_shift(by))
     other_side = [(0, 1), (1, 0)]
 
     ring = {0: split_heads(teacher_key[0], student_key[0])}
     *chosen, count = queries_for_other(place, table, teacher_query[0])
-    ring[1] = along_z(ring[0], 1, range(7))
-    ring[7] = along_z(ring[0], -1, (0, 1, 2, 3, 5, 7))
+    ring[1] = along_z(ring[0], 1)
+    ring[7] = along_z(ring[0], -1)
     pieces = [lax.ppermute(piece, "head", other_side) for piece in chosen[:-1]]
     more = lax.cond(
         count[0, 0] > SENT,
@@ -476,21 +478,21 @@
     more, ring[1], ring[7] = lax.optimization_barrier((more, ring[1], ring[7]))
     rows = prepare(place, table, teacher_query[0], student_query[0])
     mine = chunks_of(place, ring, (0,))
-    near_a = along_x(mine, 1, range(4), (0, 1, 2))
-    near_b = along_x(mine, -1, range(4), (0, 1))
-    near_c = along_x(near_a[:OTHER], 1, range(4), (1, 2))
-    near_d = along_x(near_b[OTHER:], -1, range(4), (3, 0))
+    near_a = along_x(mine, 1)
+    near_b = along_x(mine, -1)
+    near_c = along_x(near_a[:OTHER], 1)
+    near_d = along_x(near_b[OTHER:], -1)
     for step in range(2, 5):
-        ring[step] = along_z(ring[step - 1], 1, range(step - 1, 7))
+        ring[step] = along_z(ring[step - 1], 1)
         if step < 4:
-            ring[8 - step] = along_z(ring[9 - step], -1, (7, 0, 1 if step == 2 else 6))
+            ring[8 - step] = along_z(ring[9 - step], -1)
 
     rest_13 = chunks_of(place, ring, (1, 3))
-    left_13 = along_x(rest_13, 1, (1, 2, 3))
-    right_13 = along_x(rest_13, -1, (1, 2, 3))
+    left_13 = along_x(rest_13, 1)
+    right_13 = along_x(rest_13, -1)
     rest_2 = chunks_of(place, ring, (2,))
-    left_2 = along_x(rest_2, 1, (2, 3))
-    right_2 = along_x(rest_2, -1, (2, 3))
+    left_2 = along_x(rest_2, 1)
+    right_2 = along_x(rest_2, -1)
     state, rows = attend(
         place,
         table,
@@ -502,10 +504,10 @@
     left_13, right_13, state = lax.optimization_barrier((left_13, right_13, state))
     cut_1 = left_13[:CHUNK]
     cut_3 = right_13[CHUNK:]
-    far_1 = along_x(cut_1, 1, (1, 2, 3))
-    far_3 = along_x(cut_3, -1, (3,))
+    far_1 = along_x(cut_1, 1)
+    far_3 = along_x(cut_3, -1)
     left_2, right_2, state = lax.optimization_barrier((left_2, right_2, state))
-    far_2 = along_x(left_2, 1, (2, 3))
+    far_2 = along_x(left_2, 1)
     state = attend(
         place,
         table,

time: 171 us -> 146 us (0.85)
  starting transfers between devices: 135 us -> 91.5 us
  waiting for transfers between devices: 16.6 us -> 37.3 us
    all_to_all x1, starting transfers between devices: 98.3 us -> 58.6 us  [program(): terms = lax.all_to_all(sums, everyone, 0, 0, tiled=True)]
    ppermute x18, waiting for transfers between devices: 0.76 us -> 26.1 us  [the longest x11 15.9 us: program(): along_x = lambda a, by: lax.ppermute(a, 'kv_1', shift(4, by))]
    ppermute x3 -> x2, waiting for transfers between devices: 4.47 us -> 0.01 us  [program(): pieces = [lax.ppermute(piece, 'head', other_side) for piece in chosen[:-1]]]
    ppermute x18, starting transfers between devices: 35.4 us -> 32.5 us  [the longest x11 19.2 us: program(): along_x = lambda a, by: lax.ppermute(a, 'kv_1', shift(4, by))]
  transfers between devices with their start and end apart: 22 -> 21, of which waited for: 4 -> 12; matrix products, arithmetic and copies ran while one was open for 0% -> 1% of each run, Pallas kernels for 5% -> 6%
where the time goes in v10:
time: 146 us
  starting transfers between devices  91.5 us (63%)
  waiting for transfers between devices  37.3 us (26%)
  Pallas kernels  10.7 us (7%)
  local copies, waits for them, and re-layouts  4.3 us (3%)
  between operations  1.46 us (1%)
    all_to_all x1, starting transfers between devices, program(): terms = lax.all_to_all(sums, everyone, 0, 0, tiled=True)  58.6 us
    ppermute x11, starting transfers between devices, program(): along_x = lambda a, by: lax.ppermute(a, 'kv_1', shift(4, by))  19.2 us
    ppermute x11, waiting for transfers between devices, program(): along_x = lambda a, by: lax.ppermute(a, 'kv_1', shift(4, by))  15.9 us
    ppermute x7, starting transfers between devices, program(): along_z = lambda a, by: lax.ppermute(a, ('head', 'kv_0'), z_shift(by))  13.2 us
    all_to_all x1, waiting for transfers between devices, program(): terms = lax.all_to_all(sums, everyone, 0, 0, tiled=True)  11.2 us
    ppermute x7, waiting for transfers between devices, program(): along_z = lambda a, by: lax.ppermute(a, ('head', 'kv_0'), z_shift(by))  10.2 us
    pallas_call x3, Pallas kernels, attend(): pl.pallas_call(functools.partial(attend_kernel, first, last, counts, bloc...  6.05 us
    unnamed x21, local copies, waits for them, and re-layouts  4.23 us
  transfers between devices with their start and end apart: 21, of which 12 were waited for; matrix products, arithmetic and copies ran while one was open for 1% of the time, Pallas kernels for 6%

profile of v10, /device:TPU:1, one launch (start us, length us, event | category | flops | bytes accessed | tf_op | source)
XLA Modules:
  0.0 146.0 jit_solution(17674470708502067335)
XLA Ops:
  2.5 2.5 %collective-permute-start.1 = (bf16[3,256,128]{2,1,0:T(8,128)(2,1)S(1)}, bf16[3,256,128]{2,1,0:T(8,128)(2,1)S(1)}, u32[]{:S(2)}, u32[]{:S(2)}) collective-permute-start(bf16[3,256,128]{2,1,0:T(8,128)(2,1)S(1)} %split_heads.1.refs_0_), channel_id=1, source_target_pairs={{0,16},{16,4},{4,20},{20,8},{8,24},{24,12},{12,28},{28,0},{1,17},{... | collective-permute-start | bytes 589832 | tf_op jit(solution)/shard_map/ppermute | solution.py:464
  5.1 4.0 %collective-permute-start.2 = (bf16[3,256,128]{2,1,0:T(8,128)(2,1)S(1)}, bf16[3,256,128]{2,1,0:T(8,128)(2,1)S(1)}, u32[]{:S(2)}, u32[]{:S(2)}) collective-permute-start(bf16[3,256,128]{2,1,0:T(8,128)(2,1)S(1)} %split_heads.1.refs_0_), channel_id=1, source_target_pairs={{0,28},{16,0},{4,16},{20,4},{8,20},{24,8},{12,24},{28,12},{1,29},{... | collective-permute-start | bytes 589832 | tf_op jit(solution)/shard_map/ppermute | solution.py:464
  9.2 1.2 copy-done
  11.0 1.7 %queries_for_other.1 = (bf16[4,256,128]{2,1,0:T(8,128)(2,1)S(1)}, bf16[5,256,128]{2,1,0:T(8,128)(2,1)S(1)}, bf16[5,256,128]{2,1,0:T(8,128)(2,1)S(1)}, s32[1,1]{1,0:T(1,128)}) custom-call(s32[1,3]{1,0:T(1,128)S(1)} %add_bitcast_fusion.place, s32[2,14]{1,0:T(2,128)S(1)} %bitcast.21, bf16[256,1792]{1,0:T(8,128)(2,1)S(1)} %bitcast.15), custom_call_target="tpu_custom_call" | custom-call | tf_op jit(solution)/shard_map/queries_for_other/pallas_call | solution.py:108
  14.2 2.6 %collective-permute-start.10 = (bf16[5,256,128]{2,1,0:T(8,128)(2,1)S(1)}, bf16[5,256,128]{2,1,0:T(8,128)(2,1)S(1)}, u32[]{:S(2)}, u32[]{:S(2)}) collective-permute-start(bf16[5,256,128]{2,1,0:T(8,128)(2,1)S(1)} %chunks_of.4.refs_0_), channel_id=1, source_target_pairs={{0,3},{1,0},{2,1},{3,2},{4,7},{5,4},{6,5},{7,6},{8,11},{9,8},{10,9... | collective-permute-start | bytes 983048 | tf_op jit(solution)/shard_map/ppermute | solution.py:463
  16.8 2.7 %collective-permute-start.5 = (bf16[3,256,128]{2,1,0:T(8,128)(2,1)S(1)}, bf16[3,256,128]{2,1,0:T(8,128)(2,1)S(1)}, u32[]{:S(2)}, u32[]{:S(2)}) collective-permute-start(bf16[3,256,128]{2,1,0:T(8,128)(2,1)S(1)} %collective-permute-done.2.refs_5_.refs_1_), channel_id=1, source_target_pairs={{0,28},{16,0},{4,16},{20,4},{8,20},{24,8},{12,24},{28,12},{1,29},{... | collective-permute-start | bytes 589832 | tf_op jit(solution)/shard_map/ppermute | solution.py:464
  20.0 1.2 collective-permute-start.9
  22.0 3.1 %collective-permute-start.6 = (bf16[3,256,128]{2,1,0:T(8,128)(2,1)S(1)}, bf16[3,256,128]{2,1,0:T(8,128)(2,1)S(1)}, u32[]{:S(2)}, u32[]{:S(2)}) collective-permute-start(bf16[3,256,128]{2,1,0:T(8,128)(2,1)S(1)} %collective-permute-done.5.refs_3_), channel_id=1, source_target_pairs={{0,28},{16,0},{4,16},{20,4},{8,20},{24,8},{12,24},{28,12},{1,29},{... | collective-permute-start | bytes 589832 | tf_op jit(solution)/shard_map/ppermute | solution.py:464
  26.7 4.9 %collective-permute-done.6.refs_4_.refs_2_ = bf16[3,256,128]{2,1,0:T(8,128)(2,1)S(1)} collective-permute-done((bf16[3,256,128]{2,1,0:T(8,128)(2,1)S(1)}, bf16[3,256,128]{2,1,0:T(8,128)(2,1)S(1)}, u32[]{:S(2)}, u32[]{:S(2)}) %collective-permute-start.6) | collective-permute-done | bytes 196640 | tf_op jit(solution)/shard_map/ppermute | solution.py:464
  33.7 2.1 %collective-permute-start.8 = (bf16[10,256,128]{2,1,0:T(8,128)(2,1)S(1)}, bf16[10,256,128]{2,1,0:T(8,128)(2,1)S(1)}, u32[]{:S(2)}, u32[]{:S(2)}) collective-permute-start(bf16[10,256,128]{2,1,0:T(8,128)(2,1)S(1)} %chunks_of.3.refs_5_), channel_id=1, source_target_pairs={{0,3},{1,0},{2,1},{3,2},{4,7},{5,4},{6,5},{7,6},{8,11},{9,8},{10,9... | collective-permute-start | bytes 1966088 | tf_op jit(solution)/shard_map/ppermute | solution.py:463
  35.8 3.5 %collective-permute-done.13.refs_0_ = bf16[3,256,128]{2,1,0:T(8,128)(2,1)S(1)} collective-permute-done((bf16[3,256,128]{2,1,0:T(8,128)(2,1)S(1)}, bf16[3,256,128]{2,1,0:T(8,128)(2,1)S(1)}, u32[]{:S(2)}, u32[]{:S(2)}) %collective-permute-start.13) | collective-permute-done | bytes 196640 | tf_op jit(solution)/shard_map/ppermute | solution.py:464
  39.3 1.2 collective-permute-start.11
  40.6 1.1 prepare.1.refs_10_
  42.3 1.3 collective-permute-start.18
  43.6 3.5 %collective-permute-done.11.refs_3_ = bf16[2,256,128]{2,1,0:T(8,128)(2,1)S(1)} collective-permute-done((bf16[2,256,128]{2,1,0:T(8,128)(2,1)S(1)}, bf16[2,256,128]{2,1,0:T(8,128)(2,1)S(1)}, u32[]{:S(2)}, u32[]{:S(2)}) %collective-permute-start.11) | collective-permute-done | bytes 131104 | tf_op jit(solution)/shard_map/ppermute | solution.py:463
  47.3 3.2 %attend.3 = (f32[56,8,256]{2,1,0:T(8,128)S(1)}, bf16[21,256,256]{2,1,0:T(8,128)(2,1)S(1)}) custom-call(s32[1,3]{1,0:T(1,128)S(1)} %add_bitcast_fusion.place, s32[2,14]{1,0:T(2,128)S(1)} %bitcast.23, s32[2,7]{1,0:T(2,128)S(1)} %copy-done.9, bf16[5,256,128]{2,1,0:T(8,128)(2,1)S(1)} %chunks_of.4.refs_0_, ...), custom_call_target="tpu_custom_call", output_to_operand_aliasing={{1}: (13, {})} | custom-call | flops 4932501504 | bytes 2293760 | tf_op jit(solution)/shard_map/attend/pallas_call | solution.py:424
  50.6 3.5 %collective-permute-done.18.refs_2_ = bf16[5,256,128]{2,1,0:T(8,128)(2,1)S(1)} collective-permute-done((bf16[5,256,128]{2,1,0:T(8,128)(2,1)S(1)}, bf16[5,256,128]{2,1,0:T(8,128)(2,1)S(1)}, u32[]{:S(2)}, u32[]{:S(2)}) %collective-permute-start.18) | collective-permute-done | bytes 327712 | tf_op jit(solution)/shard_map/ppermute | solution.py:463
  54.1 2.0 %collective-permute-done.19.refs_3_ = bf16[5,256,128]{2,1,0:T(8,128)(2,1)S(1)} collective-permute-done((bf16[5,256,128]{2,1,0:T(8,128)(2,1)S(1)}, bf16[5,256,128]{2,1,0:T(8,128)(2,1)S(1)}, u32[]{:S(2)}, u32[]{:S(2)}) %collective-permute-start.19) | collective-permute-done | bytes 327712 | tf_op jit(solution)/shard_map/ppermute | solution.py:463
  57.1 8.2 %collective-permute-start.17 = (bf16[5,256,128]{2,1,0:T(8,128)(2,1)S(1)}, bf16[5,256,128]{2,1,0:T(8,128)(2,1)S(1)}, u32[]{:S(2)}, u32[]{:S(2)}) collective-permute-start(bf16[5,256,128]{2,1,0:T(8,128)(2,1)S(1)} %slice.18), channel_id=1, source_target_pairs={{0,3},{1,0},{2,1},{3,2},{4,7},{5,4},{6,5},{7,6},{8,11},{9,8},{10,9... | collective-permute-start | bytes 983048 | tf_op jit(solution)/shard_map/ppermute | solution.py:463
  66.2 3.3 %collective-permute-done.20.refs_2_ = bf16[5,256,128]{2,1,0:T(8,128)(2,1)S(1)} collective-permute-done((bf16[5,256,128]{2,1,0:T(8,128)(2,1)S(1)}, bf16[5,256,128]{2,1,0:T(8,128)(2,1)S(1)}, u32[]{:S(2)}, u32[]{:S(2)}) %collective-permute-start.20) | collective-permute-done | bytes 327712 | tf_op jit(solution)/shard_map/ppermute | solution.py:463
  69.5 3.5 %collective-permute-done.16.refs_0_ = bf16[5,256,128]{2,1,0:T(8,128)(2,1)S(1)} collective-permute-done((bf16[5,256,128]{2,1,0:T(8,128)(2,1)S(1)}, bf16[5,256,128]{2,1,0:T(8,128)(2,1)S(1)}, u32[]{:S(2)}, u32[]{:S(2)}) %collective-permute-start.16) | collective-permute-done | bytes 327712 | tf_op jit(solution)/shard_map/ppermute | solution.py:463
  73.0 1.9 %attend.5 = (f32[7,256]{1,0:T(8,128)S(1)}, f32[128,128]{1,0:T(8,128)}) custom-call(s32[1,3]{1,0:T(1,128)S(1)} %add_bitcast_fusion.place, s32[2,14]{1,0:T(2,128)S(1)} %bitcast.25, s32[2,3]{1,0:T(2,128)S(1)} %copy-done.7, bf16[5,256,128]{2,1,0:T(8,128)(2,1)S(1)} %collective-permute-done.16.refs_0_, bf16[5,256,128]{2,1,0:T(8,128)(2,1)S(1)} %collective-permute-done.17.refs_1_, ...), custom_call_target="tpu_custom_call" | custom-call | flops 2113929216 | bytes 983040 | tf_op jit(solution)/shard_map/attend/pallas_call | solution.py:424
  75.0 58.6 %all-to-all-start = ((f32[128,1,128]{2,1,0:T(1,128)}), f32[128,1,128]{2,1,0:T(1,128)S(1)}, u32[]{:S(2)}, u32[]{:S(2)}) async-start(f32[128,1,128]{2,1,0:T(1,128)} %bitcast.12), calls=%async_computation | async-start | bytes 131072 | tf_op jit(solution)/shard_map/all_to_all | solution.py:530
  134.1 11.2 %all-to-all-done = f32[128,1,128]{2,1,0:T(1,128)S(1)} async-done(((f32[128,1,128]{2,1,0:T(1,128)}), f32[128,1,128]{2,1,0:T(1,128)S(1)}, u32[]{:S(2)}, u32[]{:S(2)}) %all-to-all-start) | async-done | bytes 65568 | tf_op jit(solution)/shard_map/all_to_all | solution.py:530
  (56 shorter events, 12.5 us)
Async XLA Ops:
  0.6 39.9 %copy-start.6 = (s32[14,2]{0,1:T(2,128)S(1)}, s32[14,2]{0,1:T(2,128)}, u32[]{:S(2)}) copy-start(s32[14,2]{0,1:T(2,128)} %param.14) | copy-start | bytes 340
  2.5 11.1 %collective-permute-start.1 = (bf16[3,256,128]{2,1,0:T(8,128)(2,1)S(1)}, bf16[3,256,128]{2,1,0:T(8,128)(2,1)S(1)}, u32[]{:S(2)}, u32[]{:S(2)}) collective-permute-start(bf16[3,256,128]{2,1,0:T(8,128)(2,1)S(1)} %split_heads.1.refs_0_), channel_id=1, source_target_pairs={{0,16},{16,4},{4,20},{20,8},{8,24},{24,12},{12,28},{28,0},{1,17},{... | collective-permute-start | bytes 589832 | tf_op jit(solution)/shard_map/ppermute | solution.py:464
  5.1 8.5 %collective-permute-start.2 = (bf16[3,256,128]{2,1,0:T(8,128)(2,1)S(1)}, bf16[3,256,128]{2,1,0:T(8,128)(2,1)S(1)}, u32[]{:S(2)}, u32[]{:S(2)}) collective-permute-start(bf16[3,256,128]{2,1,0:T(8,128)(2,1)S(1)} %split_heads.1.refs_0_), channel_id=1, source_target_pairs={{0,28},{16,0},{4,16},{20,4},{8,20},{24,8},{12,24},{28,12},{1,29},{... | collective-permute-start | bytes 589832 | tf_op jit(solution)/shard_map/ppermute | solution.py:464
  11.0 29.5 %copy-start.1 = (bf16[1,256,1792]{2,1,0:T(8,128)(2,1)S(1)}, bf16[1,256,1792]{2,1,0:T(8,128)(2,1)}, u32[]{:S(2)}) copy-start(bf16[1,256,1792]{2,1,0:T(8,128)(2,1)} %param.10) | copy-start | bytes 2752516
  11.0 29.5 %copy-start.2 = (bf16[1,256,896]{2,1,0:T(8,128)(2,1)S(1)}, bf16[1,256,896]{2,1,0:T(8,128)(2,1)}, u32[]{:S(2)}) copy-start(bf16[1,256,896]{2,1,0:T(8,128)(2,1)} %param.12) | copy-start | bytes 1376260
  13.6 6.4 %collective-permute-start.3 = (bf16[3,256,128]{2,1,0:T(8,128)(2,1)S(1)}, bf16[3,256,128]{2,1,0:T(8,128)(2,1)S(1)}, u32[]{:S(2)}, u32[]{:S(2)}) collective-permute-start(bf16[3,256,128]{2,1,0:T(8,128)(2,1)S(1)} %collective-permute-done.1.refs_1_.refs_2_), channel_id=1, source_target_pairs={{0,16},{16,4},{4,20},{20,8},{8,24},{24,12},{12,28},{28,0},{1,17},{... | collective-permute-start | bytes 589832 | tf_op jit(solution)/shard_map/ppermute | solution.py:464
  14.2 11.0 %collective-permute-start.10 = (bf16[5,256,128]{2,1,0:T(8,128)(2,1)S(1)}, bf16[5,256,128]{2,1,0:T(8,128)(2,1)S(1)}, u32[]{:S(2)}, u32[]{:S(2)}) collective-permute-start(bf16[5,256,128]{2,1,0:T(8,128)(2,1)S(1)} %chunks_of.4.refs_0_), channel_id=1, source_target_pairs={{0,3},{1,0},{2,1},{3,2},{4,7},{5,4},{6,5},{7,6},{8,11},{9,8},{10,9... | collective-permute-start | bytes 983048 | tf_op jit(solution)/shard_map/ppermute | solution.py:463
  16.8 5.3 %collective-permute-start.5 = (bf16[3,256,128]{2,1,0:T(8,128)(2,1)S(1)}, bf16[3,256,128]{2,1,0:T(8,128)(2,1)S(1)}, u32[]{:S(2)}, u32[]{:S(2)}) collective-permute-start(bf16[3,256,128]{2,1,0:T(8,128)(2,1)S(1)} %collective-permute-done.2.refs_5_.refs_1_), channel_id=1, source_target_pairs={{0,28},{16,0},{4,16},{20,4},{8,20},{24,8},{12,24},{28,12},{1,29},{... | collective-permute-start | bytes 589832 | tf_op jit(solution)/shard_map/ppermute | solution.py:464
  20.0 5.7 %collective-permute-start.4 = (bf16[3,256,128]{2,1,0:T(8,128)(2,1)S(1)}, bf16[3,256,128]{2,1,0:T(8,128)(2,1)S(1)}, u32[]{:S(2)}, u32[]{:S(2)}) collective-permute-start(bf16[3,256,128]{2,1,0:T(8,128)(2,1)S(1)} %collective-permute-done.3.refs_0_), channel_id=1, source_target_pairs={{0,16},{16,4},{4,20},{20,8},{8,24},{24,12},{12,28},{28,0},{1,17},{... | collective-permute-start | bytes 589832 | tf_op jit(solution)/shard_map/ppermute | solution.py:464
  20.0 13.7 %collective-permute-start.9 = (bf16[5,256,128]{2,1,0:T(8,128)(2,1)S(1)}, bf16[5,256,128]{2,1,0:T(8,128)(2,1)S(1)}, u32[]{:S(2)}, u32[]{:S(2)}) collective-permute-start(bf16[5,256,128]{2,1,0:T(8,128)(2,1)S(1)} %chunks_of.4.refs_0_), channel_id=1, source_target_pairs={{0,1},{1,2},{2,3},{3,0},{4,5},{5,6},{6,7},{7,4},{8,9},{9,10},{10,1... | collective-permute-start | bytes 983048 | tf_op jit(solution)/shard_map/ppermute | solution.py:463
  21.3 11.8 %collective-permute-start.14 = (bf16[4,256,128]{2,1,0:T(8,128)(2,1)S(1)}, bf16[4,256,128]{2,1,0:T(8,128)(2,1)S(1)}, u32[]{:S(2)}, u32[]{:S(2)}) collective-permute-start(bf16[4,256,128]{2,1,0:T(8,128)(2,1)S(1)} %get-tuple-element.28), channel_id=1, source_target_pairs={{0,16},{16,0},{1,17},{17,1},{2,18},{18,2},{3,19},{19,3},{4,20},{20... | collective-permute-start | bytes 786440 | tf_op jit(solution)/shard_map/ppermute | solution.py:471
  22.0 9.5 %collective-permute-start.6 = (bf16[3,256,128]{2,1,0:T(8,128)(2,1)S(1)}, bf16[3,256,128]{2,1,0:T(8,128)(2,1)S(1)}, u32[]{:S(2)}, u32[]{:S(2)}) collective-permute-start(bf16[3,256,128]{2,1,0:T(8,128)(2,1)S(1)} %collective-permute-done.5.refs_3_), channel_id=1, source_target_pairs={{0,28},{16,0},{4,16},{20,4},{8,20},{24,8},{12,24},{28,12},{1,29},{... | collective-permute-start | bytes 589832 | tf_op jit(solution)/shard_map/ppermute | solution.py:464
  25.2 17.1 %collective-permute-start.15 = (bf16[5,256,128]{2,1,0:T(8,128)(2,1)S(1)}, bf16[5,256,128]{2,1,0:T(8,128)(2,1)S(1)}, u32[]{:S(2)}, u32[]{:S(2)}) collective-permute-start(bf16[5,256,128]{2,1,0:T(8,128)(2,1)S(1)} %get-tuple-element.29), channel_id=1, source_target_pairs={{0,16},{16,0},{1,17},{17,1},{2,18},{18,2},{3,19},{19,3},{4,20},{20... | collective-permute-start | bytes 983048 | tf_op jit(solution)/shard_map/ppermute | solution.py:471
  25.8 13.6 %collective-permute-start.13 = (bf16[3,256,128]{2,1,0:T(8,128)(2,1)S(1)}, bf16[3,256,128]{2,1,0:T(8,128)(2,1)S(1)}, u32[]{:S(2)}, u32[]{:S(2)}) collective-permute-start(bf16[3,256,128]{2,1,0:T(8,128)(2,1)S(1)} %collective-permute-done.4.refs_2_.refs_1_), channel_id=1, source_target_pairs={{0,16},{16,4},{4,20},{20,8},{8,24},{24,12},{12,28},{28,0},{1,17},{... | collective-permute-start | bytes 589832 | tf_op jit(solution)/shard_map/ppermute | solution.py:464
  31.6 15.8 %collective-permute-start.12 = (bf16[3,256,128]{2,1,0:T(8,128)(2,1)S(1)}, bf16[3,256,128]{2,1,0:T(8,128)(2,1)S(1)}, u32[]{:S(2)}, u32[]{:S(2)}) collective-permute-start(bf16[3,256,128]{2,1,0:T(8,128)(2,1)S(1)} %slice.21), channel_id=1, source_target_pairs={{0,3},{1,0},{2,1},{3,2},{4,7},{5,4},{6,5},{7,6},{8,11},{9,8},{10,9... | collective-permute-start | bytes 589832 | tf_op jit(solution)/shard_map/ppermute | solution.py:463
  33.0 17.5 %collective-permute-start.7 = (bf16[10,256,128]{2,1,0:T(8,128)(2,1)S(1)}, bf16[10,256,128]{2,1,0:T(8,128)(2,1)S(1)}, u32[]{:S(2)}, u32[]{:S(2)}) collective-permute-start(bf16[10,256,128]{2,1,0:T(8,128)(2,1)S(1)} %chunks_of.3.refs_5_), channel_id=1, source_target_pairs={{0,1},{1,2},{2,3},{3,0},{4,5},{5,6},{6,7},{7,4},{8,9},{9,10},{10,1... | collective-permute-start | bytes 1966088 | tf_op jit(solution)/shard_map/ppermute | solution.py:463
  33.7 16.8 %collective-permute-start.8 = (bf16[10,256,128]{2,1,0:T(8,128)(2,1)S(1)}, bf16[10,256,128]{2,1,0:T(8,128)(2,1)S(1)}, u32[]{:S(2)}, u32[]{:S(2)}) collective-permute-start(bf16[10,256,128]{2,1,0:T(8,128)(2,1)S(1)} %chunks_of.3.refs_5_), channel_id=1, source_target_pairs={{0,3},{1,0},{2,1},{3,2},{4,7},{5,4},{6,5},{7,6},{8,11},{9,8},{10,9... | collective-permute-start | bytes 1966088 | tf_op jit(solution)/shard_map/ppermute | solution.py:463
  39.3 7.7 %collective-permute-start.11 = (bf16[2,256,128]{2,1,0:T(8,128)(2,1)S(1)}, bf16[2,256,128]{2,1,0:T(8,128)(2,1)S(1)}, u32[]{:S(2)}, u32[]{:S(2)}) collective-permute-start(bf16[2,256,128]{2,1,0:T(8,128)(2,1)S(1)} %slice.20), channel_id=1, source_target_pairs={{0,1},{1,2},{2,3},{3,0},{4,5},{5,6},{6,7},{7,4},{8,9},{9,10},{10,1... | collective-permute-start | bytes 393224 | tf_op jit(solution)/shard_map/ppermute | solution.py:463
  42.3 11.8 %collective-permute-start.18 = (bf16[5,256,128]{2,1,0:T(8,128)(2,1)S(1)}, bf16[5,256,128]{2,1,0:T(8,128)(2,1)S(1)}, u32[]{:S(2)}, u32[]{:S(2)}) collective-permute-start(bf16[5,256,128]{2,1,0:T(8,128)(2,1)S(1)} %chunks_of.5.refs_6_), channel_id=1, source_target_pairs={{0,1},{1,2},{2,3},{3,0},{4,5},{5,6},{6,7},{7,4},{8,9},{9,10},{10,1... | collective-permute-start | bytes 983048 | tf_op jit(solution)/shard_map/ppermute | solution.py:463
  47.1 9.1 %collective-permute-start.19 = (bf16[5,256,128]{2,1,0:T(8,128)(2,1)S(1)}, bf16[5,256,128]{2,1,0:T(8,128)(2,1)S(1)}, u32[]{:S(2)}, u32[]{:S(2)}) collective-permute-start(bf16[5,256,128]{2,1,0:T(8,128)(2,1)S(1)} %chunks_of.5.refs_6_), channel_id=1, source_target_pairs={{0,3},{1,0},{2,1},{3,2},{4,7},{5,4},{6,5},{7,6},{8,11},{9,8},{10,9... | collective-permute-start | bytes 983048 | tf_op jit(solution)/shard_map/ppermute | solution.py:463
  56.1 13.4 %collective-permute-start.20 = (bf16[5,256,128]{2,1,0:T(8,128)(2,1)S(1)}, bf16[5,256,128]{2,1,0:T(8,128)(2,1)S(1)}, u32[]{:S(2)}, u32[]{:S(2)}) collective-permute-start(bf16[5,256,128]{2,1,0:T(8,128)(2,1)S(1)} %collective-permute-done.18.refs_2_), channel_id=1, source_target_pairs={{0,1},{1,2},{2,3},{3,0},{4,5},{5,6},{6,7},{7,4},{8,9},{9,10},{10,1... | collective-permute-start | bytes 983048 | tf_op jit(solution)/shard_map/ppermute | solution.py:463
  56.7 16.3 %collective-permute-start.16 = (bf16[5,256,128]{2,1,0:T(8,128)(2,1)S(1)}, bf16[5,256,128]{2,1,0:T(8,128)(2,1)S(1)}, u32[]{:S(2)}, u32[]{:S(2)}) collective-permute-start(bf16[5,256,128]{2,1,0:T(8,128)(2,1)S(1)} %slice.17), channel_id=1, source_target_pairs={{0,1},{1,2},{2,3},{3,0},{4,5},{5,6},{6,7},{7,4},{8,9},{9,10},{10,1... | collective-permute-start | bytes 983048 | tf_op jit(solution)/shard_map/ppermute | solution.py:463
  57.1 15.9 %collective-permute-start.17 = (bf16[5,256,128]{2,1,0:T(8,128)(2,1)S(1)}, bf16[5,256,128]{2,1,0:T(8,128)(2,1)S(1)}, u32[]{:S(2)}, u32[]{:S(2)}) collective-permute-start(bf16[5,256,128]{2,1,0:T(8,128)(2,1)S(1)} %slice.18), channel_id=1, source_target_pairs={{0,3},{1,0},{2,1},{3,2},{4,7},{5,4},{6,5},{7,6},{8,11},{9,8},{10,9... | collective-permute-start | bytes 983048 | tf_op jit(solution)/shard_map/ppermute | solution.py:463
  75.0 70.4 %all-to-all-start = ((f32[128,1,128]{2,1,0:T(1,128)}), f32[128,1,128]{2,1,0:T(1,128)S(1)}, u32[]{:S(2)}, u32[]{:S(2)}) async-start(f32[128,1,128]{2,1,0:T(1,128)} %bitcast.12), calls=%async_computation | async-start | bytes 131072 | tf_op jit(solution)/shard_map/all_to_all | solution.py:530
  (7 other events, 48.7 us)

commit v11 on v10

--- a/solution.py
+++ b/solution.py
@@ -480,8 +480,7 @@
     mine = chunks_of(place, ring, (0,))
     near_a = along_x(mine, 1)
     near_b = along_x(mine, -1)
-    near_c = along_x(near_a[:OTHER], 1)
-    near_d = along_x(near_b[OTHER:], -1)
+    near_c = along_x(near_a, 1)
     for step in range(2, 5):
         ring[step] = along_z(ring[step - 1], 1)
         if step < 4:
@@ -497,7 +496,7 @@
         place,
         table,
         plan_of([(0, 0), (0, -1), (0, 1), (0, 2), (1, 0), (3, 0), (2, 0)]),
-        [mine, near_a, near_b, near_c, near_d, rest_13, rest_2],
+        [mine, near_a, near_b, near_c, rest_13, rest_2],
         rows,
         queries=(*pieces, more),
     )

time: 146 us -> 132 us (0.904)
  starting transfers between devices: 91.5 us -> 70.4 us
  waiting for transfers between devices: 37.3 us -> 44.6 us
    all_to_all x1, starting transfers between devices: 58.6 us -> 44.3 us  [program(): terms = lax.all_to_all(sums, everyone, 0, 0, tiled=True)]
    ppermute x11 -> x10, waiting for transfers between devices: 15.9 us -> 22.4 us  [program(): along_x = lambda a, by: lax.ppermute(a, 'kv_1', shift(4, by))]
    ppermute x11 -> x10, starting transfers between devices: 19.2 us -> 14.2 us  [program(): along_x = lambda a, by: lax.ppermute(a, 'kv_1', shift(4, by))]
    ppermute x2, waiting for transfers between devices: 0.01 us -> 4.73 us  [program(): pieces = [lax.ppermute(piece, 'head', other_side) for piece in chosen[:-1]]]
    ppermute x7, waiting for transfers between devices: 10.2 us -> 6.25 us  [program(): along_z = lambda a, by: lax.ppermute(a, ('head', 'kv_0'), z_shift(by))]
  transfers between devices with their start and end apart: 21 -> 20, of which waited for: 12 -> 13; matrix products, arithmetic and copies ran while one was open for 1% -> 1% of each run, Pallas kernels for 6% -> 7%
where the time goes in v11:
time: 132 us
  starting transfers between devices  70.4 us (53%)
  waiting for transfers between devices  44.6 us (34%)
  Pallas kernels  10.7 us (8%)
  local copies, waits for them, and re-layouts  4.28 us (3%)
  between operations  1.43 us (1%)
    all_to_all x1, starting transfers between devices, program(): terms = lax.all_to_all(sums, everyone, 0, 0, tiled=True)  44.3 us
    ppermute x10, waiting for transfers between devices, program(): along_x = lambda a, by: lax.ppermute(a, 'kv_1', shift(4, by))  22.4 us
    ppermute x10, starting transfers between devices, program(): along_x = lambda a, by: lax.ppermute(a, 'kv_1', shift(4, by))  14.2 us
    ppermute x7, starting transfers between devices, program(): along_z = lambda a, by: lax.ppermute(a, ('head', 'kv_0'), z_shift(by))  11.9 us
    all_to_all x1, waiting for transfers between devices, program(): terms = lax.all_to_all(sums, everyone, 0, 0, tiled=True)  11.2 us
    ppermute x7, waiting for transfers between devices, program(): along_z = lambda a, by: lax.ppermute(a, ('head', 'kv_0'), z_shift(by))  6.25 us
    pallas_call x3, Pallas kernels, attend(): pl.pallas_call(functools.partial(attend_kernel, first, last, counts, bloc...  5.82 us
    ppermute x2, waiting for transfers between devices, program(): pieces = [lax.ppermute(piece, 'head', other_side) for piece in chosen[:-1]]  4.73 us
  transfers between devices with their start and end apart: 20, of which 13 were waited for; matrix products, arithmetic and copies ran while one was open for 1% of the time, Pallas kernels for 7%

profile of v11, /device:TPU:1, one launch (start us, length us, event | category | flops | bytes accessed | tf_op | source)
XLA Modules:
  0.0 132.2 jit_solution(7485599405991401167)
XLA Ops:
  2.5 2.5 %collective-permute-start.1 = (bf16[3,256,128]{2,1,0:T(8,128)(2,1)S(1)}, bf16[3,256,128]{2,1,0:T(8,128)(2,1)S(1)}, u32[]{:S(2)}, u32[]{:S(2)}) collective-permute-start(bf16[3,256,128]{2,1,0:T(8,128)(2,1)S(1)} %split_heads.1.refs_0_), channel_id=1, source_target_pairs={{0,16},{16,4},{4,20},{20,8},{8,24},{24,12},{12,28},{28,0},{1,17},{... | collective-permute-start | bytes 589832 | tf_op jit(solution)/shard_map/ppermute | solution.py:464
  5.1 4.0 %collective-permute-start.2 = (bf16[3,256,128]{2,1,0:T(8,128)(2,1)S(1)}, bf16[3,256,128]{2,1,0:T(8,128)(2,1)S(1)}, u32[]{:S(2)}, u32[]{:S(2)}) collective-permute-start(bf16[3,256,128]{2,1,0:T(8,128)(2,1)S(1)} %split_heads.1.refs_0_), channel_id=1, source_target_pairs={{0,28},{16,0},{4,16},{20,4},{8,20},{24,8},{12,24},{28,12},{1,29},{... | collective-permute-start | bytes 589832 | tf_op jit(solution)/shard_map/ppermute | solution.py:464
  11.0 1.7 %queries_for_other.1 = (bf16[4,256,128]{2,1,0:T(8,128)(2,1)S(1)}, bf16[5,256,128]{2,1,0:T(8,128)(2,1)S(1)}, bf16[5,256,128]{2,1,0:T(8,128)(2,1)S(1)}, s32[1,1]{1,0:T(1,128)}) custom-call(s32[1,3]{1,0:T(1,128)S(1)} %add_bitcast_fusion.place, s32[2,14]{1,0:T(2,128)S(1)} %bitcast.21, bf16[256,1792]{1,0:T(8,128)(2,1)S(1)} %bitcast.15), custom_call_target="tpu_custom_call" | custom-call | tf_op jit(solution)/shard_map/queries_for_other/pallas_call | solution.py:108
  13.6 2.7 %collective-permute-start.5 = (bf16[3,256,128]{2,1,0:T(8,128)(2,1)S(1)}, bf16[3,256,128]{2,1,0:T(8,128)(2,1)S(1)}, u32[]{:S(2)}, u32[]{:S(2)}) collective-permute-start(bf16[3,256,128]{2,1,0:T(8,128)(2,1)S(1)} %collective-permute-done.2.refs_5_.refs_1_), channel_id=1, source_target_pairs={{0,28},{16,0},{4,16},{20,4},{8,20},{24,8},{12,24},{28,12},{1,29},{... | collective-permute-start | bytes 589832 | tf_op jit(solution)/shard_map/ppermute | solution.py:464
  16.9 1.3 collective-permute-start.9
  18.2 1.9 %collective-permute-done.3.refs_0_ = bf16[3,256,128]{2,1,0:T(8,128)(2,1)S(1)} collective-permute-done((bf16[3,256,128]{2,1,0:T(8,128)(2,1)S(1)}, bf16[3,256,128]{2,1,0:T(8,128)(2,1)S(1)}, u32[]{:S(2)}, u32[]{:S(2)}) %collective-permute-start.3) | collective-permute-done | bytes 196640 | tf_op jit(solution)/shard_map/ppermute | solution.py:464
  20.0 2.7 %collective-permute-start.6 = (bf16[3,256,128]{2,1,0:T(8,128)(2,1)S(1)}, bf16[3,256,128]{2,1,0:T(8,128)(2,1)S(1)}, u32[]{:S(2)}, u32[]{:S(2)}) collective-permute-start(bf16[3,256,128]{2,1,0:T(8,128)(2,1)S(1)} %collective-permute-done.5.refs_3_), channel_id=1, source_target_pairs={{0,28},{16,0},{4,16},{20,4},{8,20},{24,8},{12,24},{28,12},{1,29},{... | collective-permute-start | bytes 589832 | tf_op jit(solution)/shard_map/ppermute | solution.py:464
  22.7 3.3 %collective-permute-done.4.refs_2_.refs_1_ = bf16[3,256,128]{2,1,0:T(8,128)(2,1)S(1)} collective-permute-done((bf16[3,256,128]{2,1,0:T(8,128)(2,1)S(1)}, bf16[3,256,128]{2,1,0:T(8,128)(2,1)S(1)}, u32[]{:S(2)}, u32[]{:S(2)}) %collective-permute-start.4) | collective-permute-done | bytes 196640 | tf_op jit(solution)/shard_map/ppermute | solution.py:464
  26.1 2.3 %collective-permute-start.10 = (bf16[5,256,128]{2,1,0:T(8,128)(2,1)S(1)}, bf16[5,256,128]{2,1,0:T(8,128)(2,1)S(1)}, u32[]{:S(2)}, u32[]{:S(2)}) collective-permute-start(bf16[5,256,128]{2,1,0:T(8,128)(2,1)S(1)} %chunks_of.4.refs_0_), channel_id=1, source_target_pairs={{0,3},{1,0},{2,1},{3,2},{4,7},{5,4},{6,5},{7,6},{8,11},{9,8},{10,9... | collective-permute-start | bytes 983048 | tf_op jit(solution)/shard_map/ppermute | solution.py:463
  29.0 2.1 %collective-permute-done.13.refs_6_ = bf16[4,256,128]{2,1,0:T(8,128)(2,1)S(1)} collective-permute-done((bf16[4,256,128]{2,1,0:T(8,128)(2,1)S(1)}, bf16[4,256,128]{2,1,0:T(8,128)(2,1)S(1)}, u32[]{:S(2)}, u32[]{:S(2)}) %collective-permute-start.13) | collective-permute-done | bytes 262176 | tf_op jit(solution)/shard_map/ppermute | solution.py:471
  33.1 2.5 %collective-permute-start.8 = (bf16[10,256,128]{2,1,0:T(8,128)(2,1)S(1)}, bf16[10,256,128]{2,1,0:T(8,128)(2,1)S(1)}, u32[]{:S(2)}, u32[]{:S(2)}) collective-permute-start(bf16[10,256,128]{2,1,0:T(8,128)(2,1)S(1)} %chunks_of.3.refs_4_), channel_id=1, source_target_pairs={{0,3},{1,0},{2,1},{3,2},{4,7},{5,4},{6,5},{7,6},{8,11},{9,8},{10,9... | collective-permute-start | bytes 1966088 | tf_op jit(solution)/shard_map/ppermute | solution.py:463
  37.4 2.6 %collective-permute-done.14.refs_7_ = bf16[5,256,128]{2,1,0:T(8,128)(2,1)S(1)} collective-permute-done((bf16[5,256,128]{2,1,0:T(8,128)(2,1)S(1)}, bf16[5,256,128]{2,1,0:T(8,128)(2,1)S(1)}, u32[]{:S(2)}, u32[]{:S(2)}) %collective-permute-start.14) | collective-permute-done | bytes 327712 | tf_op jit(solution)/shard_map/ppermute | solution.py:471
  41.3 1.5 %collective-permute-start.18 = (bf16[5,256,128]{2,1,0:T(8,128)(2,1)S(1)}, bf16[5,256,128]{2,1,0:T(8,128)(2,1)S(1)}, u32[]{:S(2)}, u32[]{:S(2)}) collective-permute-start(bf16[5,256,128]{2,1,0:T(8,128)(2,1)S(1)} %chunks_of.5.refs_5_), channel_id=1, source_target_pairs={{0,3},{1,0},{2,1},{3,2},{4,7},{5,4},{6,5},{7,6},{8,11},{9,8},{10,9... | collective-permute-start | bytes 983048 | tf_op jit(solution)/shard_map/ppermute | solution.py:463
  42.8 3.2 %attend.3 = (f32[56,8,256]{2,1,0:T(8,128)S(1)}, bf16[21,256,256]{2,1,0:T(8,128)(2,1)S(1)}) custom-call(s32[1,3]{1,0:T(1,128)S(1)} %add_bitcast_fusion.place, s32[2,14]{1,0:T(2,128)S(1)} %bitcast.23, s32[2,7]{1,0:T(2,128)S(1)} %copy-done.9, bf16[5,256,128]{2,1,0:T(8,128)(2,1)S(1)} %chunks_of.4.refs_0_, ...), custom_call_target="tpu_custom_call", output_to_operand_aliasing={{1}: (12, {})} | custom-call | flops 4932501504 | bytes 2293760 | tf_op jit(solution)/shard_map/attend/pallas_call | solution.py:424
  46.9 3.2 %collective-permute-done.8.refs_1_ = bf16[10,256,128]{2,1,0:T(8,128)(2,1)S(1)} collective-permute-done((bf16[10,256,128]{2,1,0:T(8,128)(2,1)S(1)}, bf16[10,256,128]{2,1,0:T(8,128)(2,1)S(1)}, u32[]{:S(2)}, u32[]{:S(2)}) %collective-permute-start.8) | collective-permute-done | bytes 655392 | tf_op jit(solution)/shard_map/ppermute | solution.py:463
  50.1 3.9 %collective-permute-done.17.refs_2_ = bf16[5,256,128]{2,1,0:T(8,128)(2,1)S(1)} collective-permute-done((bf16[5,256,128]{2,1,0:T(8,128)(2,1)S(1)}, bf16[5,256,128]{2,1,0:T(8,128)(2,1)S(1)}, u32[]{:S(2)}, u32[]{:S(2)}) %collective-permute-start.17) | collective-permute-done | bytes 327712 | tf_op jit(solution)/shard_map/ppermute | solution.py:463
  53.9 3.2 %collective-permute-done.18.refs_3_ = bf16[5,256,128]{2,1,0:T(8,128)(2,1)S(1)} collective-permute-done((bf16[5,256,128]{2,1,0:T(8,128)(2,1)S(1)}, bf16[5,256,128]{2,1,0:T(8,128)(2,1)S(1)}, u32[]{:S(2)}, u32[]{:S(2)}) %collective-permute-start.18) | collective-permute-done | bytes 327712 | tf_op jit(solution)/shard_map/ppermute | solution.py:463
  58.1 1.3 collective-permute-start.15
  59.4 2.1 %collective-permute-start.16 = (bf16[5,256,128]{2,1,0:T(8,128)(2,1)S(1)}, bf16[5,256,128]{2,1,0:T(8,128)(2,1)S(1)}, u32[]{:S(2)}, u32[]{:S(2)}) collective-permute-start(bf16[5,256,128]{2,1,0:T(8,128)(2,1)S(1)} %slice.10), channel_id=1, source_target_pairs={{0,3},{1,0},{2,1},{3,2},{4,7},{5,4},{6,5},{7,6},{8,11},{9,8},{10,9... | collective-permute-start | bytes 983048 | tf_op jit(solution)/shard_map/ppermute | solution.py:463
  62.4 4.3 %collective-permute-done.19.refs_2_ = bf16[5,256,128]{2,1,0:T(8,128)(2,1)S(1)} collective-permute-done((bf16[5,256,128]{2,1,0:T(8,128)(2,1)S(1)}, bf16[5,256,128]{2,1,0:T(8,128)(2,1)S(1)}, u32[]{:S(2)}, u32[]{:S(2)}) %collective-permute-start.19) | collective-permute-done | bytes 327712 | tf_op jit(solution)/shard_map/ppermute | solution.py:463
  66.6 7.0 %collective-permute-done.15.refs_0_ = bf16[5,256,128]{2,1,0:T(8,128)(2,1)S(1)} collective-permute-done((bf16[5,256,128]{2,1,0:T(8,128)(2,1)S(1)}, bf16[5,256,128]{2,1,0:T(8,128)(2,1)S(1)}, u32[]{:S(2)}, u32[]{:S(2)}) %collective-permute-start.15) | collective-permute-done | bytes 327712 | tf_op jit(solution)/shard_map/ppermute | solution.py:463
  73.7 1.7 %attend.5 = (f32[7,256]{1,0:T(8,128)S(1)}, f32[128,128]{1,0:T(8,128)}) custom-call(s32[1,3]{1,0:T(1,128)S(1)} %add_bitcast_fusion.place, s32[2,14]{1,0:T(2,128)S(1)} %bitcast.25, s32[2,3]{1,0:T(2,128)S(1)} %copy-done.7, bf16[5,256,128]{2,1,0:T(8,128)(2,1)S(1)} %collective-permute-done.15.refs_0_, bf16[5,256,128]{2,1,0:T(8,128)(2,1)S(1)} %collective-permute-done.16.refs_1_, ...), custom_call_target="tpu_custom_call" | custom-call | flops 2113929216 | bytes 983040 | tf_op jit(solution)/shard_map/attend/pallas_call | solution.py:424
  75.4 44.3 %all-to-all-start = ((f32[128,1,128]{2,1,0:T(1,128)}), f32[128,1,128]{2,1,0:T(1,128)S(1)}, u32[]{:S(2)}, u32[]{:S(2)}) async-start(f32[128,1,128]{2,1,0:T(1,128)} %bitcast.12), calls=%async_computation | async-start | bytes 131072 | tf_op jit(solution)/shard_map/all_to_all | solution.py:529
  120.3 11.2 %all-to-all-done = f32[128,1,128]{2,1,0:T(1,128)S(1)} async-done(((f32[128,1,128]{2,1,0:T(1,128)}), f32[128,1,128]{2,1,0:T(1,128)S(1)}, u32[]{:S(2)}, u32[]{:S(2)}) %all-to-all-start) | async-done | bytes 65568 | tf_op jit(solution)/shard_map/all_to_all | solution.py:529
  (52 shorter events, 14.4 us)
Async XLA Ops:
  0.6 34.9 %copy-start.6 = (s32[14,2]{0,1:T(2,128)S(1)}, s32[14,2]{0,1:T(2,128)}, u32[]{:S(2)}) copy-start(s32[14,2]{0,1:T(2,128)} %param.14) | copy-start | bytes 340
  2.5 11.1 %collective-permute-start.1 = (bf16[3,256,128]{2,1,0:T(8,128)(2,1)S(1)}, bf16[3,256,128]{2,1,0:T(8,128)(2,1)S(1)}, u32[]{:S(2)}, u32[]{:S(2)}) collective-permute-start(bf16[3,256,128]{2,1,0:T(8,128)(2,1)S(1)} %split_heads.1.refs_0_), channel_id=1, source_target_pairs={{0,16},{16,4},{4,20},{20,8},{8,24},{24,12},{12,28},{28,0},{1,17},{... | collective-permute-start | bytes 589832 | tf_op jit(solution)/shard_map/ppermute | solution.py:464
  5.1 8.5 %collective-permute-start.2 = (bf16[3,256,128]{2,1,0:T(8,128)(2,1)S(1)}, bf16[3,256,128]{2,1,0:T(8,128)(2,1)S(1)}, u32[]{:S(2)}, u32[]{:S(2)}) collective-permute-start(bf16[3,256,128]{2,1,0:T(8,128)(2,1)S(1)} %split_heads.1.refs_0_), channel_id=1, source_target_pairs={{0,28},{16,0},{4,16},{20,4},{8,20},{24,8},{12,24},{28,12},{1,29},{... | collective-permute-start | bytes 589832 | tf_op jit(solution)/shard_map/ppermute | solution.py:464
  11.0 24.5 %copy-start.1 = (bf16[1,256,1792]{2,1,0:T(8,128)(2,1)S(1)}, bf16[1,256,1792]{2,1,0:T(8,128)(2,1)}, u32[]{:S(2)}) copy-start(bf16[1,256,1792]{2,1,0:T(8,128)(2,1)} %param.10) | copy-start | bytes 2752516
  11.0 24.5 %copy-start.2 = (bf16[1,256,896]{2,1,0:T(8,128)(2,1)S(1)}, bf16[1,256,896]{2,1,0:T(8,128)(2,1)}, u32[]{:S(2)}) copy-start(bf16[1,256,896]{2,1,0:T(8,128)(2,1)} %param.12) | copy-start | bytes 1376260
  13.6 6.4 %collective-permute-start.3 = (bf16[3,256,128]{2,1,0:T(8,128)(2,1)S(1)}, bf16[3,256,128]{2,1,0:T(8,128)(2,1)S(1)}, u32[]{:S(2)}, u32[]{:S(2)}) collective-permute-start(bf16[3,256,128]{2,1,0:T(8,128)(2,1)S(1)} %collective-permute-done.1.refs_1_.refs_2_), channel_id=1, source_target_pairs={{0,16},{16,4},{4,20},{20,8},{8,24},{24,12},{12,28},{28,0},{1,17},{... | collective-permute-start | bytes 589832 | tf_op jit(solution)/shard_map/ppermute | solution.py:464
  13.6 6.4 %collective-permute-start.5 = (bf16[3,256,128]{2,1,0:T(8,128)(2,1)S(1)}, bf16[3,256,128]{2,1,0:T(8,128)(2,1)S(1)}, u32[]{:S(2)}, u32[]{:S(2)}) collective-permute-start(bf16[3,256,128]{2,1,0:T(8,128)(2,1)S(1)} %collective-permute-done.2.refs_5_.refs_1_), channel_id=1, source_target_pairs={{0,28},{16,0},{4,16},{20,4},{8,20},{24,8},{12,24},{28,12},{1,29},{... | collective-permute-start | bytes 589832 | tf_op jit(solution)/shard_map/ppermute | solution.py:464
  16.9 9.2 %collective-permute-start.9 = (bf16[5,256,128]{2,1,0:T(8,128)(2,1)S(1)}, bf16[5,256,128]{2,1,0:T(8,128)(2,1)S(1)}, u32[]{:S(2)}, u32[]{:S(2)}) collective-permute-start(bf16[5,256,128]{2,1,0:T(8,128)(2,1)S(1)} %chunks_of.4.refs_0_), channel_id=1, source_target_pairs={{0,1},{1,2},{2,3},{3,0},{4,5},{5,6},{6,7},{7,4},{8,9},{9,10},{10,1... | collective-permute-start | bytes 983048 | tf_op jit(solution)/shard_map/ppermute | solution.py:463
  20.0 6.0 %collective-permute-start.4 = (bf16[3,256,128]{2,1,0:T(8,128)(2,1)S(1)}, bf16[3,256,128]{2,1,0:T(8,128)(2,1)S(1)}, u32[]{:S(2)}, u32[]{:S(2)}) collective-permute-start(bf16[3,256,128]{2,1,0:T(8,128)(2,1)S(1)} %collective-permute-done.3.refs_0_), channel_id=1, source_target_pairs={{0,16},{16,4},{4,20},{20,8},{8,24},{24,12},{12,28},{28,0},{1,17},{... | collective-permute-start | bytes 589832 | tf_op jit(solution)/shard_map/ppermute | solution.py:464
  20.0 8.3 %collective-permute-start.6 = (bf16[3,256,128]{2,1,0:T(8,128)(2,1)S(1)}, bf16[3,256,128]{2,1,0:T(8,128)(2,1)S(1)}, u32[]{:S(2)}, u32[]{:S(2)}) collective-permute-start(bf16[3,256,128]{2,1,0:T(8,128)(2,1)S(1)} %collective-permute-done.5.refs_3_), channel_id=1, source_target_pairs={{0,28},{16,0},{4,16},{20,4},{8,20},{24,8},{12,24},{28,12},{1,29},{... | collective-permute-start | bytes 589832 | tf_op jit(solution)/shard_map/ppermute | solution.py:464
  22.7 8.3 %collective-permute-start.13 = (bf16[4,256,128]{2,1,0:T(8,128)(2,1)S(1)}, bf16[4,256,128]{2,1,0:T(8,128)(2,1)S(1)}, u32[]{:S(2)}, u32[]{:S(2)}) collective-permute-start(bf16[4,256,128]{2,1,0:T(8,128)(2,1)S(1)} %get-tuple-element.28), channel_id=1, source_target_pairs={{0,16},{16,0},{1,17},{17,1},{2,18},{18,2},{3,19},{19,3},{4,20},{20... | collective-permute-start | bytes 786440 | tf_op jit(solution)/shard_map/ppermute | solution.py:471
  26.1 7.0 %collective-permute-start.12 = (bf16[3,256,128]{2,1,0:T(8,128)(2,1)S(1)}, bf16[3,256,128]{2,1,0:T(8,128)(2,1)S(1)}, u32[]{:S(2)}, u32[]{:S(2)}) collective-permute-start(bf16[3,256,128]{2,1,0:T(8,128)(2,1)S(1)} %collective-permute-done.4.refs_2_.refs_1_), channel_id=1, source_target_pairs={{0,16},{16,4},{4,20},{20,8},{8,24},{24,12},{12,28},{28,0},{1,17},{... | collective-permute-start | bytes 589832 | tf_op jit(solution)/shard_map/ppermute | solution.py:464
  26.1 14.0 %collective-permute-start.14 = (bf16[5,256,128]{2,1,0:T(8,128)(2,1)S(1)}, bf16[5,256,128]{2,1,0:T(8,128)(2,1)S(1)}, u32[]{:S(2)}, u32[]{:S(2)}) collective-permute-start(bf16[5,256,128]{2,1,0:T(8,128)(2,1)S(1)} %get-tuple-element.29), channel_id=1, source_target_pairs={{0,16},{16,0},{1,17},{17,1},{2,18},{18,2},{3,19},{19,3},{4,20},{20... | collective-permute-start | bytes 983048 | tf_op jit(solution)/shard_map/ppermute | solution.py:471
  26.1 15.2 %collective-permute-start.10 = (bf16[5,256,128]{2,1,0:T(8,128)(2,1)S(1)}, bf16[5,256,128]{2,1,0:T(8,128)(2,1)S(1)}, u32[]{:S(2)}, u32[]{:S(2)}) collective-permute-start(bf16[5,256,128]{2,1,0:T(8,128)(2,1)S(1)} %chunks_of.4.refs_0_), channel_id=1, source_target_pairs={{0,3},{1,0},{2,1},{3,2},{4,7},{5,4},{6,5},{7,6},{8,11},{9,8},{10,9... | collective-permute-start | bytes 983048 | tf_op jit(solution)/shard_map/ppermute | solution.py:463
  28.3 14.4 %collective-permute-start.11 = (bf16[5,256,128]{2,1,0:T(8,128)(2,1)S(1)}, bf16[5,256,128]{2,1,0:T(8,128)(2,1)S(1)}, u32[]{:S(2)}, u32[]{:S(2)}) collective-permute-start(bf16[5,256,128]{2,1,0:T(8,128)(2,1)S(1)} %collective-permute-done.9.refs_1_), channel_id=1, source_target_pairs={{0,1},{1,2},{2,3},{3,0},{4,5},{5,6},{6,7},{7,4},{8,9},{9,10},{10,1... | collective-permute-start | bytes 983048 | tf_op jit(solution)/shard_map/ppermute | solution.py:463
  31.0 15.9 %collective-permute-start.7 = (bf16[10,256,128]{2,1,0:T(8,128)(2,1)S(1)}, bf16[10,256,128]{2,1,0:T(8,128)(2,1)S(1)}, u32[]{:S(2)}, u32[]{:S(2)}) collective-permute-start(bf16[10,256,128]{2,1,0:T(8,128)(2,1)S(1)} %chunks_of.3.refs_4_), channel_id=1, source_target_pairs={{0,1},{1,2},{2,3},{3,0},{4,5},{5,6},{6,7},{7,4},{8,9},{9,10},{10,1... | collective-permute-start | bytes 1966088 | tf_op jit(solution)/shard_map/ppermute | solution.py:463
  33.1 17.0 %collective-permute-start.8 = (bf16[10,256,128]{2,1,0:T(8,128)(2,1)S(1)}, bf16[10,256,128]{2,1,0:T(8,128)(2,1)S(1)}, u32[]{:S(2)}, u32[]{:S(2)}) collective-permute-start(bf16[10,256,128]{2,1,0:T(8,128)(2,1)S(1)} %chunks_of.3.refs_4_), channel_id=1, source_target_pairs={{0,3},{1,0},{2,1},{3,2},{4,7},{5,4},{6,5},{7,6},{8,11},{9,8},{10,9... | collective-permute-start | bytes 1966088 | tf_op jit(solution)/shard_map/ppermute | solution.py:463
  37.4 24.0 %copy-start.8 = (s32[2,6]{1,0:T(2,128)S(1)}, s32[2,6]{1,0:T(2,128)}, u32[]{:S(2)}) copy-start(s32[2,6]{1,0:T(2,128)} %constant.28.clone.plan) | copy-start | bytes 148
  40.1 13.9 %collective-permute-start.17 = (bf16[5,256,128]{2,1,0:T(8,128)(2,1)S(1)}, bf16[5,256,128]{2,1,0:T(8,128)(2,1)S(1)}, u32[]{:S(2)}, u32[]{:S(2)}) collective-permute-start(bf16[5,256,128]{2,1,0:T(8,128)(2,1)S(1)} %chunks_of.5.refs_5_), channel_id=1, source_target_pairs={{0,1},{1,2},{2,3},{3,0},{4,5},{5,6},{6,7},{7,4},{8,9},{9,10},{10,1... | collective-permute-start | bytes 983048 | tf_op jit(solution)/shard_map/ppermute | solution.py:463
  41.3 15.8 %collective-permute-start.18 = (bf16[5,256,128]{2,1,0:T(8,128)(2,1)S(1)}, bf16[5,256,128]{2,1,0:T(8,128)(2,1)S(1)}, u32[]{:S(2)}, u32[]{:S(2)}) collective-permute-start(bf16[5,256,128]{2,1,0:T(8,128)(2,1)S(1)} %chunks_of.5.refs_5_), channel_id=1, source_target_pairs={{0,3},{1,0},{2,1},{3,2},{4,7},{5,4},{6,5},{7,6},{8,11},{9,8},{10,9... | collective-permute-start | bytes 983048 | tf_op jit(solution)/shard_map/ppermute | solution.py:463
  57.1 9.5 %collective-permute-start.19 = (bf16[5,256,128]{2,1,0:T(8,128)(2,1)S(1)}, bf16[5,256,128]{2,1,0:T(8,128)(2,1)S(1)}, u32[]{:S(2)}, u32[]{:S(2)}) collective-permute-start(bf16[5,256,128]{2,1,0:T(8,128)(2,1)S(1)} %collective-permute-done.17.refs_2_), channel_id=1, source_target_pairs={{0,1},{1,2},{2,3},{3,0},{4,5},{5,6},{6,7},{7,4},{8,9},{9,10},{10,1... | collective-permute-start | bytes 983048 | tf_op jit(solution)/shard_map/ppermute | solution.py:463
  58.1 15.6 %collective-permute-start.15 = (bf16[5,256,128]{2,1,0:T(8,128)(2,1)S(1)}, bf16[5,256,128]{2,1,0:T(8,128)(2,1)S(1)}, u32[]{:S(2)}, u32[]{:S(2)}) collective-permute-start(bf16[5,256,128]{2,1,0:T(8,128)(2,1)S(1)} %slice.9), channel_id=1, source_target_pairs={{0,1},{1,2},{2,3},{3,0},{4,5},{5,6},{6,7},{7,4},{8,9},{9,10},{10,1... | collective-permute-start | bytes 983048 | tf_op jit(solution)/shard_map/ppermute | solution.py:463
  59.4 14.3 %collective-permute-start.16 = (bf16[5,256,128]{2,1,0:T(8,128)(2,1)S(1)}, bf16[5,256,128]{2,1,0:T(8,128)(2,1)S(1)}, u32[]{:S(2)}, u32[]{:S(2)}) collective-permute-start(bf16[5,256,128]{2,1,0:T(8,128)(2,1)S(1)} %slice.10), channel_id=1, source_target_pairs={{0,3},{1,0},{2,1},{3,2},{4,7},{5,4},{6,5},{7,6},{8,11},{9,8},{10,9... | collective-permute-start | bytes 983048 | tf_op jit(solution)/shard_map/ppermute | solution.py:463
  75.4 56.1 %all-to-all-start = ((f32[128,1,128]{2,1,0:T(1,128)}), f32[128,1,128]{2,1,0:T(1,128)S(1)}, u32[]{:S(2)}, u32[]{:S(2)}) async-start(f32[128,1,128]{2,1,0:T(1,128)} %bitcast.12), calls=%async_computation | async-start | bytes 131072 | tf_op jit(solution)/shard_map/all_to_all | solution.py:529
  (6 other events, 29.6 us)

commit v12 on v10

--- a/solution.py
+++ b/solution.py
@@ -496,8 +496,8 @@
     state, rows = attend(
         place,
         table,
-        plan_of([(0, 0), (0, -1), (0, 1), (0, 2), (1, 0), (3, 0), (2, 0)]),
-        [mine, near_a, near_b, near_c, near_d, rest_13, rest_2],
+        plan_of([(0, 0), (0, -1), (0, 1), (0, 2), (1, 0), (3, 0)]),
+        [mine, near_a, near_b, near_c, near_d, rest_13],
         rows,
         queries=(*pieces, more),
     )
@@ -511,8 +511,8 @@
     state = attend(
         place,
         table,
-        plan_of([(1, -1), (3, -1), (1, 1), (3, 1), (2, -1), (2, 1)]),
-        [left_13, right_13, left_2, right_2],
+        plan_of([(1, -1), (3, -1), (1, 1), (3, 1), (2, -1), (2, 1), (2, 0)]),
+        [left_13, right_13, left_2, right_2, rest_2],
         rows,
         state=state,
     )

time: 146 us -> 145 us (level)
  waiting for transfers between devices: 37.3 us -> 34.5 us
    ppermute x11, starting transfers between devices: 19.2 us -> 24.6 us  [program(): along_x = lambda a, by: lax.ppermute(a, 'kv_1', shift(4, by))]
    all_to_all x1, starting transfers between devices: 58.6 us -> 54.8 us  [program(): terms = lax.all_to_all(sums, everyone, 0, 0, tiled=True)]
    ppermute x7, waiting for transfers between devices: 10.2 us -> 6.52 us  [program(): along_z = lambda a, by: lax.ppermute(a, ('head', 'kv_0'), z_shift(by))]
    ppermute x2, waiting for transfers between devices: 0.01 us -> 2.65 us  [program(): pieces = [lax.ppermute(piece, 'head', other_side) for piece in chosen[:-1]]]
    ppermute x11, waiting for transfers between devices: 15.9 us -> 14.1 us  [program(): along_x = lambda a, by: lax.ppermute(a, 'kv_1', shift(4, by))]
  transfers between devices with their start and end apart: 21 -> 21, of which waited for: 12 -> 11; matrix products, arithmetic and copies ran while one was open for 1% -> 1% of each run, Pallas kernels for 6% -> 6%
where the time goes in v12:
time: 145 us
  starting transfers between devices  92.8 us (64%)
  waiting for transfers between devices  34.5 us (24%)
  Pallas kernels  10.7 us (7%)
  local copies, waits for them, and re-layouts  4.3 us (3%)
  between operations  1.46 us (1%)
    all_to_all x1, starting transfers between devices, program(): terms = lax.all_to_all(sums, everyone, 0, 0, tiled=True)  54.8 us
    ppermute x11, starting transfers between devices, program(): along_x = lambda a, by: lax.ppermute(a, 'kv_1', shift(4, by))  24.6 us
    ppermute x11, waiting for transfers between devices, program(): along_x = lambda a, by: lax.ppermute(a, 'kv_1', shift(4, by))  14.1 us
    ppermute x7, starting transfers between devices, program(): along_z = lambda a, by: lax.ppermute(a, ('head', 'kv_0'), z_shift(by))  13.4 us
    all_to_all x1, waiting for transfers between devices, program(): terms = lax.all_to_all(sums, everyone, 0, 0, tiled=True)  11.3 us
    ppermute x7, waiting for transfers between devices, program(): along_z = lambda a, by: lax.ppermute(a, ('head', 'kv_0'), z_shift(by))  6.52 us
    pallas_call x3, Pallas kernels, attend(): pl.pallas_call(functools.partial(attend_kernel, first, last, counts, bloc...  6.04 us
    unnamed x21, local copies, waits for them, and re-layouts  4.23 us
  transfers between devices with their start and end apart: 21, of which 11 were waited for; matrix products, arithmetic and copies ran while one was open for 1% of the time, Pallas kernels for 6%

profile of v12, /device:TPU:1, one launch (start us, length us, event | category | flops | bytes accessed | tf_op | source)
XLA Modules:
  0.0 144.6 jit_solution(10185448387429519170)
XLA Ops:
  2.5 2.5 %collective-permute-start.1 = (bf16[3,256,128]{2,1,0:T(8,128)(2,1)S(1)}, bf16[3,256,128]{2,1,0:T(8,128)(2,1)S(1)}, u32[]{:S(2)}, u32[]{:S(2)}) collective-permute-start(bf16[3,256,128]{2,1,0:T(8,128)(2,1)S(1)} %split_heads.1.refs_0_), channel_id=1, source_target_pairs={{0,16},{16,4},{4,20},{20,8},{8,24},{24,12},{12,28},{28,0},{1,17},{... | collective-permute-start | bytes 589832 | tf_op jit(solution)/shard_map/ppermute | solution.py:464
  5.1 4.0 %collective-permute-start.2 = (bf16[3,256,128]{2,1,0:T(8,128)(2,1)S(1)}, bf16[3,256,128]{2,1,0:T(8,128)(2,1)S(1)}, u32[]{:S(2)}, u32[]{:S(2)}) collective-permute-start(bf16[3,256,128]{2,1,0:T(8,128)(2,1)S(1)} %split_heads.1.refs_0_), channel_id=1, source_target_pairs={{0,28},{16,0},{4,16},{20,4},{8,20},{24,8},{12,24},{28,12},{1,29},{... | collective-permute-start | bytes 589832 | tf_op jit(solution)/shard_map/ppermute | solution.py:464
  11.0 1.7 %queries_for_other.1 = (bf16[4,256,128]{2,1,0:T(8,128)(2,1)S(1)}, bf16[5,256,128]{2,1,0:T(8,128)(2,1)S(1)}, bf16[5,256,128]{2,1,0:T(8,128)(2,1)S(1)}, s32[1,1]{1,0:T(1,128)}) custom-call(s32[1,3]{1,0:T(1,128)S(1)} %add_bitcast_fusion.place, s32[2,14]{1,0:T(2,128)S(1)} %bitcast.21, bf16[256,1792]{1,0:T(8,128)(2,1)S(1)} %bitcast.15), custom_call_target="tpu_custom_call" | custom-call | tf_op jit(solution)/shard_map/queries_for_other/pallas_call | solution.py:108
  13.6 2.7 %collective-permute-start.5 = (bf16[3,256,128]{2,1,0:T(8,128)(2,1)S(1)}, bf16[3,256,128]{2,1,0:T(8,128)(2,1)S(1)}, u32[]{:S(2)}, u32[]{:S(2)}) collective-permute-start(bf16[3,256,128]{2,1,0:T(8,128)(2,1)S(1)} %collective-permute-done.2.refs_5_.refs_1_), channel_id=1, source_target_pairs={{0,28},{16,0},{4,16},{20,4},{8,20},{24,8},{12,24},{28,12},{1,29},{... | collective-permute-start | bytes 589832 | tf_op jit(solution)/shard_map/ppermute | solution.py:464
  16.9 2.6 %collective-permute-start.10 = (bf16[5,256,128]{2,1,0:T(8,128)(2,1)S(1)}, bf16[5,256,128]{2,1,0:T(8,128)(2,1)S(1)}, u32[]{:S(2)}, u32[]{:S(2)}) collective-permute-start(bf16[5,256,128]{2,1,0:T(8,128)(2,1)S(1)} %chunks_of.4.refs_0_), channel_id=1, source_target_pairs={{0,3},{1,0},{2,1},{3,2},{4,7},{5,4},{6,5},{7,6},{8,11},{9,8},{10,9... | collective-permute-start | bytes 983048 | tf_op jit(solution)/shard_map/ppermute | solution.py:463
  20.0 2.7 %collective-permute-start.6 = (bf16[3,256,128]{2,1,0:T(8,128)(2,1)S(1)}, bf16[3,256,128]{2,1,0:T(8,128)(2,1)S(1)}, u32[]{:S(2)}, u32[]{:S(2)}) collective-permute-start(bf16[3,256,128]{2,1,0:T(8,128)(2,1)S(1)} %collective-permute-done.5.refs_3_), channel_id=1, source_target_pairs={{0,28},{16,0},{4,16},{20,4},{8,20},{24,8},{12,24},{28,12},{1,29},{... | collective-permute-start | bytes 589832 | tf_op jit(solution)/shard_map/ppermute | solution.py:464
  23.9 1.8 %collective-permute-done.4.refs_2_.refs_1_ = bf16[3,256,128]{2,1,0:T(8,128)(2,1)S(1)} collective-permute-done((bf16[3,256,128]{2,1,0:T(8,128)(2,1)S(1)}, bf16[3,256,128]{2,1,0:T(8,128)(2,1)S(1)}, u32[]{:S(2)}, u32[]{:S(2)}) %collective-permute-start.4) | collective-permute-done | bytes 196640 | tf_op jit(solution)/shard_map/ppermute | solution.py:464
  27.8 2.6 %collective-permute-done.13.refs_6_ = bf16[4,256,128]{2,1,0:T(8,128)(2,1)S(1)} collective-permute-done((bf16[4,256,128]{2,1,0:T(8,128)(2,1)S(1)}, bf16[4,256,128]{2,1,0:T(8,128)(2,1)S(1)}, u32[]{:S(2)}, u32[]{:S(2)}) %collective-permute-start.13) | collective-permute-done | bytes 262176 | tf_op jit(solution)/shard_map/ppermute | solution.py:471
  31.7 2.0 %collective-permute-start.8 = (bf16[10,256,128]{2,1,0:T(8,128)(2,1)S(1)}, bf16[10,256,128]{2,1,0:T(8,128)(2,1)S(1)}, u32[]{:S(2)}, u32[]{:S(2)}) collective-permute-start(bf16[10,256,128]{2,1,0:T(8,128)(2,1)S(1)} %chunks_of.3.refs_5_), channel_id=1, source_target_pairs={{0,3},{1,0},{2,1},{3,2},{4,7},{5,4},{6,5},{7,6},{8,11},{9,8},{10,9... | collective-permute-start | bytes 1966088 | tf_op jit(solution)/shard_map/ppermute | solution.py:463
  33.8 1.5 %collective-permute-start.12 = (bf16[3,256,128]{2,1,0:T(8,128)(2,1)S(1)}, bf16[3,256,128]{2,1,0:T(8,128)(2,1)S(1)}, u32[]{:S(2)}, u32[]{:S(2)}) collective-permute-start(bf16[3,256,128]{2,1,0:T(8,128)(2,1)S(1)} %slice.21), channel_id=1, source_target_pairs={{0,3},{1,0},{2,1},{3,2},{4,7},{5,4},{6,5},{7,6},{8,11},{9,8},{10,9... | collective-permute-start | bytes 589832 | tf_op jit(solution)/shard_map/ppermute | solution.py:463
  35.3 3.8 %collective-permute-done.17.refs_0_ = bf16[3,256,128]{2,1,0:T(8,128)(2,1)S(1)} collective-permute-done((bf16[3,256,128]{2,1,0:T(8,128)(2,1)S(1)}, bf16[3,256,128]{2,1,0:T(8,128)(2,1)S(1)}, u32[]{:S(2)}, u32[]{:S(2)}) %collective-permute-start.17) | collective-permute-done | bytes 196640 | tf_op jit(solution)/shard_map/ppermute | solution.py:464
  42.1 1.6 %collective-permute-start.18 = (bf16[5,256,128]{2,1,0:T(8,128)(2,1)S(1)}, bf16[5,256,128]{2,1,0:T(8,128)(2,1)S(1)}, u32[]{:S(2)}, u32[]{:S(2)}) collective-permute-start(bf16[5,256,128]{2,1,0:T(8,128)(2,1)S(1)} %chunks_of.5.refs_4_), channel_id=1, source_target_pairs={{0,1},{1,2},{2,3},{3,0},{4,5},{5,6},{6,7},{7,4},{8,9},{9,10},{10,1... | collective-permute-start | bytes 983048 | tf_op jit(solution)/shard_map/ppermute | solution.py:463
  43.7 3.0 %collective-permute-done.11.refs_3_ = bf16[2,256,128]{2,1,0:T(8,128)(2,1)S(1)} collective-permute-done((bf16[2,256,128]{2,1,0:T(8,128)(2,1)S(1)}, bf16[2,256,128]{2,1,0:T(8,128)(2,1)S(1)}, u32[]{:S(2)}, u32[]{:S(2)}) %collective-permute-start.11) | collective-permute-done | bytes 131104 | tf_op jit(solution)/shard_map/ppermute | solution.py:463
  46.7 2.0 %collective-permute-start.19 = (bf16[5,256,128]{2,1,0:T(8,128)(2,1)S(1)}, bf16[5,256,128]{2,1,0:T(8,128)(2,1)S(1)}, u32[]{:S(2)}, u32[]{:S(2)}) collective-permute-start(bf16[5,256,128]{2,1,0:T(8,128)(2,1)S(1)} %chunks_of.5.refs_4_), channel_id=1, source_target_pairs={{0,3},{1,0},{2,1},{3,2},{4,7},{5,4},{6,5},{7,6},{8,11},{9,8},{10,9... | collective-permute-start | bytes 983048 | tf_op jit(solution)/shard_map/ppermute | solution.py:463
  48.8 3.2 %attend.3 = (f32[56,8,256]{2,1,0:T(8,128)S(1)}, bf16[21,256,256]{2,1,0:T(8,128)(2,1)S(1)}) custom-call(s32[1,3]{1,0:T(1,128)S(1)} %add_bitcast_fusion.place, s32[2,14]{1,0:T(2,128)S(1)} %bitcast.23, s32[2,6]{1,0:T(2,128)S(1)} %copy-done.9, bf16[5,256,128]{2,1,0:T(8,128)(2,1)S(1)} %chunks_of.4.refs_0_, ...), custom_call_target="tpu_custom_call", output_to_operand_aliasing={{1}: (12, {})} | custom-call | flops 4227858432 | bytes 1966080 | tf_op jit(solution)/shard_map/attend/pallas_call | solution.py:424
  52.0 1.8 %collective-permute-done.18.refs_2_ = bf16[5,256,128]{2,1,0:T(8,128)(2,1)S(1)} collective-permute-done((bf16[5,256,128]{2,1,0:T(8,128)(2,1)S(1)}, bf16[5,256,128]{2,1,0:T(8,128)(2,1)S(1)}, u32[]{:S(2)}, u32[]{:S(2)}) %collective-permute-start.18) | collective-permute-done | bytes 327712 | tf_op jit(solution)/shard_map/ppermute | solution.py:463
  53.7 2.5 %collective-permute-done.19.refs_3_ = bf16[5,256,128]{2,1,0:T(8,128)(2,1)S(1)} collective-permute-done((bf16[5,256,128]{2,1,0:T(8,128)(2,1)S(1)}, bf16[5,256,128]{2,1,0:T(8,128)(2,1)S(1)}, u32[]{:S(2)}, u32[]{:S(2)}) %collective-permute-start.19) | collective-permute-done | bytes 327712 | tf_op jit(solution)/shard_map/ppermute | solution.py:463
  56.5 1.5 %collective-permute-start.15 = (bf16[5,256,128]{2,1,0:T(8,128)(2,1)S(1)}, bf16[5,256,128]{2,1,0:T(8,128)(2,1)S(1)}, u32[]{:S(2)}, u32[]{:S(2)}) collective-permute-start(bf16[5,256,128]{2,1,0:T(8,128)(2,1)S(1)} %slice.17), channel_id=1, source_target_pairs={{0,1},{1,2},{2,3},{3,0},{4,5},{5,6},{6,7},{7,4},{8,9},{9,10},{10,1... | collective-permute-start | bytes 983048 | tf_op jit(solution)/shard_map/ppermute | solution.py:463
  58.0 9.5 %collective-permute-start.16 = (bf16[5,256,128]{2,1,0:T(8,128)(2,1)S(1)}, bf16[5,256,128]{2,1,0:T(8,128)(2,1)S(1)}, u32[]{:S(2)}, u32[]{:S(2)}) collective-permute-start(bf16[5,256,128]{2,1,0:T(8,128)(2,1)S(1)} %slice.18), channel_id=1, source_target_pairs={{0,3},{1,0},{2,1},{3,2},{4,7},{5,4},{6,5},{7,6},{8,11},{9,8},{10,9... | collective-permute-start | bytes 983048 | tf_op jit(solution)/shard_map/ppermute | solution.py:463
  68.4 3.3 %collective-permute-done.20.refs_2_ = bf16[5,256,128]{2,1,0:T(8,128)(2,1)S(1)} collective-permute-done((bf16[5,256,128]{2,1,0:T(8,128)(2,1)S(1)}, bf16[5,256,128]{2,1,0:T(8,128)(2,1)S(1)}, u32[]{:S(2)}, u32[]{:S(2)}) %collective-permute-start.20) | collective-permute-done | bytes 327712 | tf_op jit(solution)/shard_map/ppermute | solution.py:463
  71.7 3.5 %collective-permute-done.15.refs_0_ = bf16[5,256,128]{2,1,0:T(8,128)(2,1)S(1)} collective-permute-done((bf16[5,256,128]{2,1,0:T(8,128)(2,1)S(1)}, bf16[5,256,128]{2,1,0:T(8,128)(2,1)S(1)}, u32[]{:S(2)}, u32[]{:S(2)}) %collective-permute-start.15) | collective-permute-done | bytes 327712 | tf_op jit(solution)/shard_map/ppermute | solution.py:463
  75.2 1.9 %attend.5 = (f32[7,256]{1,0:T(8,128)S(1)}, f32[128,128]{1,0:T(8,128)}) custom-call(s32[1,3]{1,0:T(1,128)S(1)} %add_bitcast_fusion.place, s32[2,14]{1,0:T(2,128)S(1)} %bitcast.25, s32[2,3]{1,0:T(2,128)S(1)} %copy-done.7, bf16[5,256,128]{2,1,0:T(8,128)(2,1)S(1)} %collective-permute-done.15.refs_0_, bf16[5,256,128]{2,1,0:T(8,128)(2,1)S(1)} %collective-permute-done.16.refs_1_, ...), custom_call_target="tpu_custom_call" | custom-call | flops 2113929216 | bytes 983040 | tf_op jit(solution)/shard_map/attend/pallas_call | solution.py:424
  77.2 54.8 %all-to-all-start = ((f32[128,1,128]{2,1,0:T(1,128)}), f32[128,1,128]{2,1,0:T(1,128)S(1)}, u32[]{:S(2)}, u32[]{:S(2)}) async-start(f32[128,1,128]{2,1,0:T(1,128)} %bitcast.12), calls=%async_computation | async-start | bytes 131072 | tf_op jit(solution)/shard_map/all_to_all | solution.py:530
  132.6 11.3 %all-to-all-done = f32[128,1,128]{2,1,0:T(1,128)S(1)} async-done(((f32[128,1,128]{2,1,0:T(1,128)}), f32[128,1,128]{2,1,0:T(1,128)S(1)}, u32[]{:S(2)}, u32[]{:S(2)}) %all-to-all-start) | async-done | bytes 65568 | tf_op jit(solution)/shard_map/all_to_all | solution.py:530
  (56 shorter events, 15.1 us)
Async XLA Ops:
  0.6 39.8 %copy-start.6 = (s32[14,2]{0,1:T(2,128)S(1)}, s32[14,2]{0,1:T(2,128)}, u32[]{:S(2)}) copy-start(s32[14,2]{0,1:T(2,128)} %param.14) | copy-start | bytes 340
  2.5 11.1 %collective-permute-start.1 = (bf16[3,256,128]{2,1,0:T(8,128)(2,1)S(1)}, bf16[3,256,128]{2,1,0:T(8,128)(2,1)S(1)}, u32[]{:S(2)}, u32[]{:S(2)}) collective-permute-start(bf16[3,256,128]{2,1,0:T(8,128)(2,1)S(1)} %split_heads.1.refs_0_), channel_id=1, source_target_pairs={{0,16},{16,4},{4,20},{20,8},{8,24},{24,12},{12,28},{28,0},{1,17},{... | collective-permute-start | bytes 589832 | tf_op jit(solution)/shard_map/ppermute | solution.py:464
  5.1 8.5 %collective-permute-start.2 = (bf16[3,256,128]{2,1,0:T(8,128)(2,1)S(1)}, bf16[3,256,128]{2,1,0:T(8,128)(2,1)S(1)}, u32[]{:S(2)}, u32[]{:S(2)}) collective-permute-start(bf16[3,256,128]{2,1,0:T(8,128)(2,1)S(1)} %split_heads.1.refs_0_), channel_id=1, source_target_pairs={{0,28},{16,0},{4,16},{20,4},{8,20},{24,8},{12,24},{28,12},{1,29},{... | collective-permute-start | bytes 589832 | tf_op jit(solution)/shard_map/ppermute | solution.py:464
  11.0 29.4 %copy-start.1 = (bf16[1,256,1792]{2,1,0:T(8,128)(2,1)S(1)}, bf16[1,256,1792]{2,1,0:T(8,128)(2,1)}, u32[]{:S(2)}) copy-start(bf16[1,256,1792]{2,1,0:T(8,128)(2,1)} %param.10) | copy-start | bytes 2752516
  11.0 29.4 %copy-start.2 = (bf16[1,256,896]{2,1,0:T(8,128)(2,1)S(1)}, bf16[1,256,896]{2,1,0:T(8,128)(2,1)}, u32[]{:S(2)}) copy-start(bf16[1,256,896]{2,1,0:T(8,128)(2,1)} %param.12) | copy-start | bytes 1376260
  13.6 6.4 %collective-permute-start.3 = (bf16[3,256,128]{2,1,0:T(8,128)(2,1)S(1)}, bf16[3,256,128]{2,1,0:T(8,128)(2,1)S(1)}, u32[]{:S(2)}, u32[]{:S(2)}) collective-permute-start(bf16[3,256,128]{2,1,0:T(8,128)(2,1)S(1)} %collective-permute-done.1.refs_1_.refs_2_), channel_id=1, source_target_pairs={{0,16},{16,4},{4,20},{20,8},{8,24},{24,12},{12,28},{28,0},{1,17},{... | collective-permute-start | bytes 589832 | tf_op jit(solution)/shard_map/ppermute | solution.py:464
  13.6 6.4 %collective-permute-start.5 = (bf16[3,256,128]{2,1,0:T(8,128)(2,1)S(1)}, bf16[3,256,128]{2,1,0:T(8,128)(2,1)S(1)}, u32[]{:S(2)}, u32[]{:S(2)}) collective-permute-start(bf16[3,256,128]{2,1,0:T(8,128)(2,1)S(1)} %collective-permute-done.2.refs_5_.refs_1_), channel_id=1, source_target_pairs={{0,28},{16,0},{4,16},{20,4},{8,20},{24,8},{12,24},{28,12},{1,29},{... | collective-permute-start | bytes 589832 | tf_op jit(solution)/shard_map/ppermute | solution.py:464
  16.9 14.8 %collective-permute-start.10 = (bf16[5,256,128]{2,1,0:T(8,128)(2,1)S(1)}, bf16[5,256,128]{2,1,0:T(8,128)(2,1)S(1)}, u32[]{:S(2)}, u32[]{:S(2)}) collective-permute-start(bf16[5,256,128]{2,1,0:T(8,128)(2,1)S(1)} %chunks_of.4.refs_0_), channel_id=1, source_target_pairs={{0,3},{1,0},{2,1},{3,2},{4,7},{5,4},{6,5},{7,6},{8,11},{9,8},{10,9... | collective-permute-start | bytes 983048 | tf_op jit(solution)/shard_map/ppermute | solution.py:463
  20.0 5.7 %collective-permute-start.4 = (bf16[3,256,128]{2,1,0:T(8,128)(2,1)S(1)}, bf16[3,256,128]{2,1,0:T(8,128)(2,1)S(1)}, u32[]{:S(2)}, u32[]{:S(2)}) collective-permute-start(bf16[3,256,128]{2,1,0:T(8,128)(2,1)S(1)} %collective-permute-done.3.refs_0_), channel_id=1, source_target_pairs={{0,16},{16,4},{4,20},{20,8},{8,24},{24,12},{12,28},{28,0},{1,17},{... | collective-permute-start | bytes 589832 | tf_op jit(solution)/shard_map/ppermute | solution.py:464
  20.0 5.7 %collective-permute-start.6 = (bf16[3,256,128]{2,1,0:T(8,128)(2,1)S(1)}, bf16[3,256,128]{2,1,0:T(8,128)(2,1)S(1)}, u32[]{:S(2)}, u32[]{:S(2)}) collective-permute-start(bf16[3,256,128]{2,1,0:T(8,128)(2,1)S(1)} %collective-permute-done.5.refs_3_), channel_id=1, source_target_pairs={{0,28},{16,0},{4,16},{20,4},{8,20},{24,8},{12,24},{28,12},{1,29},{... | collective-permute-start | bytes 589832 | tf_op jit(solution)/shard_map/ppermute | solution.py:464
  22.7 11.0 %collective-permute-start.9 = (bf16[5,256,128]{2,1,0:T(8,128)(2,1)S(1)}, bf16[5,256,128]{2,1,0:T(8,128)(2,1)S(1)}, u32[]{:S(2)}, u32[]{:S(2)}) collective-permute-start(bf16[5,256,128]{2,1,0:T(8,128)(2,1)S(1)} %chunks_of.4.refs_0_), channel_id=1, source_target_pairs={{0,1},{1,2},{2,3},{3,0},{4,5},{5,6},{6,7},{7,4},{8,9},{9,10},{10,1... | collective-permute-start | bytes 983048 | tf_op jit(solution)/shard_map/ppermute | solution.py:463
  23.9 6.6 %collective-permute-start.13 = (bf16[4,256,128]{2,1,0:T(8,128)(2,1)S(1)}, bf16[4,256,128]{2,1,0:T(8,128)(2,1)S(1)}, u32[]{:S(2)}, u32[]{:S(2)}) collective-permute-start(bf16[4,256,128]{2,1,0:T(8,128)(2,1)S(1)} %get-tuple-element.28), channel_id=1, source_target_pairs={{0,16},{16,0},{1,17},{17,1},{2,18},{18,2},{3,19},{19,3},{4,20},{20... | collective-permute-start | bytes 786440 | tf_op jit(solution)/shard_map/ppermute | solution.py:471
  25.8 16.3 %collective-permute-start.14 = (bf16[5,256,128]{2,1,0:T(8,128)(2,1)S(1)}, bf16[5,256,128]{2,1,0:T(8,128)(2,1)S(1)}, u32[]{:S(2)}, u32[]{:S(2)}) collective-permute-start(bf16[5,256,128]{2,1,0:T(8,128)(2,1)S(1)} %get-tuple-element.29), channel_id=1, source_target_pairs={{0,16},{16,0},{1,17},{17,1},{2,18},{18,2},{3,19},{19,3},{4,20},{20... | collective-permute-start | bytes 983048 | tf_op jit(solution)/shard_map/ppermute | solution.py:471
  25.8 13.4 %collective-permute-start.17 = (bf16[3,256,128]{2,1,0:T(8,128)(2,1)S(1)}, bf16[3,256,128]{2,1,0:T(8,128)(2,1)S(1)}, u32[]{:S(2)}, u32[]{:S(2)}) collective-permute-start(bf16[3,256,128]{2,1,0:T(8,128)(2,1)S(1)} %collective-permute-done.4.refs_2_.refs_1_), channel_id=1, source_target_pairs={{0,16},{16,4},{4,20},{20,8},{8,24},{24,12},{12,28},{28,0},{1,17},{... | collective-permute-start | bytes 589832 | tf_op jit(solution)/shard_map/ppermute | solution.py:464
  30.5 21.5 %collective-permute-start.7 = (bf16[10,256,128]{2,1,0:T(8,128)(2,1)S(1)}, bf16[10,256,128]{2,1,0:T(8,128)(2,1)S(1)}, u32[]{:S(2)}, u32[]{:S(2)}) collective-permute-start(bf16[10,256,128]{2,1,0:T(8,128)(2,1)S(1)} %chunks_of.3.refs_5_), channel_id=1, source_target_pairs={{0,1},{1,2},{2,3},{3,0},{4,5},{5,6},{6,7},{7,4},{8,9},{9,10},{10,1... | collective-permute-start | bytes 1966088 | tf_op jit(solution)/shard_map/ppermute | solution.py:463
  31.7 20.3 %collective-permute-start.8 = (bf16[10,256,128]{2,1,0:T(8,128)(2,1)S(1)}, bf16[10,256,128]{2,1,0:T(8,128)(2,1)S(1)}, u32[]{:S(2)}, u32[]{:S(2)}) collective-permute-start(bf16[10,256,128]{2,1,0:T(8,128)(2,1)S(1)} %chunks_of.3.refs_5_), channel_id=1, source_target_pairs={{0,3},{1,0},{2,1},{3,2},{4,7},{5,4},{6,5},{7,6},{8,11},{9,8},{10,9... | collective-permute-start | bytes 1966088 | tf_op jit(solution)/shard_map/ppermute | solution.py:463
  33.8 15.0 %collective-permute-start.12 = (bf16[3,256,128]{2,1,0:T(8,128)(2,1)S(1)}, bf16[3,256,128]{2,1,0:T(8,128)(2,1)S(1)}, u32[]{:S(2)}, u32[]{:S(2)}) collective-permute-start(bf16[3,256,128]{2,1,0:T(8,128)(2,1)S(1)} %slice.21), channel_id=1, source_target_pairs={{0,3},{1,0},{2,1},{3,2},{4,7},{5,4},{6,5},{7,6},{8,11},{9,8},{10,9... | collective-permute-start | bytes 589832 | tf_op jit(solution)/shard_map/ppermute | solution.py:463
  39.2 7.5 %collective-permute-start.11 = (bf16[2,256,128]{2,1,0:T(8,128)(2,1)S(1)}, bf16[2,256,128]{2,1,0:T(8,128)(2,1)S(1)}, u32[]{:S(2)}, u32[]{:S(2)}) collective-permute-start(bf16[2,256,128]{2,1,0:T(8,128)(2,1)S(1)} %slice.20), channel_id=1, source_target_pairs={{0,1},{1,2},{2,3},{3,0},{4,5},{5,6},{6,7},{7,4},{8,9},{9,10},{10,1... | collective-permute-start | bytes 393224 | tf_op jit(solution)/shard_map/ppermute | solution.py:463
  42.1 11.6 %collective-permute-start.18 = (bf16[5,256,128]{2,1,0:T(8,128)(2,1)S(1)}, bf16[5,256,128]{2,1,0:T(8,128)(2,1)S(1)}, u32[]{:S(2)}, u32[]{:S(2)}) collective-permute-start(bf16[5,256,128]{2,1,0:T(8,128)(2,1)S(1)} %chunks_of.5.refs_4_), channel_id=1, source_target_pairs={{0,1},{1,2},{2,3},{3,0},{4,5},{5,6},{6,7},{7,4},{8,9},{9,10},{10,1... | collective-permute-start | bytes 983048 | tf_op jit(solution)/shard_map/ppermute | solution.py:463
  46.7 9.5 %collective-permute-start.19 = (bf16[5,256,128]{2,1,0:T(8,128)(2,1)S(1)}, bf16[5,256,128]{2,1,0:T(8,128)(2,1)S(1)}, u32[]{:S(2)}, u32[]{:S(2)}) collective-permute-start(bf16[5,256,128]{2,1,0:T(8,128)(2,1)S(1)} %chunks_of.5.refs_4_), channel_id=1, source_target_pairs={{0,3},{1,0},{2,1},{3,2},{4,7},{5,4},{6,5},{7,6},{8,11},{9,8},{10,9... | collective-permute-start | bytes 983048 | tf_op jit(solution)/shard_map/ppermute | solution.py:463
  56.2 15.5 %collective-permute-start.20 = (bf16[5,256,128]{2,1,0:T(8,128)(2,1)S(1)}, bf16[5,256,128]{2,1,0:T(8,128)(2,1)S(1)}, u32[]{:S(2)}, u32[]{:S(2)}) collective-permute-start(bf16[5,256,128]{2,1,0:T(8,128)(2,1)S(1)} %collective-permute-done.18.refs_2_), channel_id=1, source_target_pairs={{0,1},{1,2},{2,3},{3,0},{4,5},{5,6},{6,7},{7,4},{8,9},{9,10},{10,1... | collective-permute-start | bytes 983048 | tf_op jit(solution)/shard_map/ppermute | solution.py:463
  56.5 18.7 %collective-permute-start.15 = (bf16[5,256,128]{2,1,0:T(8,128)(2,1)S(1)}, bf16[5,256,128]{2,1,0:T(8,128)(2,1)S(1)}, u32[]{:S(2)}, u32[]{:S(2)}) collective-permute-start(bf16[5,256,128]{2,1,0:T(8,128)(2,1)S(1)} %slice.17), channel_id=1, source_target_pairs={{0,1},{1,2},{2,3},{3,0},{4,5},{5,6},{6,7},{7,4},{8,9},{9,10},{10,1... | collective-permute-start | bytes 983048 | tf_op jit(solution)/shard_map/ppermute | solution.py:463
  58.0 17.2 %collective-permute-start.16 = (bf16[5,256,128]{2,1,0:T(8,128)(2,1)S(1)}, bf16[5,256,128]{2,1,0:T(8,128)(2,1)S(1)}, u32[]{:S(2)}, u32[]{:S(2)}) collective-permute-start(bf16[5,256,128]{2,1,0:T(8,128)(2,1)S(1)} %slice.18), channel_id=1, source_target_pairs={{0,3},{1,0},{2,1},{3,2},{4,7},{5,4},{6,5},{7,6},{8,11},{9,8},{10,9... | collective-permute-start | bytes 983048 | tf_op jit(solution)/shard_map/ppermute | solution.py:463
  77.2 66.7 %all-to-all-start = ((f32[128,1,128]{2,1,0:T(1,128)}), f32[128,1,128]{2,1,0:T(1,128)S(1)}, u32[]{:S(2)}, u32[]{:S(2)}) async-start(f32[128,1,128]{2,1,0:T(1,128)} %bitcast.12), calls=%async_computation | async-start | bytes 131072 | tf_op jit(solution)/shard_map/all_to_all | solution.py:530
  (7 other events, 51.8 us)

commit v13 on v10

--- a/solution.py
+++ b/solution.py
@@ -507,7 +507,8 @@
     far_1 = along_x(cut_1, 1)
     far_3 = along_x(cut_3, -1)
     left_2, right_2, state = lax.optimization_barrier((left_2, right_2, state))
-    far_2 = along_x(left_2, 1)
+    far_2a = along_x(left_2[:OTHER], 1)
+    far_2b = along_x(right_2[OTHER:], -1)
     state = attend(
         place,
         table,
@@ -522,7 +523,7 @@
         place,
         table,
         plan_of([(1, 2), (3, 2), (2, 2)]),
-        [far_1, far_3, far_2],
+        [far_1, far_3, far_2a, far_2b],
         rows,
         state=state,
         copies_out=devices,

time: 146 us -> 150 us (1.027)
  starting transfers between devices: 91.5 us -> 97.1 us
  waiting for transfers between devices: 37.3 us -> 35 us
    all_to_all x1, starting transfers between devices: 58.6 us -> 61.4 us  [program(): terms = lax.all_to_all(sums, everyone, 0, 0, tiled=True)]
    ppermute x11 -> x12, starting transfers between devices: 19.2 us -> 21.9 us  [program(): along_x = lambda a, by: lax.ppermute(a, 'kv_1', shift(4, by))]
    ppermute x11 -> x12, waiting for transfers between devices: 15.9 us -> 13.6 us  [program(): along_x = lambda a, by: lax.ppermute(a, 'kv_1', shift(4, by))]
  transfers between devices with their start and end apart: 21 -> 22, of which waited for: 12 -> 12; matrix products, arithmetic and copies ran while one was open for 1% -> 1% of each run, Pallas kernels for 6% -> 6%
where the time goes in v13:
time: 150 us; the launch traced here: 149 us
  starting transfers between devices  97.1 us (65%)
  waiting for transfers between devices  35 us (23%)
  Pallas kernels  10.7 us (7%)
  local copies, waits for them, and re-layouts  4.33 us (3%)
  between operations  1.5 us (1%)
    all_to_all x1, starting transfers between devices, program(): terms = lax.all_to_all(sums, everyone, 0, 0, tiled=True)  61.4 us
    ppermute x12, starting transfers between devices, program(): along_x = lambda a, by: lax.ppermute(a, 'kv_1', shift(4, by))  21.9 us
    ppermute x12, waiting for transfers between devices, program(): along_x = lambda a, by: lax.ppermute(a, 'kv_1', shift(4, by))  13.6 us
    ppermute x7, starting transfers between devices, program(): along_z = lambda a, by: lax.ppermute(a, ('head', 'kv_0'), z_shift(by))  13.2 us
    all_to_all x1, waiting for transfers between devices, program(): terms = lax.all_to_all(sums, everyone, 0, 0, tiled=True)  11.2 us
    ppermute x7, waiting for transfers between devices, program(): along_z = lambda a, by: lax.ppermute(a, ('head', 'kv_0'), z_shift(by))  10.2 us
    pallas_call x3, Pallas kernels, attend(): pl.pallas_call(functools.partial(attend_kernel, first, last, counts, bloc...  6.04 us
    unnamed x21, local copies, waits for them, and re-layouts  4.23 us
  transfers between devices with their start and end apart: 22, of which 12 were waited for; matrix products, arithmetic and copies ran while one was open for 1% of the time, Pallas kernels for 6%

profile of v13, /device:TPU:1, one launch (start us, length us, event | category | flops | bytes accessed | tf_op | source)
XLA Modules:
  0.0 149.3 jit_solution(10692327595502658614)
XLA Ops:
  2.5 2.5 %collective-permute-start.1 = (bf16[3,256,128]{2,1,0:T(8,128)(2,1)S(1)}, bf16[3,256,128]{2,1,0:T(8,128)(2,1)S(1)}, u32[]{:S(2)}, u32[]{:S(2)}) collective-permute-start(bf16[3,256,128]{2,1,0:T(8,128)(2,1)S(1)} %split_heads.1.refs_0_), channel_id=1, source_target_pairs={{0,16},{16,4},{4,20},{20,8},{8,24},{24,12},{12,28},{28,0},{1,17},{... | collective-permute-start | bytes 589832 | tf_op jit(solution)/shard_map/ppermute | solution.py:464
  5.1 4.0 %collective-permute-start.2 = (bf16[3,256,128]{2,1,0:T(8,128)(2,1)S(1)}, bf16[3,256,128]{2,1,0:T(8,128)(2,1)S(1)}, u32[]{:S(2)}, u32[]{:S(2)}) collective-permute-start(bf16[3,256,128]{2,1,0:T(8,128)(2,1)S(1)} %split_heads.1.refs_0_), channel_id=1, source_target_pairs={{0,28},{16,0},{4,16},{20,4},{8,20},{24,8},{12,24},{28,12},{1,29},{... | collective-permute-start | bytes 589832 | tf_op jit(solution)/shard_map/ppermute | solution.py:464
  9.2 1.2 copy-done
  11.0 1.7 %queries_for_other.1 = (bf16[4,256,128]{2,1,0:T(8,128)(2,1)S(1)}, bf16[5,256,128]{2,1,0:T(8,128)(2,1)S(1)}, bf16[5,256,128]{2,1,0:T(8,128)(2,1)S(1)}, s32[1,1]{1,0:T(1,128)}) custom-call(s32[1,3]{1,0:T(1,128)S(1)} %add_bitcast_fusion.place, s32[2,14]{1,0:T(2,128)S(1)} %bitcast.21, bf16[256,1792]{1,0:T(8,128)(2,1)S(1)} %bitcast.15), custom_call_target="tpu_custom_call" | custom-call | tf_op jit(solution)/shard_map/queries_for_other/pallas_call | solution.py:108
  14.2 2.6 %collective-permute-start.10 = (bf16[5,256,128]{2,1,0:T(8,128)(2,1)S(1)}, bf16[5,256,128]{2,1,0:T(8,128)(2,1)S(1)}, u32[]{:S(2)}, u32[]{:S(2)}) collective-permute-start(bf16[5,256,128]{2,1,0:T(8,128)(2,1)S(1)} %chunks_of.4.refs_0_), channel_id=1, source_target_pairs={{0,3},{1,0},{2,1},{3,2},{4,7},{5,4},{6,5},{7,6},{8,11},{9,8},{10,9... | collective-permute-start | bytes 983048 | tf_op jit(solution)/shard_map/ppermute | solution.py:463
  16.8 2.7 %collective-permute-start.5 = (bf16[3,256,128]{2,1,0:T(8,128)(2,1)S(1)}, bf16[3,256,128]{2,1,0:T(8,128)(2,1)S(1)}, u32[]{:S(2)}, u32[]{:S(2)}) collective-permute-start(bf16[3,256,128]{2,1,0:T(8,128)(2,1)S(1)} %collective-permute-done.2.refs_5_.refs_1_), channel_id=1, source_target_pairs={{0,28},{16,0},{4,16},{20,4},{8,20},{24,8},{12,24},{28,12},{1,29},{... | collective-permute-start | bytes 589832 | tf_op jit(solution)/shard_map/ppermute | solution.py:464
  20.0 1.2 collective-permute-start.9
  22.0 3.1 %collective-permute-start.6 = (bf16[3,256,128]{2,1,0:T(8,128)(2,1)S(1)}, bf16[3,256,128]{2,1,0:T(8,128)(2,1)S(1)}, u32[]{:S(2)}, u32[]{:S(2)}) collective-permute-start(bf16[3,256,128]{2,1,0:T(8,128)(2,1)S(1)} %collective-permute-done.5.refs_3_), channel_id=1, source_target_pairs={{0,28},{16,0},{4,16},{20,4},{8,20},{24,8},{12,24},{28,12},{1,29},{... | collective-permute-start | bytes 589832 | tf_op jit(solution)/shard_map/ppermute | solution.py:464
  26.7 4.9 %collective-permute-done.6.refs_4_.refs_2_ = bf16[3,256,128]{2,1,0:T(8,128)(2,1)S(1)} collective-permute-done((bf16[3,256,128]{2,1,0:T(8,128)(2,1)S(1)}, bf16[3,256,128]{2,1,0:T(8,128)(2,1)S(1)}, u32[]{:S(2)}, u32[]{:S(2)}) %collective-permute-start.6) | collective-permute-done | bytes 196640 | tf_op jit(solution)/shard_map/ppermute | solution.py:464
  33.7 2.1 %collective-permute-start.8 = (bf16[10,256,128]{2,1,0:T(8,128)(2,1)S(1)}, bf16[10,256,128]{2,1,0:T(8,128)(2,1)S(1)}, u32[]{:S(2)}, u32[]{:S(2)}) collective-permute-start(bf16[10,256,128]{2,1,0:T(8,128)(2,1)S(1)} %chunks_of.3.refs_5_), channel_id=1, source_target_pairs={{0,3},{1,0},{2,1},{3,2},{4,7},{5,4},{6,5},{7,6},{8,11},{9,8},{10,9... | collective-permute-start | bytes 1966088 | tf_op jit(solution)/shard_map/ppermute | solution.py:463
  35.8 3.5 %collective-permute-done.13.refs_0_ = bf16[3,256,128]{2,1,0:T(8,128)(2,1)S(1)} collective-permute-done((bf16[3,256,128]{2,1,0:T(8,128)(2,1)S(1)}, bf16[3,256,128]{2,1,0:T(8,128)(2,1)S(1)}, u32[]{:S(2)}, u32[]{:S(2)}) %collective-permute-start.13) | collective-permute-done | bytes 196640 | tf_op jit(solution)/shard_map/ppermute | solution.py:464
  39.3 1.2 collective-permute-start.11
  42.3 1.3 collective-permute-start.18
  43.6 3.5 %collective-permute-done.11.refs_3_ = bf16[2,256,128]{2,1,0:T(8,128)(2,1)S(1)} collective-permute-done((bf16[2,256,128]{2,1,0:T(8,128)(2,1)S(1)}, bf16[2,256,128]{2,1,0:T(8,128)(2,1)S(1)}, u32[]{:S(2)}, u32[]{:S(2)}) %collective-permute-start.11) | collective-permute-done | bytes 131104 | tf_op jit(solution)/shard_map/ppermute | solution.py:463
  47.3 3.2 %attend.3 = (f32[56,8,256]{2,1,0:T(8,128)S(1)}, bf16[21,256,256]{2,1,0:T(8,128)(2,1)S(1)}) custom-call(s32[1,3]{1,0:T(1,128)S(1)} %add_bitcast_fusion.place, s32[2,14]{1,0:T(2,128)S(1)} %bitcast.23, s32[2,7]{1,0:T(2,128)S(1)} %copy-done.9, bf16[5,256,128]{2,1,0:T(8,128)(2,1)S(1)} %chunks_of.4.refs_0_, ...), custom_call_target="tpu_custom_call", output_to_operand_aliasing={{1}: (13, {})} | custom-call | flops 4932501504 | bytes 2293760 | tf_op jit(solution)/shard_map/attend/pallas_call | solution.py:424
  50.6 3.5 %collective-permute-done.18.refs_2_ = bf16[5,256,128]{2,1,0:T(8,128)(2,1)S(1)} collective-permute-done((bf16[5,256,128]{2,1,0:T(8,128)(2,1)S(1)}, bf16[5,256,128]{2,1,0:T(8,128)(2,1)S(1)}, u32[]{:S(2)}, u32[]{:S(2)}) %collective-permute-start.18) | collective-permute-done | bytes 327712 | tf_op jit(solution)/shard_map/ppermute | solution.py:463
  54.1 2.0 %collective-permute-done.19.refs_3_ = bf16[5,256,128]{2,1,0:T(8,128)(2,1)S(1)} collective-permute-done((bf16[5,256,128]{2,1,0:T(8,128)(2,1)S(1)}, bf16[5,256,128]{2,1,0:T(8,128)(2,1)S(1)}, u32[]{:S(2)}, u32[]{:S(2)}) %collective-permute-start.19) | collective-permute-done | bytes 327712 | tf_op jit(solution)/shard_map/ppermute | solution.py:463
  56.1 8.9 %collective-permute-start.21 = (bf16[3,256,128]{2,1,0:T(8,128)(2,1)S(1)}, bf16[3,256,128]{2,1,0:T(8,128)(2,1)S(1)}, u32[]{:S(2)}, u32[]{:S(2)}) collective-permute-start(bf16[3,256,128]{2,1,0:T(8,128)(2,1)S(1)} %slice.26), channel_id=1, source_target_pairs={{0,3},{1,0},{2,1},{3,2},{4,7},{5,4},{6,5},{7,6},{8,11},{9,8},{10,9... | collective-permute-start | bytes 589832 | tf_op jit(solution)/shard_map/ppermute | solution.py:463
  65.3 2.7 %collective-permute-start.17 = (bf16[5,256,128]{2,1,0:T(8,128)(2,1)S(1)}, bf16[5,256,128]{2,1,0:T(8,128)(2,1)S(1)}, u32[]{:S(2)}, u32[]{:S(2)}) collective-permute-start(bf16[5,256,128]{2,1,0:T(8,128)(2,1)S(1)} %slice.24), channel_id=1, source_target_pairs={{0,3},{1,0},{2,1},{3,2},{4,7},{5,4},{6,5},{7,6},{8,11},{9,8},{10,9... | collective-permute-start | bytes 983048 | tf_op jit(solution)/shard_map/ppermute | solution.py:463
  68.1 1.1 attend.4.refs_5_
  70.2 3.5 %collective-permute-done.16.refs_0_ = bf16[5,256,128]{2,1,0:T(8,128)(2,1)S(1)} collective-permute-done((bf16[5,256,128]{2,1,0:T(8,128)(2,1)S(1)}, bf16[5,256,128]{2,1,0:T(8,128)(2,1)S(1)}, u32[]{:S(2)}, u32[]{:S(2)}) %collective-permute-start.16) | collective-permute-done | bytes 327712 | tf_op jit(solution)/shard_map/ppermute | solution.py:463
  73.7 1.7 %attend.5 = (f32[7,256]{1,0:T(8,128)S(1)}, f32[128,128]{1,0:T(8,128)}) custom-call(s32[1,3]{1,0:T(1,128)S(1)} %add_bitcast_fusion.place, s32[2,14]{1,0:T(2,128)S(1)} %bitcast.25, s32[2,3]{1,0:T(2,128)S(1)} %copy-done.7, bf16[5,256,128]{2,1,0:T(8,128)(2,1)S(1)} %collective-permute-done.16.refs_0_, bf16[5,256,128]{2,1,0:T(8,128)(2,1)S(1)} %collective-permute-done.17.refs_1_, ...), custom_call_target="tpu_custom_call" | custom-call | flops 2113929216 | bytes 983040 | tf_op jit(solution)/shard_map/attend/pallas_call | solution.py:424
  75.4 61.4 %all-to-all-start = ((f32[128,1,128]{2,1,0:T(1,128)}), f32[128,1,128]{2,1,0:T(1,128)S(1)}, u32[]{:S(2)}, u32[]{:S(2)}) async-start(f32[128,1,128]{2,1,0:T(1,128)} %bitcast.12), calls=%async_computation | async-start | bytes 131072 | tf_op jit(solution)/shard_map/all_to_all | solution.py:531
  137.5 11.2 %all-to-all-done = f32[128,1,128]{2,1,0:T(1,128)S(1)} async-done(((f32[128,1,128]{2,1,0:T(1,128)}), f32[128,1,128]{2,1,0:T(1,128)S(1)}, u32[]{:S(2)}, u32[]{:S(2)}) %all-to-all-start) | async-done | bytes 65568 | tf_op jit(solution)/shard_map/all_to_all | solution.py:531
  (60 shorter events, 13.0 us)
Async XLA Ops:
  0.6 39.9 %copy-start.6 = (s32[14,2]{0,1:T(2,128)S(1)}, s32[14,2]{0,1:T(2,128)}, u32[]{:S(2)}) copy-start(s32[14,2]{0,1:T(2,128)} %param.14) | copy-start | bytes 340
  2.5 11.1 %collective-permute-start.1 = (bf16[3,256,128]{2,1,0:T(8,128)(2,1)S(1)}, bf16[3,256,128]{2,1,0:T(8,128)(2,1)S(1)}, u32[]{:S(2)}, u32[]{:S(2)}) collective-permute-start(bf16[3,256,128]{2,1,0:T(8,128)(2,1)S(1)} %split_heads.1.refs_0_), channel_id=1, source_target_pairs={{0,16},{16,4},{4,20},{20,8},{8,24},{24,12},{12,28},{28,0},{1,17},{... | collective-permute-start | bytes 589832 | tf_op jit(solution)/shard_map/ppermute | solution.py:464
  5.1 8.5 %collective-permute-start.2 = (bf16[3,256,128]{2,1,0:T(8,128)(2,1)S(1)}, bf16[3,256,128]{2,1,0:T(8,128)(2,1)S(1)}, u32[]{:S(2)}, u32[]{:S(2)}) collective-permute-start(bf16[3,256,128]{2,1,0:T(8,128)(2,1)S(1)} %split_heads.1.refs_0_), channel_id=1, source_target_pairs={{0,28},{16,0},{4,16},{20,4},{8,20},{24,8},{12,24},{28,12},{1,29},{... | collective-permute-start | bytes 589832 | tf_op jit(solution)/shard_map/ppermute | solution.py:464
  11.0 29.5 %copy-start.2 = (bf16[1,256,896]{2,1,0:T(8,128)(2,1)S(1)}, bf16[1,256,896]{2,1,0:T(8,128)(2,1)}, u32[]{:S(2)}) copy-start(bf16[1,256,896]{2,1,0:T(8,128)(2,1)} %param.12) | copy-start | bytes 1376260
  13.6 6.4 %collective-permute-start.3 = (bf16[3,256,128]{2,1,0:T(8,128)(2,1)S(1)}, bf16[3,256,128]{2,1,0:T(8,128)(2,1)S(1)}, u32[]{:S(2)}, u32[]{:S(2)}) collective-permute-start(bf16[3,256,128]{2,1,0:T(8,128)(2,1)S(1)} %collective-permute-done.1.refs_1_.refs_2_), channel_id=1, source_target_pairs={{0,16},{16,4},{4,20},{20,8},{8,24},{24,12},{12,28},{28,0},{1,17},{... | collective-permute-start | bytes 589832 | tf_op jit(solution)/shard_map/ppermute | solution.py:464
  14.2 11.0 %collective-permute-start.10 = (bf16[5,256,128]{2,1,0:T(8,128)(2,1)S(1)}, bf16[5,256,128]{2,1,0:T(8,128)(2,1)S(1)}, u32[]{:S(2)}, u32[]{:S(2)}) collective-permute-start(bf16[5,256,128]{2,1,0:T(8,128)(2,1)S(1)} %chunks_of.4.refs_0_), channel_id=1, source_target_pairs={{0,3},{1,0},{2,1},{3,2},{4,7},{5,4},{6,5},{7,6},{8,11},{9,8},{10,9... | collective-permute-start | bytes 983048 | tf_op jit(solution)/shard_map/ppermute | solution.py:463
  16.8 5.3 %collective-permute-start.5 = (bf16[3,256,128]{2,1,0:T(8,128)(2,1)S(1)}, bf16[3,256,128]{2,1,0:T(8,128)(2,1)S(1)}, u32[]{:S(2)}, u32[]{:S(2)}) collective-permute-start(bf16[3,256,128]{2,1,0:T(8,128)(2,1)S(1)} %collective-permute-done.2.refs_5_.refs_1_), channel_id=1, source_target_pairs={{0,28},{16,0},{4,16},{20,4},{8,20},{24,8},{12,24},{28,12},{1,29},{... | collective-permute-start | bytes 589832 | tf_op jit(solution)/shard_map/ppermute | solution.py:464
  20.0 5.7 %collective-permute-start.4 = (bf16[3,256,128]{2,1,0:T(8,128)(2,1)S(1)}, bf16[3,256,128]{2,1,0:T(8,128)(2,1)S(1)}, u32[]{:S(2)}, u32[]{:S(2)}) collective-permute-start(bf16[3,256,128]{2,1,0:T(8,128)(2,1)S(1)} %collective-permute-done.3.refs_0_), channel_id=1, source_target_pairs={{0,16},{16,4},{4,20},{20,8},{8,24},{24,12},{12,28},{28,0},{1,17},{... | collective-permute-start | bytes 589832 | tf_op jit(solution)/shard_map/ppermute | solution.py:464
  20.0 13.7 %collective-permute-start.9 = (bf16[5,256,128]{2,1,0:T(8,128)(2,1)S(1)}, bf16[5,256,128]{2,1,0:T(8,128)(2,1)S(1)}, u32[]{:S(2)}, u32[]{:S(2)}) collective-permute-start(bf16[5,256,128]{2,1,0:T(8,128)(2,1)S(1)} %chunks_of.4.refs_0_), channel_id=1, source_target_pairs={{0,1},{1,2},{2,3},{3,0},{4,5},{5,6},{6,7},{7,4},{8,9},{9,10},{10,1... | collective-permute-start | bytes 983048 | tf_op jit(solution)/shard_map/ppermute | solution.py:463
  21.3 11.8 %collective-permute-start.14 = (bf16[4,256,128]{2,1,0:T(8,128)(2,1)S(1)}, bf16[4,256,128]{2,1,0:T(8,128)(2,1)S(1)}, u32[]{:S(2)}, u32[]{:S(2)}) collective-permute-start(bf16[4,256,128]{2,1,0:T(8,128)(2,1)S(1)} %get-tuple-element.28), channel_id=1, source_target_pairs={{0,16},{16,0},{1,17},{17,1},{2,18},{18,2},{3,19},{19,3},{4,20},{20... | collective-permute-start | bytes 786440 | tf_op jit(solution)/shard_map/ppermute | solution.py:471
  22.0 9.5 %collective-permute-start.6 = (bf16[3,256,128]{2,1,0:T(8,128)(2,1)S(1)}, bf16[3,256,128]{2,1,0:T(8,128)(2,1)S(1)}, u32[]{:S(2)}, u32[]{:S(2)}) collective-permute-start(bf16[3,256,128]{2,1,0:T(8,128)(2,1)S(1)} %collective-permute-done.5.refs_3_), channel_id=1, source_target_pairs={{0,28},{16,0},{4,16},{20,4},{8,20},{24,8},{12,24},{28,12},{1,29},{... | collective-permute-start | bytes 589832 | tf_op jit(solution)/shard_map/ppermute | solution.py:464
  25.2 17.1 %collective-permute-start.15 = (bf16[5,256,128]{2,1,0:T(8,128)(2,1)S(1)}, bf16[5,256,128]{2,1,0:T(8,128)(2,1)S(1)}, u32[]{:S(2)}, u32[]{:S(2)}) collective-permute-start(bf16[5,256,128]{2,1,0:T(8,128)(2,1)S(1)} %get-tuple-element.29), channel_id=1, source_target_pairs={{0,16},{16,0},{1,17},{17,1},{2,18},{18,2},{3,19},{19,3},{4,20},{20... | collective-permute-start | bytes 983048 | tf_op jit(solution)/shard_map/ppermute | solution.py:471
  25.8 13.6 %collective-permute-start.13 = (bf16[3,256,128]{2,1,0:T(8,128)(2,1)S(1)}, bf16[3,256,128]{2,1,0:T(8,128)(2,1)S(1)}, u32[]{:S(2)}, u32[]{:S(2)}) collective-permute-start(bf16[3,256,128]{2,1,0:T(8,128)(2,1)S(1)} %collective-permute-done.4.refs_2_.refs_1_), channel_id=1, source_target_pairs={{0,16},{16,4},{4,20},{20,8},{8,24},{24,12},{12,28},{28,0},{1,17},{... | collective-permute-start | bytes 589832 | tf_op jit(solution)/shard_map/ppermute | solution.py:464
  31.6 15.8 %collective-permute-start.12 = (bf16[3,256,128]{2,1,0:T(8,128)(2,1)S(1)}, bf16[3,256,128]{2,1,0:T(8,128)(2,1)S(1)}, u32[]{:S(2)}, u32[]{:S(2)}) collective-permute-start(bf16[3,256,128]{2,1,0:T(8,128)(2,1)S(1)} %slice.29), channel_id=1, source_target_pairs={{0,3},{1,0},{2,1},{3,2},{4,7},{5,4},{6,5},{7,6},{8,11},{9,8},{10,9... | collective-permute-start | bytes 589832 | tf_op jit(solution)/shard_map/ppermute | solution.py:463
  33.0 17.5 %collective-permute-start.7 = (bf16[10,256,128]{2,1,0:T(8,128)(2,1)S(1)}, bf16[10,256,128]{2,1,0:T(8,128)(2,1)S(1)}, u32[]{:S(2)}, u32[]{:S(2)}) collective-permute-start(bf16[10,256,128]{2,1,0:T(8,128)(2,1)S(1)} %chunks_of.3.refs_5_), channel_id=1, source_target_pairs={{0,1},{1,2},{2,3},{3,0},{4,5},{5,6},{6,7},{7,4},{8,9},{9,10},{10,1... | collective-permute-start | bytes 1966088 | tf_op jit(solution)/shard_map/ppermute | solution.py:463
  33.7 16.8 %collective-permute-start.8 = (bf16[10,256,128]{2,1,0:T(8,128)(2,1)S(1)}, bf16[10,256,128]{2,1,0:T(8,128)(2,1)S(1)}, u32[]{:S(2)}, u32[]{:S(2)}) collective-permute-start(bf16[10,256,128]{2,1,0:T(8,128)(2,1)S(1)} %chunks_of.3.refs_5_), channel_id=1, source_target_pairs={{0,3},{1,0},{2,1},{3,2},{4,7},{5,4},{6,5},{7,6},{8,11},{9,8},{10,9... | collective-permute-start | bytes 1966088 | tf_op jit(solution)/shard_map/ppermute | solution.py:463
  39.3 7.7 %collective-permute-start.11 = (bf16[2,256,128]{2,1,0:T(8,128)(2,1)S(1)}, bf16[2,256,128]{2,1,0:T(8,128)(2,1)S(1)}, u32[]{:S(2)}, u32[]{:S(2)}) collective-permute-start(bf16[2,256,128]{2,1,0:T(8,128)(2,1)S(1)} %slice.28), channel_id=1, source_target_pairs={{0,1},{1,2},{2,3},{3,0},{4,5},{5,6},{6,7},{7,4},{8,9},{9,10},{10,1... | collective-permute-start | bytes 393224 | tf_op jit(solution)/shard_map/ppermute | solution.py:463
  42.3 11.8 %collective-permute-start.18 = (bf16[5,256,128]{2,1,0:T(8,128)(2,1)S(1)}, bf16[5,256,128]{2,1,0:T(8,128)(2,1)S(1)}, u32[]{:S(2)}, u32[]{:S(2)}) collective-permute-start(bf16[5,256,128]{2,1,0:T(8,128)(2,1)S(1)} %chunks_of.5.refs_6_), channel_id=1, source_target_pairs={{0,1},{1,2},{2,3},{3,0},{4,5},{5,6},{6,7},{7,4},{8,9},{9,10},{10,1... | collective-permute-start | bytes 983048 | tf_op jit(solution)/shard_map/ppermute | solution.py:463
  47.1 9.1 %collective-permute-start.19 = (bf16[5,256,128]{2,1,0:T(8,128)(2,1)S(1)}, bf16[5,256,128]{2,1,0:T(8,128)(2,1)S(1)}, u32[]{:S(2)}, u32[]{:S(2)}) collective-permute-start(bf16[5,256,128]{2,1,0:T(8,128)(2,1)S(1)} %chunks_of.5.refs_6_), channel_id=1, source_target_pairs={{0,3},{1,0},{2,1},{3,2},{4,7},{5,4},{6,5},{7,6},{8,11},{9,8},{10,9... | collective-permute-start | bytes 983048 | tf_op jit(solution)/shard_map/ppermute | solution.py:463
  56.1 14.0 %collective-permute-start.21 = (bf16[3,256,128]{2,1,0:T(8,128)(2,1)S(1)}, bf16[3,256,128]{2,1,0:T(8,128)(2,1)S(1)}, u32[]{:S(2)}, u32[]{:S(2)}) collective-permute-start(bf16[3,256,128]{2,1,0:T(8,128)(2,1)S(1)} %slice.26), channel_id=1, source_target_pairs={{0,3},{1,0},{2,1},{3,2},{4,7},{5,4},{6,5},{7,6},{8,11},{9,8},{10,9... | collective-permute-start | bytes 589832 | tf_op jit(solution)/shard_map/ppermute | solution.py:463
  65.1 5.1 %collective-permute-start.20 = (bf16[2,256,128]{2,1,0:T(8,128)(2,1)S(1)}, bf16[2,256,128]{2,1,0:T(8,128)(2,1)S(1)}, u32[]{:S(2)}, u32[]{:S(2)}) collective-permute-start(bf16[2,256,128]{2,1,0:T(8,128)(2,1)S(1)} %slice.25), channel_id=1, source_target_pairs={{0,1},{1,2},{2,3},{3,0},{4,5},{5,6},{6,7},{7,4},{8,9},{9,10},{10,1... | collective-permute-start | bytes 393224 | tf_op jit(solution)/shard_map/ppermute | solution.py:463
  65.2 8.5 %collective-permute-start.16 = (bf16[5,256,128]{2,1,0:T(8,128)(2,1)S(1)}, bf16[5,256,128]{2,1,0:T(8,128)(2,1)S(1)}, u32[]{:S(2)}, u32[]{:S(2)}) collective-permute-start(bf16[5,256,128]{2,1,0:T(8,128)(2,1)S(1)} %slice.23), channel_id=1, source_target_pairs={{0,1},{1,2},{2,3},{3,0},{4,5},{5,6},{6,7},{7,4},{8,9},{9,10},{10,1... | collective-permute-start | bytes 983048 | tf_op jit(solution)/shard_map/ppermute | solution.py:463
  65.3 8.4 %collective-permute-start.17 = (bf16[5,256,128]{2,1,0:T(8,128)(2,1)S(1)}, bf16[5,256,128]{2,1,0:T(8,128)(2,1)S(1)}, u32[]{:S(2)}, u32[]{:S(2)}) collective-permute-start(bf16[5,256,128]{2,1,0:T(8,128)(2,1)S(1)} %slice.24), channel_id=1, source_target_pairs={{0,3},{1,0},{2,1},{3,2},{4,7},{5,4},{6,5},{7,6},{8,11},{9,8},{10,9... | collective-permute-start | bytes 983048 | tf_op jit(solution)/shard_map/ppermute | solution.py:463
  75.4 73.2 %all-to-all-start = ((f32[128,1,128]{2,1,0:T(1,128)}), f32[128,1,128]{2,1,0:T(1,128)S(1)}, u32[]{:S(2)}, u32[]{:S(2)}) async-start(f32[128,1,128]{2,1,0:T(1,128)} %bitcast.12), calls=%async_computation | async-start | bytes 131072 | tf_op jit(solution)/shard_map/all_to_all | solution.py:531
  (8 other events, 78.9 us)

commit v14 on v13

--- a/solution.py
+++ b/solution.py
@@ -370,24 +370,34 @@
         state[...] = entry[...]
         lax.fori_loop(int(first), blocks, exact_step, 0)
 
+        def settle(m_index, *sums):
+            old = state[m_index]
+            top = jnp.broadcast_to(jnp.max(old, axis=0, keepdims=True), old.shape)
+            for index in sums:
+                state[index] = state[index] * jnp.exp2(old - top)
+            state[m_index] = top
+
+        for p in range(PAIRS):
+            settle(p, TL + p, TC + p)
+        for s in range(STUDENTS):
+            settle(SM + s, SL + s)
+
     if not last:
         return
 
-    def merged(m8, l8):
-        top = jnp.max(m8, axis=0, keepdims=True)
-        factor = jnp.exp2(m8 - top)
-        total = jnp.sum(l8 * factor, axis=0, keepdims=True)
-        return factor, total, LN2 * top + jnp.log(total)
+    def merged(m_index, l_index):
+        total = jnp.sum(state[l_index], axis=0, keepdims=True)
+        return total, LN2 * state[m_index][:1] + jnp.log(total)
 
     lane = lax.broadcasted_iota(jnp.int32, (1, LANE), 1)
     line = jnp.zeros((1, LANE), jnp.float32)
     for s in range(STUDENTS):
-        _, _, s_lse = merged(state[SM + s], state[SL + s])
+        _, s_lse = merged(SM + s, SL + s)
         value = 2.0 * s_lse
         for c in range(2):
             p = 2 * s + c
-            factor, total, t_lse = merged(state[p], state[TL + p])
-            cross = jnp.sum(state[TC + p] * factor, axis=0, keepdims=True)
+            total, t_lse = merged(p, TL + p)
+            cross = jnp.sum(state[TC + p], axis=0, keepdims=True)
             value = value + (LN2 * cross / total - t_lse)
         out[s : s + 1, :] = value
         line = jnp.where(lane == s, jnp.sum(value, axis=1, keepdims=True), line)

time: 150 us -> 150 us (level)
  no operation moved by 1% of the time
where the time goes in v14:
time: 150 us; the launch traced here: 149 us
  starting transfers between devices  97.2 us (65%)
  waiting for transfers between devices  35 us (23%)
  Pallas kernels  10.7 us (7%)
  local copies, waits for them, and re-layouts  4.33 us (3%)
  between operations  1.5 us (1%)
    all_to_all x1, starting transfers between devices, program(): terms = lax.all_to_all(sums, everyone, 0, 0, tiled=True)  61.5 us
    ppermute x12, starting transfers between devices, program(): along_x = lambda a, by: lax.ppermute(a, 'kv_1', shift(4, by))  22 us
    ppermute x12, waiting for transfers between devices, program(): along_x = lambda a, by: lax.ppermute(a, 'kv_1', shift(4, by))  13.6 us
    ppermute x7, starting transfers between devices, program(): along_z = lambda a, by: lax.ppermute(a, ('head', 'kv_0'), z_shift(by))  13.2 us
    all_to_all x1, waiting for transfers between devices, program(): terms = lax.all_to_all(sums, everyone, 0, 0, tiled=True)  11.2 us
    ppermute x7, waiting for transfers between devices, program(): along_z = lambda a, by: lax.ppermute(a, ('head', 'kv_0'), z_shift(by))  10.2 us
    pallas_call x3, Pallas kernels, attend(): pl.pallas_call(functools.partial(attend_kernel, first, last, counts, bloc...  5.99 us
    unnamed x21, local copies, waits for them, and re-layouts  4.23 us
  transfers between devices with their start and end apart: 22, of which 12 were waited for; matrix products, arithmetic and copies ran while one was open for 1% of the time, Pallas kernels for 6%

profile of v14, /device:TPU:1, one launch (start us, length us, event | category | flops | bytes accessed | tf_op | source)
XLA Modules:
  0.0 149.4 jit_solution(10453113721133406587)
XLA Ops:
  2.5 2.5 %collective-permute-start.1 = (bf16[3,256,128]{2,1,0:T(8,128)(2,1)S(1)}, bf16[3,256,128]{2,1,0:T(8,128)(2,1)S(1)}, u32[]{:S(2)}, u32[]{:S(2)}) collective-permute-start(bf16[3,256,128]{2,1,0:T(8,128)(2,1)S(1)} %split_heads.1.refs_0_), channel_id=1, source_target_pairs={{0,16},{16,4},{4,20},{20,8},{8,24},{24,12},{12,28},{28,0},{1,17},{... | collective-permute-start | bytes 589832 | tf_op jit(solution)/shard_map/ppermute | solution.py:474
  5.1 4.0 %collective-permute-start.2 = (bf16[3,256,128]{2,1,0:T(8,128)(2,1)S(1)}, bf16[3,256,128]{2,1,0:T(8,128)(2,1)S(1)}, u32[]{:S(2)}, u32[]{:S(2)}) collective-permute-start(bf16[3,256,128]{2,1,0:T(8,128)(2,1)S(1)} %split_heads.1.refs_0_), channel_id=1, source_target_pairs={{0,28},{16,0},{4,16},{20,4},{8,20},{24,8},{12,24},{28,12},{1,29},{... | collective-permute-start | bytes 589832 | tf_op jit(solution)/shard_map/ppermute | solution.py:474
  9.2 1.2 copy-done
  11.0 1.7 %queries_for_other.1 = (bf16[4,256,128]{2,1,0:T(8,128)(2,1)S(1)}, bf16[5,256,128]{2,1,0:T(8,128)(2,1)S(1)}, bf16[5,256,128]{2,1,0:T(8,128)(2,1)S(1)}, s32[1,1]{1,0:T(1,128)}) custom-call(s32[1,3]{1,0:T(1,128)S(1)} %add_bitcast_fusion.place, s32[2,14]{1,0:T(2,128)S(1)} %bitcast.21, bf16[256,1792]{1,0:T(8,128)(2,1)S(1)} %bitcast.15), custom_call_target="tpu_custom_call" | custom-call | tf_op jit(solution)/shard_map/queries_for_other/pallas_call | solution.py:108
  14.2 2.6 %collective-permute-start.10 = (bf16[5,256,128]{2,1,0:T(8,128)(2,1)S(1)}, bf16[5,256,128]{2,1,0:T(8,128)(2,1)S(1)}, u32[]{:S(2)}, u32[]{:S(2)}) collective-permute-start(bf16[5,256,128]{2,1,0:T(8,128)(2,1)S(1)} %chunks_of.4.refs_0_), channel_id=1, source_target_pairs={{0,3},{1,0},{2,1},{3,2},{4,7},{5,4},{6,5},{7,6},{8,11},{9,8},{10,9... | collective-permute-start | bytes 983048 | tf_op jit(solution)/shard_map/ppermute | solution.py:473
  16.8 2.7 %collective-permute-start.5 = (bf16[3,256,128]{2,1,0:T(8,128)(2,1)S(1)}, bf16[3,256,128]{2,1,0:T(8,128)(2,1)S(1)}, u32[]{:S(2)}, u32[]{:S(2)}) collective-permute-start(bf16[3,256,128]{2,1,0:T(8,128)(2,1)S(1)} %collective-permute-done.2.refs_5_.refs_1_), channel_id=1, source_target_pairs={{0,28},{16,0},{4,16},{20,4},{8,20},{24,8},{12,24},{28,12},{1,29},{... | collective-permute-start | bytes 589832 | tf_op jit(solution)/shard_map/ppermute | solution.py:474
  20.0 1.2 collective-permute-start.9
  22.0 3.1 %collective-permute-start.6 = (bf16[3,256,128]{2,1,0:T(8,128)(2,1)S(1)}, bf16[3,256,128]{2,1,0:T(8,128)(2,1)S(1)}, u32[]{:S(2)}, u32[]{:S(2)}) collective-permute-start(bf16[3,256,128]{2,1,0:T(8,128)(2,1)S(1)} %collective-permute-done.5.refs_3_), channel_id=1, source_target_pairs={{0,28},{16,0},{4,16},{20,4},{8,20},{24,8},{12,24},{28,12},{1,29},{... | collective-permute-start | bytes 589832 | tf_op jit(solution)/shard_map/ppermute | solution.py:474
  26.7 4.9 %collective-permute-done.6.refs_4_.refs_2_ = bf16[3,256,128]{2,1,0:T(8,128)(2,1)S(1)} collective-permute-done((bf16[3,256,128]{2,1,0:T(8,128)(2,1)S(1)}, bf16[3,256,128]{2,1,0:T(8,128)(2,1)S(1)}, u32[]{:S(2)}, u32[]{:S(2)}) %collective-permute-start.6) | collective-permute-done | bytes 196640 | tf_op jit(solution)/shard_map/ppermute | solution.py:474
  33.7 2.1 %collective-permute-start.8 = (bf16[10,256,128]{2,1,0:T(8,128)(2,1)S(1)}, bf16[10,256,128]{2,1,0:T(8,128)(2,1)S(1)}, u32[]{:S(2)}, u32[]{:S(2)}) collective-permute-start(bf16[10,256,128]{2,1,0:T(8,128)(2,1)S(1)} %chunks_of.3.refs_5_), channel_id=1, source_target_pairs={{0,3},{1,0},{2,1},{3,2},{4,7},{5,4},{6,5},{7,6},{8,11},{9,8},{10,9... | collective-permute-start | bytes 1966088 | tf_op jit(solution)/shard_map/ppermute | solution.py:473
  35.8 3.5 %collective-permute-done.13.refs_0_ = bf16[3,256,128]{2,1,0:T(8,128)(2,1)S(1)} collective-permute-done((bf16[3,256,128]{2,1,0:T(8,128)(2,1)S(1)}, bf16[3,256,128]{2,1,0:T(8,128)(2,1)S(1)}, u32[]{:S(2)}, u32[]{:S(2)}) %collective-permute-start.13) | collective-permute-done | bytes 196640 | tf_op jit(solution)/shard_map/ppermute | solution.py:474
  39.3 1.2 collective-permute-start.11
  42.3 1.3 collective-permute-start.18
  43.6 3.5 %collective-permute-done.11.refs_3_ = bf16[2,256,128]{2,1,0:T(8,128)(2,1)S(1)} collective-permute-done((bf16[2,256,128]{2,1,0:T(8,128)(2,1)S(1)}, bf16[2,256,128]{2,1,0:T(8,128)(2,1)S(1)}, u32[]{:S(2)}, u32[]{:S(2)}) %collective-permute-start.11) | collective-permute-done | bytes 131104 | tf_op jit(solution)/shard_map/ppermute | solution.py:473
  47.3 3.2 %attend.3 = (f32[56,8,256]{2,1,0:T(8,128)S(1)}, bf16[21,256,256]{2,1,0:T(8,128)(2,1)S(1)}) custom-call(s32[1,3]{1,0:T(1,128)S(1)} %add_bitcast_fusion.place, s32[2,14]{1,0:T(2,128)S(1)} %bitcast.23, s32[2,7]{1,0:T(2,128)S(1)} %copy-done.9, bf16[5,256,128]{2,1,0:T(8,128)(2,1)S(1)} %chunks_of.4.refs_0_, ...), custom_call_target="tpu_custom_call", output_to_operand_aliasing={{1}: (13, {})} | custom-call | flops 4932501504 | bytes 2293760 | tf_op jit(solution)/shard_map/attend/pallas_call | solution.py:434
  50.6 3.5 %collective-permute-done.18.refs_2_ = bf16[5,256,128]{2,1,0:T(8,128)(2,1)S(1)} collective-permute-done((bf16[5,256,128]{2,1,0:T(8,128)(2,1)S(1)}, bf16[5,256,128]{2,1,0:T(8,128)(2,1)S(1)}, u32[]{:S(2)}, u32[]{:S(2)}) %collective-permute-start.18) | collective-permute-done | bytes 327712 | tf_op jit(solution)/shard_map/ppermute | solution.py:473
  54.1 2.0 %collective-permute-done.19.refs_3_ = bf16[5,256,128]{2,1,0:T(8,128)(2,1)S(1)} collective-permute-done((bf16[5,256,128]{2,1,0:T(8,128)(2,1)S(1)}, bf16[5,256,128]{2,1,0:T(8,128)(2,1)S(1)}, u32[]{:S(2)}, u32[]{:S(2)}) %collective-permute-start.19) | collective-permute-done | bytes 327712 | tf_op jit(solution)/shard_map/ppermute | solution.py:473
  56.1 9.0 %collective-permute-start.21 = (bf16[3,256,128]{2,1,0:T(8,128)(2,1)S(1)}, bf16[3,256,128]{2,1,0:T(8,128)(2,1)S(1)}, u32[]{:S(2)}, u32[]{:S(2)}) collective-permute-start(bf16[3,256,128]{2,1,0:T(8,128)(2,1)S(1)} %slice.26), channel_id=1, source_target_pairs={{0,3},{1,0},{2,1},{3,2},{4,7},{5,4},{6,5},{7,6},{8,11},{9,8},{10,9... | collective-permute-start | bytes 589832 | tf_op jit(solution)/shard_map/ppermute | solution.py:473
  65.4 2.7 %collective-permute-start.17 = (bf16[5,256,128]{2,1,0:T(8,128)(2,1)S(1)}, bf16[5,256,128]{2,1,0:T(8,128)(2,1)S(1)}, u32[]{:S(2)}, u32[]{:S(2)}) collective-permute-start(bf16[5,256,128]{2,1,0:T(8,128)(2,1)S(1)} %slice.24), channel_id=1, source_target_pairs={{0,3},{1,0},{2,1},{3,2},{4,7},{5,4},{6,5},{7,6},{8,11},{9,8},{10,9... | collective-permute-start | bytes 983048 | tf_op jit(solution)/shard_map/ppermute | solution.py:473
  68.1 1.1 attend.4.refs_5_
  70.2 3.5 %collective-permute-done.16.refs_0_ = bf16[5,256,128]{2,1,0:T(8,128)(2,1)S(1)} collective-permute-done((bf16[5,256,128]{2,1,0:T(8,128)(2,1)S(1)}, bf16[5,256,128]{2,1,0:T(8,128)(2,1)S(1)}, u32[]{:S(2)}, u32[]{:S(2)}) %collective-permute-start.16) | collective-permute-done | bytes 327712 | tf_op jit(solution)/shard_map/ppermute | solution.py:473
  73.8 1.7 %attend.5 = (f32[7,256]{1,0:T(8,128)S(1)}, f32[128,128]{1,0:T(8,128)}) custom-call(s32[1,3]{1,0:T(1,128)S(1)} %add_bitcast_fusion.place, s32[2,14]{1,0:T(2,128)S(1)} %bitcast.25, s32[2,3]{1,0:T(2,128)S(1)} %copy-done.7, bf16[5,256,128]{2,1,0:T(8,128)(2,1)S(1)} %collective-permute-done.16.refs_0_, bf16[5,256,128]{2,1,0:T(8,128)(2,1)S(1)} %collective-permute-done.17.refs_1_, ...), custom_call_target="tpu_custom_call" | custom-call | flops 2113929216 | bytes 983040 | tf_op jit(solution)/shard_map/attend/pallas_call | solution.py:434
  75.4 61.5 %all-to-all-start = ((f32[128,1,128]{2,1,0:T(1,128)}), f32[128,1,128]{2,1,0:T(1,128)S(1)}, u32[]{:S(2)}, u32[]{:S(2)}) async-start(f32[128,1,128]{2,1,0:T(1,128)} %bitcast.12), calls=%async_computation | async-start | bytes 131072 | tf_op jit(solution)/shard_map/all_to_all | solution.py:541
  137.5 11.2 %all-to-all-done = f32[128,1,128]{2,1,0:T(1,128)S(1)} async-done(((f32[128,1,128]{2,1,0:T(1,128)}), f32[128,1,128]{2,1,0:T(1,128)S(1)}, u32[]{:S(2)}, u32[]{:S(2)}) %all-to-all-start) | async-done | bytes 65568 | tf_op jit(solution)/shard_map/all_to_all | solution.py:541
  (60 shorter events, 13.0 us)
Async XLA Ops:
  0.6 39.9 %copy-start.6 = (s32[14,2]{0,1:T(2,128)S(1)}, s32[14,2]{0,1:T(2,128)}, u32[]{:S(2)}) copy-start(s32[14,2]{0,1:T(2,128)} %param.14) | copy-start | bytes 340
  2.5 11.1 %collective-permute-start.1 = (bf16[3,256,128]{2,1,0:T(8,128)(2,1)S(1)}, bf16[3,256,128]{2,1,0:T(8,128)(2,1)S(1)}, u32[]{:S(2)}, u32[]{:S(2)}) collective-permute-start(bf16[3,256,128]{2,1,0:T(8,128)(2,1)S(1)} %split_heads.1.refs_0_), channel_id=1, source_target_pairs={{0,16},{16,4},{4,20},{20,8},{8,24},{24,12},{12,28},{28,0},{1,17},{... | collective-permute-start | bytes 589832 | tf_op jit(solution)/shard_map/ppermute | solution.py:474
  5.1 8.5 %collective-permute-start.2 = (bf16[3,256,128]{2,1,0:T(8,128)(2,1)S(1)}, bf16[3,256,128]{2,1,0:T(8,128)(2,1)S(1)}, u32[]{:S(2)}, u32[]{:S(2)}) collective-permute-start(bf16[3,256,128]{2,1,0:T(8,128)(2,1)S(1)} %split_heads.1.refs_0_), channel_id=1, source_target_pairs={{0,28},{16,0},{4,16},{20,4},{8,20},{24,8},{12,24},{28,12},{1,29},{... | collective-permute-start | bytes 589832 | tf_op jit(solution)/shard_map/ppermute | solution.py:474
  11.0 29.5 %copy-start.2 = (bf16[1,256,896]{2,1,0:T(8,128)(2,1)S(1)}, bf16[1,256,896]{2,1,0:T(8,128)(2,1)}, u32[]{:S(2)}) copy-start(bf16[1,256,896]{2,1,0:T(8,128)(2,1)} %param.12) | copy-start | bytes 1376260
  13.6 6.4 %collective-permute-start.3 = (bf16[3,256,128]{2,1,0:T(8,128)(2,1)S(1)}, bf16[3,256,128]{2,1,0:T(8,128)(2,1)S(1)}, u32[]{:S(2)}, u32[]{:S(2)}) collective-permute-start(bf16[3,256,128]{2,1,0:T(8,128)(2,1)S(1)} %collective-permute-done.1.refs_1_.refs_2_), channel_id=1, source_target_pairs={{0,16},{16,4},{4,20},{20,8},{8,24},{24,12},{12,28},{28,0},{1,17},{... | collective-permute-start | bytes 589832 | tf_op jit(solution)/shard_map/ppermute | solution.py:474
  14.2 11.0 %collective-permute-start.10 = (bf16[5,256,128]{2,1,0:T(8,128)(2,1)S(1)}, bf16[5,256,128]{2,1,0:T(8,128)(2,1)S(1)}, u32[]{:S(2)}, u32[]{:S(2)}) collective-permute-start(bf16[5,256,128]{2,1,0:T(8,128)(2,1)S(1)} %chunks_of.4.refs_0_), channel_id=1, source_target_pairs={{0,3},{1,0},{2,1},{3,2},{4,7},{5,4},{6,5},{7,6},{8,11},{9,8},{10,9... | collective-permute-start | bytes 983048 | tf_op jit(solution)/shard_map/ppermute | solution.py:473
  16.8 5.3 %collective-permute-start.5 = (bf16[3,256,128]{2,1,0:T(8,128)(2,1)S(1)}, bf16[3,256,128]{2,1,0:T(8,128)(2,1)S(1)}, u32[]{:S(2)}, u32[]{:S(2)}) collective-permute-start(bf16[3,256,128]{2,1,0:T(8,128)(2,1)S(1)} %collective-permute-done.2.refs_5_.refs_1_), channel_id=1, source_target_pairs={{0,28},{16,0},{4,16},{20,4},{8,20},{24,8},{12,24},{28,12},{1,29},{... | collective-permute-start | bytes 589832 | tf_op jit(solution)/shard_map/ppermute | solution.py:474
  20.0 5.7 %collective-permute-start.4 = (bf16[3,256,128]{2,1,0:T(8,128)(2,1)S(1)}, bf16[3,256,128]{2,1,0:T(8,128)(2,1)S(1)}, u32[]{:S(2)}, u32[]{:S(2)}) collective-permute-start(bf16[3,256,128]{2,1,0:T(8,128)(2,1)S(1)} %collective-permute-done.3.refs_0_), channel_id=1, source_target_pairs={{0,16},{16,4},{4,20},{20,8},{8,24},{24,12},{12,28},{28,0},{1,17},{... | collective-permute-start | bytes 589832 | tf_op jit(solution)/shard_map/ppermute | solution.py:474
  20.0 13.7 %collective-permute-start.9 = (bf16[5,256,128]{2,1,0:T(8,128)(2,1)S(1)}, bf16[5,256,128]{2,1,0:T(8,128)(2,1)S(1)}, u32[]{:S(2)}, u32[]{:S(2)}) collective-permute-start(bf16[5,256,128]{2,1,0:T(8,128)(2,1)S(1)} %chunks_of.4.refs_0_), channel_id=1, source_target_pairs={{0,1},{1,2},{2,3},{3,0},{4,5},{5,6},{6,7},{7,4},{8,9},{9,10},{10,1... | collective-permute-start | bytes 983048 | tf_op jit(solution)/shard_map/ppermute | solution.py:473
  21.3 11.8 %collective-permute-start.14 = (bf16[4,256,128]{2,1,0:T(8,128)(2,1)S(1)}, bf16[4,256,128]{2,1,0:T(8,128)(2,1)S(1)}, u32[]{:S(2)}, u32[]{:S(2)}) collective-permute-start(bf16[4,256,128]{2,1,0:T(8,128)(2,1)S(1)} %get-tuple-element.28), channel_id=1, source_target_pairs={{0,16},{16,0},{1,17},{17,1},{2,18},{18,2},{3,19},{19,3},{4,20},{20... | collective-permute-start | bytes 786440 | tf_op jit(solution)/shard_map/ppermute | solution.py:481
  22.0 9.5 %collective-permute-start.6 = (bf16[3,256,128]{2,1,0:T(8,128)(2,1)S(1)}, bf16[3,256,128]{2,1,0:T(8,128)(2,1)S(1)}, u32[]{:S(2)}, u32[]{:S(2)}) collective-permute-start(bf16[3,256,128]{2,1,0:T(8,128)(2,1)S(1)} %collective-permute-done.5.refs_3_), channel_id=1, source_target_pairs={{0,28},{16,0},{4,16},{20,4},{8,20},{24,8},{12,24},{28,12},{1,29},{... | collective-permute-start | bytes 589832 | tf_op jit(solution)/shard_map/ppermute | solution.py:474
  25.2 17.1 %collective-permute-start.15 = (bf16[5,256,128]{2,1,0:T(8,128)(2,1)S(1)}, bf16[5,256,128]{2,1,0:T(8,128)(2,1)S(1)}, u32[]{:S(2)}, u32[]{:S(2)}) collective-permute-start(bf16[5,256,128]{2,1,0:T(8,128)(2,1)S(1)} %get-tuple-element.29), channel_id=1, source_target_pairs={{0,16},{16,0},{1,17},{17,1},{2,18},{18,2},{3,19},{19,3},{4,20},{20... | collective-permute-start | bytes 983048 | tf_op jit(solution)/shard_map/ppermute | solution.py:481
  25.8 13.6 %collective-permute-start.13 = (bf16[3,256,128]{2,1,0:T(8,128)(2,1)S(1)}, bf16[3,256,128]{2,1,0:T(8,128)(2,1)S(1)}, u32[]{:S(2)}, u32[]{:S(2)}) collective-permute-start(bf16[3,256,128]{2,1,0:T(8,128)(2,1)S(1)} %collective-permute-done.4.refs_2_.refs_1_), channel_id=1, source_target_pairs={{0,16},{16,4},{4,20},{20,8},{8,24},{24,12},{12,28},{28,0},{1,17},{... | collective-permute-start | bytes 589832 | tf_op jit(solution)/shard_map/ppermute | solution.py:474
  31.6 15.8 %collective-permute-start.12 = (bf16[3,256,128]{2,1,0:T(8,128)(2,1)S(1)}, bf16[3,256,128]{2,1,0:T(8,128)(2,1)S(1)}, u32[]{:S(2)}, u32[]{:S(2)}) collective-permute-start(bf16[3,256,128]{2,1,0:T(8,128)(2,1)S(1)} %slice.29), channel_id=1, source_target_pairs={{0,3},{1,0},{2,1},{3,2},{4,7},{5,4},{6,5},{7,6},{8,11},{9,8},{10,9... | collective-permute-start | bytes 589832 | tf_op jit(solution)/shard_map/ppermute | solution.py:473
  33.0 17.5 %collective-permute-start.7 = (bf16[10,256,128]{2,1,0:T(8,128)(2,1)S(1)}, bf16[10,256,128]{2,1,0:T(8,128)(2,1)S(1)}, u32[]{:S(2)}, u32[]{:S(2)}) collective-permute-start(bf16[10,256,128]{2,1,0:T(8,128)(2,1)S(1)} %chunks_of.3.refs_5_), channel_id=1, source_target_pairs={{0,1},{1,2},{2,3},{3,0},{4,5},{5,6},{6,7},{7,4},{8,9},{9,10},{10,1... | collective-permute-start | bytes 1966088 | tf_op jit(solution)/shard_map/ppermute | solution.py:473
  33.7 16.8 %collective-permute-start.8 = (bf16[10,256,128]{2,1,0:T(8,128)(2,1)S(1)}, bf16[10,256,128]{2,1,0:T(8,128)(2,1)S(1)}, u32[]{:S(2)}, u32[]{:S(2)}) collective-permute-start(bf16[10,256,128]{2,1,0:T(8,128)(2,1)S(1)} %chunks_of.3.refs_5_), channel_id=1, source_target_pairs={{0,3},{1,0},{2,1},{3,2},{4,7},{5,4},{6,5},{7,6},{8,11},{9,8},{10,9... | collective-permute-start | bytes 1966088 | tf_op jit(solution)/shard_map/ppermute | solution.py:473
  39.3 7.7 %collective-permute-start.11 = (bf16[2,256,128]{2,1,0:T(8,128)(2,1)S(1)}, bf16[2,256,128]{2,1,0:T(8,128)(2,1)S(1)}, u32[]{:S(2)}, u32[]{:S(2)}) collective-permute-start(bf16[2,256,128]{2,1,0:T(8,128)(2,1)S(1)} %slice.28), channel_id=1, source_target_pairs={{0,1},{1,2},{2,3},{3,0},{4,5},{5,6},{6,7},{7,4},{8,9},{9,10},{10,1... | collective-permute-start | bytes 393224 | tf_op jit(solution)/shard_map/ppermute | solution.py:473
  42.3 11.8 %collective-permute-start.18 = (bf16[5,256,128]{2,1,0:T(8,128)(2,1)S(1)}, bf16[5,256,128]{2,1,0:T(8,128)(2,1)S(1)}, u32[]{:S(2)}, u32[]{:S(2)}) collective-permute-start(bf16[5,256,128]{2,1,0:T(8,128)(2,1)S(1)} %chunks_of.5.refs_6_), channel_id=1, source_target_pairs={{0,1},{1,2},{2,3},{3,0},{4,5},{5,6},{6,7},{7,4},{8,9},{9,10},{10,1... | collective-permute-start | bytes 983048 | tf_op jit(solution)/shard_map/ppermute | solution.py:473
  47.1 9.1 %collective-permute-start.19 = (bf16[5,256,128]{2,1,0:T(8,128)(2,1)S(1)}, bf16[5,256,128]{2,1,0:T(8,128)(2,1)S(1)}, u32[]{:S(2)}, u32[]{:S(2)}) collective-permute-start(bf16[5,256,128]{2,1,0:T(8,128)(2,1)S(1)} %chunks_of.5.refs_6_), channel_id=1, source_target_pairs={{0,3},{1,0},{2,1},{3,2},{4,7},{5,4},{6,5},{7,6},{8,11},{9,8},{10,9... | collective-permute-start | bytes 983048 | tf_op jit(solution)/shard_map/ppermute | solution.py:473
  56.1 14.1 %collective-permute-start.21 = (bf16[3,256,128]{2,1,0:T(8,128)(2,1)S(1)}, bf16[3,256,128]{2,1,0:T(8,128)(2,1)S(1)}, u32[]{:S(2)}, u32[]{:S(2)}) collective-permute-start(bf16[3,256,128]{2,1,0:T(8,128)(2,1)S(1)} %slice.26), channel_id=1, source_target_pairs={{0,3},{1,0},{2,1},{3,2},{4,7},{5,4},{6,5},{7,6},{8,11},{9,8},{10,9... | collective-permute-start | bytes 589832 | tf_op jit(solution)/shard_map/ppermute | solution.py:473
  65.1 5.1 %collective-permute-start.20 = (bf16[2,256,128]{2,1,0:T(8,128)(2,1)S(1)}, bf16[2,256,128]{2,1,0:T(8,128)(2,1)S(1)}, u32[]{:S(2)}, u32[]{:S(2)}) collective-permute-start(bf16[2,256,128]{2,1,0:T(8,128)(2,1)S(1)} %slice.25), channel_id=1, source_target_pairs={{0,1},{1,2},{2,3},{3,0},{4,5},{5,6},{6,7},{7,4},{8,9},{9,10},{10,1... | collective-permute-start | bytes 393224 | tf_op jit(solution)/shard_map/ppermute | solution.py:473
  65.3 8.5 %collective-permute-start.16 = (bf16[5,256,128]{2,1,0:T(8,128)(2,1)S(1)}, bf16[5,256,128]{2,1,0:T(8,128)(2,1)S(1)}, u32[]{:S(2)}, u32[]{:S(2)}) collective-permute-start(bf16[5,256,128]{2,1,0:T(8,128)(2,1)S(1)} %slice.23), channel_id=1, source_target_pairs={{0,1},{1,2},{2,3},{3,0},{4,5},{5,6},{6,7},{7,4},{8,9},{9,10},{10,1... | collective-permute-start | bytes 983048 | tf_op jit(solution)/shard_map/ppermute | solution.py:473
  65.4 8.4 %collective-permute-start.17 = (bf16[5,256,128]{2,1,0:T(8,128)(2,1)S(1)}, bf16[5,256,128]{2,1,0:T(8,128)(2,1)S(1)}, u32[]{:S(2)}, u32[]{:S(2)}) collective-permute-start(bf16[5,256,128]{2,1,0:T(8,128)(2,1)S(1)} %slice.24), channel_id=1, source_target_pairs={{0,3},{1,0},{2,1},{3,2},{4,7},{5,4},{6,5},{7,6},{8,11},{9,8},{10,9... | collective-permute-start | bytes 983048 | tf_op jit(solution)/shard_map/ppermute | solution.py:473
  75.4 73.3 %all-to-all-start = ((f32[128,1,128]{2,1,0:T(1,128)}), f32[128,1,128]{2,1,0:T(1,128)S(1)}, u32[]{:S(2)}, u32[]{:S(2)}) async-start(f32[128,1,128]{2,1,0:T(1,128)} %bitcast.12), calls=%async_computation | async-start | bytes 131072 | tf_op jit(solution)/shard_map/all_to_all | solution.py:541
  (8 other events, 78.9 us)
